TPU v7x, 32 devices: a whole 2x2x4 slice. The times are simulated.
32 devices in a mesh: rows: 4 (over x, core), heads: 8 (over z, y).
Axes of the slice: x: 2, y: 2, z: 4, core: 2. Of those that a mesh axis runs over, the one named last changes fastest.
Arguments:
- hidden_in: bfloat16 [16, 2048, 1024], P('rows', 'heads'), may hold values from -6 to 6
- doc_ids: int32 [16, 2048], P('rows'), may hold values from 0 to 8, as said below
- cotangent: bfloat16 [16, 2048, 1024], P('rows', 'heads'), may hold values from -6 to 6
- attn_gain: float32 [1024], replicated, may hold values from 0.1 to 1.9
- query_weight: bfloat16 [1024, 1024], replicated, may hold values from -0.1875 to 0.1875
- latent_weight: bfloat16 [1024, 512], replicated, may hold values from -0.1875 to 0.1875
- key_lift_weight: bfloat16 [2, 256, 512], replicated, may hold values from -0.375 to 0.375
- value_lift_weight: bfloat16 [2, 256, 512], replicated, may hold values from -0.375 to 0.375
- output_weight: bfloat16 [1024, 1024], replicated, may hold values from -1.5 to 1.5
- ffn_gain: float32 [1024], replicated, may hold values from 0.1 to 1.9
- gate_weight: bfloat16 [1024, 2816], replicated, may hold values from -0.1875 to 0.1875
- up_weight: bfloat16 [1024, 2816], replicated, may hold values from -0.1875 to 0.1875
- down_weight: bfloat16 [2816, 1024], replicated, may hold values from -0.109375 to 0.109375
Outputs:
- hidden_out: bfloat16 [16, 2048, 1024], P('rows', 'heads')
- hidden_grad: float32 [16, 2048, 1024], P('rows', 'heads')
- attn_gain_grad: float32 [1024], P('heads')
- query_grad: float32 [1024, 1024], P('heads')
- latent_grad: float32 [1024, 512], P('heads')
- key_up_grad: float32 [2, 256, 512], P(None, 'heads')
- value_up_grad: float32 [2, 256, 512], P(None, 'heads')
- output_grad: float32 [1024, 1024], P('heads')
- ffn_gain_grad: float32 [1024], P('heads')
- gate_grad: float32 [1024, 2816], P(None, 'heads')
- up_grad: float32 [1024, 2816], P(None, 'heads')
- down_grad: float32 [2816, 1024], P('heads')
Inputs may be any that keep to these rules, and one draw needn't show every extreme that they name: `doc_ids`: in each row, ids start at 1 and rise by one at each document boundary along the row; 0 marks padding, which, where a row has any, fills its tail. A row holds at most 8 documents.
All inputs are finite; a program needn't handle non-finite values.
Results may differ from a plain program's by a relative error of at most 0.02.
Values may be sent and summed in bfloat16 or wider, within the bound.
A program may use at most 192 MiB of HBM per device.

v0:
```python
import functools

import jax
import jax.numpy as jnp
from jax import lax
from jax.sharding import PartitionSpec as P

QUERY_HEADS = 16
HEAD_WIDTH = 64


epsilon = 1e-05
blocked = -1e30


def as_sent(x):
    return jax.tree.map(lambda a: a.astype(jnp.bfloat16) if a.dtype == jnp.float32 else a, x)


def matmul(left, right):
    return jnp.dot(left, right, preferred_element_type=jnp.float32)


def matmul_back(left, right):
    return lax.dot_general(
        left, right, (((left.ndim - 1,), (1,)), ((), ())), preferred_element_type=jnp.float32
    )


def rms_inverse(value_matrix):
    return lax.rsqrt(jnp.mean(value_matrix * value_matrix, axis=-1, keepdims=True) + epsilon)


def norm_back(grad_normed, unit, inverse, gain):
    scaled = grad_normed * gain
    grad_in = inverse * (scaled - unit * jnp.mean(scaled * unit, axis=-1, keepdims=True))
    return (grad_in, jnp.sum(grad_normed * unit, axis=(0, 1)))


def tile_allow(doc, query_start, key_start, block):
    query_doc = doc[query_start : query_start + block]
    key_doc = doc[key_start : key_start + block]
    query_pos = query_start + jnp.arange(block)
    key_pos = key_start + jnp.arange(block)
    return (query_doc[:, None] == key_doc[None, :]) & (key_pos[None, :] <= query_pos[:, None])


def tile_scores(query_tile, key_tile, allow):
    scale = query_tile.shape[-1] ** (-0.5)
    raw = (
        jnp.einsum("qhd,khd->hqk", query_tile, key_tile, preferred_element_type=jnp.float32) * scale
    )
    return jnp.where(allow[None], raw, blocked)


def keep_state(state):
    return state


def attend_row(items):
    queries, key_matrix, value_matrix, doc = items
    token_length, heads, head_dim = queries.shape
    block = min(512, token_length)
    out_tiles = []
    lse_tiles = []
    for query_block in range(token_length // block):
        query_start = query_block * block
        query_tile = queries[query_start : query_start + block]
        touched = [
            jnp.any(tile_allow(doc, query_start, key_block * block, block))
            for key_block in range(query_block)
        ]

        def extend(key_block, state):
            top, total = state
            key_start = key_block * block
            allow = tile_allow(doc, query_start, key_start, block)
            masked = tile_scores(query_tile, key_matrix[key_start : key_start + block], allow)
            new_top = jnp.maximum(top, jnp.max(masked, axis=-1))
            weights = jnp.where(allow[None], jnp.exp(masked - new_top[..., None]), 0.0)
            return (new_top, total * jnp.exp(top - new_top) + jnp.sum(weights, axis=-1))

        state = extend(
            query_block,
            (
                jnp.full((heads, block), blocked, jnp.float32),
                jnp.zeros((heads, block), jnp.float32),
            ),
        )
        for key_block in range(query_block):
            state = lax.cond(
                touched[key_block], functools.partial(extend, key_block), keep_state, state
            )
        lse = state[0] + jnp.log(state[1])

        def collect(key_block, total):
            key_start = key_block * block
            allow = tile_allow(doc, query_start, key_start, block)
            masked = tile_scores(query_tile, key_matrix[key_start : key_start + block], allow)
            probs = jnp.where(allow[None], jnp.exp(masked - lse[..., None]), 0.0).astype(
                jnp.bfloat16
            )
            return total + jnp.einsum(
                "hqk,khd->qhd",
                probs,
                value_matrix[key_start : key_start + block],
                preferred_element_type=jnp.float32,
            )

        total = collect(query_block, jnp.zeros((block, heads, head_dim), jnp.float32))
        for key_block in range(query_block):
            total = lax.cond(
                touched[key_block], functools.partial(collect, key_block), keep_state, total
            )
        out_tiles.append(total)
        lse_tiles.append(lse)
    return (jnp.concatenate(out_tiles, axis=0), jnp.concatenate(lse_tiles, axis=1))


def attend_back(items):
    queries, key_matrix, value_matrix, outputs, lse, grad_out, doc = items
    token_length, heads, head_dim = queries.shape
    block = min(512, token_length)
    scale = head_dim ** (-0.5)
    delta = jnp.sum(grad_out.astype(jnp.float32) * outputs, axis=-1).T
    query_tiles = []
    key_grads = jnp.zeros((token_length, heads, head_dim), jnp.float32)
    value_grads = jnp.zeros((token_length, heads, head_dim), jnp.float32)
    for query_block in range(token_length // block):
        query_start = query_block * block
        query_tile = queries[query_start : query_start + block]
        grad_tile = grad_out[query_start : query_start + block]
        lse_tile = lse[:, query_start : query_start + block]
        delta_tile = delta[:, query_start : query_start + block]

        def tile_grads(key_block):
            key_start = key_block * block
            key_tile = key_matrix[key_start : key_start + block]
            value_tile = value_matrix[key_start : key_start + block]
            allow = tile_allow(doc, query_start, key_start, block)
            masked = tile_scores(query_tile, key_tile, allow)
            probs = jnp.where(allow[None], jnp.exp(masked - lse_tile[..., None]), 0.0)
            grad_probs = jnp.einsum(
                "qhd,khd->hqk", grad_tile, value_tile, preferred_element_type=jnp.float32
            )
            grad_scores = (probs * (grad_probs - delta_tile[..., None])).astype(jnp.bfloat16)
            return (
                jnp.einsum(
                    "hqk,khd->qhd", grad_scores, key_tile, preferred_element_type=jnp.float32
                ),
                jnp.einsum(
                    "hqk,qhd->khd", grad_scores, query_tile, preferred_element_type=jnp.float32
                ),
                jnp.einsum(
                    "hqk,qhd->khd",
                    probs.astype(jnp.bfloat16),
                    grad_tile,
                    preferred_element_type=jnp.float32,
                ),
            )

        def no_grads(key_block):
            empty = jnp.zeros((block, heads, head_dim), jnp.float32)
            return (empty, empty, empty)

        query_total = jnp.zeros((block, heads, head_dim), jnp.float32)
        for key_block in range(query_block + 1):
            key_start = key_block * block
            if key_block == query_block:
                parts = tile_grads(key_block)
            else:
                touched = jnp.any(tile_allow(doc, query_start, key_start, block))
                parts = lax.cond(
                    touched,
                    functools.partial(tile_grads, key_block),
                    functools.partial(no_grads, key_block),
                )
            query_total = query_total + parts[0]
            key_grads = key_grads.at[key_start : key_start + block].add(parts[1])
            value_grads = value_grads.at[key_start : key_start + block].add(parts[2])
        query_tiles.append(query_total)
    query_grads = jnp.concatenate(query_tiles, axis=0) * scale
    return (
        query_grads.astype(jnp.bfloat16),
        (key_grads * scale).astype(jnp.bfloat16),
        value_grads.astype(jnp.bfloat16),
    )


def shards(
    hidden_in,
    doc_ids,
    cotangent,
    attn_gain,
    query_weight,
    latent_weight,
    key_lift_weight,
    value_lift_weight,
    output_weight,
    ffn_gain,
    gate_weight,
    up_weight,
    down_weight,
):
    rows, tokens, width = hidden_in.shape
    peers = lax.axis_size("heads")
    place = lax.axis_index("heads")
    token_length = tokens * peers
    groups, latent_size, group_width = key_lift_weight.shape
    local_heads = QUERY_HEADS // peers
    local_width = local_heads * HEAD_WIDTH
    group_heads = QUERY_HEADS // groups
    peers_group = peers // groups
    own_group = place * local_heads // group_heads
    column_start = place * local_heads % group_heads * HEAD_WIDTH
    key_mine = lax.dynamic_slice_in_dim(
        lax.dynamic_index_in_dim(key_lift_weight, own_group, 0, keepdims=False),
        column_start,
        local_width,
        1,
    )
    value_mine = lax.dynamic_slice_in_dim(
        lax.dynamic_index_in_dim(value_lift_weight, own_group, 0, keepdims=False),
        column_start,
        local_width,
        1,
    )
    own_docs = lax.dynamic_slice_in_dim(doc_ids, place * tokens, tokens, 1)
    inputs = hidden_in.astype(jnp.float32)
    inverse_one = rms_inverse(inputs)
    unit_one = inputs * inverse_one
    normed_one = (unit_one * attn_gain).astype(jnp.bfloat16)
    queries = matmul(normed_one, query_weight).astype(jnp.bfloat16)
    latent_rows = (
        matmul(normed_one, latent_weight)
        .astype(jnp.bfloat16)
        .reshape(rows, tokens, groups, latent_size)
    )
    query_sent = queries.reshape(rows, tokens, peers, local_width)
    copies = jnp.broadcast_to(
        latent_rows[:, :, :, None, :], (rows, tokens, groups, peers_group, latent_size)
    ).reshape(rows, tokens, peers, latent_size)
    head_queries, head_latent = (
        lax.all_to_all(query_sent, "heads", split_axis=2, concat_axis=1, tiled=True),
        lax.all_to_all(copies, "heads", split_axis=2, concat_axis=1, tiled=True),
    )
    head_latent = head_latent.reshape(rows, token_length, latent_size)
    head_keys = (
        matmul(head_latent, key_mine)
        .astype(jnp.bfloat16)
        .reshape(rows, token_length, local_heads, HEAD_WIDTH)
    )
    head_values = (
        matmul(head_latent, value_mine)
        .astype(jnp.bfloat16)
        .reshape(rows, token_length, local_heads, HEAD_WIDTH)
    )
    head_queries = head_queries.reshape(rows, token_length, local_heads, HEAD_WIDTH)
    head_out, head_lse = lax.map(attend_row, (head_queries, head_keys, head_values, doc_ids))
    mixed_heads = head_out.astype(jnp.bfloat16).reshape(rows, token_length, 1, local_width)
    mixed = lax.all_to_all(mixed_heads, "heads", split_axis=1, concat_axis=2, tiled=True).reshape(
        rows, tokens, QUERY_HEADS * HEAD_WIDTH
    )
    resid = inputs + matmul(mixed, output_weight)
    inverse_two = rms_inverse(resid)
    unit_two = resid * inverse_two
    normed_two = (unit_two * ffn_gain).astype(jnp.bfloat16)
    gate = matmul(normed_two, gate_weight)
    up_value = matmul(normed_two, up_weight)
    sigmoid = jax.nn.sigmoid(gate)
    active = gate * sigmoid
    hidden = (active * up_value).astype(jnp.bfloat16)
    result = resid + matmul(hidden, down_weight)
    hidden_out = result.astype(jnp.bfloat16)
    keep = (own_docs != 0).astype(jnp.float32)
    grad_result = cotangent.astype(jnp.float32) * keep[:, :, None]
    ffn_back = grad_result.astype(jnp.bfloat16)
    grad_act = matmul_back(ffn_back, down_weight)
    up_back = (grad_act * active).astype(jnp.bfloat16)
    gate_back = (grad_act * up_value * sigmoid * (1.0 + gate * (1.0 - sigmoid))).astype(
        jnp.bfloat16
    )
    grad_normed_two = matmul_back(gate_back, gate_weight) + matmul_back(up_back, up_weight)
    grad_resid_norm, ffn_gain_part = norm_back(grad_normed_two, unit_two, inverse_two, ffn_gain)
    grad_resid = grad_result + grad_resid_norm
    attn_back = grad_resid.astype(jnp.bfloat16)
    output_part = jnp.einsum("rtq,rtd->qd", mixed, attn_back, preferred_element_type=jnp.float32)
    grad_mixed = (
        matmul_back(attn_back, output_weight)
        .astype(jnp.bfloat16)
        .reshape(rows, tokens, peers, local_width)
    )
    head_grads = lax.all_to_all(
        grad_mixed, "heads", split_axis=2, concat_axis=1, tiled=True
    ).reshape(rows, token_length, local_heads, HEAD_WIDTH)
    query_heads_back, key_heads_back, value_heads_back = lax.map(
        attend_back, (head_queries, head_keys, head_values, head_out, head_lse, head_grads, doc_ids)
    )
    key_flat = key_heads_back.reshape(rows, token_length, local_width)
    value_flat = value_heads_back.reshape(rows, token_length, local_width)
    latent_term = matmul_back(key_flat, key_mine) + matmul_back(value_flat, value_mine)
    zero_index = place * 0
    key_own = jnp.einsum("rsl,rsc->lc", head_latent, key_flat, preferred_element_type=jnp.float32)
    value_own = jnp.einsum(
        "rsl,rsc->lc", head_latent, value_flat, preferred_element_type=jnp.float32
    )
    key_part = lax.dynamic_update_slice(
        jnp.zeros(key_lift_weight.shape, jnp.float32),
        key_own[None],
        (own_group, zero_index, column_start),
    )
    value_part = lax.dynamic_update_slice(
        jnp.zeros(value_lift_weight.shape, jnp.float32),
        value_own[None],
        (own_group, zero_index, column_start),
    )
    query_shaped = query_heads_back.reshape(rows, token_length, 1, local_width)
    query_back = lax.all_to_all(
        as_sent(query_shaped), "heads", split_axis=1, concat_axis=2, tiled=True
    ).astype(query_shaped.dtype)
    query_back = query_back.reshape(rows, tokens, QUERY_HEADS * HEAD_WIDTH)
    latent_wide = latent_term.reshape(rows, token_length, 1, latent_size)
    latent_sums = lax.all_to_all(
        latent_wide.astype(jnp.bfloat16), "heads", split_axis=1, concat_axis=2, tiled=True
    ).astype(latent_wide.dtype)
    latent_back = jnp.sum(
        latent_sums.reshape(rows, tokens, groups, peers_group, latent_size), axis=3
    )
    latent_back = latent_back.reshape(rows, tokens, groups * latent_size).astype(jnp.bfloat16)
    query_part = jnp.einsum(
        "rtd,rtq->dq", normed_one, query_back, preferred_element_type=jnp.float32
    )
    latent_part = jnp.einsum(
        "rtd,rtl->dl", normed_one, latent_back, preferred_element_type=jnp.float32
    )
    grad_normed_one = matmul_back(query_back, query_weight) + matmul_back(
        latent_back, latent_weight
    )
    grad_in_norm, attn_gain_part = norm_back(grad_normed_one, unit_one, inverse_one, attn_gain)
    hidden_grad = grad_resid + grad_in_norm
    gate_part = jnp.einsum("rtd,rtf->df", normed_two, gate_back, preferred_element_type=jnp.float32)
    up_part = jnp.einsum("rtd,rtf->df", normed_two, up_back, preferred_element_type=jnp.float32)
    down_part = jnp.einsum("rtf,rtd->fd", hidden, ffn_back, preferred_element_type=jnp.float32)
    (
        attn_gain_share,
        query_share,
        latent_share,
        key_share,
        value_share,
        output_share,
        ffn_gain_share,
        gate_share,
        up_share,
        down_share,
    ) = (
        lax.psum_scatter(
            attn_gain_part.astype(jnp.bfloat16), "heads", scatter_dimension=0, tiled=True
        ).astype(jnp.float32),
        lax.psum_scatter(
            query_part.astype(jnp.bfloat16), "heads", scatter_dimension=0, tiled=True
        ).astype(jnp.float32),
        lax.psum_scatter(
            latent_part.astype(jnp.bfloat16), "heads", scatter_dimension=0, tiled=True
        ).astype(jnp.float32),
        lax.psum_scatter(
            key_part.astype(jnp.bfloat16), "heads", scatter_dimension=1, tiled=True
        ).astype(jnp.float32),
        lax.psum_scatter(
            value_part.astype(jnp.bfloat16), "heads", scatter_dimension=1, tiled=True
        ).astype(jnp.float32),
        lax.psum_scatter(
            output_part.astype(jnp.bfloat16), "heads", scatter_dimension=0, tiled=True
        ).astype(jnp.float32),
        lax.psum_scatter(
            ffn_gain_part.astype(jnp.bfloat16), "heads", scatter_dimension=0, tiled=True
        ).astype(jnp.float32),
        lax.psum_scatter(
            gate_part.astype(jnp.bfloat16), "heads", scatter_dimension=1, tiled=True
        ).astype(jnp.float32),
        lax.psum_scatter(
            up_part.astype(jnp.bfloat16), "heads", scatter_dimension=1, tiled=True
        ).astype(jnp.float32),
        lax.psum_scatter(
            down_part.astype(jnp.bfloat16), "heads", scatter_dimension=0, tiled=True
        ).astype(jnp.float32),
    )
    totals = (
        lax.psum(attn_gain_share.astype(jnp.bfloat16), "rows").astype(jnp.float32),
        lax.psum(query_share.astype(jnp.bfloat16), "rows").astype(jnp.float32),
        lax.psum(latent_share.astype(jnp.bfloat16), "rows").astype(jnp.float32),
        lax.psum(key_share.astype(jnp.bfloat16), "rows").astype(jnp.float32),
        lax.psum(value_share.astype(jnp.bfloat16), "rows").astype(jnp.float32),
        lax.psum(output_share.astype(jnp.bfloat16), "rows").astype(jnp.float32),
        lax.psum(ffn_gain_share.astype(jnp.bfloat16), "rows").astype(jnp.float32),
        lax.psum(gate_share.astype(jnp.bfloat16), "rows").astype(jnp.float32),
        lax.psum(up_share.astype(jnp.bfloat16), "rows").astype(jnp.float32),
        lax.psum(down_share.astype(jnp.bfloat16), "rows").astype(jnp.float32),
    )
    return (
        hidden_out,
        hidden_grad,
        totals[0],
        totals[1],
        totals[2],
        totals[3],
        totals[4],
        totals[5],
        totals[6],
        totals[7],
        totals[8],
        totals[9],
    )


def solution(mesh):
    placed = (
        P("rows", "heads", None),
        P("rows", None),
        P("rows", "heads", None),
        P(),
        P(),
        P(),
        P(),
        P(),
        P(),
        P(),
        P(),
        P(),
        P(),
    )
    return jax.shard_map(
        shards,
        mesh=mesh,
        in_specs=placed,
        out_specs=(
            P("rows", "heads", None),
            P("rows", "heads", None),
            P("heads"),
            P("heads", None),
            P("heads", None),
            P(None, "heads", None),
            P(None, "heads", None),
            P("heads", None),
            P("heads"),
            P(None, "heads"),
            P(None, "heads"),
            P("heads", None),
        ),
        check_vma=False,
    )
```

profile of v0, /device:TPU:0, one launch (start us, length us, event | category | flops | bytes accessed | tf_op | source)
XLA Modules:
  0.0 1690.8 jit_solution(11397685815972107453)
XLA Ops:
  9.6 4.0 convert_bitcast_fusion.1
  15.5 7.4 all-to-all-start.1
  25.9 45.4 %all-to-all-done.1 = bf16[4,256,8,128]{3,1,0,2:T(8,128)(2,1)} async-done(((bf16[4,256,8,128]{3,1,0,2:T(8,128)(2,1)}), bf16[4,256,8,128]{3,1,0,2:T(8,128)(2,1)}, u32[]{:S(2)}, u32[]{:S(2)}) %all-to-all-start.1) | async-done | bytes 2097184 | tf_op jit(solution)/shard_map/all_to_all | solution.py:244
  73.7 4.6 all-to-all-start
  78.4 4.5 copy.166
  82.9 4.2 reshape.2474
  87.1 83.7 %all-to-all-done = bf16[4,256,8,256]{3,1,0,2:T(8,128)(2,1)} async-done(((bf16[4,256,8,256]{3,1,0,2:T(8,128)(2,1)}), bf16[4,256,8,256]{3,1,0,2:T(8,128)(2,1)}, u32[]{:S(2)}, u32[]{:S(2)}) %all-to-all-start) | async-done | bytes 4194336 | tf_op jit(solution)/shard_map/all_to_all | solution.py:245
  173.3 4.0 convolution_convert_fusion
  181.1 231.4 %while.49 = (s32[]{:T(128)}, f32[4,2048,2,64]{1,3,2,0:T(8,128)}, f32[4,2,2048]{2,1,0:T(2,128)S(1)}, bf16[4,2048,2,64]{1,3,2,0:T(8,128)(2,1)}, s32[4,2048]{1,0:T(...) while((s32[]{:T(128)}, f32[4,2048,2,64]{1,3,2,0:T(8,128)}, ...), condition=%wide.region_52.53_spmd, body=%wide.region_1.52_spmd.sunk | while | flops 1824705024 | bytes 126708624 | solution.py:259
  412.5 3.8 convert_element_type.390
  416.3 4.2 copy.168
  420.5 4.4 all-to-all-start.2
  425.6 11.9 fusion.230
  437.5 35.2 %all-to-all-done.2 = bf16[4,2048,1,128]{3,0,2,1:T(4,128)(2,1)} async-done(((bf16[4,2048,1,128]{3,0,2,1:T(4,128)(2,1)}), bf16[4,2048,1,128]{3,0,2,1:T(4,128)(2,1)}, u32[]{:S(2)}, u32[]{:S(2)}) %all-to-all-start.2) | async-done | bytes 2097184 | tf_op jit(solution)/shard_map/all_to_all | solution.py:261
  477.2 4.2 reshape.2477
  481.4 4.7 multiply_reduce_fusion.3
  489.8 11.5 fusion.236
  501.2 22.1 %multiply_convert_fusion.12 = (bf16[4,256,2816]{2,1,0:T(8,128)(2,1)}, bf16[4,256,2816]{2,1,0:T(8,128)(2,1)}, bf16[4,256,2816]{2,1,0:T(8,128)(2,1)}) fusion(f32[4,256,2816]{2,1,0:T(8,128)} %fusion.230, f32[4,256,2816]{2,1,0:T(8,128)} %fusion.236, bf16[4,256,1024]{2,1,0:T(8,128)(2,1)} %copy-done.62, bf16[1024,2816]{1,0:T(8,128)(2,1)} %param.103), kind=kOutput, calls=%fused_computation.450 | convolution fusion | flops 5948833792 | bytes 48234496 | tf_op jit(solution)/shard_map/dot_general | solution.py:21
  523.3 10.0 fusion.234
  533.4 9.7 multiply_reduce_fusion.1
  553.0 6.5 bitcast_convert_fusion.3
  559.6 58.3 %all-to-all-done.3 = bf16[4,256,8,128]{3,1,0,2:T(8,128)(2,1)S(1)} async-done(((bf16[4,256,8,128]{3,1,0,2:T(8,128)(2,1)}), bf16[4,256,8,128]{3,1,0,2:T(8,128)(2,1)S(1)}, u32[]{:S(2)}, u32[]{:S(2)}) %all-to-all-start.3) | async-done | bytes 2097184 | tf_op jit(solution)/shard_map/all_to_all | solution.py:293
  620.8 4.2 reshape.2479
  625.0 283.4 %while.50 = (s32[]{:T(128)}, bf16[4,2048,2,64]{1,3,2,0:T(8,128)(2,1)}, bf16[4,2048,2,64]{1,3,2,0:T(8,128)(2,1)}, bf16[4,2048,2,64]{1,3,2,0:T(8,128)(2,1)}, bf16[...) while((s32[]{:T(128)}, ...), condition=%wide.region_75.76_spmd, body=%wide.region_55.75_spmd.sunk | while | flops 3416000512 | bytes 215640624 | solution.py:296
  626.1 3.9 fusion.502
  642.0 5.6 conditional.48
  652.7 5.5 conditional.49
  659.6 5.5 conditional.50
  672.3 5.5 conditional.53
  699.5 3.9 fusion.502
  715.4 5.5 conditional.48
  727.5 5.5 conditional.50
  738.8 5.5 conditional.52
  745.7 5.5 conditional.53
  772.9 3.9 fusion.502
  788.9 5.5 conditional.48
  801.0 5.5 conditional.50
  813.7 5.5 conditional.53
  840.9 3.9 fusion.502
  856.9 5.5 conditional.48
  869.0 5.5 conditional.50
  881.7 5.5 conditional.53
  908.4 4.3 convolution_bitcast_fusion.35
  918.7 11.0 bitcast_convert_fusion.2
  931.4 10.7 bitcast_convert_fusion.1
  945.3 55.7 %all_to_all.84 = bf16[4,2048,1,128]{3,0,2,1:T(4,128)(2,1)S(1)} all-to-all(bf16[4,2048,1,128]{3,0,2,1:T(4,128)(2,1)S(1)} %copy.173), channel_id=1, replica_groups=mesh['rows'=4,'heads'=8] {'heads'}, dimensions={1} | all-to-all | bytes 4194304 | tf_op jit(solution)/shard_map/all_to_all | solution.py:318
  1003.9 4.3 reshape.2481
  1008.2 5.5 bitcast_convert_fusion.4
  1015.3 10.8 bitcast_convert_fusion
  1032.3 16.0 copy.180
  1048.4 144.6 %all_to_all.85 = bf16[4,2048,1,256]{3,0,2,1:T(4,128)(2,1)} all-to-all(bf16[4,2048,1,256]{3,0,2,1:T(4,128)(2,1)S(1)} %copy.180), channel_id=1, replica_groups=mesh['rows'=4,'heads'=8] {'heads'}, dimensions={1} | all-to-all | bytes 8388608 | tf_op jit(solution)/shard_map/all_to_all | solution.py:323
  1192.9 4.7 reduce.52
  1204.7 11.4 add_convert_fusion.1
  1216.2 25.9 %reduce-scatter.19.cloned.1.call-done = bf16[1024,352]{0,1:T(8,128)(2,1)} async-done(((bf16[1024,2816]{0,1:T(8,128)(2,1)}), bf16[1024,352]{0,1:T(8,128)(2,1)}) %reduce-scatter.19.cloned.1.call-update) | async-done | bytes 720912 | tf_op jit(solution)/shard_map/reduce_scatter | solution.py:377
  1242.1 113.4 %reduce-scatter.21.cloned.1.call-done = bf16[1024,352]{0,1:T(8,128)(2,1)} async-done(((bf16[1024,2816]{0,1:T(8,128)(2,1)}), bf16[1024,352]{0,1:T(8,128)(2,1)}) %reduce-scatter.21.cloned.1.call-update) | async-done | bytes 720912 | tf_op jit(solution)/shard_map/reduce_scatter | solution.py:380
  1355.5 71.0 %reduce-scatter.9.cloned.1.call-done = bf16[128,1024]{1,0:T(8,128)(2,1)} async-done(((bf16[1024,1024]{1,0:T(8,128)(2,1)}), bf16[128,1024]{1,0:T(8,128)(2,1)}) %reduce-scatter.9.cloned.1.call-update) | async-done | bytes 262160 | tf_op jit(solution)/shard_map/reduce_scatter | solution.py:359
  1426.4 112.7 %reduce-scatter.23.cloned.1.call-done = bf16[352,1024]{1,0:T(8,128)(2,1)} async-done(((bf16[2816,1024]{1,0:T(8,128)(2,1)}), bf16[352,1024]{1,0:T(8,128)(2,1)}) %reduce-scatter.23.cloned.1.call-update) | async-done | bytes 720912 | tf_op jit(solution)/shard_map/reduce_scatter | solution.py:383
  1539.2 67.3 %reduce-scatter.11.cloned.1.call-done = bf16[128,512]{1,0:T(8,128)(2,1)} async-done(((bf16[1024,512]{1,0:T(8,128)(2,1)}), bf16[128,512]{1,0:T(8,128)(2,1)}) %reduce-scatter.11.cloned.1.call-update) | async-done | bytes 131088 | tf_op jit(solution)/shard_map/reduce_scatter | solution.py:362
  1606.5 4.7 fusion.255
  1611.3 4.3 fusion.247
  1615.6 19.4 %all-reduce.4 = (bf16[1024]{0:T(1024)(128)(2,1)S(1)}, bf16[1024]{0:T(1024)(128)(2,1)S(1)}) all-reduce(bf16[1024]{0:T(1024)(128)(2,1)S(1)} %get-tuple-element.1038, bf16[1024]{0:T(1024)(128)(2,1)S(1)} %copy-done.93), channel_id=2, replica_groups=mesh['rows'=4,'heads'=8] {'heads'}, use_global_device_ids=true, to_apply=%region_79.80.clone | all-reduce | flops 2048 | bytes 8192
  1635.2 6.3 all-reduce.5
  1642.5 5.3 fusion.246
  1647.8 27.4 %all-reduce.9.cloned.1.call-done = (bf16[128,1024]{1,0:T(8,128)(2,1)}, bf16[128,512]{1,0:T(8,128)(2,1)}, bf16[2,32,512]{2,1,0:T(8,128)(2,1)}, bf16[2,32,512]{2,1...) async-done(((bf16[128,1024]{1,0:T(8,128)(2,1)}, bf16[128,512]{1,0:T(8,128)(2,1)}, ...) | async-done | bytes 2949136 | tf_op jit(solution)/shard_map/psum | solution.py:389
  (1264 shorter events, 618.0 us)
Async XLA Ops:
  7.2 474.2 %copy-start = (bf16[1024,1024]{1,0:T(8,128)(2,1)S(1)}, bf16[1024,1024]{1,0:T(8,128)(2,1)}, u32[]{:S(2)}) copy-start(bf16[1024,1024]{1,0:T(8,128)(2,1)} %param.101) | copy-start | bytes 6291460
  9.6 13.3 copy-start.86
  15.5 7.4 copy-start.68
  15.5 55.8 %all-to-all-start.1 = ((bf16[4,256,8,128]{3,1,0,2:T(8,128)(2,1)}), bf16[4,256,8,128]{3,1,0,2:T(8,128)(2,1)}, u32[]{:S(2)}, u32[]{:S(2)}) async-start(bf16[4,256,8,128]{3,1,0,2:T(8,128)(2,1)} %bitcast.720), calls=%async_computation.1 | async-start | bytes 4194304 | tf_op jit(solution)/shard_map/all_to_all | solution.py:244
  73.7 97.1 %all-to-all-start = ((bf16[4,256,8,256]{3,1,0,2:T(8,128)(2,1)}), bf16[4,256,8,256]{3,1,0,2:T(8,128)(2,1)}, u32[]{:S(2)}, u32[]{:S(2)}) async-start(bf16[4,256,8,256]{3,1,0,2:T(8,128)(2,1)} %bitcast.701), calls=%async_computation | async-start | bytes 8388608 | tf_op jit(solution)/shard_map/all_to_all | solution.py:245
  173.3 7.8 copy-start.6
  194.5 12.5 copy-start.60
  213.9 4.2 copy-start.14
  235.7 3.8 copy-start.58
  254.9 10.1 copy-start.60
  274.4 4.2 copy-start.14
  287.0 3.1 copy-start.76
  296.1 3.8 copy-start.58
  315.3 10.1 copy-start.60
  332.4 4.2 copy-start.14
  351.1 3.8 copy-start.58
  370.3 10.1 copy-start.60
  387.3 4.2 copy-start.14
  406.1 3.8 copy-start.58
  420.5 52.1 %all-to-all-start.2 = ((bf16[4,2048,1,128]{3,0,2,1:T(4,128)(2,1)}), bf16[4,2048,1,128]{3,0,2,1:T(4,128)(2,1)}, u32[]{:S(2)}, u32[]{:S(2)}) async-start(bf16[4,2048,1,128]{3,0,2,1:T(4,128)(2,1)} %copy.168), calls=%async_computation.2 | async-start | bytes 4194304 | tf_op jit(solution)/shard_map/all_to_all | solution.py:261
  425.6 117.5 %copy-start.89 = (f32[4,256]{1,0:T(4,128)}, f32[4,256]{1,0:T(4,128)S(1)}, u32[]{:S(2)}) copy-start(f32[4,256]{1,0:T(4,128)S(1)} %fusion.289) | copy-start | bytes 12292
  481.4 6.6 copy-start.88
  523.3 10.0 copy-start.52
  523.3 10.0 copy-start.95
  533.4 9.8 copy-start.66
  548.9 69.0 %all-to-all-start.3 = ((bf16[4,256,8,128]{3,1,0,2:T(8,128)(2,1)}), bf16[4,256,8,128]{3,1,0,2:T(8,128)(2,1)S(1)}, u32[]{:S(2)}, u32[]{:S(2)}) async-start(bf16[4,256,8,128]{3,1,0,2:T(8,128)(2,1)} %bitcast.719), calls=%async_computation.3 | async-start | bytes 4194304 | tf_op jit(solution)/shard_map/all_to_all | solution.py:293
  552.5 663.7 %reduce-scatter.17.cloned.1.call-start = ((), (), s32[]{:S(2)}) async-start(), calls=%async_computation.18 | async-start | bytes 2359296 | tf_op jit(solution)/shard_map/reduce_scatter | solution.py:371
  559.5 656.6 %reduce-scatter.13.cloned.1.call-start = ((), (), s32[]{:S(2)}) async-start(), calls=%async_computation.16 | async-start | bytes 589824 | tf_op jit(solution)/shard_map/reduce_scatter | solution.py:365
  625.2 7.7 copy-start.82
  632.9 5.2 copy-start.11
  647.6 3.1 copy-start.23
  647.6 3.1 copy-start.39
  698.6 7.7 copy-start.82
  706.3 5.2 copy-start.11
  721.0 3.1 copy-start.23
  721.0 3.1 copy-start.39
  772.1 7.7 copy-start.82
  779.8 5.2 copy-start.11
  794.4 3.1 copy-start.23
  794.4 3.1 copy-start.39
  840.1 7.7 copy-start.82
  847.8 5.2 copy-start.11
  862.4 3.1 copy-start.23
  862.4 3.1 copy-start.39
  908.4 5.6 copy-start.56
  913.9 302.2 %reduce-scatter.15.cloned.1.call-start = ((), (), s32[]{:S(2)}) async-start(), calls=%async_computation.17 | async-start | bytes 589824 | tf_op jit(solution)/shard_map/reduce_scatter | solution.py:368
  918.7 323.4 %reduce-scatter.19.cloned.1.call-start = ((), (), s32[]{:S(2)}) async-start(), calls=%async_computation.19 | async-start | bytes 6488064 | tf_op jit(solution)/shard_map/reduce_scatter | solution.py:377
  929.8 425.6 %reduce-scatter.21.cloned.1.call-start = ((), (), s32[]{:S(2)}) async-start(), calls=%async_computation.20 | async-start | bytes 6488064 | tf_op jit(solution)/shard_map/reduce_scatter | solution.py:380
  942.1 484.3 %reduce-scatter.9.cloned.1.call-start = ((), (), s32[]{:S(2)}) async-start(), calls=%async_computation.14 | async-start | bytes 2359296 | tf_op jit(solution)/shard_map/reduce_scatter | solution.py:359
  1003.9 4.3 copy-start.49
  1003.9 4.3 copy-start.87
  1003.9 4.3 copy-start.92
  1013.7 525.5 %reduce-scatter.23.cloned.1.call-start = ((), (), s32[]{:S(2)}) async-start(), calls=%async_computation.21 | async-start | bytes 6488064 | tf_op jit(solution)/shard_map/reduce_scatter | solution.py:383
  1026.1 580.4 %reduce-scatter.11.cloned.1.call-start = ((), (), s32[]{:S(2)}) async-start(), calls=%async_computation.15 | async-start | bytes 1179648 | tf_op jit(solution)/shard_map/reduce_scatter | solution.py:362
  1199.6 3.9 copy-start.94
  1203.4 471.8 %all-reduce.9.cloned.1.call-start = ((), (), s32[]{:S(2)}) async-start(), calls=%async_computation.22 | async-start | bytes 5898240 | tf_op jit(solution)/shard_map/psum | solution.py:389
  1606.5 4.8 copy-start.59
  1606.5 4.8 copy-start.69
  1611.3 4.3 copy-start.93
  1675.2 3.8 copy-start.72
  1677.7 3.4 copy-start.77
  1679.0 3.7 copy-start.85
  1679.0 5.0 copy-start.1
  1679.0 4.4 copy-start.84
  (209 other events, 354.4 us)
Sparse Core Ops, SparseCore 0:
  559.6 99.2 reduce-scatter.16
  914.1 80.8 reduce-scatter.12
  999.2 64.2 reduce-scatter.14
  1067.0 175.0 reduce-scatter.18
  1245.6 109.8 reduce-scatter.20
  1358.8 67.5 reduce-scatter.8
  1430.1 109.0 reduce-scatter.22
  1543.1 63.2 reduce-scatter.10
  1609.6 65.6 all-reduce.8
where the time goes:
time: 1710 us; the launch traced here: 1690 us
  waiting for transfers between devices  640 us (37%)
  matrix products  464 us (27%)
  blocking collectives  226 us (13%)
  local copies, waits for them, and re-layouts  168 us (10%)
  other arithmetic  118 us (7%)
  loops' own time  38.1 us (2%)
  starting transfers between devices  20.7 us (1%)
    all_to_all x1, blocking collectives, shards(): lax.all_to_all(latent_wide.astype(jnp.bfloat16), 'heads', split_axis=1, c...  145 us
    reduce_scatter x1, waiting for transfers between devices, shards(): lax.psum_scatter(up_part.astype(jnp.bfloat16), 'heads', scatter_dimension...  113 us
    reduce_scatter x1, waiting for transfers between devices, shards(): lax.psum_scatter(down_part.astype(jnp.bfloat16), 'heads', scatter_dimensi...  113 us
    dot_general x60, matrix products, tile_scores(): jnp.einsum('qhd,khd->hqk', query_tile, key_tile, preferred_element_type=j...  106 us
    dot_general x30, matrix products, collect(): jnp.einsum('hqk,khd->qhd', probs, value_matrix[key_start:key_start + bloc...  84 us
    all_to_all x1, waiting for transfers between devices, shards(): lax.all_to_all(copies, 'heads', split_axis=2, concat_axis=1, tiled=True)  83.7 us
    reduce_scatter x1, waiting for transfers between devices, shards(): lax.psum_scatter(query_part.astype(jnp.bfloat16), 'heads', scatter_dimens...  71 us
    reduce_scatter x1, waiting for transfers between devices, shards(): lax.psum_scatter(latent_part.astype(jnp.bfloat16), 'heads', scatter_dimen...  67.3 us
  transfers between devices with their start and end apart: 13, of which 10 were waited for; matrix products, arithmetic and copies ran while one was open for 23% of the time, Pallas kernels for 0%

commit v1 on v0

v1 whole, which is shorter than its diff:
```python
import functools
import math

import jax
import jax.numpy as jnp
from jax import lax
from jax.experimental import pallas as pl
from jax.experimental.pallas import tpu as pltpu
from jax.sharding import PartitionSpec as P

HEAD_WIDTH = 64
epsilon = 1e-05
blocked = -1e30
LOG2E = math.log2(math.e)
LN2 = math.log(2.0)
QUAD = 4
f32 = jnp.float32
bf16 = jnp.bfloat16


def matmul(left, right):
    return jnp.dot(left, right, preferred_element_type=f32)


def matmul_nt(left, right):
    return lax.dot_general(
        left, right, (((left.ndim - 1,), (right.ndim - 1,)), ((), ())), preferred_element_type=f32
    )


def matmul_tn(left, right):
    return lax.dot_general(left, right, (((0,), (0,)), ((), ())), preferred_element_type=f32)


def rms_inverse(value_matrix):
    return lax.rsqrt(jnp.mean(value_matrix * value_matrix, axis=-1, keepdims=True) + epsilon)


def norm_back(grad_normed, unit, inverse, gain):
    scaled = grad_normed * gain
    grad_in = inverse * (scaled - unit * jnp.mean(scaled * unit, axis=-1, keepdims=True))
    return (grad_in, jnp.sum(grad_normed * unit, axis=0))


def expand_heads(source, weights, factor, out_ref):
    quads, wide, deep = weights.shape
    latent = wide // QUAD
    for quad in range(quads):
        product = matmul_nt(weights[quad], source[:, quad * deep : (quad + 1) * deep])
        if factor != 1.0:
            product = product * factor
        product = product.astype(bf16)
        for h in range(QUAD):
            out_ref[quad * QUAD + h] = product[h * latent : (h + 1) * latent]


def seg_mask(diagonal, base, start):
    keys = start.shape[-1]
    key_at = lax.broadcasted_iota(jnp.int32, (keys, keys), 0)
    allow = key_at >= (start - base)
    if diagonal:
        allow = allow & (key_at <= lax.broadcasted_iota(jnp.int32, (keys, keys), 1))
    return allow


def attend_kernel(count, first, last, diagonal_at, lo, bases, *refs):
    refs = list(refs)
    take = lambda k: [refs.pop(0) for _ in range(k)]
    query_ref, start_ref, key_lift_ref = take(3)
    segs = take(count)
    if not first:
        top_in, total_in, mix_in = take(3)
    if last:
        (value_lift_ref,) = take(1)
        out_ref, lse_ref, mix_ref = take(3)
    else:
        top_out, total_out, mix_out = take(3)
    expanded, top, total, mix = take(4)
    heads = expanded.shape[0]
    tokens = query_ref.shape[1]
    row = pl.program_id(0)
    scale = HEAD_WIDTH ** (-0.5) * LOG2E
    expand_heads(query_ref[0], key_lift_ref, scale, expanded)
    if first:
        top[...] = jnp.full_like(top, blocked)
        total[...] = jnp.zeros_like(total)
        mix[...] = jnp.zeros_like(mix)
    else:
        top[...] = top_in[0]
        total[...] = total_in[0]
        mix[...] = mix_in[0]
    start = start_ref[0]
    for i in range(count):

        @pl.when((bases[i] >= 0) & (bases[i] + tokens - 1 >= lo[row]))
        def _():
            latent = segs[i][0]
            latent_t = latent.T
            allow = seg_mask(i == diagonal_at, bases[i], start)
            for h in range(heads):
                score = jnp.where(allow, matmul(latent, expanded[h]), blocked)
                old = top[h : h + 1]
                new = jnp.maximum(old, jnp.max(score, axis=0, keepdims=True))
                probs = jnp.exp2(score - new)
                fade = jnp.exp2(old - new)
                top[h : h + 1] = new
                total[h : h + 1] = total[h : h + 1] * fade + jnp.sum(probs, axis=0, keepdims=True)
                mix[h] = mix[h] * fade + matmul(latent_t, probs.astype(bf16))

    if not last:
        top_out[0] = top[...]
        total_out[0] = total[...]
        mix_out[0] = mix[...]
        return
    lse_ref[0] = top[...] + jnp.log2(total[...])
    inverse = 1.0 / total[...]
    quads, deep, wide = value_lift_ref.shape
    for h in range(heads):
        mix_ref[0, h] = (mix[h] * inverse[h : h + 1]).astype(bf16)
    for quad in range(quads):
        part = mix_ref[0, quad * QUAD : (quad + 1) * QUAD].reshape(wide, tokens)
        lifted = matmul(value_lift_ref[quad], part)
        out_ref[0, :, quad * deep : (quad + 1) * deep] = lifted.T.astype(bf16)


def whole(array):
    return pl.BlockSpec(array.shape, lambda *_: (0,) * array.ndim)


def by_row(shape):
    return pl.BlockSpec((1,) + tuple(shape[1:]), lambda r, *_: (r,) + (0,) * (len(shape) - 1))


def attend_part(queries, start, key_lift, value_lift, lo, segs, bases, diagonal_at, state, last):
    rows, tokens, width = queries.shape
    heads = width // HEAD_WIDTH
    latent = segs[0].shape[-1]
    state_shapes = [(rows, heads, tokens), (rows, heads, tokens), (rows, heads, latent, tokens)]
    args = [queries, start, key_lift, *segs]
    specs = [by_row(queries.shape), by_row(start.shape), whole(key_lift)]
    specs += [by_row(s.shape) for s in segs]
    if state is not None:
        args += list(state)
        specs += [by_row(s) for s in state_shapes]
    if last:
        args.append(value_lift)
        specs.append(whole(value_lift))
        outs = [
            jax.ShapeDtypeStruct(queries.shape, bf16),
            jax.ShapeDtypeStruct(state_shapes[0], f32),
            jax.ShapeDtypeStruct(state_shapes[2], bf16),
        ]
    else:
        outs = [jax.ShapeDtypeStruct(s, f32) for s in state_shapes]
    blocks = rows * heads * len(segs)
    return pl.pallas_call(
        functools.partial(attend_kernel, len(segs), state is None, last, diagonal_at),
        out_shape=outs,
        grid_spec=pltpu.PrefetchScalarGridSpec(
            num_scalar_prefetch=2,
            grid=(rows,),
            in_specs=specs,
            out_specs=[by_row(o.shape) for o in outs],
            scratch_shapes=[
                pltpu.VMEM((heads, latent, tokens), bf16),
                pltpu.VMEM((heads, tokens), f32),
                pltpu.VMEM((heads, tokens), f32),
                pltpu.VMEM((heads, latent, tokens), f32),
            ],
        ),
        compiler_params=pltpu.CompilerParams(
            dimension_semantics=("arbitrary",), vmem_limit_bytes=48 << 20
        ),
        cost_estimate=pl.CostEstimate(
            flops=blocks * tokens * tokens * latent * 4,
            bytes_accessed=rows * heads * latent * tokens * 4,
            transcendentals=blocks * tokens * tokens,
        ),
        name="attend",
    )(lo, bases, *args)


def attend_back_kernel(count, first, last, diagonal_at, lo, bases, *refs):
    refs = list(refs)
    take = lambda k: [refs.pop(0) for _ in range(k)]
    query_ref, grad_ref, lse_ref, mix_ref, start_ref, key_lift_ref, value_lift_ref = take(7)
    segs = take(count)
    if not first:
        (back_in,) = take(1)
    if last:
        (key_lift_t_ref,) = take(1)
    seg_grads = take(count)
    if last:
        query_back_ref, key_up_ref, value_up_ref = take(3)
    else:
        (back_out,) = take(1)
    expanded, expanded_grad, delta, back, part_key, part_value = take(6)
    heads, latent_size, tokens = expanded.shape
    row = pl.program_id(0)
    scale = HEAD_WIDTH ** (-0.5)
    expand_heads(query_ref[0], key_lift_ref, scale * LOG2E, expanded)
    expand_heads(grad_ref[0], value_lift_ref, 1.0, expanded_grad)
    for h in range(heads):
        delta[h : h + 1] = jnp.sum(
            mix_ref[0, h].astype(f32) * expanded_grad[h].astype(f32), axis=0, keepdims=True
        )
    if first:
        back[...] = jnp.zeros_like(back)
    else:
        back[...] = back_in[0]
    start = start_ref[0]
    for i in range(count):
        touched = (bases[i] >= 0) & (bases[i] + tokens - 1 >= lo[row])

        @pl.when(touched)
        def _():
            latent = segs[i][0]
            latent_t = latent.T
            allow = seg_mask(i == diagonal_at, bases[i], start)
            for h in range(heads):
                score = matmul(latent, expanded[h])
                probs = jnp.where(allow, jnp.exp2(score - lse_ref[0, h : h + 1]), 0.0)
                dprobs = matmul(latent, expanded_grad[h])
                dscore = (probs * (dprobs - delta[h : h + 1])).astype(bf16)
                back[h] += matmul(latent_t, dscore)
                by_key = matmul_nt(dscore, expanded[h])
                by_value = matmul_nt(probs.astype(bf16), expanded_grad[h])
                if h == 0:
                    part_key[...] = by_key
                    part_value[...] = by_value
                else:
                    part_key[...] += by_key
                    part_value[...] += by_value
            seg_grads[i][0] = (part_key[...] * LN2 + part_value[...]).astype(bf16)

        @pl.when(jnp.logical_not(touched))
        def _():
            seg_grads[i][0] = jnp.zeros((tokens, latent_size), bf16)

    if not last:
        back_out[0] = back[...]
        return

    @pl.when(row == 0)
    def _():
        key_up_ref[...] = jnp.zeros_like(key_up_ref)
        value_up_ref[...] = jnp.zeros_like(value_up_ref)

    quads, deep, wide = key_lift_t_ref.shape
    for quad in range(quads):
        part = (back[quad * QUAD : (quad + 1) * QUAD].reshape(wide, tokens) * scale).astype(bf16)
        lifted = matmul(key_lift_t_ref[quad], part)
        query_back_ref[0, :, quad * deep : (quad + 1) * deep] = lifted.T.astype(bf16)
        key_up_ref[quad] += matmul(part, query_ref[0, :, quad * deep : (quad + 1) * deep])
        mixed = mix_ref[0, quad * QUAD : (quad + 1) * QUAD].reshape(wide, tokens)
        value_up_ref[quad] += matmul(mixed, grad_ref[0, :, quad * deep : (quad + 1) * deep])


def attend_back_part(
    queries, grads, lse, mix, start, key_lift, value_lift, key_lift_t, lo, segs, bases,
    diagonal_at, state, last,
):
    rows, tokens, width = queries.shape
    heads = width // HEAD_WIDTH
    latent = segs[0].shape[-1]
    state_shape = (rows, heads, latent, tokens)
    args = [queries, grads, lse, mix, start, key_lift, value_lift, *segs]
    specs = [by_row(a.shape) for a in (queries, grads, lse, mix, start)]
    specs += [whole(key_lift), whole(value_lift)]
    specs += [by_row(s.shape) for s in segs]
    if state is not None:
        args.append(state)
        specs.append(by_row(state_shape))
    outs = [jax.ShapeDtypeStruct(s.shape, bf16) for s in segs]
    out_specs = [by_row(s.shape) for s in segs]
    if last:
        args.append(key_lift_t)
        specs.append(whole(key_lift_t))
        outs.append(jax.ShapeDtypeStruct(queries.shape, bf16))
        out_specs.append(by_row(queries.shape))
        for _ in range(2):
            outs.append(jax.ShapeDtypeStruct(key_lift.shape, f32))
            out_specs.append(whole(key_lift))
    else:
        outs.append(jax.ShapeDtypeStruct(state_shape, f32))
        out_specs.append(by_row(state_shape))
    blocks = rows * heads * len(segs)
    return pl.pallas_call(
        functools.partial(attend_back_kernel, len(segs), state is None, last, diagonal_at),
        out_shape=outs,
        grid_spec=pltpu.PrefetchScalarGridSpec(
            num_scalar_prefetch=2,
            grid=(rows,),
            in_specs=specs,
            out_specs=out_specs,
            scratch_shapes=[
                pltpu.VMEM((heads, latent, tokens), bf16),
                pltpu.VMEM((heads, latent, tokens), bf16),
                pltpu.VMEM((heads, tokens), f32),
                pltpu.VMEM((heads, latent, tokens), f32),
                pltpu.VMEM((tokens, latent), f32),
                pltpu.VMEM((tokens, latent), f32),
            ],
        ),
        compiler_params=pltpu.CompilerParams(
            dimension_semantics=("arbitrary",), vmem_limit_bytes=48 << 20
        ),
        cost_estimate=pl.CostEstimate(
            flops=blocks * tokens * tokens * latent * 10,
            bytes_accessed=rows * heads * latent * tokens * 8,
            transcendentals=blocks * tokens * tokens,
        ),
        name="attend_back",
    )(lo, bases, *args)


def quad_lift(lift):
    latent, width = lift.shape
    deep = QUAD * HEAD_WIDTH
    quads = width // deep
    tall = jnp.tile(lift.reshape(latent, quads, deep).transpose(1, 0, 2), (1, QUAD, 1))
    row_head = lax.broadcasted_iota(jnp.int32, tall.shape, 1) // latent
    column_head = lax.broadcasted_iota(jnp.int32, tall.shape, 2) // HEAD_WIDTH
    return jnp.where(row_head == column_head, tall, jnp.zeros_like(tall))


def quad_unlift(quad_grad):
    quads, wide, deep = quad_grad.shape
    latent = wide // QUAD
    column_head = lax.broadcasted_iota(jnp.int32, (latent, deep), 1) // HEAD_WIDTH
    parts = []
    for quad in range(quads):
        part = quad_grad[quad, :latent]
        for h in range(1, QUAD):
            part = jnp.where(column_head == h, quad_grad[quad, h * latent : (h + 1) * latent], part)
        parts.append(part)
    return jnp.concatenate(parts, axis=1)


def flip(array, axis, bit):
    size = lax.axis_size(axis)
    return lax.ppermute(array, axis, [(i, i ^ (1 << bit)) for i in range(size)])


def add_sent(mine, other):
    return (mine.astype(f32) + other.astype(f32)).astype(bf16)


def reduce_rest(part):
    row_bits = lax.axis_size("rows").bit_length() - 1
    head_bits = lax.axis_size("heads").bit_length() - 1
    row_at = lax.axis_index("rows")
    head_at = lax.axis_index("heads")
    for bit in range(1, row_bits):
        mine = (row_at >> bit) & 1
        half = part.shape[-1] // 2
        keep = lax.dynamic_slice_in_dim(part, mine * half, half, 2)
        send = lax.dynamic_slice_in_dim(part, (1 - mine) * half, half, 2)
        part = add_sent(keep, flip(send, "rows", bit))
    for bit in range(head_bits):
        mine = (head_at >> bit) & 1
        pairs = part.reshape((part.shape[0] // 2, 2) + part.shape[1:])
        keep = lax.dynamic_index_in_dim(pairs, mine, 1, keepdims=False)
        send = lax.dynamic_index_in_dim(pairs, 1 - mine, 1, keepdims=False)
        part = add_sent(keep, flip(send, "heads", bit))
    return part[0]


def gather_columns(part):
    row_bits = lax.axis_size("rows").bit_length() - 1
    row_at = lax.axis_index("rows")
    for bit in reversed(range(row_bits)):
        mine = (row_at >> bit) & 1
        other = flip(part, "rows", bit)
        low = jnp.where(mine == 0, part, other)
        high = jnp.where(mine == 0, other, part)
        part = jnp.stack([low, high]) if bit == 0 else jnp.concatenate([low, high], axis=1)
    return part


def shards(
    hidden_in,
    doc_ids,
    cotangent,
    attn_gain,
    query_weight,
    latent_weight,
    key_lift_weight,
    value_lift_weight,
    output_weight,
    ffn_gain,
    gate_weight,
    up_weight,
    down_weight,
):
    rows, tokens, width = hidden_in.shape
    peers = lax.axis_size("heads")
    place = lax.axis_index("heads")
    core = lax.axis_index("rows") & 1
    groups, latent_size, group_width = key_lift_weight.shape
    count = rows * tokens
    steps = peers // 2
    side = place & 1
    level = place // 2
    swap = lambda a: flip(a, "rows", 0)
    mine = lambda a, axis: lax.dynamic_slice_in_dim(a, core * (a.shape[axis] // 2), a.shape[axis] // 2, axis)
    theirs = lambda a, axis: lax.dynamic_slice_in_dim(
        a, (1 - core) * (a.shape[axis] // 2), a.shape[axis] // 2, axis
    )

    own_base = place * tokens
    own_docs = lax.dynamic_slice_in_dim(doc_ids, own_base, tokens, 1)
    position = own_base + jnp.arange(tokens, dtype=jnp.int32)
    before = (doc_ids[:, None, :] == own_docs[:, :, None]) & (
        jnp.arange(doc_ids.shape[1], dtype=jnp.int32)[None, None, :] <= position[None, :, None]
    )
    own_start = position[None, :] + 1 - jnp.sum(before.astype(jnp.int32), axis=-1)
    start = jnp.concatenate([own_start, swap(own_start)], axis=0)
    lo = start[:, 0]
    start = start[:, None, :]

    inputs = hidden_in.reshape(count, width).astype(f32)
    inverse_one = rms_inverse(inputs)
    normed_one = (inputs * inverse_one * attn_gain).astype(bf16)
    latent_mine = matmul(normed_one, mine(latent_weight, 1)).astype(bf16)
    latent_sent = matmul(normed_one, theirs(latent_weight, 1)).astype(bf16)
    latent_got = swap(latent_sent)
    own_seg = jnp.concatenate([latent_mine, latent_got], axis=0).reshape(2 * rows, tokens, latent_size)
    query_mine = matmul(normed_one, mine(query_weight, 1)).astype(bf16)
    query_sent = matmul(normed_one, theirs(query_weight, 1)).astype(bf16)
    queries = jnp.concatenate([query_mine, swap(query_sent)], axis=0).reshape(2 * rows, tokens, group_width)

    key_mine = lax.dynamic_index_in_dim(key_lift_weight, core, 0, keepdims=False)
    value_mine = lax.dynamic_index_in_dim(value_lift_weight, core, 0, keepdims=False)
    key_lift = quad_lift(key_mine)
    value_lift = quad_lift(value_mine)
    key_lift_t = key_lift.transpose(0, 2, 1)
    value_lift_t = value_lift.transpose(0, 2, 1)

    up_chain = [(i, i + 2) for i in range(peers - 2)]
    down_chain = [(i + 2, i) for i in range(peers - 2)]
    segs = []
    bases = []
    moving = own_seg
    for k in range(steps):
        if k > 0:
            moving = lax.ppermute(moving, "heads", up_chain)
        segs.append((moving, flip(moving, "heads", 0)))
        base = ((level - k) * 2 + side) * tokens
        other = ((level - k) * 2 + 1 - side) * tokens
        there = level >= k
        bases.append(
            (jnp.where(there, base, -1), jnp.where(there & (other < own_base), other, -1))
        )

    def pick(ks):
        return (
            [s for k in ks for s in segs[k]],
            jnp.stack([b for k in ks for b in bases[k]]).astype(jnp.int32),
        )

    parts = [range(0, steps - 1), range(steps - 1, steps)]
    state = None
    for i, ks in enumerate(parts):
        seg_list, base_list = pick(ks)
        state = attend_part(
            queries, start, key_lift, value_lift_t, lo, seg_list, base_list,
            0 if i == 0 else -1, state, i == len(parts) - 1,
        )
    head_out, lse, head_mix = state
    mixed_mine = head_out[:rows].reshape(count, group_width)
    mixed_got = swap(head_out[rows:]).reshape(count, group_width)
    mixed = jnp.where(
        core == 0,
        jnp.concatenate([mixed_mine, mixed_got], axis=1),
        jnp.concatenate([mixed_got, mixed_mine], axis=1),
    )

    resid = inputs + matmul(mixed, output_weight)
    inverse_two = rms_inverse(resid)
    unit_two = resid * inverse_two
    normed_two = (unit_two * ffn_gain).astype(bf16)
    gate = matmul(normed_two, gate_weight)
    up_value = matmul(normed_two, up_weight)
    sigmoid = jax.nn.sigmoid(gate)
    active = gate * sigmoid
    hidden = (active * up_value).astype(bf16)
    result = resid + matmul(hidden, down_weight)
    hidden_out = result.astype(bf16)
    keep = (own_docs != 0).astype(f32).reshape(count, 1)
    grad_result = cotangent.reshape(count, width).astype(f32) * keep
    ffn_back = grad_result.astype(bf16)
    grad_act = matmul_nt(ffn_back, down_weight)
    up_back = (grad_act * active).astype(bf16)
    gate_back = (grad_act * up_value * sigmoid * (1.0 + gate * (1.0 - sigmoid))).astype(bf16)
    grad_two = matmul_nt(gate_back, gate_weight) + matmul_nt(up_back, up_weight)
    grad_norm, ffn_gain_part = norm_back(grad_two, unit_two, inverse_two, ffn_gain)
    grad_resid = grad_result + grad_norm
    attn_back = grad_resid.astype(bf16)
    grad_mixed_mine = matmul_nt(attn_back, mine(output_weight, 0)).astype(bf16)
    grad_mixed_sent = matmul_nt(attn_back, theirs(output_weight, 0)).astype(bf16)
    head_grads = jnp.concatenate([grad_mixed_mine, swap(grad_mixed_sent)], axis=0).reshape(
        2 * rows, tokens, group_width
    )

    def halves(left, right):
        return (
            matmul_tn(left, mine(right, 1)).astype(bf16),
            matmul_tn(left, theirs(right, 1)).astype(bf16),
        )

    def core_sum(pair):
        total = add_sent(pair[0], swap(pair[1]))
        return total.reshape((peers, total.shape[0] // peers, total.shape[1]))

    gate_sum = core_sum(halves(gate_back, normed_two))
    up_sum = core_sum(halves(up_back, normed_two))
    down_sum = core_sum(halves(hidden, ffn_back))
    output_sum = core_sum(halves(mixed, attn_back))
    early_one = reduce_rest(jnp.concatenate([gate_sum, output_sum], axis=1))
    early_two = reduce_rest(jnp.concatenate([up_sum, down_sum], axis=1))

    back_parts = [[k] for k in range(steps - 1, 1, -1)] + [list(range(min(1, steps - 1), -1, -1))]
    state = None
    passing = None
    for i, ks in enumerate(back_parts):
        seg_list, base_list = pick(ks)
        done = i == len(back_parts) - 1
        outs = attend_back_part(
            queries, head_grads, lse, head_mix, start, key_lift, value_lift, key_lift_t, lo,
            seg_list, base_list, 2 * len(ks) - 2 if done else -1, state, done,
        )
        for j, k in enumerate(ks):
            total = outs[2 * j].astype(f32) + flip(outs[2 * j + 1], "heads", 0).astype(f32)
            if passing is not None:
                total = total + passing.astype(f32)
            passing = total.astype(bf16)
            if k > 0:
                passing = lax.ppermute(passing, "heads", down_chain)
        if done:
            query_grads, key_up_quads, value_up_quads = outs[2 * len(ks) :]
        else:
            state = outs[2 * len(ks)]
    latent_grads = passing

    query_back_mine = query_grads[:rows].reshape(count, group_width)
    query_back_got = swap(query_grads[rows:]).reshape(count, group_width)
    latent_back_mine = latent_grads[:rows].reshape(count, latent_size)
    latent_back_got = swap(latent_grads[rows:]).reshape(count, latent_size)
    query_sum = core_sum(
        (
            matmul_tn(normed_one, query_back_mine).astype(bf16),
            matmul_tn(normed_one, query_back_got).astype(bf16),
        )
    )
    latent_sum = core_sum(
        (
            matmul_tn(normed_one, latent_back_mine).astype(bf16),
            matmul_tn(normed_one, latent_back_got).astype(bf16),
        )
    )
    grad_one = (
        matmul_nt(query_back_mine, mine(query_weight, 1))
        + matmul_nt(query_back_got, theirs(query_weight, 1))
        + matmul_nt(latent_back_mine, mine(latent_weight, 1))
        + matmul_nt(latent_back_got, theirs(latent_weight, 1))
    )
    unit_one = inputs * inverse_one
    grad_in_norm, attn_gain_part = norm_back(grad_one, unit_one, inverse_one, attn_gain)
    hidden_grad = (grad_resid + grad_in_norm).reshape(rows, tokens, width)

    share = width // peers
    spread = lambda a: jnp.pad(a.astype(bf16).reshape(peers, 1, share), ((0, 0), (0, 7), (0, group_width - share)))
    gain_sum = add_sent(
        spread(jnp.where(core == 0, attn_gain_part, ffn_gain_part)),
        swap(spread(jnp.where(core == 0, ffn_gain_part, attn_gain_part))),
    )
    lift_share = latent_size // peers
    key_sum = quad_unlift(key_up_quads).astype(bf16).reshape(peers, lift_share, group_width)
    value_sum = quad_unlift(value_up_quads).astype(bf16).reshape(peers, lift_share, group_width)
    folded = latent_sum.reshape(peers, 2, latent_sum.shape[1] // 2, latent_sum.shape[2])
    latent_fold = jnp.concatenate([folded[:, 0], folded[:, 1]], axis=-1)
    late = reduce_rest(
        jnp.concatenate([query_sum, latent_fold, key_sum, value_sum, gain_sum], axis=1)
    )

    full = gather_columns(jnp.concatenate([early_one, early_two, late], axis=0)).astype(f32)
    at = 0

    def cut(size):
        nonlocal at
        piece = full[:, at : at + size]
        at += size
        return piece

    beside = lambda pair: jnp.concatenate([pair[0], pair[1]], axis=-1)
    ff_share = gate_weight.shape[1] // peers
    gate_share = beside(cut(ff_share)).T
    output_share = beside(cut(share))
    up_share = beside(cut(ff_share)).T
    down_share = beside(cut(ff_share))
    query_share = beside(cut(share))
    fold = cut(share // 2)
    latent_share = jnp.concatenate(
        [
            jnp.concatenate([fold[0, :, :latent_size], fold[1, :, :latent_size]], axis=-1),
            jnp.concatenate([fold[0, :, latent_size:], fold[1, :, latent_size:]], axis=-1),
        ],
        axis=0,
    )
    key_share = cut(lift_share)
    value_share = cut(lift_share)
    gains = cut(8)
    return (
        hidden_out.reshape(rows, tokens, width),
        hidden_grad,
        gains[0, 0, :share],
        query_share,
        latent_share,
        key_share,
        value_share,
        output_share,
        gains[1, 0, :share],
        gate_share,
        up_share,
        down_share,
    )


def solution(mesh):
    placed = (
        P("rows", "heads", None),
        P("rows", None),
        P("rows", "heads", None),
        P(),
        P(),
        P(),
        P(),
        P(),
        P(),
        P(),
        P(),
        P(),
        P(),
    )
    return jax.shard_map(
        shards,
        mesh=mesh,
        in_specs=placed,
        out_specs=(
            P("rows", "heads", None),
            P("rows", "heads", None),
            P("heads"),
            P("heads", None),
            P("heads", None),
            P(None, "heads", None),
            P(None, "heads", None),
            P("heads", None),
            P("heads"),
            P(None, "heads"),
            P(None, "heads"),
            P("heads", None),
        ),
        check_vma=False,
    )
```

time: 1710 us -> 753 us (0.44)
  waiting for transfers between devices: 640 us -> 232 us
  matrix products: 464 us -> 149 us
  blocking collectives: 226 us -> 0 us
  local copies, waits for them, and re-layouts: 168 us -> 25.2 us
  starting transfers between devices: 20.7 us -> 163 us
  Pallas kernels: 0 us -> 115 us
  other arithmetic: 118 us -> 52.1 us
  loops' own time: 38.1 us -> 0 us
    reduce_scatter x8 -> x0, waiting for transfers between devices: 390 us -> none  [the longest x1 113 us: shards(): lax.psum_scatter(up_part.astype(jnp.bfloat16), 'heads', scatter_dimension...]
    dot_general x234 -> x29, matrix products: 464 us -> 149 us  [the longest x12 55 us: matmul_tn(): lax.dot_general(left, right, (((0,), (0,)), ((), ())), preferred_element_...]
    ppermute x0 -> x42, waiting for transfers between devices: none -> 232 us  [the longest x36 114 us: flip(): return lax.ppermute(array, axis, [(i, i ^ 1 << bit) for i in range(size)])]
    all_to_all x4 -> x0, waiting for transfers between devices: 223 us -> none  [the longest x1 83.7 us: shards(): lax.all_to_all(copies, 'heads', split_axis=2, concat_axis=1, tiled=True)]
    all_to_all x2 -> x0, blocking collectives: 200 us -> none  [the longest x1 145 us: shards(): lax.all_to_all(latent_wide.astype(jnp.bfloat16), 'heads', split_axis=1, c...]
    ppermute x0 -> x42, starting transfers between devices: none -> 163 us  [the longest x36 143 us: flip(): return lax.ppermute(array, axis, [(i, i ^ 1 << bit) for i in range(size)])]
    pallas_call x0 -> x5, Pallas kernels: none -> 115 us  [the longest x3 82.6 us: attend_back_part(): pl.pallas_call(functools.partial(attend_back_kernel, len(segs), state is...]
    another operation x74 -> x0, loops' own time: 38.1 us -> none  [the longest x1 18.5 us: shards(): lax.map(attend_back, (head_queries, head_keys, head_values, head_out, hea...]
  transfers between devices with their start and end apart: 13 -> 42, of which waited for: 10 -> 17; matrix products, arithmetic and copies ran while one was open for 23% -> 15% of each run, Pallas kernels for 0% -> 14%
where the time goes in v1:
time: 753 us; the launch traced here: 739 us
  waiting for transfers between devices  232 us (31%)
  starting transfers between devices  163 us (22%)
  matrix products  149 us (20%)
  Pallas kernels  115 us (15%)
  other arithmetic  52.1 us (7%)
  local copies, waits for them, and re-layouts  25.2 us (3%)
    ppermute x36, starting transfers between devices, flip(): return lax.ppermute(array, axis, [(i, i ^ 1 << bit) for i in range(size)])  143 us
    ppermute x36, waiting for transfers between devices, flip(): return lax.ppermute(array, axis, [(i, i ^ 1 << bit) for i in range(size)])  114 us
    pallas_call x3, Pallas kernels, attend_back_part(): pl.pallas_call(functools.partial(attend_back_kernel, len(segs), state is...  82.6 us
    ppermute x3, waiting for transfers between devices, shards(): passing = lax.ppermute(passing, 'heads', down_chain)  79.6 us
    dot_general x12, matrix products, matmul_tn(): lax.dot_general(left, right, (((0,), (0,)), ((), ())), preferred_element_...  55 us
    dot_general x9, matrix products, matmul_nt(): lax.dot_general(left, right, (((left.ndim - 1,), (right.ndim - 1,)), ((),...  50.6 us
    dot_general x8, matrix products, matmul(): return jnp.dot(left, right, preferred_element_type=f32)  43.8 us
    ppermute x3, waiting for transfers between devices, shards(): moving = lax.ppermute(moving, 'heads', up_chain)  38 us
  transfers between devices with their start and end apart: 42, of which 17 were waited for; matrix products, arithmetic and copies ran while one was open for 15% of the time, Pallas kernels for 14%

profile of v1, /device:TPU:0, one launch (start us, length us, event | category | flops | bytes accessed | tf_op | source)
XLA Modules:
  0.0 739.4 jit_solution(4174789178673704128)
XLA Ops:
  12.1 5.5 collective-permute-start.3
  19.5 20.5 %collective-permute-done.3.refs_5_.refs_7_ = bf16[8,256,256]{2,1,0:T(8,128)(2,1)} collective-permute-done((bf16[8,256,256]{2,1,0:T(8,128)(2,1)}, bf16[8,256,256]{2,1,0:T(8,128)(2,1)}, u32[]{:S(2)}, u32[]{:S(2)}) %collective-permute-start.3) | collective-permute-done | bytes 1048608 | tf_op jit(solution)/shard_map/ppermute | solution.py:447
  40.0 5.4 collective-permute-start.4
  45.3 3.9 convolution_convert_fusion.10
  58.5 8.5 %collective-permute-done.4.refs_7_ = bf16[8,256,256]{2,1,0:T(8,128)(2,1)} collective-permute-done((bf16[8,256,256]{2,1,0:T(8,128)(2,1)}, bf16[8,256,256]{2,1,0:T(8,128)(2,1)}, u32[]{:S(2)}, u32[]{:S(2)}) %collective-permute-start.4) | collective-permute-done | bytes 1048608 | tf_op jit(solution)/shard_map/ppermute | solution.py:447
  68.5 5.4 collective-permute-start.5
  73.8 3.0 fusion.22
  76.9 2.4 copy.78.refs_2_.refs_5_
  79.4 2.8 convolution_convert_fusion.11
  82.4 2.8 pad_maximum_fusion
  85.2 9.1 %collective-permute-done.5.refs_3_.refs_7_ = bf16[8,256,256]{2,1,0:T(8,128)(2,1)} collective-permute-done((bf16[8,256,256]{2,1,0:T(8,128)(2,1)}, bf16[8,256,256]{2,1,0:T(8,128)(2,1)}, u32[]{:S(2)}, u32[]{:S(2)}) %collective-permute-start.5) | collective-permute-done | bytes 1048608 | tf_op jit(solution)/shard_map/ppermute | solution.py:447
  94.8 10.5 %collective-permute-done.8.refs_6_.refs_8_ = bf16[8,256,256]{2,1,0:T(8,128)(2,1)} collective-permute-done((bf16[8,256,256]{2,1,0:T(8,128)(2,1)}, bf16[8,256,256]{2,1,0:T(8,128)(2,1)}, u32[]{:S(2)}, u32[]{:S(2)}) %collective-permute-start.8) | collective-permute-done | bytes 1048608 | tf_op jit(solution)/shard_map/ppermute | solution.py:342
  105.3 22.5 %collective-permute-done.9.refs_8_ = bf16[8,256,256]{2,1,0:T(8,128)(2,1)} collective-permute-done((bf16[8,256,256]{2,1,0:T(8,128)(2,1)}, bf16[8,256,256]{2,1,0:T(8,128)(2,1)}, u32[]{:S(2)}, u32[]{:S(2)}) %collective-permute-start.9) | collective-permute-done | bytes 1048608 | tf_op jit(solution)/shard_map/ppermute | solution.py:342
  127.7 17.8 %attend.2 = (f32[8,8,256]{2,1,0:T(8,128)S(1)}, f32[8,8,256]{2,1,0:T(8,128)S(1)}, f32[8,8,256,256]{3,2,1,0:T(8,128)}) custom-call(s32[8]{0:T(128)S(1)} %fusion.98.lo, s32[6]{0:T(128)S(1)} %stack.63.bases, bf16[8,256,512]{2,1,0:T(8,128)(2,1)} %bitcast.258, s32[8,1,256]{2,1,0:T(1,128)S(1)} %broadcast_in_dim.2.refs_1_.refs_4_, ...), custom_call_target="tpu_custom_call" | custom-call | flops 25769803776 | bytes 16777216 | tf_op jit(solution)/shard_map/attend/pallas_call | solution.py:156
  145.5 3.6 collective-permute-done.6.refs_4_.refs_8_
  149.2 14.8 %attend.3 = (bf16[8,256,512]{2,1,0:T(8,128)(2,1)}, f32[8,8,256]{2,1,0:T(8,128)S(1)}, bf16[8,8,256,256]{3,2,1,0:T(8,128)(2,1)}) custom-call(s32[8]{0:T(128)S(1)} %fusion.98.lo, s32[2]{0:T(128)S(1)} %pad_add_fusion.1.bases, bf16[8,256,512]{2,1,0:T(8,128)(2,1)} %bitcast.259, s32[8,1,256]{2,1,0:T(1,128)S(1)} %broadcast_in_dim.2.refs_1_.refs_4_, ...), custom_call_target="tpu_custom_call" | custom-call | flops 8589934592 | bytes 16777216 | tf_op jit(solution)/shard_map/attend/pallas_call | solution.py:156
  163.9 3.0 fusion.110
  168.7 3.5 fusion.2
  172.3 4.8 multiply_reduce_fusion.2
  179.5 8.7 %fusion.113 = f32[1024,2816]{1,0:T(8,128)} fusion(bf16[1024,1024]{1,0:T(8,128)(2,1)S(1)} %multiply_convert_fusion.3, bf16[1024,2816]{1,0:T(8,128)(2,1)S(1)} %bitcast.299), kind=kOutput, calls=%fused_computation.258 | convolution fusion | flops 5905580032 | bytes 19398656 | tf_op jit(solution)/shard_map/dot_general | solution.py:22
  188.3 8.8 %fusion.112 = f32[1024,2816]{1,0:T(8,128)} fusion(bf16[1024,1024]{1,0:T(8,128)(2,1)S(1)} %multiply_convert_fusion.3, bf16[1024,2816]{1,0:T(8,128)(2,1)S(1)} %bitcast.297), kind=kOutput, calls=%fused_computation.257 | convolution fusion | flops 5905580032 | bytes 19398656 | tf_op jit(solution)/shard_map/dot_general | solution.py:22
  197.1 22.0 %multiply_convert_fusion = (bf16[1024,2816]{1,0:T(8,128)(2,1)}, bf16[1024,2816]{1,0:T(8,128)(2,1)}, bf16[1024,2816]{1,0:T(8,128)(2,1)}) fusion(f32[1024,2816]{1,0:T(8,128)} %fusion.112, f32[1024,2816]{1,0:T(8,128)} %fusion.113, bf16[1024,1024]{1,0:T(8,128)(2,1)} %fusion.2, bf16[2816,1024]{1,0:T(8,128)(2,1)} %param.25), kind=kOutput, calls=%fused_computation | convolution fusion | flops 5948833792 | bytes 48234496 | tf_op jit(solution)/shard_map/dot_general | solution.py:26
  219.1 7.9 %convolution_convert_fusion.4 = bf16[2816,512]{1,0:T(8,128)(2,1)} fusion(bf16[1024,2816]{1,0:T(8,128)(2,1)} %get-tuple-element.59, bf16[1024,1024]{1,0:T(8,128)(2,1)} %copy-done.22, s32[]{:T(128)S(6)} %select_n.281), kind=kOutput, calls=%fused_computation.20 | convolution fusion | flops 2954231808 | bytes 9699332 | tf_op jit(solution)/shard_map/dot_general | solution.py:32
  227.0 8.3 %fusion.114 = f32[1024,1024]{1,0:T(8,128)S(1)} fusion(bf16[1024,2816]{1,0:T(8,128)(2,1)S(1)} %copy-done.47, bf16[1024,2816]{1,0:T(8,128)(2,1)} %param.23), kind=kOutput, calls=%fused_computation.259 | convolution fusion | flops 5905580032 | bytes 15728640 | tf_op jit(solution)/shard_map/dot_general | solution.py:26
  235.4 9.6 %multiply_reduce_fusion = (bf16[1024]{0:T(1024)(128)(2,1)}, f32[1024]{0:T(1024)S(1)}, f32[1024,1024]{1,0:T(8,128)S(1)}) fusion(f32[1024,1024]{1,0:T(8,128)S(1)} %copy-done.9, f32[1024]{0:T(1024)S(1)} %add_rsqrt_fusion, f32[1024]{0:T(1024)S(1)} %copy-done.37, f32[1024,1024]{1,0:T(8,128)S(1)} %fusion.114, bf16[1024,2816]{1,0:T(8,128)(2,1)} %get-tuple-element.58, ...), kind=kOutput, calls=%fused_computation.42 | convolution fusion | flops 5912918016 | bytes 24131584 | tf_op jit(solution)/shard_map/dot_general | solution.py:26
  245.0 3.3 fusion.105
  248.3 4.0 convolution_convert_fusion.6
  252.4 3.1 convolution_convert_fusion.7
  257.0 4.8 convolution_convert_fusion
  264.1 4.6 convolution_convert_fusion.2
  268.7 3.0 collective-permute-done.11
  273.1 17.1 %attend_back.3 = (bf16[8,256,256]{2,1,0:T(8,128)(2,1)S(1)}, bf16[8,256,256]{2,1,0:T(8,128)(2,1)S(1)}, f32[8,8,256,256]{3,2,1,0:T(8,128)}) custom-call(s32[8]{0:T(128)S(1)} %fusion.98.lo, s32[2]{0:T(128)S(1)} %pad_add_fusion.1.bases, bf16[8,256,512]{2,1,0:T(8,128)(2,1)} %bitcast.260, bf16[8,256,512]{2,1,0:T(8,128)(2,1)} %bitcast.263, ...), custom_call_target="tpu_custom_call" | custom-call | flops 21474836480 | bytes 33554432 | tf_op jit(solution)/shard_map/attend_back/pallas_call | solution.py:288
  290.3 20.7 %attend_back.4 = (bf16[8,256,256]{2,1,0:T(8,128)(2,1)S(1)}, bf16[8,256,256]{2,1,0:T(8,128)(2,1)S(1)}, f32[8,8,256,256]{3,2,1,0:T(8,128)}) custom-call(s32[8]{0:T(128)S(1)} %fusion.98.lo, s32[2]{0:T(128)S(1)} %pad_add_fusion.3.bases, bf16[8,256,512]{2,1,0:T(8,128)(2,1)} %bitcast.261, bf16[8,256,512]{2,1,0:T(8,128)(2,1)} %bitcast.264, ...), custom_call_target="tpu_custom_call" | custom-call | flops 21474836480 | bytes 33554432 | tf_op jit(solution)/shard_map/attend_back/pallas_call | solution.py:288
  310.9 5.8 collective-permute-start.15
  316.8 44.8 %attend_back.5 = (bf16[8,256,256]{2,1,0:T(8,128)(2,1)S(1)}, bf16[8,256,256]{2,1,0:T(8,128)(2,1)S(1)}, bf16[8,256,256]{2,1,0:T(8,128)(2,1)S(1)}, bf16[8,256,256]{...) custom-call(s32[8]{0:T(128)S(1)} %fusion.98.lo, ...), custom_call_target="tpu_custom_call" | custom-call | flops 42949672960 | bytes 33554432 | tf_op jit(solution)/shard_map/attend_back/pallas_call | solution.py:288
  367.9 2.5 bitcast_convert_fusion
  371.7 24.2 %collective-permute-start.13 = (bf16[8,256,256]{2,1,0:T(8,128)(2,1)S(1)}, bf16[8,256,256]{2,1,0:T(8,128)(2,1)}, u32[]{:S(2)}, u32[]{:S(2)}) collective-permute-start(bf16[8,256,256]{2,1,0:T(8,128)(2,1)S(1)} %get-tuple-element.41), channel_id=1, source_target_pairs={{0,1},{1,0},{2,3},{3,2},{4,5},{5,4},{6,7},{7,6},{8,9},{9,8},{10,11... | collective-permute-start | bytes 3145736 | tf_op jit(solution)/shard_map/ppermute | solution.py:342
  395.9 44.4 %collective-permute-done.17 = bf16[8,256,256]{2,1,0:T(8,128)(2,1)S(1)} collective-permute-done((bf16[8,256,256]{2,1,0:T(8,128)(2,1)S(1)}, bf16[8,256,256]{2,1,0:T(8,128)(2,1)S(1)}, u32[]{:S(2)}, u32[]{:S(2)}) %collective-permute-start.17) | collective-permute-done | bytes 1048608 | tf_op jit(solution)/shard_map/ppermute | solution.py:539
  440.3 10.1 %collective-permute-start.14 = (bf16[8,256,256]{2,1,0:T(8,128)(2,1)S(1)}, bf16[8,256,256]{2,1,0:T(8,128)(2,1)S(1)}, u32[]{:S(2)}, u32[]{:S(2)}) collective-permute-start(bf16[8,256,256]{2,1,0:T(8,128)(2,1)S(1)} %get-tuple-element.43), channel_id=1, source_target_pairs={{0,1},{1,0},{2,3},{3,2},{4,5},{5,4},{6,7},{7,6},{8,9},{9,8},{10,11... | collective-permute-start | bytes 3145736 | tf_op jit(solution)/shard_map/ppermute | solution.py:342
  453.3 6.6 add_convert_fusion.3
  461.5 6.6 add_convert_fusion.1
  468.1 4.9 collective-permute-done.14
  473.0 9.2 %collective-permute-start.23 = (bf16[8,480,256]{2,1,0:T(8,128)(2,1)S(1)}, bf16[8,480,256]{2,1,0:T(8,128)(2,1)S(1)}, u32[]{:S(2)}, u32[]{:S(2)}) collective-permute-start(bf16[8,480,256]{2,1,0:T(8,128)(2,1)S(1)} %fusion.19), channel_id=1, source_target_pairs={{0,16},{8,24},{16,0},{24,8},{1,17},{9,25},{17,1},{25,9},{2,18},{10... | collective-permute-start | bytes 5898248 | tf_op jit(solution)/shard_map/ppermute | solution.py:342
  482.2 11.0 %collective-permute-done.18 = bf16[8,256,256]{2,1,0:T(8,128)(2,1)S(1)} collective-permute-done((bf16[8,256,256]{2,1,0:T(8,128)(2,1)S(1)}, bf16[8,256,256]{2,1,0:T(8,128)(2,1)S(1)}, u32[]{:S(2)}, u32[]{:S(2)}) %collective-permute-start.18) | collective-permute-done | bytes 1048608 | tf_op jit(solution)/shard_map/ppermute | solution.py:539
  495.9 6.8 add_convert_fusion.2
  502.9 7.4 %collective-permute-start.29 = (bf16[8,704,256]{2,1,0:T(8,128)(2,1)S(1)}, bf16[8,704,256]{2,1,0:T(8,128)(2,1)}, u32[]{:S(2)}, u32[]{:S(2)}) collective-permute-start(bf16[8,704,256]{2,1,0:T(8,128)(2,1)S(1)} %fusion.16), channel_id=1, source_target_pairs={{0,16},{8,24},{16,0},{24,8},{1,17},{9,25},{17,1},{25,9},{2,18},{10... | collective-permute-start | bytes 8650760 | tf_op jit(solution)/shard_map/ppermute | solution.py:342
  510.3 2.7 add_convert_fusion.7
  513.1 24.2 %collective-permute-done.19 = bf16[8,256,256]{2,1,0:T(8,128)(2,1)} collective-permute-done((bf16[8,256,256]{2,1,0:T(8,128)(2,1)}, bf16[8,256,256]{2,1,0:T(8,128)(2,1)}, u32[]{:S(2)}, u32[]{:S(2)}) %collective-permute-start.19) | collective-permute-done | bytes 1048608 | tf_op jit(solution)/shard_map/ppermute | solution.py:539
  544.0 2.9 fusion.26
  548.9 4.4 fusion.12
  553.7 32.1 %collective-permute-done.29 = bf16[8,704,256]{2,1,0:T(8,128)(2,1)} collective-permute-done((bf16[8,704,256]{2,1,0:T(8,128)(2,1)S(1)}, bf16[8,704,256]{2,1,0:T(8,128)(2,1)}, u32[]{:S(2)}, u32[]{:S(2)}) %collective-permute-start.29) | collective-permute-done | bytes 2883616 | tf_op jit(solution)/shard_map/ppermute | solution.py:342
  585.8 2.6 add_convert_fusion
  588.4 2.7 fusion.29
  598.8 14.6 %collective-permute-start.25 = (bf16[2,480,256]{2,1,0:T(8,128)(2,1)S(1)}, bf16[2,480,256]{2,1,0:T(8,128)(2,1)S(1)}, u32[]{:S(2)}, u32[]{:S(2)}) collective-permute-start(bf16[2,480,256]{2,1,0:T(8,128)(2,1)S(1)} %dynamic-slice_bitcast_fusion.4), channel_id=1, source_target_pairs={{0,2},{1,3},{2,0},{3,1},{4,6},{5,7},{6,4},{7,5},{8,10},{9,11},{10,... | collective-permute-start | bytes 1474568 | tf_op jit(solution)/shard_map/ppermute | solution.py:342
  613.4 3.2 collective-permute-done.36
  619.4 10.7 %collective-permute-done.30 = bf16[4,704,256]{2,1,0:T(8,128)(2,1)S(1)} collective-permute-done((bf16[4,704,256]{2,1,0:T(8,128)(2,1)}, bf16[4,704,256]{2,1,0:T(8,128)(2,1)S(1)}, u32[]{:S(2)}, u32[]{:S(2)}) %collective-permute-start.30) | collective-permute-done | bytes 1441824 | tf_op jit(solution)/shard_map/ppermute | solution.py:342
  630.6 14.6 %collective-permute-start.31 = (bf16[2,704,256]{2,1,0:T(8,128)(2,1)S(1)}, bf16[2,704,256]{2,1,0:T(8,128)(2,1)S(1)}, u32[]{:S(2)}, u32[]{:S(2)}) collective-permute-start(bf16[2,704,256]{2,1,0:T(8,128)(2,1)S(1)} %dynamic-slice_bitcast_fusion.2), channel_id=1, source_target_pairs={{0,2},{1,3},{2,0},{3,1},{4,6},{5,7},{6,4},{7,5},{8,10},{9,11},{10,... | collective-permute-start | bytes 2162696 | tf_op jit(solution)/shard_map/ppermute | solution.py:342
  645.3 17.0 %collective-permute-start.26 = (bf16[1,480,256]{2,1,0:T(8,128)(2,1)S(1)}, bf16[1,480,256]{2,1,0:T(8,128)(2,1)S(1)}, u32[]{:S(2)}, u32[]{:S(2)}) collective-permute-start(bf16[1,480,256]{2,1,0:T(8,128)(2,1)S(1)} %constant_dynamic-slice_fusion.3), channel_id=1, source_target_pairs={{0,4},{1,5},{2,6},{3,7},{4,0},{5,1},{6,2},{7,3},{8,12},{9,13},{10,... | collective-permute-start | bytes 737288 | tf_op jit(solution)/shard_map/ppermute | solution.py:342
  662.9 18.0 %collective-permute-start.32 = (bf16[1,704,256]{2,1,0:T(8,128)(2,1)S(1)}, bf16[1,704,256]{2,1,0:T(8,128)(2,1)S(1)}, u32[]{:S(2)}, u32[]{:S(2)}) collective-permute-start(bf16[1,704,256]{2,1,0:T(8,128)(2,1)S(1)} %constant_dynamic-slice_fusion.2), channel_id=1, source_target_pairs={{0,4},{1,5},{2,6},{3,7},{4,0},{5,1},{6,2},{7,3},{8,12},{9,13},{10,... | collective-permute-start | bytes 1081352 | tf_op jit(solution)/shard_map/ppermute | solution.py:342
  681.1 8.5 %collective-permute-start.39 = (bf16[1,264,256]{2,1,0:T(8,128)(2,1)S(1)}, bf16[1,264,256]{2,1,0:T(8,128)(2,1)S(1)}, u32[]{:S(2)}, u32[]{:S(2)}) collective-permute-start(bf16[1,264,256]{2,1,0:T(8,128)(2,1)S(1)} %constant_dynamic-slice_fusion), channel_id=1, source_target_pairs={{0,4},{1,5},{2,6},{3,7},{4,0},{5,1},{6,2},{7,3},{8,12},{9,13},{10,... | collective-permute-start | bytes 405512 | tf_op jit(solution)/shard_map/ppermute | solution.py:342
  689.5 7.7 %collective-permute-done.32 = bf16[1,704,256]{2,1,0:T(8,128)(2,1)S(1)} collective-permute-done((bf16[1,704,256]{2,1,0:T(8,128)(2,1)S(1)}, bf16[1,704,256]{2,1,0:T(8,128)(2,1)S(1)}, u32[]{:S(2)}, u32[]{:S(2)}) %collective-permute-start.32) | collective-permute-done | bytes 360480 | tf_op jit(solution)/shard_map/ppermute | solution.py:342
  700.4 14.8 %collective-permute-done.40 = bf16[1448,256]{1,0:T(8,128)(2,1)} collective-permute-done((bf16[1448,256]{1,0:T(8,128)(2,1)}, bf16[1448,256]{1,0:T(8,128)(2,1)}, u32[]{:S(2)}, u32[]{:S(2)}) %collective-permute-start.40) | collective-permute-done | bytes 741408 | tf_op jit(solution)/shard_map/ppermute | solution.py:342
  716.8 10.9 %add_convert_fusion.4 = bf16[1024,1024]{1,0:T(8,128)(2,1)} fusion(f32[1024,1024]{1,0:T(8,128)S(1)} %copy-done.10, bf16[1024,2816]{1,0:T(8,128)(2,1)} %get-tuple-element.60, bf16[2816,1024]{1,0:T(8,128)(2,1)} %param.25), kind=kOutput, calls=%fused_computation.45 | convolution fusion | flops 5907677184 | bytes 17825792 | tf_op jit(solution)/shard_map/dot_general | solution.py:22
  727.8 2.7 fusion.11
  (275 shorter events, 83.5 us)
Async XLA Ops:
  0.6 44.7 %copy-start = (bf16[1024,1024]{1,0:T(8,128)(2,1)S(1)}, bf16[1024,1024]{1,0:T(8,128)(2,1)}, u32[]{:S(2)}) copy-start(bf16[1024,1024]{1,0:T(8,128)(2,1)} %param.17) | copy-start | bytes 6291460
  7.2 2.8 collective-permute-start.2
  7.7 9.9 %copy-start.35 = (s32[4,2048]{1,0:T(4,128)S(1)}, s32[4,2048]{1,0:T(4,128)}, u32[]{:S(2)}) copy-start(s32[4,2048]{1,0:T(4,128)} %param.14) | copy-start | bytes 98308
  12.1 27.9 %collective-permute-start.3 = (bf16[8,256,256]{2,1,0:T(8,128)(2,1)}, bf16[8,256,256]{2,1,0:T(8,128)(2,1)}, u32[]{:S(2)}, u32[]{:S(2)}) collective-permute-start(bf16[8,256,256]{2,1,0:T(8,128)(2,1)} %bitcast.6.refs_3_.refs_9_), channel_id=1, source_target_pairs={{0,2},{1,3},{2,4},{3,5},{4,6},{5,7},{8,10},{9,11},{10,12},{11,13},... | collective-permute-start | bytes 3145736 | tf_op jit(solution)/shard_map/ppermute | solution.py:447
  40.0 27.0 %collective-permute-start.4 = (bf16[8,256,256]{2,1,0:T(8,128)(2,1)}, bf16[8,256,256]{2,1,0:T(8,128)(2,1)}, u32[]{:S(2)}, u32[]{:S(2)}) collective-permute-start(bf16[8,256,256]{2,1,0:T(8,128)(2,1)} %collective-permute-done.3.refs_5_.refs_7_), channel_id=1, source_target_pairs={{0,2},{1,3},{2,4},{3,5},{4,6},{5,7},{8,10},{9,11},{10,12},{11,13},... | collective-permute-start | bytes 3145736 | tf_op jit(solution)/shard_map/ppermute | solution.py:447
  45.3 23.1 %collective-permute-start = (s32[4,256]{1,0:T(4,128)S(1)}, s32[4,256]{1,0:T(4,128)S(1)}, u32[]{:S(2)}, u32[]{:S(2)}) collective-permute-start(s32[4,256]{1,0:T(4,128)S(1)} %broadcast_subtract_fusion), channel_id=1, source_target_pairs={{0,8},{8,0},{16,24},{24,16},{1,9},{9,1},{17,25},{25,17},{2,10},{10... | collective-permute-start | bytes 12296 | tf_op jit(solution)/shard_map/ppermute | solution.py:342
  49.2 33.2 %collective-permute-start.1 = (bf16[1024,512]{1,0:T(8,128)(2,1)}, bf16[1024,512]{1,0:T(8,128)(2,1)}, u32[]{:S(2)}, u32[]{:S(2)}) collective-permute-start(bf16[1024,512]{1,0:T(8,128)(2,1)} %convolution_convert_fusion.10), channel_id=1, source_target_pairs={{0,8},{8,0},{16,24},{24,16},{1,9},{9,1},{17,25},{25,17},{2,10},{10... | collective-permute-start | bytes 3145736 | tf_op jit(solution)/shard_map/ppermute | solution.py:342
  49.7 24.1 %copy-start.38 = (s32[256]{0:T(256)}, s32[256]{0:T(256)S(1)}, u32[]{:S(2)}) copy-start(s32[256]{0:T(256)S(1)} %get-tuple-element.127) | copy-start | bytes 3076
  49.7 24.1 %copy-start.40 = (s32[256]{0:T(256)}, s32[256]{0:T(256)S(1)}, u32[]{:S(2)}) copy-start(s32[256]{0:T(256)S(1)} %get-tuple-element.128) | copy-start | bytes 3076
  49.8 24.1 %copy-start.43 = (pred[256]{0:T(512)(128)(4,1)}, pred[256]{0:T(512)(128)(4,1)S(1)}, u32[]{:S(2)}) copy-start(pred[256]{0:T(512)(128)(4,1)S(1)} %compare_and_fusion) | copy-start | bytes 772
  56.4 38.3 %collective-permute-start.7 = (bf16[8,256,256]{2,1,0:T(8,128)(2,1)}, bf16[8,256,256]{2,1,0:T(8,128)(2,1)}, u32[]{:S(2)}, u32[]{:S(2)}) collective-permute-start(bf16[8,256,256]{2,1,0:T(8,128)(2,1)} %bitcast.6.refs_3_.refs_9_), channel_id=1, source_target_pairs={{0,1},{1,0},{2,3},{3,2},{4,5},{5,4},{6,7},{7,6},{8,9},{9,8},{10,11... | collective-permute-start | bytes 3145736 | tf_op jit(solution)/shard_map/ppermute | solution.py:342
  58.0 47.3 %collective-permute-start.8 = (bf16[8,256,256]{2,1,0:T(8,128)(2,1)}, bf16[8,256,256]{2,1,0:T(8,128)(2,1)}, u32[]{:S(2)}, u32[]{:S(2)}) collective-permute-start(bf16[8,256,256]{2,1,0:T(8,128)(2,1)} %collective-permute-done.3.refs_5_.refs_7_), channel_id=1, source_target_pairs={{0,1},{1,0},{2,3},{3,2},{4,5},{5,4},{6,7},{7,6},{8,9},{9,8},{10,11... | collective-permute-start | bytes 3145736 | tf_op jit(solution)/shard_map/ppermute | solution.py:342
  66.9 60.8 %collective-permute-start.9 = (bf16[8,256,256]{2,1,0:T(8,128)(2,1)}, bf16[8,256,256]{2,1,0:T(8,128)(2,1)}, u32[]{:S(2)}, u32[]{:S(2)}) collective-permute-start(bf16[8,256,256]{2,1,0:T(8,128)(2,1)} %collective-permute-done.4.refs_7_), channel_id=1, source_target_pairs={{0,1},{1,0},{2,3},{3,2},{4,5},{5,4},{6,7},{7,6},{8,9},{9,8},{10,11... | collective-permute-start | bytes 3145736 | tf_op jit(solution)/shard_map/ppermute | solution.py:342
  68.5 25.8 %collective-permute-start.5 = (bf16[8,256,256]{2,1,0:T(8,128)(2,1)}, bf16[8,256,256]{2,1,0:T(8,128)(2,1)}, u32[]{:S(2)}, u32[]{:S(2)}) collective-permute-start(bf16[8,256,256]{2,1,0:T(8,128)(2,1)} %collective-permute-done.4.refs_7_), channel_id=1, source_target_pairs={{0,2},{1,3},{2,4},{3,5},{4,6},{5,7},{8,10},{9,11},{10,12},{11,13},... | collective-permute-start | bytes 3145736 | tf_op jit(solution)/shard_map/ppermute | solution.py:447
  82.3 45.4 %copy-start.1 = (bf16[2,1024,256]{2,1,0:T(8,128)(2,1)S(1)}, bf16[2,1024,256]{2,1,0:T(8,128)(2,1)}, u32[]{:S(2)}) copy-start(bf16[2,1024,256]{2,1,0:T(8,128)(2,1)} %copy.78.refs_2_.refs_5_) | copy-start | bytes 3145732
  94.3 54.9 %collective-permute-start.6 = (bf16[8,256,256]{2,1,0:T(8,128)(2,1)}, bf16[8,256,256]{2,1,0:T(8,128)(2,1)S(1)}, u32[]{:S(2)}, u32[]{:S(2)}) collective-permute-start(bf16[8,256,256]{2,1,0:T(8,128)(2,1)} %collective-permute-done.5.refs_3_.refs_7_), channel_id=1, source_target_pairs={{0,1},{1,0},{2,3},{3,2},{4,5},{5,4},{6,7},{7,6},{8,9},{9,8},{10,11... | collective-permute-start | bytes 3145736 | tf_op jit(solution)/shard_map/ppermute | solution.py:342
  149.2 14.8 %copy-start.4 = (bf16[8,256,256]{2,1,0:T(8,128)(2,1)}, bf16[8,256,256]{2,1,0:T(8,128)(2,1)S(1)}, u32[]{:S(2)}) copy-start(bf16[8,256,256]{2,1,0:T(8,128)(2,1)S(1)} %collective-permute-done.6.refs_4_.refs_8_) | copy-start | bytes 3145732
  167.0 5.3 collective-permute-start.10
  168.7 10.8 %slice-start.2 = ((s8[5767168]{0:T(1024)(128)(4,1)}), s8[4194304]{0:T(1024)(128)(4,1)S(1)}, s32[]{:S(2)}) async-start(s8[5767168]{0:T(1024)(128)(4,1)} %bitcast.298), calls=%async_computation.2 | async-start | bytes 8388608
  179.1 9.2 %slice-start = ((s8[5767168]{0:T(1024)(128)(4,1)}), s8[4194304]{0:T(1024)(128)(4,1)S(1)}, s32[]{:S(2)}) async-start(s8[5767168]{0:T(1024)(128)(4,1)} %bitcast.296), calls=%async_computation | async-start | bytes 8388608
  179.5 8.8 %copy-start.22 = (bf16[1024,1024]{1,0:T(8,128)(2,1)}, bf16[1024,1024]{1,0:T(8,128)(2,1)S(1)}, u32[]{:S(2)}) copy-start(bf16[1024,1024]{1,0:T(8,128)(2,1)S(1)} %multiply_convert_fusion.3) | copy-start | bytes 6291460
  179.5 8.8 %slice-start.1 = ((s8[5767168]{0:T(1024)(128)(4,1)}), s8[1572864]{0:T(1024)(128)(4,1)S(1)}, s32[]{:S(2)}) async-start(s8[5767168]{0:T(1024)(128)(4,1)} %bitcast.296), calls=%async_computation.1 | async-start | bytes 3145728
  219.1 16.2 %slice-start.4 = ((s8[5767168]{0:T(1024)(128)(4,1)}), s8[4194304]{0:T(1024)(128)(4,1)S(1)}, s32[]{:S(2)}) async-start(s8[5767168]{0:T(1024)(128)(4,1)} %bitcast.300), calls=%async_computation.4 | async-start | bytes 8388608
  227.0 8.4 %slice-start.5 = ((s8[5767168]{0:T(1024)(128)(4,1)}), s8[1572864]{0:T(1024)(128)(4,1)S(1)}, s32[]{:S(2)}) async-start(s8[5767168]{0:T(1024)(128)(4,1)} %bitcast.300), calls=%async_computation.5 | async-start | bytes 3145728
  235.4 9.6 %copy-start.15 = (bf16[4,256,1024]{2,1,0:T(8,128)(2,1)S(1)}, bf16[4,256,1024]{2,1,0:T(8,128)(2,1)}, u32[]{:S(2)}) copy-start(bf16[4,256,1024]{2,1,0:T(8,128)(2,1)} %param.15) | copy-start | bytes 6291460
  248.3 8.4 %slice-start.6 = ((s8[5767168]{0:T(1024)(128)(4,1)}), s8[4194304]{0:T(1024)(128)(4,1)S(1)}, s32[]{:S(2)}) async-start(s8[5767168]{0:T(1024)(128)(4,1)} %bitcast.303), calls=%async_computation.6 | async-start | bytes 8388608
  261.8 198.3 %collective-permute-start.28 = (bf16[2816,512]{1,0:T(8,128)(2,1)}, bf16[2816,512]{1,0:T(8,128)(2,1)}, u32[]{:S(2)}, u32[]{:S(2)}) collective-permute-start(bf16[2816,512]{1,0:T(8,128)(2,1)} %convolution_convert_fusion), channel_id=1, source_target_pairs={{0,8},{8,0},{16,24},{24,16},{1,9},{9,1},{17,25},{25,17},{2,10},{10... | collective-permute-start | bytes 8650760 | tf_op jit(solution)/shard_map/ppermute | solution.py:342
  262.3 189.7 %collective-permute-start.21 = (bf16[2816,512]{1,0:T(8,128)(2,1)}, bf16[2816,512]{1,0:T(8,128)(2,1)}, u32[]{:S(2)}, u32[]{:S(2)}) collective-permute-start(bf16[2816,512]{1,0:T(8,128)(2,1)} %convolution_convert_fusion.4), channel_id=1, source_target_pairs={{0,8},{8,0},{16,24},{24,16},{1,9},{9,1},{17,25},{25,17},{2,10},{10... | collective-permute-start | bytes 8650760 | tf_op jit(solution)/shard_map/ppermute | solution.py:342
  262.3 9.4 %collective-permute-start.11 = (bf16[1024,512]{1,0:T(8,128)(2,1)S(1)}, bf16[1024,512]{1,0:T(8,128)(2,1)S(1)}, u32[]{:S(2)}, u32[]{:S(2)}) collective-permute-start(bf16[1024,512]{1,0:T(8,128)(2,1)S(1)} %convolution_convert_fusion.8), channel_id=1, source_target_pairs={{0,8},{8,0},{16,24},{24,16},{1,9},{9,1},{17,25},{25,17},{2,10},{10... | collective-permute-start | bytes 3145736 | tf_op jit(solution)/shard_map/ppermute | solution.py:342
  262.8 100.6 %collective-permute-start.22 = (bf16[1024,512]{1,0:T(8,128)(2,1)}, bf16[1024,512]{1,0:T(8,128)(2,1)S(1)}, u32[]{:S(2)}, u32[]{:S(2)}) collective-permute-start(bf16[1024,512]{1,0:T(8,128)(2,1)} %convolution_convert_fusion.6), channel_id=1, source_target_pairs={{0,8},{8,0},{16,24},{24,16},{1,9},{9,1},{17,25},{25,17},{2,10},{10... | collective-permute-start | bytes 3145736 | tf_op jit(solution)/shard_map/ppermute | solution.py:342
  310.9 60.8 %collective-permute-start.15 = (bf16[8,256,256]{2,1,0:T(8,128)(2,1)S(1)}, bf16[8,256,256]{2,1,0:T(8,128)(2,1)}, u32[]{:S(2)}, u32[]{:S(2)}) collective-permute-start(bf16[8,256,256]{2,1,0:T(8,128)(2,1)S(1)} %get-tuple-element.45), channel_id=1, source_target_pairs={{0,1},{1,0},{2,3},{3,2},{4,5},{5,4},{6,7},{7,6},{8,9},{9,8},{10,11... | collective-permute-start | bytes 3145736 | tf_op jit(solution)/shard_map/ppermute | solution.py:342
  316.7 48.5 %collective-permute-start.16 = (bf16[8,256,256]{2,1,0:T(8,128)(2,1)S(1)}, bf16[8,256,256]{2,1,0:T(8,128)(2,1)S(1)}, u32[]{:S(2)}, u32[]{:S(2)}) collective-permute-start(bf16[8,256,256]{2,1,0:T(8,128)(2,1)S(1)} %get-tuple-element.47), channel_id=1, source_target_pairs={{0,1},{1,0},{2,3},{3,2},{4,5},{5,4},{6,7},{7,6},{8,9},{9,8},{10,11... | collective-permute-start | bytes 3145736 | tf_op jit(solution)/shard_map/ppermute | solution.py:342
  363.4 4.4 collective-permute-start.12
  365.5 74.8 %collective-permute-start.17 = (bf16[8,256,256]{2,1,0:T(8,128)(2,1)S(1)}, bf16[8,256,256]{2,1,0:T(8,128)(2,1)S(1)}, u32[]{:S(2)}, u32[]{:S(2)}) collective-permute-start(bf16[8,256,256]{2,1,0:T(8,128)(2,1)S(1)} %add_convert_fusion.12), channel_id=1, source_target_pairs={{2,0},{3,1},{4,2},{5,3},{6,4},{7,5},{10,8},{11,9},{12,10},{13,11},... | collective-permute-start | bytes 3145736 | tf_op jit(solution)/shard_map/ppermute | solution.py:539
  367.8 128.1 %collective-permute-start.27 = (bf16[2816,512]{1,0:T(8,128)(2,1)}, bf16[2816,512]{1,0:T(8,128)(2,1)}, u32[]{:S(2)}, u32[]{:S(2)}) collective-permute-start(bf16[2816,512]{1,0:T(8,128)(2,1)} %convolution_convert_fusion.2), channel_id=1, source_target_pairs={{0,8},{8,0},{16,24},{24,16},{1,9},{9,1},{17,25},{25,17},{2,10},{10... | collective-permute-start | bytes 8650760 | tf_op jit(solution)/shard_map/ppermute | solution.py:342
  371.7 81.6 %copy-start.24 = (bf16[1024,1024]{1,0:T(8,128)(2,1)S(1)}, bf16[1024,1024]{1,0:T(8,128)(2,1)}, u32[]{:S(2)}) copy-start(bf16[1024,1024]{1,0:T(8,128)(2,1)} %copy-done.22) | copy-start | bytes 6291460
  371.7 141.3 %collective-permute-start.13 = (bf16[8,256,256]{2,1,0:T(8,128)(2,1)S(1)}, bf16[8,256,256]{2,1,0:T(8,128)(2,1)}, u32[]{:S(2)}, u32[]{:S(2)}) collective-permute-start(bf16[8,256,256]{2,1,0:T(8,128)(2,1)S(1)} %get-tuple-element.41), channel_id=1, source_target_pairs={{0,1},{1,0},{2,3},{3,2},{4,5},{5,4},{6,7},{7,6},{8,9},{9,8},{10,11... | collective-permute-start | bytes 3145736 | tf_op jit(solution)/shard_map/ppermute | solution.py:342
  440.3 32.7 %collective-permute-start.14 = (bf16[8,256,256]{2,1,0:T(8,128)(2,1)S(1)}, bf16[8,256,256]{2,1,0:T(8,128)(2,1)S(1)}, u32[]{:S(2)}, u32[]{:S(2)}) collective-permute-start(bf16[8,256,256]{2,1,0:T(8,128)(2,1)S(1)} %get-tuple-element.43), channel_id=1, source_target_pairs={{0,1},{1,0},{2,3},{3,2},{4,5},{5,4},{6,7},{7,6},{8,9},{9,8},{10,11... | collective-permute-start | bytes 3145736 | tf_op jit(solution)/shard_map/ppermute | solution.py:342
  452.0 41.2 %collective-permute-start.18 = (bf16[8,256,256]{2,1,0:T(8,128)(2,1)S(1)}, bf16[8,256,256]{2,1,0:T(8,128)(2,1)S(1)}, u32[]{:S(2)}, u32[]{:S(2)}) collective-permute-start(bf16[8,256,256]{2,1,0:T(8,128)(2,1)S(1)} %add_convert_fusion.11), channel_id=1, source_target_pairs={{2,0},{3,1},{4,2},{5,3},{6,4},{7,5},{10,8},{11,9},{12,10},{13,11},... | collective-permute-start | bytes 3145736 | tf_op jit(solution)/shard_map/ppermute | solution.py:539
  460.1 50.2 %collective-permute-start.33 = (bf16[1024,512]{1,0:T(8,128)(2,1)}, bf16[1024,512]{1,0:T(8,128)(2,1)}, u32[]{:S(2)}, u32[]{:S(2)}) collective-permute-start(bf16[1024,512]{1,0:T(8,128)(2,1)} %bitcast_convert_fusion), channel_id=1, source_target_pairs={{0,8},{8,0},{16,24},{24,16},{1,9},{9,1},{17,25},{25,17},{2,10},{10... | collective-permute-start | bytes 3145736 | tf_op jit(solution)/shard_map/ppermute | solution.py:342
  473.0 67.0 %collective-permute-start.23 = (bf16[8,480,256]{2,1,0:T(8,128)(2,1)S(1)}, bf16[8,480,256]{2,1,0:T(8,128)(2,1)S(1)}, u32[]{:S(2)}, u32[]{:S(2)}) collective-permute-start(bf16[8,480,256]{2,1,0:T(8,128)(2,1)S(1)} %fusion.19), channel_id=1, source_target_pairs={{0,16},{8,24},{16,0},{24,8},{1,17},{9,25},{17,1},{25,9},{2,18},{10... | collective-permute-start | bytes 5898248 | tf_op jit(solution)/shard_map/ppermute | solution.py:342
  494.6 42.7 %collective-permute-start.19 = (bf16[8,256,256]{2,1,0:T(8,128)(2,1)}, bf16[8,256,256]{2,1,0:T(8,128)(2,1)}, u32[]{:S(2)}, u32[]{:S(2)}) collective-permute-start(bf16[8,256,256]{2,1,0:T(8,128)(2,1)} %add_convert_fusion.10), channel_id=1, source_target_pairs={{2,0},{3,1},{4,2},{5,3},{6,4},{7,5},{10,8},{11,9},{12,10},{13,11},... | collective-permute-start | bytes 3145736 | tf_op jit(solution)/shard_map/ppermute | solution.py:539
  502.9 82.9 %collective-permute-start.29 = (bf16[8,704,256]{2,1,0:T(8,128)(2,1)S(1)}, bf16[8,704,256]{2,1,0:T(8,128)(2,1)}, u32[]{:S(2)}, u32[]{:S(2)}) collective-permute-start(bf16[8,704,256]{2,1,0:T(8,128)(2,1)S(1)} %fusion.16), channel_id=1, source_target_pairs={{0,16},{8,24},{16,0},{24,8},{1,17},{9,25},{17,1},{25,9},{2,18},{10... | collective-permute-start | bytes 8650760 | tf_op jit(solution)/shard_map/ppermute | solution.py:342
  540.1 3.9 collective-permute-start.20
  541.8 55.1 %collective-permute-start.24 = (bf16[4,480,256]{2,1,0:T(8,128)(2,1)}, bf16[4,480,256]{2,1,0:T(8,128)(2,1)}, u32[]{:S(2)}, u32[]{:S(2)}) collective-permute-start(bf16[4,480,256]{2,1,0:T(8,128)(2,1)} %dynamic-slice_bitcast_fusion.1), channel_id=1, source_target_pairs={{0,1},{1,0},{2,3},{3,2},{4,5},{5,4},{6,7},{7,6},{8,9},{9,8},{10,11... | collective-permute-start | bytes 2949128 | tf_op jit(solution)/shard_map/ppermute | solution.py:342
  546.9 41.5 %collective-permute-start.34 = (bf16[1024,256]{1,0:T(8,128)(2,1)}, bf16[1024,256]{1,0:T(8,128)(2,1)}, u32[]{:S(2)}, u32[]{:S(2)}) collective-permute-start(bf16[1024,256]{1,0:T(8,128)(2,1)} %fusion.26), channel_id=1, source_target_pairs={{0,8},{8,0},{16,24},{24,16},{1,9},{9,1},{17,25},{25,17},{2,10},{10... | collective-permute-start | bytes 1572872 | tf_op jit(solution)/shard_map/ppermute | solution.py:342
  553.3 35.0 %collective-permute-start.35 = (bf16[8,8,512]{2,0,1:T(8,128)(2,1)S(1)}, bf16[8,8,512]{2,0,1:T(8,128)(2,1)S(1)}, u32[]{:S(2)}, u32[]{:S(2)}) collective-permute-start(bf16[8,8,512]{2,0,1:T(8,128)(2,1)S(1)} %pad.8), channel_id=1, source_target_pairs={{0,8},{8,0},{16,24},{24,16},{1,9},{9,1},{17,25},{25,17},{2,10},{10... | collective-permute-start | bytes 196616 | tf_op jit(solution)/shard_map/ppermute | solution.py:342
  592.4 24.1 %collective-permute-start.36 = (bf16[8,264,256]{2,1,0:T(8,128)(2,1)}, bf16[8,264,256]{2,1,0:T(8,128)(2,1)}, u32[]{:S(2)}, u32[]{:S(2)}) collective-permute-start(bf16[8,264,256]{2,1,0:T(8,128)(2,1)} %constant_dynamic-slice_fusion.1), channel_id=1, source_target_pairs={{0,16},{8,24},{16,0},{24,8},{1,17},{9,25},{17,1},{25,9},{2,18},{10... | collective-permute-start | bytes 3244040 | tf_op jit(solution)/shard_map/ppermute | solution.py:342
  595.4 34.7 %collective-permute-start.30 = (bf16[4,704,256]{2,1,0:T(8,128)(2,1)}, bf16[4,704,256]{2,1,0:T(8,128)(2,1)S(1)}, u32[]{:S(2)}, u32[]{:S(2)}) collective-permute-start(bf16[4,704,256]{2,1,0:T(8,128)(2,1)} %dynamic-slice_bitcast_fusion), channel_id=1, source_target_pairs={{0,1},{1,0},{2,3},{3,2},{4,5},{5,4},{6,7},{7,6},{8,9},{9,8},{10,11... | collective-permute-start | bytes 4325384 | tf_op jit(solution)/shard_map/ppermute | solution.py:342
  596.8 19.8 %copy-start.18 = (bf16[8,264,512]{2,1,0:T(8,128)(2,1)S(1)}, bf16[8,264,512]{2,1,0:T(8,128)(2,1)}, u32[]{:S(2)}) copy-start(bf16[8,264,512]{2,1,0:T(8,128)(2,1)} %copy-done.17) | copy-start | bytes 6488068
  598.7 31.4 %copy-start.14 = (bf16[8,704,256]{2,1,0:T(8,128)(2,1)S(1)}, bf16[8,704,256]{2,1,0:T(8,128)(2,1)}, u32[]{:S(2)}) copy-start(bf16[8,704,256]{2,1,0:T(8,128)(2,1)} %copy-done.13) | copy-start | bytes 8650756
  598.8 46.4 %collective-permute-start.25 = (bf16[2,480,256]{2,1,0:T(8,128)(2,1)S(1)}, bf16[2,480,256]{2,1,0:T(8,128)(2,1)S(1)}, u32[]{:S(2)}, u32[]{:S(2)}) collective-permute-start(bf16[2,480,256]{2,1,0:T(8,128)(2,1)S(1)} %dynamic-slice_bitcast_fusion.4), channel_id=1, source_target_pairs={{0,2},{1,3},{2,0},{3,1},{4,6},{5,7},{6,4},{7,5},{8,10},{9,11},{10,... | collective-permute-start | bytes 1474568 | tf_op jit(solution)/shard_map/ppermute | solution.py:342
  618.2 44.2 %collective-permute-start.37 = (bf16[4,264,256]{2,1,0:T(8,128)(2,1)S(1)}, bf16[4,264,256]{2,1,0:T(8,128)(2,1)S(1)}, u32[]{:S(2)}, u32[]{:S(2)}) collective-permute-start(bf16[4,264,256]{2,1,0:T(8,128)(2,1)S(1)} %dynamic-slice_bitcast_fusion.3), channel_id=1, source_target_pairs={{0,1},{1,0},{2,3},{3,2},{4,5},{5,4},{6,7},{7,6},{8,9},{9,8},{10,11... | collective-permute-start | bytes 1622024 | tf_op jit(solution)/shard_map/ppermute | solution.py:342
  630.6 32.1 %collective-permute-start.31 = (bf16[2,704,256]{2,1,0:T(8,128)(2,1)S(1)}, bf16[2,704,256]{2,1,0:T(8,128)(2,1)S(1)}, u32[]{:S(2)}, u32[]{:S(2)}) collective-permute-start(bf16[2,704,256]{2,1,0:T(8,128)(2,1)S(1)} %dynamic-slice_bitcast_fusion.2), channel_id=1, source_target_pairs={{0,2},{1,3},{2,0},{3,1},{4,6},{5,7},{6,4},{7,5},{8,10},{9,11},{10,... | collective-permute-start | bytes 2162696 | tf_op jit(solution)/shard_map/ppermute | solution.py:342
  645.3 35.6 %collective-permute-start.26 = (bf16[1,480,256]{2,1,0:T(8,128)(2,1)S(1)}, bf16[1,480,256]{2,1,0:T(8,128)(2,1)S(1)}, u32[]{:S(2)}, u32[]{:S(2)}) collective-permute-start(bf16[1,480,256]{2,1,0:T(8,128)(2,1)S(1)} %constant_dynamic-slice_fusion.3), channel_id=1, source_target_pairs={{0,4},{1,5},{2,6},{3,7},{4,0},{5,1},{6,2},{7,3},{8,12},{9,13},{10,... | collective-permute-start | bytes 737288 | tf_op jit(solution)/shard_map/ppermute | solution.py:342
  662.6 18.4 %collective-permute-start.38 = (bf16[2,264,256]{2,1,0:T(8,128)(2,1)S(1)}, bf16[2,264,256]{2,1,0:T(8,128)(2,1)S(1)}, u32[]{:S(2)}, u32[]{:S(2)}) collective-permute-start(bf16[2,264,256]{2,1,0:T(8,128)(2,1)S(1)} %dynamic-slice_bitcast_fusion.5), channel_id=1, source_target_pairs={{0,2},{1,3},{2,0},{3,1},{4,6},{5,7},{6,4},{7,5},{8,10},{9,11},{10,... | collective-permute-start | bytes 811016 | tf_op jit(solution)/shard_map/ppermute | solution.py:342
  662.9 34.3 %collective-permute-start.32 = (bf16[1,704,256]{2,1,0:T(8,128)(2,1)S(1)}, bf16[1,704,256]{2,1,0:T(8,128)(2,1)S(1)}, u32[]{:S(2)}, u32[]{:S(2)}) collective-permute-start(bf16[1,704,256]{2,1,0:T(8,128)(2,1)S(1)} %constant_dynamic-slice_fusion.2), channel_id=1, source_target_pairs={{0,4},{1,5},{2,6},{3,7},{4,0},{5,1},{6,2},{7,3},{8,12},{9,13},{10,... | collective-permute-start | bytes 1081352 | tf_op jit(solution)/shard_map/ppermute | solution.py:342
  681.1 17.6 %collective-permute-start.39 = (bf16[1,264,256]{2,1,0:T(8,128)(2,1)S(1)}, bf16[1,264,256]{2,1,0:T(8,128)(2,1)S(1)}, u32[]{:S(2)}, u32[]{:S(2)}) collective-permute-start(bf16[1,264,256]{2,1,0:T(8,128)(2,1)S(1)} %constant_dynamic-slice_fusion), channel_id=1, source_target_pairs={{0,4},{1,5},{2,6},{3,7},{4,0},{5,1},{6,2},{7,3},{8,12},{9,13},{10,... | collective-permute-start | bytes 405512 | tf_op jit(solution)/shard_map/ppermute | solution.py:342
  699.6 15.6 %collective-permute-start.40 = (bf16[1448,256]{1,0:T(8,128)(2,1)}, bf16[1448,256]{1,0:T(8,128)(2,1)}, u32[]{:S(2)}, u32[]{:S(2)}) collective-permute-start(bf16[1448,256]{1,0:T(8,128)(2,1)} %pad_maximum_fusion.5), channel_id=1, source_target_pairs={{0,16},{8,24},{16,0},{24,8},{1,17},{9,25},{17,1},{25,9},{2,18},{10... | collective-permute-start | bytes 2224136 | tf_op jit(solution)/shard_map/ppermute | solution.py:342
  700.4 16.4 %copy-start.10 = (f32[1024,1024]{1,0:T(8,128)S(1)}, f32[1024,1024]{1,0:T(8,128)}, u32[]{:S(2)}) copy-start(f32[1024,1024]{1,0:T(8,128)} %copy-done.8) | copy-start | bytes 12582916
  716.7 11.0 %copy-start.7 = (bf16[4,256,1024]{2,1,0:T(8,128)(2,1)S(1)}, bf16[4,256,1024]{2,1,0:T(8,128)(2,1)}, u32[]{:S(2)}) copy-start(bf16[4,256,1024]{2,1,0:T(8,128)(2,1)} %param.13) | copy-start | bytes 6291460
  716.7 13.7 %collective-permute-start.41 = (bf16[1448,512]{1,0:T(8,128)(2,1)S(1)}, bf16[1448,512]{1,0:T(8,128)(2,1)S(1)}, u32[]{:S(2)}, u32[]{:S(2)}) collective-permute-start(bf16[1448,512]{1,0:T(8,128)(2,1)S(1)} %pad_maximum_fusion.2), channel_id=1, source_target_pairs={{0,8},{8,0},{16,24},{24,16},{1,9},{9,1},{17,25},{25,17},{2,10},{10... | collective-permute-start | bytes 4448264 | tf_op jit(solution)/shard_map/ppermute | solution.py:342
  716.8 10.9 %copy-start.11 = (f32[1024,1024]{1,0:T(8,128)S(1)}, f32[1024,1024]{1,0:T(8,128)}, u32[]{:S(2)}) copy-start(f32[1024,1024]{1,0:T(8,128)} %get-tuple-element.55) | copy-start | bytes 12582916
  716.8 10.9 %copy-start.12 = (f32[1024,1024]{1,0:T(8,128)S(1)}, f32[1024,1024]{1,0:T(8,128)}, u32[]{:S(2)}) copy-start(f32[1024,1024]{1,0:T(8,128)} %get-tuple-element.120) | copy-start | bytes 12582916
  (36 other events, 144.8 us)

commit v2 on v1

--- a/solution.py
+++ b/solution.py
@@ -337,6 +337,162 @@
     return jnp.concatenate(parts, axis=1)
 
 
+def feed_kernel(core_ref, *refs):
+    (
+        inputs_ref, mine_ref, got_ref, output_ref, gain_ref, cotangent_ref, keep_ref,
+        gate_t_ref, up_t_ref, down_ref, gate_ref, up_ref, down_t_ref,
+        hidden_out_ref, grad_resid_ref, attn_back_ref, head_mine_ref, head_sent_ref, gain_grad_ref,
+        grads_ref,
+        normed, normed_t, back, back_t, resid, inverse, result_t, grad_t, staged, staged_out, sems, out_sem,
+    ) = refs
+    step = pl.program_id(0)
+    steps = pl.num_programs(0)
+    count, width = inputs_ref.shape
+    pieces, _, piece = grads_ref.shape
+    chunk = gate_t_ref.shape[0]
+    ff = down_t_ref.shape[1] * steps
+    block = min(256, count)
+    core = core_ref[0]
+    slot = step % 2
+
+    def put(ref, value, at=0):
+        for j in range(pieces):
+            ref[j, pl.ds(at, value.shape[0])] = value[:, j * piece : (j + 1) * piece].astype(bf16)
+
+    def leave(at, kind, place):
+        return pltpu.make_async_copy(
+            staged.at[at, kind],
+            grads_ref.at[:, pl.ds(pl.multiple_of(kind * ff + place * chunk, chunk), chunk)],
+            sems.at[at, kind],
+        )
+
+    @pl.when(step >= 2)
+    def _():
+        for kind in range(3):
+            leave(slot, kind, step - 2).wait()
+
+    @pl.when(step == 0)
+    def _():
+        for t in range(0, count, block):
+            at = slice(t, t + block)
+            row = inputs_ref[at].astype(f32) + (
+                matmul(mine_ref[at], output_ref[core]) + matmul(got_ref[at], output_ref[1 - core])
+            )
+            resid[at] = row
+            scale = lax.rsqrt(jnp.mean(row * row, axis=-1, keepdims=True) + epsilon)
+            inverse[at] = scale
+            unit = (row * scale * gain_ref[...]).astype(bf16)
+            normed[at] = unit
+            normed_t[:, at] = unit.T
+            kept = (cotangent_ref[at].astype(f32) * keep_ref[at]).astype(bf16)
+            back[at] = kept
+            back_t[:, at] = kept.T
+        result_t[...] = jnp.zeros_like(result_t)
+        grad_t[...] = jnp.zeros_like(grad_t)
+
+    gate = matmul(gate_t_ref[...], normed_t[...])
+    up = matmul(up_t_ref[...], normed_t[...])
+    grad_act = matmul(down_ref[...], back_t[...])
+    sigmoid = 1.0 / (1.0 + jnp.exp(-gate))
+    active = gate * sigmoid
+    hidden = (active * up).astype(bf16)
+    up_back = (grad_act * active).astype(bf16)
+    gate_back = (grad_act * up * (sigmoid * (1.0 + gate * (1.0 - sigmoid)))).astype(bf16)
+    put(staged.at[slot, 2], matmul(hidden, back[...]))
+    put(staged.at[slot, 1], matmul(up_back, normed[...]))
+    put(staged.at[slot, 0], matmul(gate_back, normed[...]))
+    for kind in range(3):
+        leave(slot, kind, step).start()
+    result_t[...] += matmul(down_t_ref[...], hidden)
+    grad_t[...] += matmul(gate_ref[...], gate_back) + matmul(up_ref[...], up_back)
+
+    @pl.when(step == steps - 1)
+    def _():
+        gain_total = jnp.zeros((1, width), f32)
+        for t in range(0, count, block):
+            at = slice(t, t + block)
+            row = resid[at]
+            hidden_out_ref[at] = (row + result_t[:, at].T).astype(bf16)
+            scale = inverse[at]
+            unit = row * scale
+            grad = grad_t[:, at].T
+            gain_total += jnp.sum(grad * unit, axis=0, keepdims=True)
+            scaled = grad * gain_ref[...]
+            grad = back[at].astype(f32) + scale * (
+                scaled - unit * jnp.mean(scaled * unit, axis=-1, keepdims=True)
+            )
+            grad_resid_ref[at] = grad
+            low = grad.astype(bf16)
+            attn_back_ref[at] = low
+            head_mine_ref[at] = matmul_nt(low, output_ref[core]).astype(bf16)
+            head_sent_ref[at] = matmul_nt(low, output_ref[1 - core]).astype(bf16)
+        gain_grad_ref[...] = gain_total
+        half = mine_ref.shape[1]
+        put(staged_out, matmul_tn(mine_ref[...], attn_back_ref[...]), core * half)
+        put(staged_out, matmul_tn(got_ref[...], attn_back_ref[...]), (1 - core) * half)
+        last = pltpu.make_async_copy(staged_out, grads_ref.at[:, pl.ds(3 * ff, width)], out_sem)
+        last.start()
+        for kind in range(3):
+            leave(1 - slot, kind, step - 1).wait()
+            leave(slot, kind, step).wait()
+        last.wait()
+
+
+def feed(core, inputs, mixed_mine, mixed_got, output_weight, gain, cotangent, keep, weights, pieces):
+    count, width = inputs.shape
+    ff = weights[0].shape[0]
+    chunk = 256
+    piece = width // pieces
+    output_weight = output_weight.reshape(2, -1, width)
+    once = lambda a: pl.BlockSpec(a.shape, lambda *_: (0,) * len(a.shape), pipeline_mode=pl.Buffered(1))
+    by_rows = pl.BlockSpec((chunk, width), lambda c, *_: (c, 0))
+    by_columns = pl.BlockSpec((width, chunk), lambda c, *_: (0, c))
+    shape = jax.ShapeDtypeStruct
+    firsts = [inputs, mixed_mine, mixed_got, output_weight, gain.reshape(1, width), cotangent, keep]
+    outs = [
+        shape((count, width), bf16),
+        shape((count, width), f32),
+        shape((count, width), bf16),
+        shape(mixed_mine.shape, bf16),
+        shape(mixed_mine.shape, bf16),
+        shape((1, width), f32),
+        shape((pieces, 3 * ff + width, piece), bf16),
+    ]
+    return pl.pallas_call(
+        feed_kernel,
+        out_shape=outs,
+        grid_spec=pltpu.PrefetchScalarGridSpec(
+            num_scalar_prefetch=1,
+            grid=(ff // chunk,),
+            in_specs=[once(a) for a in firsts] + [by_rows] * 3 + [by_columns] * 3,
+            out_specs=[once(o) for o in outs[:6]] + [pl.BlockSpec(memory_space=pl.ANY)],
+            scratch_shapes=[
+                pltpu.VMEM((count, width), bf16),
+                pltpu.VMEM((width, count), bf16),
+                pltpu.VMEM((count, width), bf16),
+                pltpu.VMEM((width, count), bf16),
+                pltpu.VMEM((count, width), f32),
+                pltpu.VMEM((count, 1), f32),
+                pltpu.VMEM((width, count), f32),
+                pltpu.VMEM((width, count), f32),
+                pltpu.VMEM((2, 3, pieces, chunk, piece), bf16),
+                pltpu.VMEM((pieces, width, piece), bf16),
+                pltpu.SemaphoreType.DMA((2, 3)),
+                pltpu.SemaphoreType.DMA,
+            ],
+        ),
+        compiler_params=pltpu.CompilerParams(
+            dimension_semantics=("arbitrary",), vmem_limit_bytes=60 << 20
+        ),
+        cost_estimate=pl.CostEstimate(
+            flops=count * width * (ff * 18 + width * 6),
+            bytes_accessed=width * ff * 18 + count * width * 16,
+            transcendentals=count * ff,
+        ),
+        name="feed",
+    )(core.reshape(1), *firsts, *weights)
+
+
 def flip(array, axis, bit):
     size = lax.axis_size(axis)
     return lax.ppermute(array, axis, [(i, i ^ (1 << bit)) for i in range(size)])
@@ -346,36 +502,263 @@
     return (mine.astype(f32) + other.astype(f32)).astype(bf16)
 
 
-def reduce_rest(part):
-    row_bits = lax.axis_size("rows").bit_length() - 1
-    head_bits = lax.axis_size("heads").bit_length() - 1
+def finish_kernel(
+    shares, early_ref, own_ref, sent_ref, out_ref, late_got, late_from, got_first, got_next,
+    core_sems, along_sems, first_sems, first_late_sems, next_sems, out_sems,
+):
+    along, count, late_rows, piece = own_ref.shape
+    shared_rows = sent_ref.shape[2]
+    early_rows = sum(shares)
+    bits = count.bit_length() - 1
     row_at = lax.axis_index("rows")
-    head_at = lax.axis_index("heads")
-    for bit in range(1, row_bits):
-        mine = (row_at >> bit) & 1
-        half = part.shape[-1] // 2
-        keep = lax.dynamic_slice_in_dim(part, mine * half, half, 2)
-        send = lax.dynamic_slice_in_dim(part, (1 - mine) * half, half, 2)
-        part = add_sent(keep, flip(send, "rows", bit))
-    for bit in range(head_bits):
-        mine = (head_at >> bit) & 1
-        pairs = part.reshape((part.shape[0] // 2, 2) + part.shape[1:])
-        keep = lax.dynamic_index_in_dim(pairs, mine, 1, keepdims=False)
-        send = lax.dynamic_index_in_dim(pairs, 1 - mine, 1, keepdims=False)
-        part = add_sent(keep, flip(send, "heads", bit))
-    return part[0]
-
-
-def gather_columns(part):
-    row_bits = lax.axis_size("rows").bit_length() - 1
-    row_at = lax.axis_index("rows")
-    for bit in reversed(range(row_bits)):
-        mine = (row_at >> bit) & 1
-        other = flip(part, "rows", bit)
-        low = jnp.where(mine == 0, part, other)
-        high = jnp.where(mine == 0, other, part)
-        part = jnp.stack([low, high]) if bit == 0 else jnp.concatenate([low, high], axis=1)
-    return part
+    place = lax.axis_index("heads")
+    core = row_at % 2
+    x_at = row_at // 2
+    mesh = pl.DeviceIdType.MESH
+    early_part = slice(0, early_rows)
+    late_part = slice(early_rows, early_rows + late_rows)
+
+    def turned(which):
+        at = place
+        for bit in which:
+            at = at + (1 << bit) * (1 - 2 * ((place // (1 << bit)) % 2))
+        return at
+
+    core_peer = (row_at + 1 - 2 * core, place)
+    x_others = [(x_at + d) % along for d in range(1, along)]
+    x_peers = [(x * 2 + core, place) for x in x_others]
+    head_peers = [(row_at, turned([bit])) for bit in range(bits)]
+    barrier = pltpu.get_barrier_semaphore()
+    everyone = [core_peer] + x_peers + head_peers
+    for peer in everyone:
+        pl.semaphore_signal(barrier, inc=1, device_id=peer, device_id_type=mesh)
+    pl.semaphore_wait(barrier, len(everyone))
+
+    def remote(source, target, sems, index, peer):
+        return pltpu.make_async_remote_copy(
+            src_ref=source, dst_ref=target, send_sem=sems.at[(0,) + index], recv_sem=sems.at[(1,) + index],
+            device_id=peer, device_id_type=mesh,
+        )
+
+    def orders(bit):
+        rest = list(range(bit + 1, bits))
+        return [
+            [b for i, b in enumerate(rest) if not (mask >> (len(rest) - 1 - i)) & 1]
+            for mask in range(1 << len(rest))
+        ]
+
+    def add_rows(target, other, size):
+        block = size if size <= 600 else size // 2
+
+        def one(i, carry):
+            at = pl.ds(pl.multiple_of(i * block, 16), block)
+            target[at] = (target[at].astype(f32) + other[at].astype(f32)).astype(bf16)
+            return carry
+
+        lax.fori_loop(0, size // block, one, 0)
+
+    first = orders(0)
+    sections = []
+    at, row = 0, 0
+    for share in shares:
+        sections.append((at, row, share))
+        at += share * count
+        row += share
+
+    pending = []
+    core_copy = remote(sent_ref, late_got, core_sems, (0,), core_peer)
+    core_copy.start()
+
+    def first_early(i, n):
+        start, row, share = sections[n]
+        shard = turned([0] + first[i])
+        return remote(
+            early_ref.at[pl.ds(pl.multiple_of(start + shard * share, 16), share)],
+            got_first.at[i, pl.ds(row, share)],
+            first_sems, (i, n), head_peers[0],
+        )
+
+    for i in range(len(first)):
+        for n in range(len(sections)):
+            first_early(i, n).start()
+
+    core_copy.wait()
+
+    def core_add(i, carry):
+        j, s = i // count, i % count
+        late_got[j, s] = (own_ref[j, s, :shared_rows].astype(f32) + late_got[j, s].astype(f32)).astype(bf16)
+        return carry
+
+    lax.fori_loop(0, along * count, core_add, 0)
+    x_copies = []
+    for d, (x, peer) in enumerate(zip(x_others, x_peers)):
+        x_copies.append(
+            remote(late_got.at[x], late_from.at[d, :, pl.ds(0, shared_rows)], along_sems, (d, 0), peer)
+        )
+        x_copies.append(
+            remote(
+                own_ref.at[x, :, pl.ds(shared_rows, late_rows - shared_rows)],
+                late_from.at[d, :, pl.ds(shared_rows, late_rows - shared_rows)],
+                along_sems, (d, 1), peer,
+            )
+        )
+    for copy in x_copies:
+        copy.start()
+
+    def next_copy(bit, j, i, part, which):
+        rows = pl.ds(part.start, part.stop - part.start)
+        return remote(
+            got_first.at[i, rows], got_next[bit - 1].at[j, rows], next_sems[bit - 1], (j, which), head_peers[bit]
+        )
+
+    def settle(i, part, which):
+        rest = first[i]
+        level = rest[0] if rest else bits
+        size = part.stop - part.start
+        rows = pl.ds(part.start, size)
+        for bit in range(1, level):
+            j = orders(bit).index(rest)
+            next_copy(bit, j, i, part, which).wait_recv()
+            add_rows(got_first.at[i, rows], got_next[bit - 1].at[j, rows], size)
+        if rest:
+            copy = next_copy(level, orders(level).index(rest[1:]), i, part, which)
+            copy.start()
+            pending.append(copy)
+
+    def early_step(i):
+        shard = turned(first[i])
+        for n, (start, row, share) in enumerate(sections):
+            first_early(i, n).wait()
+            add_rows(
+                got_first.at[i, pl.ds(row, share)],
+                early_ref.at[pl.ds(pl.multiple_of(start + shard * share, 16), share)],
+                share,
+            )
+        settle(i, early_part, 0)
+
+    def first_late(i):
+        return remote(
+            late_from.at[0, turned([0] + first[i])],
+            got_first.at[i, pl.ds(early_rows, late_rows)],
+            first_late_sems, (i,), head_peers[0],
+        )
+
+    def late_begin():
+        for copy in x_copies:
+            copy.wait()
+
+        def x_add(s, carry):
+            shared = late_got[x_at, s].astype(f32)
+            alone = own_ref[x_at, s, shared_rows:].astype(f32)
+            for d in range(along - 1):
+                shared = shared + late_from[d, s, :shared_rows].astype(f32)
+                alone = alone + late_from[d, s, shared_rows:].astype(f32)
+            late_from[0, s, :shared_rows] = shared.astype(bf16)
+            late_from[0, s, shared_rows:] = alone.astype(bf16)
+            return carry
+
+        lax.fori_loop(0, count, x_add, 0)
+        for i in range(len(first)):
+            first_late(i).start()
+
+    def late_step(i):
+        first_late(i).wait()
+        add_rows(got_first.at[i, pl.ds(early_rows, late_rows)], late_from.at[0, turned(first[i])], late_rows)
+        settle(i, late_part, 1)
+
+    final = len(first) - 1
+    half = max(1, len(first) // 2)
+    for i in range(half):
+        early_step(i)
+    late_begin()
+    for i in range(half, final):
+        early_step(i)
+    for i in range(final):
+        late_step(i)
+
+    def spread(part, which):
+        size = part.stop - part.start
+        rows = pl.ds(part.start, size)
+        out_ref[row_at, rows] = got_first[final, rows]
+        copies = [remote(out_ref.at[row_at, rows], out_ref.at[row_at, rows], out_sems, (which, 0), core_peer)]
+        for d, peer in enumerate(x_peers):
+            copies.append(
+                remote(out_ref.at[row_at, rows], out_ref.at[row_at, rows], out_sems, (which, 1 + d), peer)
+            )
+        for copy in copies:
+            copy.start()
+        return copies
+
+    def pass_on(part, which, copies):
+        rows = pl.ds(part.start, part.stop - part.start)
+        more = []
+        for d in range(along - 1):
+            copies[1 + d].wait_recv()
+            source = ((x_at + along - 1 - d) % along) * 2 + core
+            more.append(
+                remote(
+                    out_ref.at[source, rows], out_ref.at[source, rows], out_sems, (which, along + d), core_peer
+                )
+            )
+            more[-1].start()
+        return more
+
+    early_step(final)
+    early_out = spread(early_part, 0)
+    late_step(final)
+    late_out = spread(late_part, 1)
+    early_more = pass_on(early_part, 0, early_out)
+    late_more = pass_on(late_part, 1, late_out)
+    for copies, more in ((early_out, early_more), (late_out, late_more)):
+        copies[0].wait()
+        for copy in copies[1:]:
+            copy.wait_send()
+        for copy in more:
+            copy.wait()
+    for copy in pending:
+        copy.wait_send()
+
+
+def finish(early, own, sent, shares):
+    along, count, late_rows, piece = own.shape
+    bits = count.bit_length() - 1
+    total = sum(shares) + late_rows
+    vmem = pl.BlockSpec(memory_space=pltpu.VMEM)
+    dma = pltpu.SemaphoreType.DMA
+
+    def body(early_ref, own_ref, sent_ref, out_ref, late_got, late_from, got_first, *rest):
+        got_next = rest[: bits - 1]
+        core_sems, along_sems, first_sems, first_late_sems = rest[bits - 1 : bits + 3]
+        next_sems = rest[bits + 3 : 2 * bits + 2]
+        finish_kernel(
+            shares, early_ref, own_ref, sent_ref, out_ref, late_got, late_from, got_first, got_next,
+            core_sems, along_sems, first_sems, first_late_sems, next_sems, rest[-1],
+        )
+
+    return pl.pallas_call(
+        body,
+        out_shape=jax.ShapeDtypeStruct((2 * along, total, piece), bf16),
+        in_specs=[vmem] * 3,
+        out_specs=vmem,
+        scratch_shapes=[
+            pltpu.VMEM(sent.shape, bf16),
+            pltpu.VMEM((along - 1, count, late_rows, piece), bf16),
+            pltpu.VMEM((count // 2, total, piece), bf16),
+        ]
+        + [pltpu.VMEM((count >> (bit + 1), total, piece), bf16) for bit in range(1, bits)]
+        + [
+            dma((2, 1)),
+            dma((2, along - 1, 2)),
+            dma((2, count // 2, len(shares))),
+            dma((2, count // 2)),
+        ]
+        + [dma((2, count >> (bit + 1), 2)) for bit in range(1, bits)]
+        + [dma((2, 2, 2 * along))],
+        compiler_params=pltpu.CompilerParams(
+            collective_id=0, has_side_effects=True, vmem_limit_bytes=48 << 20
+        ),
+        name="finish",
+    )(early, own, sent)
 
 
 def shards(
@@ -400,6 +783,8 @@
     groups, latent_size, group_width = key_lift_weight.shape
     count = rows * tokens
     steps = peers // 2
+    pieces = lax.axis_size("rows")
+    share = width // peers
     side = place & 1
     level = place // 2
     swap = lambda a: flip(a, "rows", 0)
@@ -439,12 +824,19 @@
 
     up_chain = [(i, i + 2) for i in range(peers - 2)]
     down_chain = [(i + 2, i) for i in range(peers - 2)]
+    weights = [gate_weight.T, up_weight.T, down_weight, gate_weight, up_weight, down_weight.T]
+    queries, weights[0], weights[1], weights[5] = lax.optimization_barrier(
+        (queries, weights[0], weights[1], weights[5])
+    )
     segs = []
     bases = []
     moving = own_seg
     for k in range(steps):
         if k > 0:
             moving = lax.ppermute(moving, "heads", up_chain)
+            if k > 1:
+                moving, crossed = lax.optimization_barrier((moving, segs[-1][1]))
+                segs[-1] = (segs[-1][0], crossed)
         segs.append((moving, flip(moving, "heads", 0)))
         base = ((level - k) * 2 + side) * tokens
         other = ((level - k) * 2 + 1 - side) * tokens
@@ -470,55 +862,20 @@
     head_out, lse, head_mix = state
     mixed_mine = head_out[:rows].reshape(count, group_width)
     mixed_got = swap(head_out[rows:]).reshape(count, group_width)
-    mixed = jnp.where(
-        core == 0,
-        jnp.concatenate([mixed_mine, mixed_got], axis=1),
-        jnp.concatenate([mixed_got, mixed_mine], axis=1),
-    )
-
-    resid = inputs + matmul(mixed, output_weight)
-    inverse_two = rms_inverse(resid)
-    unit_two = resid * inverse_two
-    normed_two = (unit_two * ffn_gain).astype(bf16)
-    gate = matmul(normed_two, gate_weight)
-    up_value = matmul(normed_two, up_weight)
-    sigmoid = jax.nn.sigmoid(gate)
-    active = gate * sigmoid
-    hidden = (active * up_value).astype(bf16)
-    result = resid + matmul(hidden, down_weight)
-    hidden_out = result.astype(bf16)
     keep = (own_docs != 0).astype(f32).reshape(count, 1)
-    grad_result = cotangent.reshape(count, width).astype(f32) * keep
-    ffn_back = grad_result.astype(bf16)
-    grad_act = matmul_nt(ffn_back, down_weight)
-    up_back = (grad_act * active).astype(bf16)
-    gate_back = (grad_act * up_value * sigmoid * (1.0 + gate * (1.0 - sigmoid))).astype(bf16)
-    grad_two = matmul_nt(gate_back, gate_weight) + matmul_nt(up_back, up_weight)
-    grad_norm, ffn_gain_part = norm_back(grad_two, unit_two, inverse_two, ffn_gain)
-    grad_resid = grad_result + grad_norm
-    attn_back = grad_resid.astype(bf16)
-    grad_mixed_mine = matmul_nt(attn_back, mine(output_weight, 0)).astype(bf16)
-    grad_mixed_sent = matmul_nt(attn_back, theirs(output_weight, 0)).astype(bf16)
+    (
+        hidden_out, grad_resid, attn_back, grad_mixed_mine, grad_mixed_sent, ffn_gain_part,
+        grads,
+    ) = feed(
+        core, hidden_in.reshape(count, width), mixed_mine, mixed_got, output_weight, ffn_gain,
+        cotangent.reshape(count, width), keep, weights, pieces,
+    )
+    ffn_gain_part = ffn_gain_part[0]
     head_grads = jnp.concatenate([grad_mixed_mine, swap(grad_mixed_sent)], axis=0).reshape(
         2 * rows, tokens, group_width
     )
 
-    def halves(left, right):
-        return (
-            matmul_tn(left, mine(right, 1)).astype(bf16),
-            matmul_tn(left, theirs(right, 1)).astype(bf16),
-        )
-
-    def core_sum(pair):
-        total = add_sent(pair[0], swap(pair[1]))
-        return total.reshape((peers, total.shape[0] // peers, total.shape[1]))
-
-    gate_sum = core_sum(halves(gate_back, normed_two))
-    up_sum = core_sum(halves(up_back, normed_two))
-    down_sum = core_sum(halves(hidden, ffn_back))
-    output_sum = core_sum(halves(mixed, attn_back))
-    early_one = reduce_rest(jnp.concatenate([gate_sum, output_sum], axis=1))
-    early_two = reduce_rest(jnp.concatenate([up_sum, down_sum], axis=1))
+    early = lax.psum_scatter(grads, "rows", scatter_dimension=0, tiled=True)[0]
 
     back_parts = [[k] for k in range(steps - 1, 1, -1)] + [list(range(min(1, steps - 1), -1, -1))]
     state = None
@@ -547,18 +904,25 @@
     query_back_got = swap(query_grads[rows:]).reshape(count, group_width)
     latent_back_mine = latent_grads[:rows].reshape(count, latent_size)
     latent_back_got = swap(latent_grads[rows:]).reshape(count, latent_size)
-    query_sum = core_sum(
-        (
-            matmul_tn(normed_one, query_back_mine).astype(bf16),
-            matmul_tn(normed_one, query_back_got).astype(bf16),
-        )
-    )
-    latent_sum = core_sum(
-        (
-            matmul_tn(normed_one, latent_back_mine).astype(bf16),
-            matmul_tn(normed_one, latent_back_got).astype(bf16),
-        )
-    )
+    along = pieces // 2
+    piece = width // pieces
+
+    def to_pieces(array, shards_first):
+        array = array.reshape(shards_first, array.shape[0] // shards_first, along, piece)
+        return array.transpose(2, 0, 1, 3)
+
+    def latent_fold(array):
+        array = array.reshape(peers, 2, array.shape[0] // peers // 2, array.shape[1])
+        return jnp.concatenate([array[:, 0], array[:, 1]], axis=-1).reshape(-1, 2 * array.shape[-1])
+
+    def late_pieces(query_part, latent_part, gains):
+        gains = jnp.pad(gains.astype(bf16).reshape(peers, 1, share), ((0, 0), (0, 15), (0, group_width - share)))
+        return [
+            to_pieces(query_part.astype(bf16), peers),
+            to_pieces(latent_fold(latent_part.astype(bf16)), peers),
+            to_pieces(gains.reshape(peers * 16, group_width), peers),
+        ]
+
     grad_one = (
         matmul_nt(query_back_mine, mine(query_weight, 1))
         + matmul_nt(query_back_got, theirs(query_weight, 1))
@@ -569,36 +933,46 @@
     grad_in_norm, attn_gain_part = norm_back(grad_one, unit_one, inverse_one, attn_gain)
     hidden_grad = (grad_resid + grad_in_norm).reshape(rows, tokens, width)
 
-    share = width // peers
-    spread = lambda a: jnp.pad(a.astype(bf16).reshape(peers, 1, share), ((0, 0), (0, 7), (0, group_width - share)))
-    gain_sum = add_sent(
-        spread(jnp.where(core == 0, attn_gain_part, ffn_gain_part)),
-        swap(spread(jnp.where(core == 0, ffn_gain_part, attn_gain_part))),
-    )
     lift_share = latent_size // peers
-    key_sum = quad_unlift(key_up_quads).astype(bf16).reshape(peers, lift_share, group_width)
-    value_sum = quad_unlift(value_up_quads).astype(bf16).reshape(peers, lift_share, group_width)
-    folded = latent_sum.reshape(peers, 2, latent_sum.shape[1] // 2, latent_sum.shape[2])
-    latent_fold = jnp.concatenate([folded[:, 0], folded[:, 1]], axis=-1)
-    late = reduce_rest(
-        jnp.concatenate([query_sum, latent_fold, key_sum, value_sum, gain_sum], axis=1)
-    )
-
-    full = gather_columns(jnp.concatenate([early_one, early_two, late], axis=0)).astype(f32)
+    ff_share = gate_weight.shape[1] // peers
+    key_part = quad_unlift(key_up_quads).astype(bf16)
+    value_part = quad_unlift(value_up_quads).astype(bf16)
+    own = jnp.concatenate(
+        late_pieces(
+            matmul_tn(normed_one, query_back_mine),
+            matmul_tn(normed_one, latent_back_mine),
+            jnp.where(core == 0, attn_gain_part, ffn_gain_part),
+        )
+        + [to_pieces(key_part, peers), to_pieces(value_part, peers)],
+        axis=2,
+    )
+    sent = jnp.concatenate(
+        late_pieces(
+            matmul_tn(normed_one, query_back_got),
+            matmul_tn(normed_one, latent_back_got),
+            jnp.where(core == 0, ffn_gain_part, attn_gain_part),
+        ),
+        axis=2,
+    )
+    full = finish(early, own, sent, (ff_share, ff_share, ff_share, share))
+
+    early_rows = 3 * ff_share + share
+    early_full = full[:, :early_rows].transpose(1, 0, 2).reshape(early_rows, width).astype(f32)
+    gate_share = early_full[:ff_share].T
+    up_share = early_full[ff_share : 2 * ff_share].T
+    down_share = early_full[2 * ff_share : 3 * ff_share]
+    output_share = early_full[3 * ff_share :]
+    late_full = full[:, early_rows:].reshape(along, 2, -1, piece).transpose(1, 2, 0, 3)
+    late_full = late_full.reshape(2, -1, group_width).astype(f32)
     at = 0
 
     def cut(size):
         nonlocal at
-        piece = full[:, at : at + size]
+        found = late_full[:, at : at + size]
         at += size
-        return piece
+        return found
 
     beside = lambda pair: jnp.concatenate([pair[0], pair[1]], axis=-1)
-    ff_share = gate_weight.shape[1] // peers
-    gate_share = beside(cut(ff_share)).T
-    output_share = beside(cut(share))
-    up_share = beside(cut(ff_share)).T
-    down_share = beside(cut(ff_share))
     query_share = beside(cut(share))
     fold = cut(share // 2)
     latent_share = jnp.concatenate(
@@ -608,9 +982,9 @@
         ],
         axis=0,
     )
+    gains = cut(16)
     key_share = cut(lift_share)
     value_share = cut(lift_share)
-    gains = cut(8)
     return (
         hidden_out.reshape(rows, tokens, width),
         hidden_grad,

time: 753 us -> 670 us (0.89)
  Pallas kernels: 115 us -> 333 us
  matrix products: 149 us -> 26.6 us
  waiting for transfers between devices: 232 us -> 116 us
  starting transfers between devices: 163 us -> 51.1 us
  local copies, waits for them, and re-layouts: 25.2 us -> 84.8 us
  other arithmetic: 52.1 us -> 31.7 us
  between operations: 2.22 us -> 14.9 us
    pallas_call x0 -> x2, Pallas kernels: none -> 215 us  [the longest x1 137 us: finish(): pl.pallas_call(body, out_shape=jax.ShapeDtypeStruct((2 * along, total, pi...]
    ppermute x36 -> x15, starting transfers between devices: 143 us -> 31.1 us  [flip(): return lax.ppermute(array, axis, [(i, i ^ 1 << bit) for i in range(size)])]
    ppermute x36 -> x15, waiting for transfers between devices: 114 us -> 49.5 us  [flip(): return lax.ppermute(array, axis, [(i, i ^ 1 << bit) for i in range(size)])]
    dot_general x12 -> x4, matrix products: 55 us -> 8.29 us  [matmul_tn(): lax.dot_general(left, right, (((0,), (0,)), ((), ())), preferred_element_...]
    dot_general x9 -> x4, matrix products: 50.6 us -> 8.45 us  [matmul_nt(): lax.dot_general(left, right, (((left.ndim - 1,), (right.ndim - 1,)), ((),...]
    unnamed x121 -> x101, local copies, waits for them, and re-layouts: 5.9 us -> 44.9 us
    ppermute x3, waiting for transfers between devices: 79.6 us -> 42.4 us  [shards(): passing = lax.ppermute(passing, 'heads', down_chain)]
    dot_general x8 -> x4, matrix products: 43.8 us -> 9.86 us  [matmul(): return jnp.dot(left, right, preferred_element_type=f32)]
  transfers between devices with their start and end apart: 42 -> 22, of which waited for: 17 -> 9; matrix products, arithmetic and copies ran while one was open for 15% -> 16% of each run, Pallas kernels for 14% -> 16%
where the time goes in v2:
time: 670 us; the launch traced here: 659 us
  Pallas kernels  333 us (50%)
  waiting for transfers between devices  116 us (17%)
  local copies, waits for them, and re-layouts  84.8 us (13%)
  starting transfers between devices  51.1 us (8%)
  other arithmetic  31.7 us (5%)
  matrix products  26.6 us (4%)
  between operations  14.9 us (2%)
    pallas_call x1, Pallas kernels, finish(): pl.pallas_call(body, out_shape=jax.ShapeDtypeStruct((2 * along, total, pi...  137 us
    pallas_call x3, Pallas kernels, attend_back_part(): pl.pallas_call(functools.partial(attend_back_kernel, len(segs), state is...  86.3 us
    pallas_call x1, Pallas kernels, feed(): pl.pallas_call(feed_kernel, out_shape=outs, grid_spec=pltpu.PrefetchScala...  78.1 us
    ppermute x15, waiting for transfers between devices, flip(): return lax.ppermute(array, axis, [(i, i ^ 1 << bit) for i in range(size)])  49.5 us
    unnamed x101, local copies, waits for them, and re-layouts  44.9 us
    ppermute x3, waiting for transfers between devices, shards(): passing = lax.ppermute(passing, 'heads', down_chain)  42.4 us
    pallas_call x2, Pallas kernels, attend_part(): pl.pallas_call(functools.partial(attend_kernel, len(segs), state is None,...  32.5 us
    ppermute x15, starting transfers between devices, flip(): return lax.ppermute(array, axis, [(i, i ^ 1 << bit) for i in range(size)])  31.1 us
  transfers between devices with their start and end apart: 22, of which 9 were waited for; matrix products, arithmetic and copies ran while one was open for 16% of the time, Pallas kernels for 16%

profile of v2, /device:TPU:0, one launch (start us, length us, event | category | flops | bytes accessed | tf_op | source)
XLA Modules:
  0.0 658.5 jit_solution(15554079046235424701)
XLA Ops:
  7.3 2.2 fusion
  10.1 2.2 multiply_convert_fusion
  12.4 1.5 convolution_convert_fusion.2
  14.3 2.3 convolution_convert_fusion.3
  16.6 2.1 pad_maximum_fusion.3
  18.8 4.5 collective-permute-start.3
  23.7 1.6 convert_reduce_fusion
  25.3 21.3 %collective-permute-done.3.refs_5_.refs_7_ = bf16[8,256,256]{2,1,0:T(8,128)(2,1)S(1)} collective-permute-done((bf16[8,256,256]{2,1,0:T(8,128)(2,1)}, bf16[8,256,256]{2,1,0:T(8,128)(2,1)S(1)}, u32[]{:S(2)}, u32[]{:S(2)}) %collective-permute-start.3) | collective-permute-done | bytes 1048608 | tf_op jit(solution)/shard_map/ppermute | solution.py:836
  46.6 1.5 collective-permute-start.5
  48.1 5.3 collective-permute-start.4
  53.5 3.8 convolution_convert_fusion
  57.8 1.9 constant_dynamic-slice_fusion
  60.8 1.8 copy.125
  62.6 2.2 tile.8
  64.8 2.6 tile.9
  68.6 2.6 tile.21
  71.7 2.7 collective-permute-done.4.refs_7_
  74.9 5.5 collective-permute-start.6
  80.4 3.2 fusion.3
  83.6 2.2 convolution_convert_fusion.1
  85.9 2.5 copy.85.refs_2_.refs_5_
  88.4 8.3 %copy.79 = bf16[1024,2816]{0,1:T(8,128)(2,1)} copy(bf16[1024,2816]{1,0:T(8,128)(2,1)} %refs_10_.1) | data formatting | bytes 11534336 | tf_op args[10]
  96.7 8.3 %copy.80 = bf16[1024,2816]{0,1:T(8,128)(2,1)} copy(bf16[1024,2816]{1,0:T(8,128)(2,1)} %refs_11_.1) | data formatting | bytes 11534336 | tf_op args[11]
  105.0 8.4 %copy.81 = bf16[2816,1024]{0,1:T(8,128)(2,1)} copy(bf16[2816,1024]{1,0:T(8,128)(2,1)} %refs_9_.1) | data formatting | bytes 11534336 | tf_op args[12]
  113.6 3.2 pad_maximum_fusion
  116.8 2.2 collective-permute-done.7.refs_8_
  119.6 17.6 %attend.2 = (f32[8,8,256]{2,1,0:T(8,128)S(1)}, f32[8,8,256]{2,1,0:T(8,128)S(1)}, f32[8,8,256,256]{3,2,1,0:T(8,128)}) custom-call(s32[8]{0:T(128)S(1)} %fusion.45.lo, s32[6]{0:T(128)S(1)} %stack.54.bases, bf16[8,256,512]{2,1,0:T(8,128)(2,1)} %bitcast.215, s32[8,1,256]{2,1,0:T(1,128)S(1)} %broadcast_in_dim.2.refs_1_.refs_4_, ...), custom_call_target="tpu_custom_call" | custom-call | flops 25769803776 | bytes 16777216 | tf_op jit(solution)/shard_map/attend/pallas_call | solution.py:156
  137.2 6.3 collective-permute-done.8.refs_4_.refs_8_
  143.5 14.9 %attend.3 = (bf16[8,256,512]{2,1,0:T(8,128)(2,1)}, f32[8,8,256]{2,1,0:T(8,128)S(1)}, bf16[8,8,256,256]{3,2,1,0:T(8,128)(2,1)}) custom-call(s32[8]{0:T(128)S(1)} %fusion.45.lo, s32[2]{0:T(128)S(1)} %pad_add_fusion.1.bases, bf16[8,256,512]{2,1,0:T(8,128)(2,1)} %bitcast.216, s32[8,1,256]{2,1,0:T(1,128)S(1)} %broadcast_in_dim.2.refs_1_.refs_4_, ...), custom_call_target="tpu_custom_call" | custom-call | flops 8589934592 | bytes 16777216 | tf_op jit(solution)/shard_map/attend/pallas_call | solution.py:156
  158.4 3.0 fusion.59
  162.4 2.0 collective-permute-done.10
  164.3 78.1 %feed.1 = (bf16[1024,1024]{1,0:T(8,128)(2,1)}, f32[1024,1024]{1,0:T(8,128)}, bf16[1024,1024]{1,0:T(8,128)(2,1)}, bf16[1024,512]{1,0:T(8,128)(2,1)}, bf16[1024,51...) custom-call(s32[1]{0:T(128)} %bitcast.core_ref, bf16[1024,1024]{1,0:T(8,128)(2,1)} %bitcast.201, ...), custom_call_target="tpu_custom_call" | custom-call | flops 59592671232 | bytes 68681728 | tf_op jit(solution)/shard_map/feed/pallas_call | solution.py:461
  245.5 3.2 pad_maximum_fusion.1
  248.7 17.2 %attend_back.3 = (bf16[8,256,256]{2,1,0:T(8,128)(2,1)S(1)}, bf16[8,256,256]{2,1,0:T(8,128)(2,1)S(1)}, f32[8,8,256,256]{3,2,1,0:T(8,128)}) custom-call(s32[8]{0:T(128)S(1)} %fusion.45.lo, s32[2]{0:T(128)S(1)} %pad_add_fusion.1.bases, bf16[8,256,512]{2,1,0:T(8,128)(2,1)} %bitcast.217, bf16[8,256,512]{2,1,0:T(8,128)(2,1)} %bitcast.220, ...), custom_call_target="tpu_custom_call" | custom-call | flops 21474836480 | bytes 33554432 | tf_op jit(solution)/shard_map/attend_back/pallas_call | solution.py:288
  265.9 3.2 collective-permute-start.16
  269.1 24.3 %attend_back.4 = (bf16[8,256,256]{2,1,0:T(8,128)(2,1)S(1)}, bf16[8,256,256]{2,1,0:T(8,128)(2,1)S(1)}, f32[8,8,256,256]{3,2,1,0:T(8,128)}) custom-call(s32[8]{0:T(128)S(1)} %fusion.45.lo, s32[2]{0:T(128)S(1)} %pad_add_fusion.3.bases, bf16[8,256,512]{2,1,0:T(8,128)(2,1)} %bitcast.218, bf16[8,256,512]{2,1,0:T(8,128)(2,1)} %bitcast.221, ...), custom_call_target="tpu_custom_call" | custom-call | flops 21474836480 | bytes 33554432 | tf_op jit(solution)/shard_map/attend_back/pallas_call | solution.py:288
  294.4 1.7 collective-permute-start.17
  296.1 44.8 %attend_back.5 = (bf16[8,256,256]{2,1,0:T(8,128)(2,1)S(1)}, bf16[8,256,256]{2,1,0:T(8,128)(2,1)S(1)}, bf16[8,256,256]{2,1,0:T(8,128)(2,1)S(1)}, bf16[8,256,256]{...) custom-call(s32[8]{0:T(128)S(1)} %fusion.45.lo, ...), custom_call_target="tpu_custom_call" | custom-call | flops 42949672960 | bytes 33554432 | tf_op jit(solution)/shard_map/attend_back/pallas_call | solution.py:288
  340.9 3.0 fusion.58
  343.9 22.8 %collective-permute-start.13 = (bf16[8,256,256]{2,1,0:T(8,128)(2,1)}, bf16[8,256,256]{2,1,0:T(8,128)(2,1)}, u32[]{:S(2)}, u32[]{:S(2)}) collective-permute-start(bf16[8,256,256]{2,1,0:T(8,128)(2,1)} %get-tuple-element.67), channel_id=1, source_target_pairs={{0,1},{1,0},{2,3},{3,2},{4,5},{5,4},{6,7},{7,6},{8,9},{9,8},{10,11... | collective-permute-start | bytes 3145736 | tf_op jit(solution)/shard_map/ppermute | solution.py:498
  367.3 1.6 collective-permute-start.18
  370.0 2.5 bitcast_convert_fusion.1
  372.5 3.2 fusion.10
  375.7 37.5 %collective-permute-done.14 = bf16[8,256,256]{2,1,0:T(8,128)(2,1)S(1)} collective-permute-done((bf16[8,256,256]{2,1,0:T(8,128)(2,1)S(1)}, bf16[8,256,256]{2,1,0:T(8,128)(2,1)S(1)}, u32[]{:S(2)}, u32[]{:S(2)}) %collective-permute-start.14) | collective-permute-done | bytes 1048608 | tf_op jit(solution)/shard_map/ppermute | solution.py:498
  413.2 11.1 %collective-permute-done.18 = bf16[8,256,256]{2,1,0:T(8,128)(2,1)S(1)} collective-permute-done((bf16[8,256,256]{2,1,0:T(8,128)(2,1)S(1)}, bf16[8,256,256]{2,1,0:T(8,128)(2,1)S(1)}, u32[]{:S(2)}, u32[]{:S(2)}) %collective-permute-start.18) | collective-permute-done | bytes 1048608 | tf_op jit(solution)/shard_map/ppermute | solution.py:896
  425.7 1.5 collective-permute-start.19
  428.9 1.7 convert_element_type.171
  430.7 2.1 reshape.304
  432.8 2.5 bitcast_dynamic-update-slice_fusion
  435.3 3.7 bitcast_convert_fusion
  439.0 2.1 reshape.305
  442.6 2.5 fusion.7
  445.1 31.3 %collective-permute-done.19 = bf16[8,256,256]{2,1,0:T(8,128)(2,1)} collective-permute-done((bf16[8,256,256]{2,1,0:T(8,128)(2,1)}, bf16[8,256,256]{2,1,0:T(8,128)(2,1)}, u32[]{:S(2)}, u32[]{:S(2)}) %collective-permute-start.19) | collective-permute-done | bytes 1048608 | tf_op jit(solution)/shard_map/ppermute | solution.py:896
  476.3 1.9 add_convert_fusion
  478.4 1.4 copy-done.11
  483.1 1.4 copy-done.12
  484.6 2.0 multiply_reduce_fusion
  491.4 2.8 multiply_add_fusion
  494.2 1.5 copy-done.1
  495.7 1.6 copy-done.2
  497.3 136.6 %finish.1 = bf16[4,1456,256]{2,1,0:T(8,128)(2,1)} custom-call(bf16[9472,256]{1,0:T(8,128)(2,1)} %bitcast.206, bf16[2,8,272,256]{3,2,1,0:T(8,128)(2,1)S(1)} %copy-done.2, bf16[2,8,208,256]{3,2,1,0:T(8,128)(2,1)S(1)} %copy-done.1), custom_call_target="tpu_custom_call" | custom-call | tf_op jit(solution)/shard_map/finish/pallas_call | solution.py:738
  638.4 2.4 slice_bitcast_fusion
  643.8 2.1 copy.116
  645.9 2.7 copy.135
  (174 shorter events, 36.0 us)
Async XLA Ops:
  7.2 46.3 %copy-start = (bf16[1024,1024]{1,0:T(8,128)(2,1)S(1)}, bf16[1024,1024]{1,0:T(8,128)(2,1)}, u32[]{:S(2)}) copy-start(bf16[1024,1024]{1,0:T(8,128)(2,1)} %param.17) | copy-start | bytes 6291460
  7.2 2.9 copy-start.34
  7.2 487.0 %reduce-scatter.2.cloned.1.call-start = ((), (), s32[]{:S(2)}) async-start(), calls=%async_computation.1 | async-start | bytes 24248320 | tf_op jit(solution)/shard_map/reduce_scatter | solution.py:878
  10.1 2.2 copy-start.31
  10.1 2.3 copy-start.21
  12.3 1.5 copy-start.17
  13.9 2.8 collective-permute-start.2
  16.6 6.7 %copy-start.33 = (s32[4,2048]{1,0:T(4,128)S(1)}, s32[4,2048]{1,0:T(4,128)}, u32[]{:S(2)}) copy-start(s32[4,2048]{1,0:T(4,128)} %param.14) | copy-start | bytes 98308
  18.8 27.9 %collective-permute-start.3 = (bf16[8,256,256]{2,1,0:T(8,128)(2,1)}, bf16[8,256,256]{2,1,0:T(8,128)(2,1)S(1)}, u32[]{:S(2)}, u32[]{:S(2)}) collective-permute-start(bf16[8,256,256]{2,1,0:T(8,128)(2,1)} %bitcast.10.refs_3_.refs_9_), channel_id=1, source_target_pairs={{0,2},{1,3},{2,4},{3,5},{4,6},{5,7},{8,10},{9,11},{10,12},{11,13},... | collective-permute-start | bytes 3145736 | tf_op jit(solution)/shard_map/ppermute | solution.py:836
  46.6 10.7 %copy-start.6 = (bf16[8,256,256]{2,1,0:T(8,128)(2,1)}, bf16[8,256,256]{2,1,0:T(8,128)(2,1)S(1)}, u32[]{:S(2)}) copy-start(bf16[8,256,256]{2,1,0:T(8,128)(2,1)S(1)} %collective-permute-done.3.refs_5_.refs_7_) | copy-start | bytes 3145732
  46.6 25.1 %collective-permute-start.5 = (bf16[8,256,256]{2,1,0:T(8,128)(2,1)S(1)}, bf16[8,256,256]{2,1,0:T(8,128)(2,1)}, u32[]{:S(2)}, u32[]{:S(2)}) collective-permute-start(bf16[8,256,256]{2,1,0:T(8,128)(2,1)S(1)} %collective-permute-done.3.refs_5_.refs_7_), channel_id=1, source_target_pairs={{0,1},{1,0},{2,3},{3,2},{4,5},{5,4},{6,7},{7,6},{8,9},{9,8},{10,11... | collective-permute-start | bytes 3145736 | tf_op jit(solution)/shard_map/ppermute | solution.py:498
  48.1 26.3 %collective-permute-start.4 = (bf16[8,256,256]{2,1,0:T(8,128)(2,1)S(1)}, bf16[8,256,256]{2,1,0:T(8,128)(2,1)}, u32[]{:S(2)}, u32[]{:S(2)}) collective-permute-start(bf16[8,256,256]{2,1,0:T(8,128)(2,1)S(1)} %collective-permute-done.3.refs_5_.refs_7_), channel_id=1, source_target_pairs={{0,2},{1,3},{2,4},{3,5},{4,6},{5,7},{8,10},{9,11},{10,12},{11,13},... | collective-permute-start | bytes 3145736 | tf_op jit(solution)/shard_map/ppermute | solution.py:836
  53.5 60.0 %collective-permute-start = (s32[4,256]{1,0:T(4,128)S(1)}, s32[4,256]{1,0:T(4,128)S(1)}, u32[]{:S(2)}, u32[]{:S(2)}) collective-permute-start(s32[4,256]{1,0:T(4,128)S(1)} %broadcast_subtract_fusion), channel_id=1, source_target_pairs={{0,8},{8,0},{16,24},{24,16},{1,9},{9,1},{17,25},{25,17},{2,10},{10... | collective-permute-start | bytes 12296 | tf_op jit(solution)/shard_map/ppermute | solution.py:498
  57.3 56.3 %collective-permute-start.1 = (bf16[1024,512]{1,0:T(8,128)(2,1)}, bf16[1024,512]{1,0:T(8,128)(2,1)}, u32[]{:S(2)}, u32[]{:S(2)}) collective-permute-start(bf16[1024,512]{1,0:T(8,128)(2,1)} %convolution_convert_fusion), channel_id=1, source_target_pairs={{0,8},{8,0},{16,24},{24,16},{1,9},{9,1},{17,25},{25,17},{2,10},{10... | collective-permute-start | bytes 3145736 | tf_op jit(solution)/shard_map/ppermute | solution.py:498
  57.8 22.6 %copy-start.36 = (s32[256]{0:T(256)}, s32[256]{0:T(256)S(1)}, u32[]{:S(2)}) copy-start(s32[256]{0:T(256)S(1)} %get-tuple-element.148) | copy-start | bytes 3076
  57.8 22.6 %copy-start.38 = (s32[256]{0:T(256)}, s32[256]{0:T(256)S(1)}, u32[]{:S(2)}) copy-start(s32[256]{0:T(256)S(1)} %get-tuple-element.149) | copy-start | bytes 3076
  59.7 20.7 %copy-start.42 = (pred[256]{0:T(512)(128)(4,1)}, pred[256]{0:T(512)(128)(4,1)S(1)}, u32[]{:S(2)}) copy-start(pred[256]{0:T(512)(128)(4,1)S(1)} %compare_and_fusion) | copy-start | bytes 772
  71.2 48.4 %collective-permute-start.9 = (bf16[8,256,256]{2,1,0:T(8,128)(2,1)}, bf16[8,256,256]{2,1,0:T(8,128)(2,1)}, u32[]{:S(2)}, u32[]{:S(2)}) collective-permute-start(bf16[8,256,256]{2,1,0:T(8,128)(2,1)} %bitcast.10.refs_3_.refs_9_), channel_id=1, source_target_pairs={{0,1},{1,0},{2,3},{3,2},{4,5},{5,4},{6,7},{7,6},{8,9},{9,8},{10,11... | collective-permute-start | bytes 3145736 | tf_op jit(solution)/shard_map/ppermute | solution.py:498
  74.4 44.6 %collective-permute-start.7 = (bf16[8,256,256]{2,1,0:T(8,128)(2,1)}, bf16[8,256,256]{2,1,0:T(8,128)(2,1)}, u32[]{:S(2)}, u32[]{:S(2)}) collective-permute-start(bf16[8,256,256]{2,1,0:T(8,128)(2,1)} %collective-permute-done.4.refs_7_), channel_id=1, source_target_pairs={{0,1},{1,0},{2,3},{3,2},{4,5},{5,4},{6,7},{7,6},{8,9},{9,8},{10,11... | collective-permute-start | bytes 3145736 | tf_op jit(solution)/shard_map/ppermute | solution.py:498
  74.9 44.1 %collective-permute-start.6 = (bf16[8,256,256]{2,1,0:T(8,128)(2,1)}, bf16[8,256,256]{2,1,0:T(8,128)(2,1)}, u32[]{:S(2)}, u32[]{:S(2)}) collective-permute-start(bf16[8,256,256]{2,1,0:T(8,128)(2,1)} %collective-permute-done.4.refs_7_), channel_id=1, source_target_pairs={{0,2},{1,3},{2,4},{3,5},{4,6},{5,7},{8,10},{9,11},{10,12},{11,13},... | collective-permute-start | bytes 3145736 | tf_op jit(solution)/shard_map/ppermute | solution.py:836
  80.4 3.2 copy-start.18
  113.6 6.0 copy-start.3
  113.6 6.0 copy-start.7
  119.0 24.4 %collective-permute-start.8 = (bf16[8,256,256]{2,1,0:T(8,128)(2,1)}, bf16[8,256,256]{2,1,0:T(8,128)(2,1)S(1)}, u32[]{:S(2)}, u32[]{:S(2)}) collective-permute-start(bf16[8,256,256]{2,1,0:T(8,128)(2,1)} %collective-permute-done.6.refs_3_.refs_7_), channel_id=1, source_target_pairs={{0,1},{1,0},{2,3},{3,2},{4,5},{5,4},{6,7},{7,6},{8,9},{9,8},{10,11... | collective-permute-start | bytes 3145736 | tf_op jit(solution)/shard_map/ppermute | solution.py:498
  143.5 14.9 %copy-start.8 = (bf16[8,256,256]{2,1,0:T(8,128)(2,1)}, bf16[8,256,256]{2,1,0:T(8,128)(2,1)S(1)}, u32[]{:S(2)}) copy-start(bf16[8,256,256]{2,1,0:T(8,128)(2,1)S(1)} %collective-permute-done.8.refs_4_.refs_8_) | copy-start | bytes 3145732
  161.3 3.0 collective-permute-start.10
  242.5 3.1 collective-permute-start.11
  245.5 3.2 copy-start.4
  245.5 3.2 copy-start.5
  265.9 28.2 %collective-permute-start.16 = (bf16[8,256,256]{2,1,0:T(8,128)(2,1)S(1)}, bf16[8,256,256]{2,1,0:T(8,128)(2,1)S(1)}, u32[]{:S(2)}, u32[]{:S(2)}) collective-permute-start(bf16[8,256,256]{2,1,0:T(8,128)(2,1)S(1)} %get-tuple-element.73), channel_id=1, source_target_pairs={{0,1},{1,0},{2,3},{3,2},{4,5},{5,4},{6,7},{7,6},{8,9},{9,8},{10,11... | collective-permute-start | bytes 3145736 | tf_op jit(solution)/shard_map/ppermute | solution.py:498
  293.4 73.4 %collective-permute-start.15 = (bf16[8,256,256]{2,1,0:T(8,128)(2,1)S(1)}, bf16[8,256,256]{2,1,0:T(8,128)(2,1)S(1)}, u32[]{:S(2)}, u32[]{:S(2)}) collective-permute-start(bf16[8,256,256]{2,1,0:T(8,128)(2,1)S(1)} %get-tuple-element.71), channel_id=1, source_target_pairs={{0,1},{1,0},{2,3},{3,2},{4,5},{5,4},{6,7},{7,6},{8,9},{9,8},{10,11... | collective-permute-start | bytes 3145736 | tf_op jit(solution)/shard_map/ppermute | solution.py:498
  294.4 72.4 %collective-permute-start.17 = (bf16[8,256,256]{2,1,0:T(8,128)(2,1)S(1)}, bf16[8,256,256]{2,1,0:T(8,128)(2,1)S(1)}, u32[]{:S(2)}, u32[]{:S(2)}) collective-permute-start(bf16[8,256,256]{2,1,0:T(8,128)(2,1)S(1)} %add_convert_fusion.3), channel_id=1, source_target_pairs={{2,0},{3,1},{4,2},{5,3},{6,4},{7,5},{10,8},{11,9},{12,10},{13,11},... | collective-permute-start | bytes 3145736 | tf_op jit(solution)/shard_map/ppermute | solution.py:896
  340.9 27.9 %copy-start.26 = (f32[2,1024,256]{2,1,0:T(8,128)S(1)}, f32[2,1024,256]{2,1,0:T(8,128)}, u32[]{:S(2)}) copy-start(f32[2,1024,256]{2,1,0:T(8,128)} %get-tuple-element.77) | copy-start | bytes 6291460
  343.9 91.4 %collective-permute-start.12 = (bf16[4,256,512]{2,1,0:T(8,128)(2,1)}, bf16[4,256,512]{2,1,0:T(8,128)(2,1)}, u32[]{:S(2)}, u32[]{:S(2)}) collective-permute-start(bf16[4,256,512]{2,1,0:T(8,128)(2,1)} %get-tuple-element.113), channel_id=1, source_target_pairs={{0,8},{8,0},{16,24},{24,16},{1,9},{9,1},{17,25},{25,17},{2,10},{10... | collective-permute-start | bytes 3145736 | tf_op jit(solution)/shard_map/ppermute | solution.py:498
  343.9 101.1 %collective-permute-start.13 = (bf16[8,256,256]{2,1,0:T(8,128)(2,1)}, bf16[8,256,256]{2,1,0:T(8,128)(2,1)}, u32[]{:S(2)}, u32[]{:S(2)}) collective-permute-start(bf16[8,256,256]{2,1,0:T(8,128)(2,1)} %get-tuple-element.67), channel_id=1, source_target_pairs={{0,1},{1,0},{2,3},{3,2},{4,5},{5,4},{6,7},{7,6},{8,9},{9,8},{10,11... | collective-permute-start | bytes 3145736 | tf_op jit(solution)/shard_map/ppermute | solution.py:498
  366.7 46.5 %collective-permute-start.14 = (bf16[8,256,256]{2,1,0:T(8,128)(2,1)S(1)}, bf16[8,256,256]{2,1,0:T(8,128)(2,1)S(1)}, u32[]{:S(2)}, u32[]{:S(2)}) collective-permute-start(bf16[8,256,256]{2,1,0:T(8,128)(2,1)S(1)} %get-tuple-element.69), channel_id=1, source_target_pairs={{0,1},{1,0},{2,3},{3,2},{4,5},{5,4},{6,7},{7,6},{8,9},{9,8},{10,11... | collective-permute-start | bytes 3145736 | tf_op jit(solution)/shard_map/ppermute | solution.py:498
  366.8 2.1 copy-start.25
  366.8 2.1 copy-start.37
  366.8 2.1 copy-start.39
  366.8 2.1 copy-start.43
  366.8 3.0 copy-start.19
  367.2 2.8 copy-start.9
  367.3 2.8 copy-start.35
  367.3 2.8 copy-start.40
  367.3 57.1 %collective-permute-start.18 = (bf16[8,256,256]{2,1,0:T(8,128)(2,1)S(1)}, bf16[8,256,256]{2,1,0:T(8,128)(2,1)S(1)}, u32[]{:S(2)}, u32[]{:S(2)}) collective-permute-start(bf16[8,256,256]{2,1,0:T(8,128)(2,1)S(1)} %add_convert_fusion.2), channel_id=1, source_target_pairs={{2,0},{3,1},{4,2},{5,3},{6,4},{7,5},{10,8},{11,9},{12,10},{13,11},... | collective-permute-start | bytes 3145736 | tf_op jit(solution)/shard_map/ppermute | solution.py:896
  425.7 50.6 %collective-permute-start.19 = (bf16[8,256,256]{2,1,0:T(8,128)(2,1)}, bf16[8,256,256]{2,1,0:T(8,128)(2,1)}, u32[]{:S(2)}, u32[]{:S(2)}) collective-permute-start(bf16[8,256,256]{2,1,0:T(8,128)(2,1)} %add_convert_fusion.1), channel_id=1, source_target_pairs={{2,0},{3,1},{4,2},{5,3},{6,4},{7,5},{10,8},{11,9},{12,10},{13,11},... | collective-permute-start | bytes 3145736 | tf_op jit(solution)/shard_map/ppermute | solution.py:896
  432.8 2.5 copy-start.10
  478.3 1.6 copy-start.11
  478.4 4.8 collective-permute-start.20
  480.9 1.4 copy-start.22
  482.4 2.2 copy-start.12
  482.4 2.2 copy-start.32
  484.6 2.0 copy-start.41
  487.8 2.0 copy-start.20
  487.8 3.5 copy-start.16
  494.2 1.5 copy-start.1
  495.7 1.6 copy-start.2
  635.1 3.0 copy-start.14
  638.4 3.0 copy-start.13
  643.8 4.8 copy-start.15
  648.6 2.2 copy-start.27
  648.6 2.2 copy-start.28
  648.6 2.2 copy-start.29
  648.6 2.2 copy-start.30
  (3 other events, 4.0 us)
Sparse Core Ops, SparseCore 0:
  242.6 163.9 reduce-scatter.1

commit v3 on v2

v3 whole, which is shorter than its diff:
```python
import functools
import math

import jax
import jax.numpy as jnp
from jax import lax
from jax.experimental import pallas as pl
from jax.experimental.pallas import tpu as pltpu
from jax.sharding import PartitionSpec as P

HEAD_WIDTH = 64
epsilon = 1e-05
blocked = -1e30
LOG2E = math.log2(math.e)
LN2 = math.log(2.0)
QUAD = 4
FORWARD_GROUP = 1
BACKWARD_GROUP = 8
f32 = jnp.float32
bf16 = jnp.bfloat16


def matmul(left, right):
    return jnp.dot(left, right, preferred_element_type=f32)


def matmul_nt(left, right):
    return lax.dot_general(
        left, right, (((left.ndim - 1,), (right.ndim - 1,)), ((), ())), preferred_element_type=f32
    )


def matmul_tn(left, right):
    return lax.dot_general(left, right, (((0,), (0,)), ((), ())), preferred_element_type=f32)


def rms_inverse(value_matrix):
    return lax.rsqrt(jnp.mean(value_matrix * value_matrix, axis=-1, keepdims=True) + epsilon)


def expand_heads(source, weights, factor, out_ref):
    tokens = source.shape[0]
    quads, wide, deep = weights.shape
    latent = wide // QUAD
    for quad in range(quads):
        product = matmul_nt(weights[quad], source[:, quad * deep : (quad + 1) * deep])
        if factor != 1.0:
            product = product * factor
        product = product.astype(bf16)
        for h in range(QUAD):
            at = (quad * QUAD + h) * tokens
            out_ref[:, at : at + tokens] = product[h * latent : (h + 1) * latent]


def lift_heads(source, weights, tokens):
    parts = [
        matmul(weights[h], source[:, h * tokens : (h + 1) * tokens]) for h in range(weights.shape[0])
    ]
    return jnp.concatenate(parts, axis=0)


def lift_grad(left, right, tokens, out_ref):
    latent = left.shape[0]
    deep = QUAD * HEAD_WIDTH
    head = lax.broadcasted_iota(jnp.int32, (latent, deep), 1) // HEAD_WIDTH
    for quad in range(right.shape[1] // deep):
        columns = slice(quad * deep, (quad + 1) * deep)
        found = None
        for h in range(QUAD):
            at = (quad * QUAD + h) * tokens
            part = matmul(left[:, at : at + tokens], right[:, columns])
            found = part if h == 0 else jnp.where(head == h, part, found)
        out_ref[:, columns] += found


def seg_mask(diagonal, base, start, heads):
    tokens = start.shape[-1]
    start = jnp.concatenate([start - base] * heads, axis=1)
    key_at = lax.broadcasted_iota(jnp.int32, (tokens, heads * tokens), 0)
    allow = key_at >= start
    if diagonal:
        at = lax.broadcasted_iota(jnp.int32, (1, tokens), 1)
        allow = allow & (key_at <= jnp.concatenate([at] * heads, axis=1))
    return allow


def attend_kernel(count, first, last, diagonal_at, lo, bases, *refs):
    refs = list(refs)
    take = lambda k: [refs.pop(0) for _ in range(k)]
    query_ref, start_ref, key_lift_ref = take(3)
    segs = take(count)
    if not first:
        top_in, total_in, mix_in = take(3)
    if last:
        (value_lift_ref,) = take(1)
        out_ref, lse_ref, mix_ref = take(3)
    else:
        top_out, total_out, mix_out = take(3)
    expanded, top, total, mix = take(4)
    tokens = query_ref.shape[1]
    heads = expanded.shape[1] // tokens
    row = pl.program_id(0)
    scale = HEAD_WIDTH ** (-0.5) * LOG2E
    touches = [(bases[i] >= 0) & (bases[i] + tokens - 1 >= lo[row]) for i in range(count)]
    if first:
        expand_heads(query_ref[0], key_lift_ref, scale, expanded)
        top[...] = jnp.full_like(top, blocked)
        total[...] = jnp.zeros_like(total)
        mix[...] = jnp.zeros_like(mix)
    else:
        top[...] = top_in[0]
        total[...] = total_in[0]
        mix[...] = mix_in[0].astype(f32)

        @pl.when(functools.reduce(jnp.logical_or, touches))
        def _():
            expand_heads(query_ref[0], key_lift_ref, scale, expanded)

    start = start_ref[0]
    for i in range(count):

        @pl.when(touches[i])
        def _():
            latent = segs[i][0]
            latent_t = latent.T
            allow = seg_mask(i == diagonal_at, bases[i], start, FORWARD_GROUP)
            for g in range(0, heads, FORWARD_GROUP):
                at = slice(g * tokens, (g + FORWARD_GROUP) * tokens)
                score = jnp.where(allow, matmul(latent, expanded[:, at]), blocked)
                old = top[:, at]
                new = jnp.maximum(old, jnp.max(score, axis=0, keepdims=True))
                probs = jnp.exp2(score - new)
                fade = jnp.exp2(old - new)
                top[:, at] = new
                total[:, at] = total[:, at] * fade + jnp.sum(probs, axis=0, keepdims=True)
                mix[:, at] = mix[:, at] * fade + matmul(latent_t, probs.astype(bf16))

    if not last:
        top_out[0] = top[...]
        total_out[0] = total[...]
        mix_out[0] = mix[...].astype(bf16)
        return
    lse_ref[0] = top[...] + jnp.log2(total[...])
    mix_ref[0] = (mix[...] * (1.0 / total[...])).astype(bf16)
    out_ref[0] = lift_heads(mix_ref[0], value_lift_ref, tokens).T.astype(bf16)


def whole(array):
    return pl.BlockSpec(array.shape, lambda *_: (0,) * len(array.shape))


def by_row(shape):
    return pl.BlockSpec((1,) + tuple(shape[1:]), lambda r, *_: (r,) + (0,) * (len(shape) - 1))


def attend_part(queries, start, key_lift, value_lift_t, lo, segs, bases, diagonal_at, state, last):
    rows, tokens, width = queries.shape
    heads = width // HEAD_WIDTH
    latent = segs[0].shape[-1]
    shape = jax.ShapeDtypeStruct
    stat = shape((rows, 1, heads * tokens), f32)
    state_shapes = [stat, stat, shape((rows, latent, heads * tokens), bf16)]
    args = [queries, start, key_lift, *segs]
    specs = [by_row(queries.shape), by_row(start.shape), whole(key_lift)]
    specs += [by_row(s.shape) for s in segs]
    if state is not None:
        args += list(state)
        specs += [by_row(s.shape) for s in state_shapes]
    if last:
        args.append(value_lift_t)
        specs.append(whole(value_lift_t))
        outs = [shape(queries.shape, bf16), stat, state_shapes[2]]
    else:
        outs = state_shapes
    blocks = rows * heads * len(segs)
    return pl.pallas_call(
        functools.partial(attend_kernel, len(segs), state is None, last, diagonal_at),
        out_shape=outs,
        grid_spec=pltpu.PrefetchScalarGridSpec(
            num_scalar_prefetch=2,
            grid=(rows,),
            in_specs=specs,
            out_specs=[by_row(o.shape) for o in outs],
            scratch_shapes=[
                pltpu.VMEM((latent, heads * tokens), bf16),
                pltpu.VMEM((1, heads * tokens), f32),
                pltpu.VMEM((1, heads * tokens), f32),
                pltpu.VMEM((latent, heads * tokens), f32),
            ],
        ),
        compiler_params=pltpu.CompilerParams(
            dimension_semantics=("arbitrary",), vmem_limit_bytes=48 << 20
        ),
        cost_estimate=pl.CostEstimate(
            flops=blocks * tokens * tokens * latent * 4,
            bytes_accessed=rows * heads * latent * tokens * 4,
            transcendentals=blocks * tokens * tokens,
        ),
        name="attend",
    )(lo, bases, *args)


def attend_back_kernel(count, first, last, diagonal_at, lo, bases, *refs):
    refs = list(refs)
    take = lambda k: [refs.pop(0) for _ in range(k)]
    query_ref, grad_ref, lse_ref, mix_ref, start_ref, key_lift_ref, value_lift_ref, key_lift_t_ref = take(8)
    segs = take(count)
    if not first:
        query_back_in, key_up_in = take(2)
    seg_grads = take(count)
    query_back_ref, key_up_ref = take(2)
    if last:
        (value_up_ref,) = take(1)
    expanded, expanded_grad, delta, back, query_back = take(5)
    latent_size = expanded.shape[0]
    tokens = query_ref.shape[1]
    heads = expanded.shape[1] // tokens
    row = pl.program_id(0)
    scale = HEAD_WIDTH ** (-0.5)
    touches = [(bases[i] >= 0) & (bases[i] + tokens - 1 >= lo[row]) for i in range(count)]

    @pl.when(row == 0)
    def _():
        key_up_ref[...] = jnp.zeros_like(key_up_ref) if first else key_up_in[...]
        if last:
            value_up_ref[...] = jnp.zeros_like(value_up_ref)

    query_back[...] = jnp.zeros_like(query_back) if first else query_back_in[0]

    @pl.when(functools.reduce(jnp.logical_or, touches))
    def _():
        expand_heads(query_ref[0], key_lift_ref, scale * LOG2E, expanded)
        expand_heads(grad_ref[0], value_lift_ref, 1.0, expanded_grad)
        delta[...] = jnp.sum(mix_ref[0].astype(f32) * expanded_grad[...].astype(f32), axis=0, keepdims=True)
        back[...] = jnp.zeros_like(back)

    start = start_ref[0]
    for i in range(count):

        @pl.when(touches[i])
        def _():
            latent = segs[i][0]
            latent_t = latent.T
            allow = seg_mask(i == diagonal_at, bases[i], start, BACKWARD_GROUP)
            by_key = by_value = None
            for g in range(0, heads, BACKWARD_GROUP):
                at = slice(g * tokens, (g + BACKWARD_GROUP) * tokens)
                score = matmul(latent, expanded[:, at])
                dprobs = matmul(latent, expanded_grad[:, at])
                probs = jnp.where(allow, jnp.exp2(score - lse_ref[0, :, at]), 0.0)
                dscore = (probs * (dprobs - delta[:, at])).astype(bf16)
                key_term = matmul_nt(dscore, expanded[:, at])
                value_term = matmul_nt(probs.astype(bf16), expanded_grad[:, at])
                by_key = key_term if g == 0 else by_key + key_term
                by_value = value_term if g == 0 else by_value + value_term
                back[:, at] += matmul(latent_t, dscore)
            seg_grads[i][0] = (by_key * LN2 + by_value).astype(bf16)

        @pl.when(jnp.logical_not(touches[i]))
        def _():
            seg_grads[i][0] = jnp.zeros((tokens, latent_size), bf16)

    @pl.when(functools.reduce(jnp.logical_or, touches))
    def _():
        part = (back[...] * scale).astype(bf16)
        query_back[...] += lift_heads(part, key_lift_t_ref, tokens)
        lift_grad(part, query_ref[0], tokens, key_up_ref)

    if last:
        lift_grad(mix_ref[0], grad_ref[0], tokens, value_up_ref)
        query_back_ref[0] = query_back[...].T.astype(bf16)
    else:
        query_back_ref[0] = query_back[...]


def attend_back_part(
    queries, grads, lse, mix, start, key_lift, value_lift, key_lift_t, lo, segs, bases,
    diagonal_at, state, last,
):
    rows, tokens, width = queries.shape
    heads = width // HEAD_WIDTH
    latent = segs[0].shape[-1]
    shape = jax.ShapeDtypeStruct
    back_shape = shape((rows, width, tokens), f32)
    up_shape = shape((latent, width), f32)
    args = [queries, grads, lse, mix, start, key_lift, value_lift, key_lift_t, *segs]
    specs = [by_row(a.shape) for a in (queries, grads, lse, mix, start)]
    specs += [whole(key_lift), whole(value_lift), whole(key_lift_t)]
    specs += [by_row(s.shape) for s in segs]
    if state is not None:
        args += list(state)
        specs += [by_row(back_shape.shape), whole(up_shape)]
    outs = [shape(s.shape, bf16) for s in segs]
    out_specs = [by_row(s.shape) for s in segs]
    outs += [shape(queries.shape, bf16) if last else back_shape, up_shape]
    out_specs += [by_row(outs[-2].shape), whole(up_shape)]
    if last:
        outs.append(up_shape)
        out_specs.append(whole(up_shape))
    blocks = rows * heads * len(segs)
    return pl.pallas_call(
        functools.partial(attend_back_kernel, len(segs), state is None, last, diagonal_at),
        out_shape=outs,
        grid_spec=pltpu.PrefetchScalarGridSpec(
            num_scalar_prefetch=2,
            grid=(rows,),
            in_specs=specs,
            out_specs=out_specs,
            scratch_shapes=[
                pltpu.VMEM((latent, heads * tokens), bf16),
                pltpu.VMEM((latent, heads * tokens), bf16),
                pltpu.VMEM((1, heads * tokens), f32),
                pltpu.VMEM((latent, heads * tokens), f32),
                pltpu.VMEM((width, tokens), f32),
            ],
        ),
        compiler_params=pltpu.CompilerParams(
            dimension_semantics=("arbitrary",), vmem_limit_bytes=48 << 20
        ),
        cost_estimate=pl.CostEstimate(
            flops=blocks * tokens * tokens * latent * 10,
            bytes_accessed=rows * heads * latent * tokens * 8,
            transcendentals=blocks * tokens * tokens,
        ),
        name="attend_back",
    )(lo, bases, *args)


def quad_lift(lift):
    latent, width = lift.shape
    deep = QUAD * HEAD_WIDTH
    quads = width // deep
    tall = jnp.tile(lift.reshape(latent, quads, deep).transpose(1, 0, 2), (1, QUAD, 1))
    row_head = lax.broadcasted_iota(jnp.int32, tall.shape, 1) // latent
    column_head = lax.broadcasted_iota(jnp.int32, tall.shape, 2) // HEAD_WIDTH
    return jnp.where(row_head == column_head, tall, jnp.zeros_like(tall))


def head_lift(lift):
    latent, width = lift.shape
    return lift.T.reshape(width // HEAD_WIDTH, HEAD_WIDTH, latent)


def put_pieces(ref, value, at=0):
    pieces, _, piece = ref.shape
    for j in range(pieces):
        ref[j, pl.ds(at, value.shape[0])] = value[:, j * piece : (j + 1) * piece].astype(bf16)


def feed_kernel(core_ref, *refs):
    (
        inputs_ref, mine_ref, got_ref, output_ref, gain_ref, cotangent_ref, keep_ref,
        gate_ref, up_ref, down_ref,
        hidden_out_ref, resid, normed, back, active_ref, slope_ref, down_grad_ref,
        result,
    ) = refs
    step = pl.program_id(0)
    count = inputs_ref.shape[0]
    block = min(256, count)
    core = core_ref[0]

    @pl.when(step == 0)
    def _():
        for t in range(0, count, block):
            at = slice(t, t + block)
            row = inputs_ref[at].astype(f32) + (
                matmul(mine_ref[at], output_ref[core]) + matmul(got_ref[at], output_ref[1 - core])
            )
            resid[at] = row
            scale = lax.rsqrt(jnp.mean(row * row, axis=-1, keepdims=True) + epsilon)
            normed[at] = (row * scale * gain_ref[...]).astype(bf16)
            back[at] = (cotangent_ref[at].astype(f32) * keep_ref[at]).astype(bf16)
        result[...] = jnp.zeros_like(result)

    gate = matmul(normed[...], gate_ref[...])
    up = matmul(normed[...], up_ref[...])
    sigmoid = 1.0 / (1.0 + jnp.exp(-gate))
    active = gate * sigmoid
    hidden = (active * up).astype(bf16)
    active_ref[...] = active.astype(bf16)
    slope_ref[...] = (up * (sigmoid * (1.0 + gate * (1.0 - sigmoid)))).astype(bf16)
    put_pieces(down_grad_ref, matmul_tn(hidden, back[...]))
    result[...] += matmul(hidden, down_ref[...])

    @pl.when(step == pl.num_programs(0) - 1)
    def _():
        hidden_out_ref[...] = (resid[...] + result[...]).astype(bf16)


def feed_back_kernel(core_ref, *refs):
    (
        mine_ref, got_ref, output_ref, gain_ref, resid_ref, normed, back,
        active_ref, slope_ref, gate_ref, up_ref, down_ref,
        grad_resid_ref, head_mine_ref, head_sent_ref, gain_grad_ref, grads_ref,
        grad_two, low, staged, staged_out, sems, out_sem,
    ) = refs
    step = pl.program_id(0)
    steps = pl.num_programs(0)
    count, width = resid_ref.shape
    chunk = down_ref.shape[0]
    ff = (grads_ref.shape[1] - width) // 2
    block = min(256, count)
    core = core_ref[0]
    slot = step % 2

    def leave(at, kind, place):
        return pltpu.make_async_copy(
            staged.at[at, kind],
            grads_ref.at[:, pl.ds(pl.multiple_of(kind * ff + place * chunk, chunk), chunk)],
            sems.at[at, kind],
        )

    @pl.when(step >= 2)
    def _():
        for kind in range(2):
            leave(slot, kind, step - 2).wait()

    @pl.when(step == 0)
    def _():
        grad_two[...] = jnp.zeros_like(grad_two)

    grad_act = matmul_nt(back[...], down_ref[...])
    up_back = (grad_act * active_ref[...].astype(f32)).astype(bf16)
    gate_back = (grad_act * slope_ref[...].astype(f32)).astype(bf16)
    put_pieces(staged.at[slot, 1], matmul_tn(up_back, normed[...]))
    put_pieces(staged.at[slot, 0], matmul_tn(gate_back, normed[...]))
    for kind in range(2):
        leave(slot, kind, step).start()
    grad_two[...] += matmul_nt(gate_back, gate_ref[...]) + matmul_nt(up_back, up_ref[...])

    @pl.when(step == steps - 1)
    def _():
        gain_total = jnp.zeros((1, width), f32)
        for t in range(0, count, block):
            at = slice(t, t + block)
            row = resid_ref[at]
            scale = lax.rsqrt(jnp.mean(row * row, axis=-1, keepdims=True) + epsilon)
            unit = row * scale
            grad = grad_two[at]
            gain_total += jnp.sum(grad * unit, axis=0, keepdims=True)
            scaled = grad * gain_ref[...]
            grad = back[at].astype(f32) + scale * (
                scaled - unit * jnp.mean(scaled * unit, axis=-1, keepdims=True)
            )
            grad_resid_ref[at] = grad
            low[at] = grad.astype(bf16)
            head_mine_ref[at] = matmul_nt(low[at], output_ref[core]).astype(bf16)
            head_sent_ref[at] = matmul_nt(low[at], output_ref[1 - core]).astype(bf16)
        gain_grad_ref[...] = gain_total
        half = mine_ref.shape[1]
        put_pieces(staged_out, matmul_tn(mine_ref[...], low[...]), core * half)
        put_pieces(staged_out, matmul_tn(got_ref[...], low[...]), (1 - core) * half)
        last = pltpu.make_async_copy(staged_out, grads_ref.at[:, pl.ds(2 * ff, width)], out_sem)
        last.start()
        for kind in range(2):
            leave(1 - slot, kind, step - 1).wait()
            leave(slot, kind, step).wait()
        last.wait()


def once(array):
    return pl.BlockSpec(array.shape, lambda *_: (0,) * len(array.shape), pipeline_mode=pl.Buffered(1))


def feed(core, inputs, mixed_mine, mixed_got, output_weight, gain, cotangent, keep, weights, pieces):
    count, width = inputs.shape
    gate_weight, up_weight, down_weight = weights
    ff = gate_weight.shape[1]
    chunk = 256
    piece = width // pieces
    output_weight = output_weight.reshape(2, -1, width)
    gain = gain.reshape(1, width)
    by_rows = pl.BlockSpec((chunk, width), lambda c, *_: (c, 0))
    by_columns = pl.BlockSpec((width, chunk), lambda c, *_: (0, c))
    kept_columns = pl.BlockSpec((count, chunk), lambda c, *_: (0, c))
    shape = jax.ShapeDtypeStruct
    params = pltpu.CompilerParams(dimension_semantics=("arbitrary",), vmem_limit_bytes=60 << 20)
    full_bf, full_f = shape((count, width), bf16), shape((count, width), f32)
    kept = shape((count, ff), bf16)
    firsts = [inputs, mixed_mine, mixed_got, output_weight, gain, cotangent, keep]
    outs = [full_bf, full_f, full_bf, full_bf, kept, kept, shape((pieces, ff, piece), bf16)]
    hidden_out, resid, normed, back, active, slope, down_grad = pl.pallas_call(
        feed_kernel,
        out_shape=outs,
        grid_spec=pltpu.PrefetchScalarGridSpec(
            num_scalar_prefetch=1,
            grid=(ff // chunk,),
            in_specs=[once(a) for a in firsts] + [by_columns, by_columns, by_rows],
            out_specs=[once(o) for o in outs[:4]]
            + [kept_columns, kept_columns, pl.BlockSpec((pieces, chunk, piece), lambda c, *_: (0, c, 0))],
            scratch_shapes=[pltpu.VMEM((count, width), f32)],
        ),
        compiler_params=params,
        cost_estimate=pl.CostEstimate(
            flops=count * width * (ff * 8 + width * 2),
            bytes_accessed=width * ff * 8 + count * width * 16 + count * ff * 4,
            transcendentals=count * ff,
        ),
        name="feed",
    )(core.reshape(1), *firsts, *weights)
    firsts = [mixed_mine, mixed_got, output_weight, gain, resid, normed, back]
    outs = [
        full_f,
        shape(mixed_mine.shape, bf16),
        shape(mixed_mine.shape, bf16),
        shape((1, width), f32),
        shape((pieces, 2 * ff + width, piece), bf16),
    ]
    grad_resid, head_mine, head_sent, gain_grad, grads = pl.pallas_call(
        feed_back_kernel,
        out_shape=outs,
        grid_spec=pltpu.PrefetchScalarGridSpec(
            num_scalar_prefetch=1,
            grid=(ff // chunk,),
            in_specs=[once(a) for a in firsts]
            + [kept_columns, kept_columns, by_columns, by_columns, by_rows],
            out_specs=[once(o) for o in outs[:4]] + [pl.BlockSpec(memory_space=pl.ANY)],
            scratch_shapes=[
                pltpu.VMEM((count, width), f32),
                pltpu.VMEM((count, width), bf16),
                pltpu.VMEM((2, 2, pieces, chunk, piece), bf16),
                pltpu.VMEM((pieces, width, piece), bf16),
                pltpu.SemaphoreType.DMA((2, 2)),
                pltpu.SemaphoreType.DMA,
            ],
        ),
        compiler_params=params,
        cost_estimate=pl.CostEstimate(
            flops=count * width * (ff * 10 + width * 4),
            bytes_accessed=width * ff * 10 + count * width * 20 + count * ff * 4,
            transcendentals=0,
        ),
        name="feed_back",
    )(core.reshape(1), *firsts, active, slope, *weights)
    return hidden_out, grad_resid, head_mine, head_sent, gain_grad, down_grad, grads


def flip(array, axis, bit):
    size = lax.axis_size(axis)
    return lax.ppermute(array, axis, [(i, i ^ (1 << bit)) for i in range(size)])


def late_parts(core, inputs_ref, gain_ref, back_refs, query_ref, latent_ref, resid_ref, other_gain_ref, up_refs, normed, own, sent, grad_ref):
    along, count, _, piece = own.shape
    tokens, width = inputs_ref.shape
    query_mine, query_got, latent_mine, latent_got = back_refs
    share = width // count
    fold = share // 2
    latent = latent_mine.shape[1]
    half = query_mine.shape[1]
    block = min(256, tokens)
    mine = lambda ref, size: ref[:, pl.ds(pl.multiple_of(core * size, size), size)]
    theirs = lambda ref, size: ref[:, pl.ds(pl.multiple_of((1 - core) * size, size), size)]
    gain_total = jnp.zeros((1, width), f32)
    for t in range(0, tokens, block):
        at = slice(t, t + block)
        row = inputs_ref[at].astype(f32)
        scale = lax.rsqrt(jnp.mean(row * row, axis=-1, keepdims=True) + epsilon)
        unit = row * scale
        normed[at] = (unit * gain_ref[...]).astype(bf16)
        grad = (
            matmul_nt(query_mine[at], mine(query_ref, half))
            + matmul_nt(query_got[at], theirs(query_ref, half))
            + matmul_nt(latent_mine[at], mine(latent_ref, latent))
            + matmul_nt(latent_got[at], theirs(latent_ref, latent))
        )
        gain_total += jnp.sum(grad * unit, axis=0, keepdims=True)
        scaled = grad * gain_ref[...]
        grad_ref[at] = resid_ref[at] + scale * (
            scaled - unit * jnp.mean(scaled * unit, axis=-1, keepdims=True)
        )
    other = other_gain_ref[...]
    gains = (jnp.where(core == 0, gain_total, other), jnp.where(core == 0, other, gain_total))
    lane = max(share, 128)
    for target, query, latents, gain in (
        (own, query_mine, latent_mine, gains[0]),
        (sent, query_got, latent_got, gains[1]),
    ):
        query_grad = matmul_tn(normed[...], query[...]).astype(bf16)
        latent_grad = matmul_tn(normed[...], latents[...]).astype(bf16)
        for s in range(count):
            first = s * share
            begin = first // lane * lane
            for j in range(along):
                target[j, s, :share] = query_grad[first : first + share, j * piece : (j + 1) * piece]
                side, column = divmod(j * piece, latent)
                target[j, s, share : share + fold] = latent_grad[
                    first + side * fold : first + (side + 1) * fold, column : column + piece
                ]
                rows = slice(share + fold, share + fold + 16)
                if j == 0:
                    kept = jnp.broadcast_to(gain[:, begin : begin + lane], (16, lane)).astype(bf16)
                    target[j, s, rows, :lane] = kept
                    if piece > lane:
                        target[j, s, rows, lane:] = jnp.zeros((16, piece - lane), bf16)
                else:
                    target[j, s, rows] = jnp.zeros((16, piece), bf16)
    lift = latent // count
    at = share + fold + 16
    for ref in up_refs:
        for s in range(count):
            for j in range(along):
                own[j, s, at : at + lift] = ref[s * lift : (s + 1) * lift, j * piece : (j + 1) * piece].astype(bf16)
        at += lift


def finish_kernel(
    sections, early_refs, late_compute, own_ref, sent_ref, out_ref, late_got, late_from, got_first, got_next,
    core_sems, along_sems, first_sems, first_late_sems, next_sems, out_sems,
):
    along, count, late_rows, piece = own_ref.shape
    shared_rows = sent_ref.shape[2]
    early_rows = sum(section[2] for section in sections)
    bits = count.bit_length() - 1
    row_at = lax.axis_index("rows")
    place = lax.axis_index("heads")
    core = row_at % 2
    x_at = row_at // 2
    mesh = pl.DeviceIdType.MESH
    early_part = slice(0, early_rows)
    late_part = slice(early_rows, early_rows + late_rows)

    def turned(which):
        at = place
        for bit in which:
            at = at + (1 << bit) * (1 - 2 * ((place // (1 << bit)) % 2))
        return at

    core_peer = (row_at + 1 - 2 * core, place)
    x_others = [(x_at + d) % along for d in range(1, along)]
    x_peers = [(x * 2 + core, place) for x in x_others]
    head_peers = [(row_at, turned([bit])) for bit in range(bits)]
    barrier = pltpu.get_barrier_semaphore()
    everyone = [core_peer] + x_peers + head_peers
    for peer in everyone:
        pl.semaphore_signal(barrier, inc=1, device_id=peer, device_id_type=mesh)
    pl.semaphore_wait(barrier, len(everyone))

    def remote(source, target, sems, index, peer):
        return pltpu.make_async_remote_copy(
            src_ref=source, dst_ref=target, send_sem=sems.at[(0,) + index], recv_sem=sems.at[(1,) + index],
            device_id=peer, device_id_type=mesh,
        )

    def orders(bit):
        rest = list(range(bit + 1, bits))
        return [
            [b for i, b in enumerate(rest) if not (mask >> (len(rest) - 1 - i)) & 1]
            for mask in range(1 << len(rest))
        ]

    def add_rows(target, other, size):
        block = size if size <= 600 else size // 2

        def one(i, carry):
            at = pl.ds(pl.multiple_of(i * block, 16), block)
            target[at] = (target[at].astype(f32) + other[at].astype(f32)).astype(bf16)
            return carry

        lax.fori_loop(0, size // block, one, 0)

    first = orders(0)
    pending = []

    def early_rows_of(n, shard):
        which, start, share, _ = sections[n]
        return early_refs[which].at[pl.ds(pl.multiple_of(start + shard * share, 16), share)]

    def first_early(i, n):
        _, _, share, row = sections[n]
        return remote(
            early_rows_of(n, turned([0] + first[i])), got_first.at[i, pl.ds(row, share)],
            first_sems, (i, n), head_peers[0],
        )

    for i in range(len(first)):
        for n in range(len(sections)):
            first_early(i, n).start()

    late_compute(core)
    core_copy = remote(sent_ref, late_got, core_sems, (0,), core_peer)
    core_copy.start()
    core_copy.wait()

    def core_add(i, carry):
        j, s = i // count, i % count
        late_got[j, s] = (own_ref[j, s, :shared_rows].astype(f32) + late_got[j, s].astype(f32)).astype(bf16)
        return carry

    lax.fori_loop(0, along * count, core_add, 0)
    x_copies = []
    for d, (x, peer) in enumerate(zip(x_others, x_peers)):
        x_copies.append(
            remote(late_got.at[x], late_from.at[d, :, pl.ds(0, shared_rows)], along_sems, (d, 0), peer)
        )
        x_copies.append(
            remote(
                own_ref.at[x, :, pl.ds(shared_rows, late_rows - shared_rows)],
                late_from.at[d, :, pl.ds(shared_rows, late_rows - shared_rows)],
                along_sems, (d, 1), peer,
            )
        )
    for copy in x_copies:
        copy.start()

    def next_copy(bit, j, i, part, which):
        rows = pl.ds(part.start, part.stop - part.start)
        return remote(
            got_first.at[i, rows], got_next[bit - 1].at[j, rows], next_sems[bit - 1], (j, which), head_peers[bit]
        )

    def settle(i, part, which):
        rest = first[i]
        level = rest[0] if rest else bits
        size = part.stop - part.start
        rows = pl.ds(part.start, size)
        for bit in range(1, level):
            j = orders(bit).index(rest)
            next_copy(bit, j, i, part, which).wait_recv()
            add_rows(got_first.at[i, rows], got_next[bit - 1].at[j, rows], size)
        if rest:
            copy = next_copy(level, orders(level).index(rest[1:]), i, part, which)
            copy.start()
            pending.append(copy)

    def early_step(i):
        for n, (_, _, share, row) in enumerate(sections):
            first_early(i, n).wait()
            add_rows(got_first.at[i, pl.ds(row, share)], early_rows_of(n, turned(first[i])), share)
        settle(i, early_part, 0)

    def first_late(i):
        return remote(
            late_from.at[0, turned([0] + first[i])],
            got_first.at[i, pl.ds(early_rows, late_rows)],
            first_late_sems, (i,), head_peers[0],
        )

    def late_begin():
        for copy in x_copies:
            copy.wait()

        def x_add(s, carry):
            shared = late_got[x_at, s].astype(f32)
            alone = own_ref[x_at, s, shared_rows:].astype(f32)
            for d in range(along - 1):
                shared = shared + late_from[d, s, :shared_rows].astype(f32)
                alone = alone + late_from[d, s, shared_rows:].astype(f32)
            late_from[0, s, :shared_rows] = shared.astype(bf16)
            late_from[0, s, shared_rows:] = alone.astype(bf16)
            return carry

        lax.fori_loop(0, count, x_add, 0)
        for i in range(len(first)):
            first_late(i).start()

    def late_step(i):
        first_late(i).wait()
        add_rows(got_first.at[i, pl.ds(early_rows, late_rows)], late_from.at[0, turned(first[i])], late_rows)
        settle(i, late_part, 1)

    final = len(first) - 1
    half = max(1, len(first) // 2)
    for i in range(half):
        early_step(i)
    late_begin()
    for i in range(half, final):
        early_step(i)
    for i in range(final):
        late_step(i)

    def spread(part, which):
        rows = pl.ds(part.start, part.stop - part.start)
        out_ref[row_at, rows] = got_first[final, rows]
        copies = [remote(out_ref.at[row_at, rows], out_ref.at[row_at, rows], out_sems, (which, 0), core_peer)]
        for d, peer in enumerate(x_peers):
            copies.append(
                remote(out_ref.at[row_at, rows], out_ref.at[row_at, rows], out_sems, (which, 1 + d), peer)
            )
        for copy in copies:
            copy.start()
        return copies

    def pass_on(part, which, copies):
        rows = pl.ds(part.start, part.stop - part.start)
        more = []
        for d in range(along - 1):
            copies[1 + d].wait_recv()
            source = ((x_at + along - 1 - d) % along) * 2 + core
            more.append(
                remote(
                    out_ref.at[source, rows], out_ref.at[source, rows], out_sems, (which, along + d), core_peer
                )
            )
            more[-1].start()
        return more

    early_step(final)
    early_out = spread(early_part, 0)
    late_step(final)
    late_out = spread(late_part, 1)
    early_more = pass_on(early_part, 0, early_out)
    late_more = pass_on(late_part, 1, late_out)
    for copies, more in ((early_out, early_more), (late_out, late_more)):
        copies[0].wait()
        for copy in copies[1:]:
            copy.wait_send()
        for copy in more:
            copy.wait()
    for copy in pending:
        copy.wait_send()


def finish(early, shares, count, late_args):
    inputs = late_args[0]
    tokens, width = inputs.shape
    piece = early[0].shape[1]
    along = width // piece // 2
    share = width // count
    bits = count.bit_length() - 1
    shared_rows = share + share // 2 + 16
    late_rows = shared_rows + 2 * (late_args[4].shape[1] // count)
    sections = []
    row = 0
    for which, of_one in enumerate(shares):
        start = 0
        for size in of_one:
            sections.append((which, start, size, row))
            start += size * count
            row += size
    total = row + late_rows
    vmem = pl.BlockSpec(memory_space=pltpu.VMEM)
    dma = pltpu.SemaphoreType.DMA

    def body(*refs):
        refs = list(refs)
        take = lambda k: [refs.pop(0) for _ in range(k)]
        early_refs = take(len(early))
        late_refs = take(len(late_args))
        out_ref, grad_ref = take(2)
        normed, own_ref, sent_ref, late_got, late_from, got_first = take(6)
        got_next = take(bits - 1)
        core_sems, along_sems, first_sems, first_late_sems = take(4)
        next_sems = take(bits - 1)
        (out_sems,) = take(1)
        (
            inputs_ref, gain_ref, query_mine, query_got, latent_mine, latent_got,
            query_ref, latent_ref, resid_ref, other_gain_ref, key_up, value_up,
        ) = late_refs

        def late_compute(core):
            late_parts(
                core, inputs_ref, gain_ref, (query_mine, query_got, latent_mine, latent_got),
                query_ref, latent_ref, resid_ref, other_gain_ref, (key_up, value_up),
                normed, own_ref, sent_ref, grad_ref,
            )

        finish_kernel(
            sections, early_refs, late_compute, own_ref, sent_ref, out_ref, late_got, late_from,
            got_first, got_next, core_sems, along_sems, first_sems, first_late_sems, next_sems, out_sems,
        )

    return pl.pallas_call(
        body,
        out_shape=[
            jax.ShapeDtypeStruct((2 * along, total, piece), bf16),
            jax.ShapeDtypeStruct((tokens, width), f32),
        ],
        in_specs=[vmem] * (len(early) + len(late_args)),
        out_specs=[vmem] * 2,
        scratch_shapes=[
            pltpu.VMEM((tokens, width), bf16),
            pltpu.VMEM((along, count, late_rows, piece), bf16),
            pltpu.VMEM((along, count, shared_rows, piece), bf16),
            pltpu.VMEM((along, count, shared_rows, piece), bf16),
            pltpu.VMEM((along - 1, count, late_rows, piece), bf16),
            pltpu.VMEM((count // 2, total, piece), bf16),
        ]
        + [pltpu.VMEM((count >> (bit + 1), total, piece), bf16) for bit in range(1, bits)]
        + [
            dma((2, 1)),
            dma((2, along - 1, 2)),
            dma((2, count // 2, len(sections))),
            dma((2, count // 2)),
        ]
        + [dma((2, count >> (bit + 1), 2)) for bit in range(1, bits)]
        + [dma((2, 2, 2 * along))],
        compiler_params=pltpu.CompilerParams(
            collective_id=0, has_side_effects=True, vmem_limit_bytes=60 << 20
        ),
        name="finish",
    )(*early, *late_args)


def lay_out_kernel(rows, latent, full_ref, gate_ref, up_ref, output_ref, down_ref, query_ref, latent_ref, key_ref, value_ref, gains_ref):
    pieces, _, piece = full_ref.shape
    at = 0
    for ref, size, turn in zip((gate_ref, up_ref, output_ref, down_ref), rows, (True, True, False, False)):
        for j in range(pieces):
            value = full_ref[j, at : at + size].astype(f32)
            if turn:
                ref[j * piece : (j + 1) * piece] = value.T
            else:
                ref[:, j * piece : (j + 1) * piece] = value
        at += size
    share = query_ref.shape[0]
    fold = share // 2
    lift = key_ref.shape[1]
    half = key_ref.shape[2]
    lane = gains_ref.shape[1]
    for j in range(pieces):
        x, core = divmod(j, 2)
        row = at
        query_ref[:, core * half + x * piece : core * half + (x + 1) * piece] = full_ref[
            j, row : row + share
        ].astype(f32)
        row += share
        side, column = divmod(x * piece, latent)
        column += core * latent
        latent_ref[side * fold : (side + 1) * fold, column : column + piece] = full_ref[
            j, row : row + fold
        ].astype(f32)
        row += fold
        if x == 0:
            gains_ref[core : core + 1] = full_ref[j, row : row + 16, :lane].astype(f32)[:1]
        row += 16
        for ref in (key_ref, value_ref):
            ref[core, :, x * piece : (x + 1) * piece] = full_ref[j, row : row + lift].astype(f32)
            row += lift


def lay_out(full, rows, share, latent, half, count, width):
    shape = jax.ShapeDtypeStruct
    gate, up, output, down = rows
    lift = latent // count
    vmem = pl.BlockSpec(memory_space=pltpu.VMEM)
    outs = [
        shape((width, gate), f32),
        shape((width, up), f32),
        shape((output, width), f32),
        shape((down, width), f32),
        shape((share, width), f32),
        shape((share, 2 * latent), f32),
        shape((2, lift, half), f32),
        shape((2, lift, half), f32),
        shape((2, max(share, 128)), f32),
    ]
    return pl.pallas_call(
        functools.partial(lay_out_kernel, rows, latent),
        out_shape=outs,
        in_specs=[vmem],
        out_specs=[vmem] * len(outs),
        compiler_params=pltpu.CompilerParams(vmem_limit_bytes=48 << 20),
        name="lay_out",
    )(full)


def shards(
    hidden_in,
    doc_ids,
    cotangent,
    attn_gain,
    query_weight,
    latent_weight,
    key_lift_weight,
    value_lift_weight,
    output_weight,
    ffn_gain,
    gate_weight,
    up_weight,
    down_weight,
):
    rows, tokens, width = hidden_in.shape
    peers = lax.axis_size("heads")
    place = lax.axis_index("heads")
    core = lax.axis_index("rows") & 1
    groups, latent_size, group_width = key_lift_weight.shape
    count = rows * tokens
    steps = peers // 2
    pieces = lax.axis_size("rows")
    share = width // peers
    side = place & 1
    level = place // 2
    swap = lambda a: flip(a, "rows", 0)
    mine = lambda a, axis: lax.dynamic_slice_in_dim(a, core * (a.shape[axis] // 2), a.shape[axis] // 2, axis)
    theirs = lambda a, axis: lax.dynamic_slice_in_dim(
        a, (1 - core) * (a.shape[axis] // 2), a.shape[axis] // 2, axis
    )

    own_base = place * tokens
    own_docs = lax.dynamic_slice_in_dim(doc_ids, own_base, tokens, 1)
    position = own_base + jnp.arange(tokens, dtype=jnp.int32)
    before = (doc_ids[:, None, :] == own_docs[:, :, None]) & (
        jnp.arange(doc_ids.shape[1], dtype=jnp.int32)[None, None, :] <= position[None, :, None]
    )
    own_start = position[None, :] + 1 - jnp.sum(before.astype(jnp.int32), axis=-1)
    start = jnp.concatenate([own_start, swap(own_start)], axis=0)
    lo = start[:, 0]
    start = start[:, None, :]

    inputs = hidden_in.reshape(count, width).astype(f32)
    inverse_one = rms_inverse(inputs)
    normed_one = (inputs * inverse_one * attn_gain).astype(bf16)
    latent_mine = matmul(normed_one, mine(latent_weight, 1)).astype(bf16)
    latent_sent = matmul(normed_one, theirs(latent_weight, 1)).astype(bf16)
    latent_got = swap(latent_sent)
    own_seg = jnp.concatenate([latent_mine, latent_got], axis=0).reshape(2 * rows, tokens, latent_size)
    query_mine = matmul(normed_one, mine(query_weight, 1)).astype(bf16)
    query_sent = matmul(normed_one, theirs(query_weight, 1)).astype(bf16)
    queries = jnp.concatenate([query_mine, swap(query_sent)], axis=0).reshape(2 * rows, tokens, group_width)

    key_mine = lax.dynamic_index_in_dim(key_lift_weight, core, 0, keepdims=False)
    value_mine = lax.dynamic_index_in_dim(value_lift_weight, core, 0, keepdims=False)
    key_lift = quad_lift(key_mine)
    value_lift = quad_lift(value_mine)
    key_lift_t = head_lift(key_mine)
    value_lift_t = head_lift(value_mine)

    up_chain = [(i, i + 2) for i in range(peers - 2)]
    down_chain = [(i + 2, i) for i in range(peers - 2)]
    segs = []
    bases = []
    moving = own_seg
    for k in range(steps):
        if k > 0:
            moving = lax.ppermute(moving, "heads", up_chain)
            if k > 1:
                moving, crossed = lax.optimization_barrier((moving, segs[-1][1]))
                segs[-1] = (segs[-1][0], crossed)
        segs.append((moving, flip(moving, "heads", 0)))
        base = ((level - k) * 2 + side) * tokens
        other = ((level - k) * 2 + 1 - side) * tokens
        there = level >= k
        bases.append(
            (jnp.where(there, base, -1), jnp.where(there & (other < own_base), other, -1))
        )

    def pick(ks):
        return (
            [s for k in ks for s in segs[k]],
            jnp.stack([b for k in ks for b in bases[k]]).astype(jnp.int32),
        )

    parts = [range(0, steps - 1), range(steps - 1, steps)]
    state = None
    for i, ks in enumerate(parts):
        seg_list, base_list = pick(ks)
        state = attend_part(
            queries, start, key_lift, value_lift_t, lo, seg_list, base_list,
            0 if i == 0 else -1, state, i == len(parts) - 1,
        )
    head_out, lse, head_mix = state
    mixed_mine = head_out[:rows].reshape(count, group_width)
    mixed_got = swap(head_out[rows:]).reshape(count, group_width)
    keep = (own_docs != 0).astype(f32).reshape(count, 1)
    hidden_out, grad_resid, grad_mixed_mine, grad_mixed_sent, ffn_gain_part, down_grad, feed_grads = feed(
        core, hidden_in.reshape(count, width), mixed_mine, mixed_got, output_weight, ffn_gain,
        cotangent.reshape(count, width), keep, (gate_weight, up_weight, down_weight), pieces,
    )
    head_grads = jnp.concatenate([grad_mixed_mine, swap(grad_mixed_sent)], axis=0).reshape(
        2 * rows, tokens, group_width
    )
    early_down = lax.psum_scatter(down_grad, "rows", scatter_dimension=0, tiled=True)[0]
    early_feed = lax.psum_scatter(feed_grads, "rows", scatter_dimension=0, tiled=True)[0]

    back_parts = [[(k, 0), (k, 1)] for k in range(steps - 1, 0, -1)]
    back_parts[-1].append((0, 1))
    back_parts.append([(0, 0)])
    state = None
    seg_grads = {}
    passing = None
    for i, items in enumerate(back_parts):
        done = i == len(back_parts) - 1
        outs = attend_back_part(
            queries, head_grads, lse, head_mix, start, key_lift, value_lift, key_lift_t, lo,
            [segs[k][j] for k, j in items],
            jnp.stack([bases[k][j] for k, j in items]).astype(jnp.int32),
            0 if done else -1, state, done,
        )
        for item, out in zip(items, outs):
            seg_grads[item] = out
        state = outs[len(items) :]
        if not done:
            k = items[0][0]
            total = seg_grads[(k, 0)].astype(f32) + flip(seg_grads[(k, 1)], "heads", 0).astype(f32)
            if passing is not None:
                total = total + passing.astype(f32)
            passing = lax.ppermute(total.astype(bf16), "heads", down_chain)
            if k == 1:
                crossed = flip(seg_grads[(0, 1)], "heads", 0)
    query_grads, key_part, value_part = state
    latent_grads = (
        seg_grads[(0, 0)].astype(f32) + crossed.astype(f32) + passing.astype(f32)
    ).astype(bf16)

    query_back_mine = query_grads[:rows].reshape(count, group_width)
    query_back_got = swap(query_grads[rows:]).reshape(count, group_width)
    latent_back_mine = latent_grads[:rows].reshape(count, latent_size)
    latent_back_got = swap(latent_grads[rows:]).reshape(count, latent_size)
    ff_share = gate_weight.shape[1] // peers
    full, hidden_grad = finish(
        (early_feed, early_down),
        ((ff_share, ff_share, share), (ff_share,)),
        peers,
        (
            hidden_in.reshape(count, width), attn_gain.reshape(1, width),
            query_back_mine, query_back_got, latent_back_mine, latent_back_got,
            query_weight, latent_weight, grad_resid, ffn_gain_part, key_part, value_part,
        ),
    )
    (
        gate_share, up_share, output_share, down_share, query_share, latent_share, key_share, value_share, gains,
    ) = lay_out(full, (ff_share, ff_share, share, ff_share), share, latent_size, group_width, peers, width)
    gains = lax.dynamic_slice_in_dim(gains, (place * share) % gains.shape[1], share, 1)
    return (
        hidden_out.reshape(rows, tokens, width),
        hidden_grad.reshape(rows, tokens, width),
        gains[0],
        query_share,
        latent_share,
        key_share,
        value_share,
        output_share,
        gains[1],
        gate_share,
        up_share,
        down_share,
    )


def solution(mesh):
    placed = (
        P("rows", "heads", None),
        P("rows", None),
        P("rows", "heads", None),
        P(),
        P(),
        P(),
        P(),
        P(),
        P(),
        P(),
        P(),
        P(),
        P(),
    )
    return jax.shard_map(
        shards,
        mesh=mesh,
        in_specs=placed,
        out_specs=(
            P("rows", "heads", None),
            P("rows", "heads", None),
            P("heads"),
            P("heads", None),
            P("heads", None),
            P(None, "heads", None),
            P(None, "heads", None),
            P("heads", None),
            P("heads"),
            P(None, "heads"),
            P(None, "heads"),
            P("heads", None),
        ),
        check_vma=False,
    )
```

time: 670 us -> 577 us (0.86); the launches traced: 659 us -> 575 us
  local copies, waits for them, and re-layouts: 84.8 us -> 22.7 us
  waiting for transfers between devices: 116 us -> 145 us
  other arithmetic: 31.7 us -> 14.9 us
  Pallas kernels: 333 us -> 317 us
  matrix products: 26.6 us -> 11.2 us
    pallas_call x1 -> x3, Pallas kernels: 137 us -> 183 us  [the longest x1 121 us: finish(): pl.pallas_call(body, out_shape=[jax.ShapeDtypeStruct((2 * along, total, p...]
    pallas_call x1, Pallas kernels: 78.1 us -> 42.2 us  [feed(): pl.pallas_call(feed_kernel, out_shape=outs, grid_spec=pltpu.PrefetchScala...]
    unnamed x101 -> x43, local copies, waits for them, and re-layouts: 44.9 us -> 13 us
    ppermute x15, waiting for transfers between devices: 49.5 us -> 78 us  [flip(): return lax.ppermute(array, axis, [(i, i ^ 1 << bit) for i in range(size)])]
    pallas_call x3 -> x4, Pallas kernels: 86.3 us -> 64.6 us  [attend_back_part(): pl.pallas_call(functools.partial(attend_back_kernel, len(segs), state is...]
    dot_general x8 -> x0, matrix products: 16.7 us -> none  [the longest x4 8.45 us: matmul_nt(): lax.dot_general(left, right, (((left.ndim - 1,), (right.ndim - 1,)), ((),...]
    another operation x5 -> x0, local copies, waits for them, and re-layouts: 8.58 us -> none  [the longest x4 8.57 us: quad_lift(): jnp.tile(lift.reshape(latent, quads, deep).transpose(1, 0, 2), (1, QUAD, 1))]
    slice x8 -> x0, local copies, waits for them, and re-layouts: 8.08 us -> none  [the longest x1 2.66 us: shards(): up_share = early_full[ff_share:2 * ff_share].T]
  transfers between devices with their start and end apart: 22 -> 23, of which waited for: 9 -> 13; matrix products, arithmetic and copies ran while one was open for 16% -> 5% of each run, Pallas kernels for 16% -> 25%
where the time goes in v3:
time: 577 us; the launch traced here: 575 us
  Pallas kernels  317 us (55%)
  waiting for transfers between devices  145 us (25%)
  starting transfers between devices  49 us (8%)
  local copies, waits for them, and re-layouts  22.7 us (4%)
  other arithmetic  14.9 us (3%)
  between operations  14.9 us (3%)
  matrix products  11.2 us (2%)
    pallas_call x1, Pallas kernels, finish(): pl.pallas_call(body, out_shape=[jax.ShapeDtypeStruct((2 * along, total, p...  121 us
    ppermute x15, waiting for transfers between devices, flip(): return lax.ppermute(array, axis, [(i, i ^ 1 << bit) for i in range(size)])  78 us
    pallas_call x4, Pallas kernels, attend_back_part(): pl.pallas_call(functools.partial(attend_back_kernel, len(segs), state is...  64.6 us
    pallas_call x1, Pallas kernels, feed(): pl.pallas_call(feed_back_kernel, out_shape=outs, grid_spec=pltpu.Prefetch...  60.3 us
    ppermute x3, waiting for transfers between devices, shards(): passing = lax.ppermute(total.astype(bf16), 'heads', down_chain)  42.2 us
    pallas_call x1, Pallas kernels, feed(): pl.pallas_call(feed_kernel, out_shape=outs, grid_spec=pltpu.PrefetchScala...  42.2 us
    ppermute x15, starting transfers between devices, flip(): return lax.ppermute(array, axis, [(i, i ^ 1 << bit) for i in range(size)])  29.7 us
    pallas_call x2, Pallas kernels, attend_part(): pl.pallas_call(functools.partial(attend_kernel, len(segs), state is None,...  27.4 us
  transfers between devices with their start and end apart: 23, of which 13 were waited for; matrix products, arithmetic and copies ran while one was open for 5% of the time, Pallas kernels for 25%

profile of v3, /device:TPU:0, one launch (start us, length us, event | category | flops | bytes accessed | tf_op | source)
XLA Modules:
  0.0 574.8 jit_solution(16728468092627402925)
XLA Ops:
  7.3 2.2 multiply_reduce_fusion
  9.5 0.5 multiply_convert_fusion
  10.1 0.7 copy-done.13
  10.7 0.7 convolution_convert_fusion.2
  11.5 0.6 copy-done.12
  12.1 0.5 collective-permute-start.2
  12.5 2.3 convolution_convert_fusion.3
  14.9 4.5 collective-permute-start.3
  19.9 22.6 %collective-permute-done.3.refs_5_.refs_8_ = bf16[8,256,256]{2,1,0:T(8,128)(2,1)S(1)} collective-permute-done((bf16[8,256,256]{2,1,0:T(8,128)(2,1)S(1)}, bf16[8,256,256]{2,1,0:T(8,128)(2,1)S(1)}, u32[]{:S(2)}, u32[]{:S(2)}) %collective-permute-start.3) | collective-permute-done | bytes 1048608 | tf_op jit(solution)/shard_map/ppermute | solution.py:1026
  42.5 1.5 collective-permute-start.5
  44.0 5.4 collective-permute-start.4
  49.3 1.6 convert_reduce_fusion
  51.0 4.1 convolution_convert_fusion
  55.1 0.5 collective-permute-start.1
  55.6 0.6 collective-permute-start.9
  56.2 12.4 %collective-permute-done.5.refs_6_.refs_9_ = bf16[8,256,256]{2,1,0:T(8,128)(2,1)S(1)} collective-permute-done((bf16[8,256,256]{2,1,0:T(8,128)(2,1)S(1)}, bf16[8,256,256]{2,1,0:T(8,128)(2,1)S(1)}, u32[]{:S(2)}, u32[]{:S(2)}) %collective-permute-start.5) | collective-permute-done | bytes 1048608 | tf_op jit(solution)/shard_map/ppermute | solution.py:540
  68.5 1.8 collective-permute-done.4.refs_7_.refs_8_
  70.4 0.5 collective-permute-start.7
  70.9 5.4 collective-permute-start.6
  76.4 1.1 constant_dynamic-slice_fusion
  77.4 4.1 convolution_convert_fusion.1
  81.9 0.8 copy.39
  82.7 0.8 copy.38
  83.5 0.8 copy.42
  84.5 2.2 fusion
  86.9 3.2 pad_maximum_fusion
  90.1 22.2 %collective-permute-done.7.refs_8_.refs_9_ = bf16[8,256,256]{2,1,0:T(8,128)(2,1)} collective-permute-done((bf16[8,256,256]{2,1,0:T(8,128)(2,1)}, bf16[8,256,256]{2,1,0:T(8,128)(2,1)}, u32[]{:S(2)}, u32[]{:S(2)}) %collective-permute-start.7) | collective-permute-done | bytes 1048608 | tf_op jit(solution)/shard_map/ppermute | solution.py:540
  112.3 1.5 collective-permute-start.8
  113.9 16.3 %attend.2 = (f32[8,1,2048]{2,1,0:T(1,128)S(1)}, f32[8,1,2048]{2,1,0:T(1,128)S(1)}, bf16[8,256,2048]{2,1,0:T(8,128)(2,1)}) custom-call(s32[8]{0:T(128)S(1)} %fusion.9.lo, s32[6]{0:T(128)S(1)} %stack.54.bases, bf16[8,256,512]{2,1,0:T(8,128)(2,1)} %bitcast.79, s32[8,1,256]{2,1,0:T(1,128)S(1)} %broadcast_in_dim.4.refs_1_.refs_4_, ...), custom_call_target="tpu_custom_call" | custom-call | flops 25769803776 | bytes 16777216 | tf_op jit(solution)/shard_map/attend/pallas_call | solution.py:176
  130.1 6.3 %collective-permute-done.8.refs_4_.refs_9_ = bf16[8,256,256]{2,1,0:T(8,128)(2,1)S(1)} collective-permute-done((bf16[8,256,256]{2,1,0:T(8,128)(2,1)}, bf16[8,256,256]{2,1,0:T(8,128)(2,1)S(1)}, u32[]{:S(2)}, u32[]{:S(2)}) %collective-permute-start.8) | collective-permute-done | bytes 1048608 | tf_op jit(solution)/shard_map/ppermute | solution.py:540
  136.4 11.1 %attend.3 = (bf16[8,256,512]{2,1,0:T(8,128)(2,1)S(1)}, f32[8,1,2048]{2,1,0:T(1,128)S(1)}, bf16[8,256,2048]{2,1,0:T(8,128)(2,1)}) custom-call(s32[8]{0:T(128)S(1)} %fusion.9.lo, s32[2]{0:T(128)S(1)} %pad_add_fusion.1.bases, bf16[8,256,512]{2,1,0:T(8,128)(2,1)} %bitcast.80, s32[8,1,256]{2,1,0:T(1,128)S(1)} %broadcast_in_dim.4.refs_1_.refs_4_, ...), custom_call_target="tpu_custom_call" | custom-call | flops 8589934592 | bytes 16777216 | tf_op jit(solution)/shard_map/attend/pallas_call | solution.py:176
  147.6 1.4 fusion.16
  149.1 1.0 copy.51
  150.1 2.0 collective-permute-done.10
  152.0 42.2 %feed.1 = (bf16[1024,1024]{1,0:T(8,128)(2,1)}, f32[1024,1024]{1,0:T(8,128)}, bf16[1024,1024]{1,0:T(8,128)(2,1)}, bf16[1024,1024]{1,0:T(8,128)(2,1)}, bf16[1024,2...) custom-call(s32[1]{0:T(128)} %bitcast.core_ref, bf16[1024,1024]{1,0:T(8,128)(2,1)} %bitcast.73, ...), custom_call_target="tpu_custom_call" | custom-call | flops 25769803776 | bytes 51380224 | tf_op jit(solution)/shard_map/feed/pallas_call | solution.py:482
  194.3 60.3 %feed_back.1 = (f32[1024,1024]{1,0:T(8,128)}, bf16[1024,512]{1,0:T(8,128)(2,1)}, bf16[1024,512]{1,0:T(8,128)(2,1)}, f32[1,1024]{1,0:T(1,128)}, bf16[4,6656,256]{2,1,0:T(8,128)(2,1)}) custom-call(s32[1]{0:T(128)} %bitcast.core_ref, bf16[1024,512]{1,0:T(8,128)(2,1)} %bitcast.94, bf16[1024,512]{1,0:T(8,128)(2,1)} %bitcast.19.refs_2_.refs_1_, ...), custom_call_target="tpu_custom_call" | custom-call | flops 33822867456 | bytes 61341696 | tf_op jit(solution)/shard_map/feed_back/pallas_call | solution.py:509
  254.9 2.7 collective-permute-done.11
  257.5 2.7 pad_maximum_fusion.1
  260.2 9.7 %attend_back.4 = (bf16[8,256,256]{2,1,0:T(8,128)(2,1)S(1)}, bf16[8,256,256]{2,1,0:T(8,128)(2,1)S(1)}, f32[8,512,256]{2,1,0:T(8,128)}, f32[256,512]{1,0:T(8,128)S(1)}) custom-call(s32[8]{0:T(128)S(1)} %fusion.9.lo, s32[2]{0:T(128)S(1)} %pad_add_fusion.1.bases, bf16[8,256,512]{2,1,0:T(8,128)(2,1)} %bitcast.81, bf16[8,256,512]{2,1,0:T(8,128)(2,1)} %bitcast.85, ...), custom_call_target="tpu_custom_call" | custom-call | flops 21474836480 | bytes 33554432 | tf_op jit(solution)/shard_map/attend_back/pallas_call | solution.py:301
  269.9 3.0 collective-permute-start.16
  272.9 10.4 %attend_back.5 = (bf16[8,256,256]{2,1,0:T(8,128)(2,1)S(1)}, bf16[8,256,256]{2,1,0:T(8,128)(2,1)S(1)}, f32[8,512,256]{2,1,0:T(8,128)}, f32[256,512]{1,0:T(8,128)S(1)}) custom-call(s32[8]{0:T(128)S(1)} %fusion.9.lo, s32[2]{0:T(128)S(1)} %pad_add_fusion.3.bases, bf16[8,256,512]{2,1,0:T(8,128)(2,1)} %bitcast.82, bf16[8,256,512]{2,1,0:T(8,128)(2,1)} %bitcast.86, ...), custom_call_target="tpu_custom_call" | custom-call | flops 21474836480 | bytes 33554432 | tf_op jit(solution)/shard_map/attend_back/pallas_call | solution.py:301
  283.4 13.5 %collective-permute-done.16 = bf16[8,256,256]{2,1,0:T(8,128)(2,1)S(1)} collective-permute-done((bf16[8,256,256]{2,1,0:T(8,128)(2,1)S(1)}, bf16[8,256,256]{2,1,0:T(8,128)(2,1)S(1)}, u32[]{:S(2)}, u32[]{:S(2)}) %collective-permute-start.16) | collective-permute-done | bytes 1048608 | tf_op jit(solution)/shard_map/ppermute | solution.py:540
  297.2 1.3 collective-permute-start.17
  298.5 12.8 %attend_back.6 = (bf16[8,256,256]{2,1,0:T(8,128)(2,1)S(1)}, bf16[8,256,256]{2,1,0:T(8,128)(2,1)S(1)}, bf16[8,256,256]{2,1,0:T(8,128)(2,1)S(1)}, f32[8,512,256]{2,1,0:T(8,128)}, f32[256,512]{1,0:T(8,128)S(1)}) custom-call(s32[8]{0:T(128)S(1)} %fusion.9.lo, s32[3]{0:T(128)S(1)} %pad_add_fusion.2.bases, bf16[8,256,512]{2,1,0:T(8,128)(2,1)} %bitcast.83, ...), custom_call_target="tpu_custom_call" | custom-call | flops 32212254720 | bytes 33554432 | tf_op jit(solution)/shard_map/attend_back/pallas_call | solution.py:301
  311.2 19.9 %collective-permute-start.14 = (bf16[8,256,256]{2,1,0:T(8,128)(2,1)S(1)}, bf16[8,256,256]{2,1,0:T(8,128)(2,1)S(1)}, u32[]{:S(2)}, u32[]{:S(2)}) collective-permute-start(bf16[8,256,256]{2,1,0:T(8,128)(2,1)S(1)} %get-tuple-element.92), channel_id=1, source_target_pairs={{0,1},{1,0},{2,3},{3,2},{4,5},{5,4},{6,7},{7,6},{8,9},{9,8},{10,11... | collective-permute-start | bytes 3145736 | tf_op jit(solution)/shard_map/ppermute | solution.py:540
  331.1 3.7 collective-permute-done.17
  335.2 1.3 collective-permute-start.18
  336.5 1.5 collective-permute-start.13
  338.0 17.2 %collective-permute-done.14 = bf16[8,256,256]{2,1,0:T(8,128)(2,1)S(1)} collective-permute-done((bf16[8,256,256]{2,1,0:T(8,128)(2,1)S(1)}, bf16[8,256,256]{2,1,0:T(8,128)(2,1)S(1)}, u32[]{:S(2)}, u32[]{:S(2)}) %collective-permute-start.14) | collective-permute-done | bytes 1048608 | tf_op jit(solution)/shard_map/ppermute | solution.py:540
  355.2 29.8 %collective-permute-done.18 = bf16[8,256,256]{2,1,0:T(8,128)(2,1)S(1)} collective-permute-done((bf16[8,256,256]{2,1,0:T(8,128)(2,1)S(1)}, bf16[8,256,256]{2,1,0:T(8,128)(2,1)S(1)}, u32[]{:S(2)}, u32[]{:S(2)}) %collective-permute-start.18) | collective-permute-done | bytes 1048608 | tf_op jit(solution)/shard_map/ppermute | solution.py:1088
  385.4 1.3 collective-permute-start.19
  386.7 31.8 %attend_back.7 = (bf16[8,256,256]{2,1,0:T(8,128)(2,1)S(1)}, bf16[8,256,512]{2,1,0:T(8,128)(2,1)}, f32[256,512]{1,0:T(8,128)S(1)}, f32[256,512]{1,0:T(8,128)S(1)}) custom-call(s32[8]{0:T(128)S(1)} %fusion.9.lo, s32[1]{0:T(128)} %bitcast.9.bases, bf16[8,256,512]{2,1,0:T(8,128)(2,1)} %bitcast.84, bf16[8,256,512]{2,1,0:T(8,128)(2,1)} %bitcast.88, ...), custom_call_target="tpu_custom_call" | custom-call | flops 10737418240 | bytes 33554432 | tf_op jit(solution)/shard_map/attend_back/pallas_call | solution.py:301
  418.5 3.0 fusion.15
  421.6 8.8 %collective-permute-done.19 = bf16[8,256,256]{2,1,0:T(8,128)(2,1)S(1)} collective-permute-done((bf16[8,256,256]{2,1,0:T(8,128)(2,1)S(1)}, bf16[8,256,256]{2,1,0:T(8,128)(2,1)S(1)}, u32[]{:S(2)}, u32[]{:S(2)}) %collective-permute-start.19) | collective-permute-done | bytes 1048608 | tf_op jit(solution)/shard_map/ppermute | solution.py:1088
  430.8 0.9 fusion.17
  431.7 1.9 collective-permute-done.20
  433.6 0.8 copy-done.15
  434.4 120.8 %finish.1 = (bf16[4,1456,256]{2,1,0:T(8,128)(2,1)}, f32[1024,1024]{1,0:T(8,128)}) custom-call(bf16[6656,256]{1,0:T(8,128)(2,1)} %bitcast.77, bf16[2816,256]{1,0:T(8,128)(2,1)} %bitcast.90, bf16[1024,1024]{1,0:T(8,128)(2,1)} %bitcast.74, f32[1,1024]{1,0:T(1,128)} %bitcast.99, bf16[1024,512]{1,0:T(8,128)(2,1)} %bitcast.76, bf16[1024,512]{1,0:T(8,128)(2,1)} %bitcast.91, ...), custom_call_target="tpu_custom_call" | custom-call | tf_op jit(solution)/shard_map/finish/pallas_call | solution.py:863
  555.1 1.8 copy-done
  557.0 2.1 lay_out.1
  559.1 0.5 slice_bitcast_fusion
  559.6 1.6 copy.45
  561.2 1.6 copy.46
  562.8 4.8 copy.53
  (77 shorter events, 3.4 us)
Async XLA Ops:
  7.2 2.3 copy-start.11
  7.2 2.3 copy-start.17
  7.2 426.4 %reduce-scatter.5.cloned.1.call-start = ((), (), s32[]{:S(2)}) async-start(), calls=%async_computation.3 | async-start | bytes 7208960 | tf_op jit(solution)/shard_map/reduce_scatter | solution.py:1063
  9.5 1.2 copy-start.13
  10.7 1.3 copy-start.12
  12.1 2.8 collective-permute-start.2
  14.8 4.7 copy-start.16
  14.9 27.6 %collective-permute-start.3 = (bf16[8,256,256]{2,1,0:T(8,128)(2,1)S(1)}, bf16[8,256,256]{2,1,0:T(8,128)(2,1)S(1)}, u32[]{:S(2)}, u32[]{:S(2)}) collective-permute-start(bf16[8,256,256]{2,1,0:T(8,128)(2,1)S(1)} %bitcast.63), channel_id=1, source_target_pairs={{0,2},{1,3},{2,4},{3,5},{4,6},{5,7},{8,10},{9,11},{10,12},{11,13},... | collective-permute-start | bytes 3145736 | tf_op jit(solution)/shard_map/ppermute | solution.py:1026
  42.5 12.6 %copy-start.6 = (bf16[8,256,256]{2,1,0:T(8,128)(2,1)}, bf16[8,256,256]{2,1,0:T(8,128)(2,1)S(1)}, u32[]{:S(2)}) copy-start(bf16[8,256,256]{2,1,0:T(8,128)(2,1)S(1)} %collective-permute-done.3.refs_5_.refs_8_) | copy-start | bytes 3145732
  42.5 26.1 %collective-permute-start.5 = (bf16[8,256,256]{2,1,0:T(8,128)(2,1)S(1)}, bf16[8,256,256]{2,1,0:T(8,128)(2,1)S(1)}, u32[]{:S(2)}, u32[]{:S(2)}) collective-permute-start(bf16[8,256,256]{2,1,0:T(8,128)(2,1)S(1)} %collective-permute-done.3.refs_5_.refs_8_), channel_id=1, source_target_pairs={{0,1},{1,0},{2,3},{3,2},{4,5},{5,4},{6,7},{7,6},{8,9},{9,8},{10,11... | collective-permute-start | bytes 3145736 | tf_op jit(solution)/shard_map/ppermute | solution.py:540
  44.0 26.4 %collective-permute-start.4 = (bf16[8,256,256]{2,1,0:T(8,128)(2,1)S(1)}, bf16[8,256,256]{2,1,0:T(8,128)(2,1)}, u32[]{:S(2)}, u32[]{:S(2)}) collective-permute-start(bf16[8,256,256]{2,1,0:T(8,128)(2,1)S(1)} %collective-permute-done.3.refs_5_.refs_8_), channel_id=1, source_target_pairs={{0,2},{1,3},{2,4},{3,5},{4,6},{5,7},{8,10},{9,11},{10,12},{11,13},... | collective-permute-start | bytes 3145736 | tf_op jit(solution)/shard_map/ppermute | solution.py:1026
  50.9 35.8 %collective-permute-start = (s32[4,256]{1,0:T(4,128)S(1)}, s32[4,256]{1,0:T(4,128)S(1)}, u32[]{:S(2)}, u32[]{:S(2)}) collective-permute-start(s32[4,256]{1,0:T(4,128)S(1)} %broadcast_subtract_fusion), channel_id=1, source_target_pairs={{0,8},{8,0},{16,24},{24,16},{1,9},{9,1},{17,25},{25,17},{2,10},{10... | collective-permute-start | bytes 12296 | tf_op jit(solution)/shard_map/ppermute | solution.py:540
  55.1 31.8 %collective-permute-start.1 = (bf16[1024,512]{1,0:T(8,128)(2,1)}, bf16[1024,512]{1,0:T(8,128)(2,1)}, u32[]{:S(2)}, u32[]{:S(2)}) collective-permute-start(bf16[1024,512]{1,0:T(8,128)(2,1)} %convolution_convert_fusion), channel_id=1, source_target_pairs={{0,8},{8,0},{16,24},{24,16},{1,9},{9,1},{17,25},{25,17},{2,10},{10... | collective-permute-start | bytes 3145736 | tf_op jit(solution)/shard_map/ppermute | solution.py:540
  55.6 58.2 %collective-permute-start.9 = (bf16[8,256,256]{2,1,0:T(8,128)(2,1)S(1)}, bf16[8,256,256]{2,1,0:T(8,128)(2,1)}, u32[]{:S(2)}, u32[]{:S(2)}) collective-permute-start(bf16[8,256,256]{2,1,0:T(8,128)(2,1)S(1)} %bitcast.64), channel_id=1, source_target_pairs={{0,1},{1,0},{2,3},{3,2},{4,5},{5,4},{6,7},{7,6},{8,9},{9,8},{10,11... | collective-permute-start | bytes 3145736 | tf_op jit(solution)/shard_map/ppermute | solution.py:540
  68.5 13.0 %copy-start.8 = (bf16[8,256,256]{2,1,0:T(8,128)(2,1)}, bf16[8,256,256]{2,1,0:T(8,128)(2,1)S(1)}, u32[]{:S(2)}) copy-start(bf16[8,256,256]{2,1,0:T(8,128)(2,1)S(1)} %collective-permute-done.5.refs_6_.refs_9_) | copy-start | bytes 3145732
  70.4 41.9 %collective-permute-start.7 = (bf16[8,256,256]{2,1,0:T(8,128)(2,1)}, bf16[8,256,256]{2,1,0:T(8,128)(2,1)}, u32[]{:S(2)}, u32[]{:S(2)}) collective-permute-start(bf16[8,256,256]{2,1,0:T(8,128)(2,1)} %collective-permute-done.4.refs_7_.refs_8_), channel_id=1, source_target_pairs={{0,1},{1,0},{2,3},{3,2},{4,5},{5,4},{6,7},{7,6},{8,9},{9,8},{10,11... | collective-permute-start | bytes 3145736 | tf_op jit(solution)/shard_map/ppermute | solution.py:540
  70.9 41.4 %collective-permute-start.6 = (bf16[8,256,256]{2,1,0:T(8,128)(2,1)}, bf16[8,256,256]{2,1,0:T(8,128)(2,1)}, u32[]{:S(2)}, u32[]{:S(2)}) collective-permute-start(bf16[8,256,256]{2,1,0:T(8,128)(2,1)} %collective-permute-done.4.refs_7_.refs_8_), channel_id=1, source_target_pairs={{0,2},{1,3},{2,4},{3,5},{4,6},{5,7},{8,10},{9,11},{10,12},{11,13},... | collective-permute-start | bytes 3145736 | tf_op jit(solution)/shard_map/ppermute | solution.py:1026
  86.7 186.2 %copy-start.1 = (bf16[2,1024,256]{2,1,0:T(8,128)(2,1)}, bf16[2,1024,256]{2,1,0:T(8,128)(2,1)S(1)}, u32[]{:S(2)}) copy-start(bf16[2,1024,256]{2,1,0:T(8,128)(2,1)S(1)} %get-tuple-element.156.refs_6_) | copy-start | bytes 3145732
  86.8 27.0 %copy-start.7 = (bf16[8,256,256]{2,1,0:T(8,128)(2,1)S(1)}, bf16[8,256,256]{2,1,0:T(8,128)(2,1)}, u32[]{:S(2)}) copy-start(bf16[8,256,256]{2,1,0:T(8,128)(2,1)} %copy-done.6) | copy-start | bytes 3145732
  86.8 27.0 %copy-start.9 = (bf16[8,256,256]{2,1,0:T(8,128)(2,1)S(1)}, bf16[8,256,256]{2,1,0:T(8,128)(2,1)}, u32[]{:S(2)}) copy-start(bf16[8,256,256]{2,1,0:T(8,128)(2,1)} %copy-done.8) | copy-start | bytes 3145732
  112.3 24.1 %collective-permute-start.8 = (bf16[8,256,256]{2,1,0:T(8,128)(2,1)}, bf16[8,256,256]{2,1,0:T(8,128)(2,1)S(1)}, u32[]{:S(2)}, u32[]{:S(2)}) collective-permute-start(bf16[8,256,256]{2,1,0:T(8,128)(2,1)} %collective-permute-done.6.refs_3_.refs_8_), channel_id=1, source_target_pairs={{0,1},{1,0},{2,3},{3,2},{4,5},{5,4},{6,7},{7,6},{8,9},{9,8},{10,11... | collective-permute-start | bytes 3145736 | tf_op jit(solution)/shard_map/ppermute | solution.py:540
  113.8 22.6 %copy-start.5 = (bf16[512,256]{1,0:T(8,128)(2,1)S(1)}, bf16[512,256]{1,0:T(8,128)(2,1)}, u32[]{:S(2)}) copy-start(bf16[512,256]{1,0:T(8,128)(2,1)} %copy.39) | copy-start | bytes 786436
  136.4 11.1 %copy-start.10 = (bf16[8,256,256]{2,1,0:T(8,128)(2,1)}, bf16[8,256,256]{2,1,0:T(8,128)(2,1)S(1)}, u32[]{:S(2)}) copy-start(bf16[8,256,256]{2,1,0:T(8,128)(2,1)S(1)} %collective-permute-done.8.refs_4_.refs_9_) | copy-start | bytes 3145732
  149.0 3.0 collective-permute-start.10
  194.3 239.3 %reduce-scatter.3.cloned.1.call-start = ((), (), s32[]{:S(2)}) async-start(), calls=%async_computation.2 | async-start | bytes 17039360 | tf_op jit(solution)/shard_map/reduce_scatter | solution.py:1064
  254.6 2.9 collective-permute-start.11
  269.9 26.9 %collective-permute-start.16 = (bf16[8,256,256]{2,1,0:T(8,128)(2,1)S(1)}, bf16[8,256,256]{2,1,0:T(8,128)(2,1)S(1)}, u32[]{:S(2)}, u32[]{:S(2)}) collective-permute-start(bf16[8,256,256]{2,1,0:T(8,128)(2,1)S(1)} %get-tuple-element.96), channel_id=1, source_target_pairs={{0,1},{1,0},{2,3},{3,2},{4,5},{5,4},{6,7},{7,6},{8,9},{9,8},{10,11... | collective-permute-start | bytes 3145736 | tf_op jit(solution)/shard_map/ppermute | solution.py:540
  283.3 47.8 %collective-permute-start.15 = (bf16[8,256,256]{2,1,0:T(8,128)(2,1)S(1)}, bf16[8,256,256]{2,1,0:T(8,128)(2,1)S(1)}, u32[]{:S(2)}, u32[]{:S(2)}) collective-permute-start(bf16[8,256,256]{2,1,0:T(8,128)(2,1)S(1)} %get-tuple-element.94), channel_id=1, source_target_pairs={{0,1},{1,0},{2,3},{3,2},{4,5},{5,4},{6,7},{7,6},{8,9},{9,8},{10,11... | collective-permute-start | bytes 3145736 | tf_op jit(solution)/shard_map/ppermute | solution.py:540
  297.2 37.6 %collective-permute-start.17 = (bf16[8,256,256]{2,1,0:T(8,128)(2,1)S(1)}, bf16[8,256,256]{2,1,0:T(8,128)(2,1)S(1)}, u32[]{:S(2)}, u32[]{:S(2)}) collective-permute-start(bf16[8,256,256]{2,1,0:T(8,128)(2,1)S(1)} %add_convert_fusion.3), channel_id=1, source_target_pairs={{2,0},{3,1},{4,2},{5,3},{6,4},{7,5},{10,8},{11,9},{12,10},{13,11},... | collective-permute-start | bytes 3145736 | tf_op jit(solution)/shard_map/ppermute | solution.py:1088
  311.2 44.0 %collective-permute-start.14 = (bf16[8,256,256]{2,1,0:T(8,128)(2,1)S(1)}, bf16[8,256,256]{2,1,0:T(8,128)(2,1)S(1)}, u32[]{:S(2)}, u32[]{:S(2)}) collective-permute-start(bf16[8,256,256]{2,1,0:T(8,128)(2,1)S(1)} %get-tuple-element.92), channel_id=1, source_target_pairs={{0,1},{1,0},{2,3},{3,2},{4,5},{5,4},{6,7},{7,6},{8,9},{9,8},{10,11... | collective-permute-start | bytes 3145736 | tf_op jit(solution)/shard_map/ppermute | solution.py:540
  335.2 49.7 %collective-permute-start.18 = (bf16[8,256,256]{2,1,0:T(8,128)(2,1)S(1)}, bf16[8,256,256]{2,1,0:T(8,128)(2,1)S(1)}, u32[]{:S(2)}, u32[]{:S(2)}) collective-permute-start(bf16[8,256,256]{2,1,0:T(8,128)(2,1)S(1)} %add_convert_fusion.2), channel_id=1, source_target_pairs={{2,0},{3,1},{4,2},{5,3},{6,4},{7,5},{10,8},{11,9},{12,10},{13,11},... | collective-permute-start | bytes 3145736 | tf_op jit(solution)/shard_map/ppermute | solution.py:1088
  336.5 85.0 %collective-permute-start.13 = (bf16[8,256,256]{2,1,0:T(8,128)(2,1)S(1)}, bf16[8,256,256]{2,1,0:T(8,128)(2,1)S(1)}, u32[]{:S(2)}, u32[]{:S(2)}) collective-permute-start(bf16[8,256,256]{2,1,0:T(8,128)(2,1)S(1)} %get-tuple-element.90), channel_id=1, source_target_pairs={{0,1},{1,0},{2,3},{3,2},{4,5},{5,4},{6,7},{7,6},{8,9},{9,8},{10,11... | collective-permute-start | bytes 3145736 | tf_op jit(solution)/shard_map/ppermute | solution.py:540
  385.0 1.8 copy-start.2
  385.4 44.9 %collective-permute-start.19 = (bf16[8,256,256]{2,1,0:T(8,128)(2,1)S(1)}, bf16[8,256,256]{2,1,0:T(8,128)(2,1)S(1)}, u32[]{:S(2)}, u32[]{:S(2)}) collective-permute-start(bf16[8,256,256]{2,1,0:T(8,128)(2,1)S(1)} %add_convert_fusion.1), channel_id=1, source_target_pairs={{2,0},{3,1},{4,2},{5,3},{6,4},{7,5},{10,8},{11,9},{12,10},{13,11},... | collective-permute-start | bytes 3145736 | tf_op jit(solution)/shard_map/ppermute | solution.py:1088
  418.5 3.0 copy-start.3
  418.5 3.0 copy-start.4
  421.6 10.1 %collective-permute-start.12 = (bf16[4,256,512]{2,1,0:T(8,128)(2,1)S(1)}, bf16[4,256,512]{2,1,0:T(8,128)(2,1)S(1)}, u32[]{:S(2)}, u32[]{:S(2)}) collective-permute-start(bf16[4,256,512]{2,1,0:T(8,128)(2,1)S(1)} %get-tuple-element.150), channel_id=1, source_target_pairs={{0,8},{8,0},{16,24},{24,16},{1,9},{9,1},{17,25},{25,17},{2,10},{10... | collective-permute-start | bytes 3145736 | tf_op jit(solution)/shard_map/ppermute | solution.py:540
  431.7 1.9 collective-permute-start.20
  431.7 1.9 copy-start.14
  433.6 0.8 copy-start.15
  555.1 1.8 copy-start
Sparse Core Ops, SparseCore 0:
  194.4 78.2 reduce-scatter.4
  275.4 109.5 reduce-scatter.2

commit v4 on v3

--- a/solution.py
+++ b/solution.py
@@ -14,8 +14,6 @@
 LOG2E = math.log2(math.e)
 LN2 = math.log(2.0)
 QUAD = 4
-FORWARD_GROUP = 1
-BACKWARD_GROUP = 8
 f32 = jnp.float32
 bf16 = jnp.bfloat16
 
@@ -73,22 +71,18 @@
         out_ref[:, columns] += found
 
 
-def seg_mask(diagonal, base, start, heads):
+def seg_mask(base, own_base, start):
     tokens = start.shape[-1]
-    start = jnp.concatenate([start - base] * heads, axis=1)
-    key_at = lax.broadcasted_iota(jnp.int32, (tokens, heads * tokens), 0)
-    allow = key_at >= start
-    if diagonal:
-        at = lax.broadcasted_iota(jnp.int32, (1, tokens), 1)
-        allow = allow & (key_at <= jnp.concatenate([at] * heads, axis=1))
-    return allow
-
-
-def attend_kernel(count, first, last, diagonal_at, lo, bases, *refs):
+    key_at = lax.broadcasted_iota(jnp.int32, (tokens, tokens), 0)
+    query_at = lax.broadcasted_iota(jnp.int32, (tokens, tokens), 1)
+    return (key_at >= start - base) & (key_at <= query_at + (own_base - base))
+
+
+def attend_kernel(count, first, last, lo, bases, *refs):
     refs = list(refs)
     take = lambda k: [refs.pop(0) for _ in range(k)]
     query_ref, start_ref, key_lift_ref = take(3)
-    segs = take(count)
+    seg_refs = take(count)
     if not first:
         top_in, total_in, mix_in = take(3)
     if last:
@@ -96,12 +90,12 @@
         out_ref, lse_ref, mix_ref = take(3)
     else:
         top_out, total_out, mix_out = take(3)
-    expanded, top, total, mix = take(4)
+    expanded, top, total, mix, segs = take(5)
     tokens = query_ref.shape[1]
     heads = expanded.shape[1] // tokens
     row = pl.program_id(0)
     scale = HEAD_WIDTH ** (-0.5) * LOG2E
-    touches = [(bases[i] >= 0) & (bases[i] + tokens - 1 >= lo[row]) for i in range(count)]
+    touched = lambda i: (bases[i] >= 0) & (bases[i] + tokens - 1 >= lo[row])
     if first:
         expand_heads(query_ref[0], key_lift_ref, scale, expanded)
         top[...] = jnp.full_like(top, blocked)
@@ -112,20 +106,22 @@
         total[...] = total_in[0]
         mix[...] = mix_in[0].astype(f32)
 
-        @pl.when(functools.reduce(jnp.logical_or, touches))
+        @pl.when(functools.reduce(jnp.logical_or, [touched(i) for i in range(count)]))
         def _():
             expand_heads(query_ref[0], key_lift_ref, scale, expanded)
 
-    start = start_ref[0]
     for i in range(count):
-
-        @pl.when(touches[i])
+        segs[i] = seg_refs[i][0]
+
+    @pl.loop(0, count)
+    def _(i):
+        @pl.when(touched(i))
         def _():
-            latent = segs[i][0]
+            latent = segs[i]
             latent_t = latent.T
-            allow = seg_mask(i == diagonal_at, bases[i], start, FORWARD_GROUP)
-            for g in range(0, heads, FORWARD_GROUP):
-                at = slice(g * tokens, (g + FORWARD_GROUP) * tokens)
+            allow = seg_mask(bases[i], bases[count], start_ref[0])
+            for h in range(heads):
+                at = slice(h * tokens, (h + 1) * tokens)
                 score = jnp.where(allow, matmul(latent, expanded[:, at]), blocked)
                 old = top[:, at]
                 new = jnp.maximum(old, jnp.max(score, axis=0, keepdims=True))
@@ -149,11 +145,11 @@
     return pl.BlockSpec(array.shape, lambda *_: (0,) * len(array.shape))
 
 
-def by_row(shape):
-    return pl.BlockSpec((1,) + tuple(shape[1:]), lambda r, *_: (r,) + (0,) * (len(shape) - 1))
-
-
-def attend_part(queries, start, key_lift, value_lift_t, lo, segs, bases, diagonal_at, state, last):
+def by_row(shape, begin=0):
+    return pl.BlockSpec((1,) + tuple(shape[1:]), lambda r, *_: (r + begin,) + (0,) * (len(shape) - 1))
+
+
+def attend_part(queries, start, key_lift, value_lift_t, lo, segs, bases, state, last):
     rows, tokens, width = queries.shape
     heads = width // HEAD_WIDTH
     latent = segs[0].shape[-1]
@@ -174,7 +170,7 @@
         outs = state_shapes
     blocks = rows * heads * len(segs)
     return pl.pallas_call(
-        functools.partial(attend_kernel, len(segs), state is None, last, diagonal_at),
+        functools.partial(attend_kernel, len(segs), state is None, last),
         out_shape=outs,
         grid_spec=pltpu.PrefetchScalarGridSpec(
             num_scalar_prefetch=2,
@@ -186,6 +182,7 @@
                 pltpu.VMEM((1, heads * tokens), f32),
                 pltpu.VMEM((1, heads * tokens), f32),
                 pltpu.VMEM((latent, heads * tokens), f32),
+                pltpu.VMEM((len(segs), tokens, latent), bf16),
             ],
         ),
         compiler_params=pltpu.CompilerParams(
@@ -194,73 +191,72 @@
         cost_estimate=pl.CostEstimate(
             flops=blocks * tokens * tokens * latent * 4,
             bytes_accessed=rows * heads * latent * tokens * 4,
-            transcendentals=blocks * tokens * tokens,
+            transcendentals=0,
         ),
         name="attend",
     )(lo, bases, *args)
 
 
-def attend_back_kernel(count, first, last, diagonal_at, lo, bases, *refs):
+def attend_back_kernel(count, begin, first, last, lo, bases, *refs):
     refs = list(refs)
     take = lambda k: [refs.pop(0) for _ in range(k)]
     query_ref, grad_ref, lse_ref, mix_ref, start_ref, key_lift_ref, value_lift_ref, key_lift_t_ref = take(8)
-    segs = take(count)
+    seg_refs = take(count)
     if not first:
         query_back_in, key_up_in = take(2)
-    seg_grads = take(count)
+        if last:
+            (value_up_in,) = take(1)
+    grad_refs = take(count)
     query_back_ref, key_up_ref = take(2)
     if last:
         (value_up_ref,) = take(1)
-    expanded, expanded_grad, delta, back, query_back = take(5)
+    expanded, expanded_grad, delta, back, query_back, segs, seg_grads = take(7)
     latent_size = expanded.shape[0]
     tokens = query_ref.shape[1]
     heads = expanded.shape[1] // tokens
     row = pl.program_id(0)
     scale = HEAD_WIDTH ** (-0.5)
-    touches = [(bases[i] >= 0) & (bases[i] + tokens - 1 >= lo[row]) for i in range(count)]
+    touched = lambda i: (bases[i] >= 0) & (bases[i] + tokens - 1 >= lo[row + begin])
+    any_touched = functools.reduce(jnp.logical_or, [touched(i) for i in range(count)])
 
     @pl.when(row == 0)
     def _():
         key_up_ref[...] = jnp.zeros_like(key_up_ref) if first else key_up_in[...]
         if last:
-            value_up_ref[...] = jnp.zeros_like(value_up_ref)
+            value_up_ref[...] = value_up_in[...]
 
     query_back[...] = jnp.zeros_like(query_back) if first else query_back_in[0]
-
-    @pl.when(functools.reduce(jnp.logical_or, touches))
+    seg_grads[...] = jnp.zeros_like(seg_grads)
+
+    @pl.when(any_touched)
     def _():
         expand_heads(query_ref[0], key_lift_ref, scale * LOG2E, expanded)
         expand_heads(grad_ref[0], value_lift_ref, 1.0, expanded_grad)
         delta[...] = jnp.sum(mix_ref[0].astype(f32) * expanded_grad[...].astype(f32), axis=0, keepdims=True)
         back[...] = jnp.zeros_like(back)
-
-    start = start_ref[0]
+        for i in range(count):
+            segs[i] = seg_refs[i][0]
+
+    @pl.loop(0, count)
+    def _(i):
+        @pl.when(touched(i))
+        def _():
+            latent = segs[i]
+            allow = seg_mask(bases[i], bases[count], start_ref[0])
+            allow = jnp.concatenate([allow] * heads, axis=1)
+            score = matmul(latent, expanded[...])
+            probs = jnp.where(allow, jnp.exp2(score - lse_ref[0]), 0.0)
+            dprobs = matmul(latent, expanded_grad[...])
+            dscore = (probs * (dprobs - delta[...])).astype(bf16)
+            by_key = matmul_nt(dscore, expanded[...])
+            by_value = matmul_nt(probs.astype(bf16), expanded_grad[...])
+            seg_grads[i] = (by_key * LN2 + by_value).astype(bf16)
+            back[...] += matmul(latent.T, dscore)
+
     for i in range(count):
-
-        @pl.when(touches[i])
-        def _():
-            latent = segs[i][0]
-            latent_t = latent.T
-            allow = seg_mask(i == diagonal_at, bases[i], start, BACKWARD_GROUP)
-            by_key = by_value = None
-            for g in range(0, heads, BACKWARD_GROUP):
-                at = slice(g * tokens, (g + BACKWARD_GROUP) * tokens)
-                score = matmul(latent, expanded[:, at])
-                dprobs = matmul(latent, expanded_grad[:, at])
-                probs = jnp.where(allow, jnp.exp2(score - lse_ref[0, :, at]), 0.0)
-                dscore = (probs * (dprobs - delta[:, at])).astype(bf16)
-                key_term = matmul_nt(dscore, expanded[:, at])
-                value_term = matmul_nt(probs.astype(bf16), expanded_grad[:, at])
-                by_key = key_term if g == 0 else by_key + key_term
-                by_value = value_term if g == 0 else by_value + value_term
-                back[:, at] += matmul(latent_t, dscore)
-            seg_grads[i][0] = (by_key * LN2 + by_value).astype(bf16)
-
-        @pl.when(jnp.logical_not(touches[i]))
-        def _():
-            seg_grads[i][0] = jnp.zeros((tokens, latent_size), bf16)
-
-    @pl.when(functools.reduce(jnp.logical_or, touches))
+        grad_refs[i][0] = seg_grads[i]
+
+    @pl.when(any_touched)
     def _():
         part = (back[...] * scale).astype(bf16)
         query_back[...] += lift_heads(part, key_lift_t_ref, tokens)
@@ -274,32 +270,31 @@
 
 
 def attend_back_part(
-    queries, grads, lse, mix, start, key_lift, value_lift, key_lift_t, lo, segs, bases,
-    diagonal_at, state, last,
+    queries, grads, lse, mix, start, key_lift, value_lift, key_lift_t, lo, segs, bases, state, last, begin, rows,
 ):
-    rows, tokens, width = queries.shape
+    _, tokens, width = queries.shape
     heads = width // HEAD_WIDTH
     latent = segs[0].shape[-1]
     shape = jax.ShapeDtypeStruct
     back_shape = shape((rows, width, tokens), f32)
     up_shape = shape((latent, width), f32)
     args = [queries, grads, lse, mix, start, key_lift, value_lift, key_lift_t, *segs]
-    specs = [by_row(a.shape) for a in (queries, grads, lse, mix, start)]
+    specs = [by_row(a.shape, begin) for a in (queries, grads, lse, mix, start)]
     specs += [whole(key_lift), whole(value_lift), whole(key_lift_t)]
-    specs += [by_row(s.shape) for s in segs]
+    specs += [by_row(s.shape, begin) for s in segs]
     if state is not None:
         args += list(state)
-        specs += [by_row(back_shape.shape), whole(up_shape)]
-    outs = [shape(s.shape, bf16) for s in segs]
-    out_specs = [by_row(s.shape) for s in segs]
-    outs += [shape(queries.shape, bf16) if last else back_shape, up_shape]
-    out_specs += [by_row(outs[-2].shape), whole(up_shape)]
+        specs.append(by_row(state[0].shape, begin))
+        specs += [whole(up_shape)] * (len(state) - 1)
+    outs = [shape((rows, tokens, latent), bf16) for _ in segs]
+    outs += [shape((rows, tokens, width), bf16) if last else back_shape, up_shape]
+    out_specs = [by_row(o.shape) for o in outs[:-1]] + [whole(up_shape)]
     if last:
         outs.append(up_shape)
         out_specs.append(whole(up_shape))
     blocks = rows * heads * len(segs)
     return pl.pallas_call(
-        functools.partial(attend_back_kernel, len(segs), state is None, last, diagonal_at),
+        functools.partial(attend_back_kernel, len(segs), begin, state is None, last),
         out_shape=outs,
         grid_spec=pltpu.PrefetchScalarGridSpec(
             num_scalar_prefetch=2,
@@ -312,15 +307,17 @@
                 pltpu.VMEM((1, heads * tokens), f32),
                 pltpu.VMEM((latent, heads * tokens), f32),
                 pltpu.VMEM((width, tokens), f32),
+                pltpu.VMEM((len(segs), tokens, latent), bf16),
+                pltpu.VMEM((len(segs), tokens, latent), bf16),
             ],
         ),
         compiler_params=pltpu.CompilerParams(
             dimension_semantics=("arbitrary",), vmem_limit_bytes=48 << 20
         ),
         cost_estimate=pl.CostEstimate(
-            flops=blocks * tokens * tokens * latent * 10,
-            bytes_accessed=rows * heads * latent * tokens * 8,
-            transcendentals=blocks * tokens * tokens,
+            flops=blocks * tokens * tokens * latent,
+            bytes_accessed=rows * heads * latent * tokens,
+            transcendentals=0,
         ),
         name="attend_back",
     )(lo, bases, *args)
@@ -352,7 +349,7 @@
         inputs_ref, mine_ref, got_ref, output_ref, gain_ref, cotangent_ref, keep_ref,
         gate_ref, up_ref, down_ref,
         hidden_out_ref, resid, normed, back, active_ref, slope_ref, down_grad_ref,
-        result,
+        result, hidden,
     ) = refs
     step = pl.program_id(0)
     count = inputs_ref.shape[0]
@@ -372,15 +369,18 @@
             back[at] = (cotangent_ref[at].astype(f32) * keep_ref[at]).astype(bf16)
         result[...] = jnp.zeros_like(result)
 
-    gate = matmul(normed[...], gate_ref[...])
-    up = matmul(normed[...], up_ref[...])
-    sigmoid = 1.0 / (1.0 + jnp.exp(-gate))
-    active = gate * sigmoid
-    hidden = (active * up).astype(bf16)
-    active_ref[...] = active.astype(bf16)
-    slope_ref[...] = (up * (sigmoid * (1.0 + gate * (1.0 - sigmoid)))).astype(bf16)
-    put_pieces(down_grad_ref, matmul_tn(hidden, back[...]))
-    result[...] += matmul(hidden, down_ref[...])
+    part = count // 4
+    for t in range(0, count, part):
+        at = slice(t, t + part)
+        gate = matmul(normed[at], gate_ref[...])
+        up = matmul(normed[at], up_ref[...])
+        sigmoid = 1.0 / (1.0 + jnp.exp(-gate))
+        active = gate * sigmoid
+        hidden[at] = (active * up).astype(bf16)
+        active_ref[at] = active.astype(bf16)
+        slope_ref[at] = (up * (sigmoid * (1.0 + gate * (1.0 - sigmoid)))).astype(bf16)
+    put_pieces(down_grad_ref, matmul_tn(hidden[...], back[...]))
+    result[...] += matmul(hidden[...], down_ref[...])
 
     @pl.when(step == pl.num_programs(0) - 1)
     def _():
@@ -392,7 +392,7 @@
         mine_ref, got_ref, output_ref, gain_ref, resid_ref, normed, back,
         active_ref, slope_ref, gate_ref, up_ref, down_ref,
         grad_resid_ref, head_mine_ref, head_sent_ref, gain_grad_ref, grads_ref,
-        grad_two, low, staged, staged_out, sems, out_sem,
+        grad_two, both, low, staged, staged_out, sems, out_sem,
     ) = refs
     step = pl.program_id(0)
     steps = pl.num_programs(0)
@@ -419,14 +419,19 @@
     def _():
         grad_two[...] = jnp.zeros_like(grad_two)
 
-    grad_act = matmul_nt(back[...], down_ref[...])
-    up_back = (grad_act * active_ref[...].astype(f32)).astype(bf16)
-    gate_back = (grad_act * slope_ref[...].astype(f32)).astype(bf16)
-    put_pieces(staged.at[slot, 1], matmul_tn(up_back, normed[...]))
-    put_pieces(staged.at[slot, 0], matmul_tn(gate_back, normed[...]))
+    part = count // 4
+    for t in range(0, count, part):
+        at = slice(t, t + part)
+        grad_act = matmul_nt(back[at], down_ref[...])
+        both[at, :chunk] = (grad_act * slope_ref[at].astype(f32)).astype(bf16)
+        both[at, chunk:] = (grad_act * active_ref[at].astype(f32)).astype(bf16)
     for kind in range(2):
+        put_pieces(staged.at[slot, kind], matmul_tn(both[:, kind * chunk : (kind + 1) * chunk], normed[...]))
         leave(slot, kind, step).start()
-    grad_two[...] += matmul_nt(gate_back, gate_ref[...]) + matmul_nt(up_back, up_ref[...])
+    weights = jnp.concatenate([gate_ref[...], up_ref[...]], axis=1)
+    for t in range(0, count, part):
+        at = slice(t, t + part)
+        grad_two[at] += matmul_nt(both[at], weights)
 
     @pl.when(step == steps - 1)
     def _():
@@ -488,7 +493,7 @@
             in_specs=[once(a) for a in firsts] + [by_columns, by_columns, by_rows],
             out_specs=[once(o) for o in outs[:4]]
             + [kept_columns, kept_columns, pl.BlockSpec((pieces, chunk, piece), lambda c, *_: (0, c, 0))],
-            scratch_shapes=[pltpu.VMEM((count, width), f32)],
+            scratch_shapes=[pltpu.VMEM((count, width), f32), pltpu.VMEM((count, chunk), bf16)],
         ),
         compiler_params=params,
         cost_estimate=pl.CostEstimate(
@@ -517,6 +522,7 @@
             out_specs=[once(o) for o in outs[:4]] + [pl.BlockSpec(memory_space=pl.ANY)],
             scratch_shapes=[
                 pltpu.VMEM((count, width), f32),
+                pltpu.VMEM((count, 2 * chunk), bf16),
                 pltpu.VMEM((count, width), bf16),
                 pltpu.VMEM((2, 2, pieces, chunk, piece), bf16),
                 pltpu.VMEM((pieces, width, piece), bf16),
@@ -540,7 +546,7 @@
     return lax.ppermute(array, axis, [(i, i ^ (1 << bit)) for i in range(size)])
 
 
-def late_parts(core, inputs_ref, gain_ref, back_refs, query_ref, latent_ref, resid_ref, other_gain_ref, up_refs, normed, own, sent, grad_ref):
+def late_parts(core, inputs_ref, gain_ref, back_refs, before, query_ref, latent_ref, resid_ref, other_gain_ref, up_refs, normed, own, sent, grad_ref):
     along, count, _, piece = own.shape
     tokens, width = inputs_ref.shape
     query_mine, query_got, latent_mine, latent_got = back_refs
@@ -551,13 +557,18 @@
     block = min(256, tokens)
     mine = lambda ref, size: ref[:, pl.ds(pl.multiple_of(core * size, size), size)]
     theirs = lambda ref, size: ref[:, pl.ds(pl.multiple_of((1 - core) * size, size), size)]
+    for t in range(0, tokens, block):
+        at = slice(t, t + block)
+        row = inputs_ref[at].astype(f32)
+        scale = lax.rsqrt(jnp.mean(row * row, axis=-1, keepdims=True) + epsilon)
+        normed[at] = (row * scale * gain_ref[...]).astype(bf16)
+    before()
     gain_total = jnp.zeros((1, width), f32)
     for t in range(0, tokens, block):
         at = slice(t, t + block)
         row = inputs_ref[at].astype(f32)
         scale = lax.rsqrt(jnp.mean(row * row, axis=-1, keepdims=True) + epsilon)
         unit = row * scale
-        normed[at] = (unit * gain_ref[...]).astype(bf16)
         grad = (
             matmul_nt(query_mine[at], mine(query_ref, half))
             + matmul_nt(query_got[at], theirs(query_ref, half))
@@ -605,8 +616,8 @@
 
 
 def finish_kernel(
-    sections, early_refs, late_compute, own_ref, sent_ref, out_ref, late_got, late_from, got_first, got_next,
-    core_sems, along_sems, first_sems, first_late_sems, next_sems, out_sems,
+    sections, early_refs, late_compute, chain_refs, own_ref, sent_ref, out_ref, late_got, late_from, got_first, got_next,
+    chain_sems, core_sems, along_sems, first_sems, first_late_sems, next_sems, out_sems,
 ):
     along, count, late_rows, piece = own_ref.shape
     shared_rows = sent_ref.shape[2]
@@ -631,7 +642,9 @@
     x_peers = [(x * 2 + core, place) for x in x_others]
     head_peers = [(row_at, turned([bit])) for bit in range(bits)]
     barrier = pltpu.get_barrier_semaphore()
-    everyone = [core_peer] + x_peers + head_peers
+    above = (row_at, (place + 2) % count)
+    below = (row_at, (place + count - 2) % count)
+    everyone = [core_peer, above, below] + x_peers + head_peers
     for peer in everyone:
         pl.semaphore_signal(barrier, inc=1, device_id=peer, device_id_type=mesh)
     pl.semaphore_wait(barrier, len(everyone))
@@ -673,35 +686,27 @@
             first_sems, (i, n), head_peers[0],
         )
 
+    query_grad_ref, latent_grad_ref, joined_ref, chain_got, query_got, latent_low, latent_got = chain_refs
+    chain_copy = remote(joined_ref, chain_got, chain_sems, (0,), below)
+    chain_copy.start()
+    query_copy = remote(query_grad_ref.at[1], query_got, chain_sems, (1,), core_peer)
+    query_copy.start()
+    latent_copy = remote(latent_low.at[1], latent_got, chain_sems, (2,), core_peer)
     for i in range(len(first)):
         for n in range(len(sections)):
             first_early(i, n).start()
 
-    late_compute(core)
-    core_copy = remote(sent_ref, late_got, core_sems, (0,), core_peer)
-    core_copy.start()
-    core_copy.wait()
-
-    def core_add(i, carry):
-        j, s = i // count, i % count
-        late_got[j, s] = (own_ref[j, s, :shared_rows].astype(f32) + late_got[j, s].astype(f32)).astype(bf16)
-        return carry
-
-    lax.fori_loop(0, along * count, core_add, 0)
-    x_copies = []
-    for d, (x, peer) in enumerate(zip(x_others, x_peers)):
-        x_copies.append(
-            remote(late_got.at[x], late_from.at[d, :, pl.ds(0, shared_rows)], along_sems, (d, 0), peer)
-        )
-        x_copies.append(
-            remote(
-                own_ref.at[x, :, pl.ds(shared_rows, late_rows - shared_rows)],
-                late_from.at[d, :, pl.ds(shared_rows, late_rows - shared_rows)],
-                along_sems, (d, 1), peer,
-            )
-        )
-    for copy in x_copies:
-        copy.start()
+    def settle_latents():
+        chain_copy.wait()
+        for side in (1, 0):
+            size = latent_low.shape[1] // 2
+            for t in range(2):
+                at = slice(t * size, (t + 1) * size)
+                latent_low[side, at] = (latent_grad_ref[side, at] + chain_got[side, at].astype(f32)).astype(bf16)
+            if side == 1:
+                latent_copy.start()
+        query_copy.wait()
+        latent_copy.wait()
 
     def next_copy(bit, j, i, part, which):
         rows = pl.ds(part.start, part.stop - part.start)
@@ -763,8 +768,35 @@
     half = max(1, len(first) // 2)
     for i in range(half):
         early_step(i)
+    late_compute(core, settle_latents)
+    core_copy = remote(sent_ref, late_got, core_sems, (0,), core_peer)
+    core_copy.start()
+    core_copy.wait()
+
+    def core_add(i, carry):
+        j, s = i // count, i % count
+        late_got[j, s] = (own_ref[j, s, :shared_rows].astype(f32) + late_got[j, s].astype(f32)).astype(bf16)
+        return carry
+
+    lax.fori_loop(0, along * count, core_add, 0)
+    x_copies = []
+    for d, (x, peer) in enumerate(zip(x_others, x_peers)):
+        x_copies.append(
+            remote(late_got.at[x], late_from.at[d, :, pl.ds(0, shared_rows)], along_sems, (d, 0), peer)
+        )
+        x_copies.append(
+            remote(
+                own_ref.at[x, :, pl.ds(shared_rows, late_rows - shared_rows)],
+                late_from.at[d, :, pl.ds(shared_rows, late_rows - shared_rows)],
+                along_sems, (d, 1), peer,
+            )
+        )
+    for copy in x_copies:
+        copy.start()
+
+    early_step(half)
     late_begin()
-    for i in range(half, final):
+    for i in range(half + 1, final):
         early_step(i)
     for i in range(final):
         late_step(i)
@@ -819,7 +851,7 @@
     share = width // count
     bits = count.bit_length() - 1
     shared_rows = share + share // 2 + 16
-    late_rows = shared_rows + 2 * (late_args[4].shape[1] // count)
+    late_rows = shared_rows + 2 * (late_args[3].shape[2] // count)
     sections = []
     row = 0
     for which, of_one in enumerate(shares):
@@ -840,24 +872,27 @@
         out_ref, grad_ref = take(2)
         normed, own_ref, sent_ref, late_got, late_from, got_first = take(6)
         got_next = take(bits - 1)
+        chain_got, query_got, latent_low, latent_got, chain_sems = take(5)
         core_sems, along_sems, first_sems, first_late_sems = take(4)
         next_sems = take(bits - 1)
         (out_sems,) = take(1)
         (
-            inputs_ref, gain_ref, query_mine, query_got, latent_mine, latent_got,
+            inputs_ref, gain_ref, query_grad_ref, latent_grad_ref, joined_ref,
             query_ref, latent_ref, resid_ref, other_gain_ref, key_up, value_up,
         ) = late_refs
 
-        def late_compute(core):
+        def late_compute(core, before):
             late_parts(
-                core, inputs_ref, gain_ref, (query_mine, query_got, latent_mine, latent_got),
+                core, inputs_ref, gain_ref, (query_grad_ref.at[0], query_got, latent_low.at[0], latent_got), before,
                 query_ref, latent_ref, resid_ref, other_gain_ref, (key_up, value_up),
                 normed, own_ref, sent_ref, grad_ref,
             )
 
         finish_kernel(
-            sections, early_refs, late_compute, own_ref, sent_ref, out_ref, late_got, late_from,
-            got_first, got_next, core_sems, along_sems, first_sems, first_late_sems, next_sems, out_sems,
+            sections, early_refs, late_compute,
+            (query_grad_ref, latent_grad_ref, joined_ref, chain_got, query_got, latent_low, latent_got),
+            own_ref, sent_ref, out_ref, late_got, late_from,
+            got_first, got_next, chain_sems, core_sems, along_sems, first_sems, first_late_sems, next_sems, out_sems,
         )
 
     return pl.pallas_call(
@@ -878,6 +913,11 @@
         ]
         + [pltpu.VMEM((count >> (bit + 1), total, piece), bf16) for bit in range(1, bits)]
         + [
+            pltpu.VMEM(late_args[4].shape, bf16),
+            pltpu.VMEM(late_args[2].shape[1:], bf16),
+            pltpu.VMEM(late_args[4].shape, bf16),
+            pltpu.VMEM(late_args[4].shape[1:], bf16),
+            dma((2, 3)),
             dma((2, 1)),
             dma((2, along - 1, 2)),
             dma((2, count // 2, len(sections))),
@@ -1035,19 +1075,18 @@
             (jnp.where(there, base, -1), jnp.where(there & (other < own_base), other, -1))
         )
 
-    def pick(ks):
+    def pick(items):
         return (
-            [s for k in ks for s in segs[k]],
-            jnp.stack([b for k in ks for b in bases[k]]).astype(jnp.int32),
+            [segs[k][j] for k, j in items],
+            jnp.stack([bases[k][j] for k, j in items] + [own_base]).astype(jnp.int32),
         )
 
     parts = [range(0, steps - 1), range(steps - 1, steps)]
     state = None
     for i, ks in enumerate(parts):
-        seg_list, base_list = pick(ks)
+        seg_list, base_list = pick([(k, j) for k in ks for j in range(2)])
         state = attend_part(
-            queries, start, key_lift, value_lift_t, lo, seg_list, base_list,
-            0 if i == 0 else -1, state, i == len(parts) - 1,
+            queries, start, key_lift, value_lift_t, lo, seg_list, base_list, state, i == len(parts) - 1
         )
     head_out, lse, head_mix = state
     mixed_mine = head_out[:rows].reshape(count, group_width)
@@ -1063,40 +1102,43 @@
     early_down = lax.psum_scatter(down_grad, "rows", scatter_dimension=0, tiled=True)[0]
     early_feed = lax.psum_scatter(feed_grads, "rows", scatter_dimension=0, tiled=True)[0]
 
-    back_parts = [[(k, 0), (k, 1)] for k in range(steps - 1, 0, -1)]
-    back_parts[-1].append((0, 1))
-    back_parts.append([(0, 0)])
+    calls = [[(k, 0), (k, 1)] for k in range(steps - 1, 0, -1)]
+    calls[-1].append((0, 1))
+    calls.append([(0, 0)])
     state = None
-    seg_grads = {}
+    pieces_in = []
+    waiting = []
     passing = None
-    for i, items in enumerate(back_parts):
-        done = i == len(back_parts) - 1
-        outs = attend_back_part(
-            queries, head_grads, lse, head_mix, start, key_lift, value_lift, key_lift_t, lo,
-            [segs[k][j] for k, j in items],
-            jnp.stack([bases[k][j] for k, j in items]).astype(jnp.int32),
-            0 if done else -1, state, done,
-        )
-        for item, out in zip(items, outs):
-            seg_grads[item] = out
-        state = outs[len(items) :]
-        if not done:
-            k = items[0][0]
-            total = seg_grads[(k, 0)].astype(f32) + flip(seg_grads[(k, 1)], "heads", 0).astype(f32)
-            if passing is not None:
-                total = total + passing.astype(f32)
-            passing = lax.ppermute(total.astype(bf16), "heads", down_chain)
-            if k == 1:
-                crossed = flip(seg_grads[(0, 1)], "heads", 0)
+    now = queries
+
+    def join(parts):
+        total = parts[0].astype(f32) + parts[1].astype(f32)
+        if passing is not None:
+            total = total + passing.astype(f32)
+        return total.astype(bf16)
+
+    for i, items in enumerate(calls):
+        if len(waiting) == 2:
+            now, joined = lax.optimization_barrier((queries, join(waiting.pop(0))))
+            passing = lax.ppermute(joined, "heads", down_chain)
+        seg_list, base_list = pick(items)
+        made = attend_back_part(
+            now, head_grads, lse, head_mix, start, key_lift, value_lift, key_lift_t, lo,
+            seg_list, base_list, state, len(items) == 1, 0, 2 * rows,
+        )
+        state = list(made[len(items) :])
+        k = items[0][0]
+        if k == 0:
+            pieces_in.append(made[0])
+            continue
+        waiting.append((made[0], flip(made[1], "heads", 0)))
+        if k == 1:
+            state.append(jnp.zeros_like(state[1]))
+            pieces_in.append(flip(made[2], "heads", 0))
+    joined = join(waiting.pop())
     query_grads, key_part, value_part = state
-    latent_grads = (
-        seg_grads[(0, 0)].astype(f32) + crossed.astype(f32) + passing.astype(f32)
-    ).astype(bf16)
-
-    query_back_mine = query_grads[:rows].reshape(count, group_width)
-    query_back_got = swap(query_grads[rows:]).reshape(count, group_width)
-    latent_back_mine = latent_grads[:rows].reshape(count, latent_size)
-    latent_back_got = swap(latent_grads[rows:]).reshape(count, latent_size)
+    latent_grads = sum(p.astype(f32) for p in pieces_in)
+
     ff_share = gate_weight.shape[1] // peers
     full, hidden_grad = finish(
         (early_feed, early_down),
@@ -1104,7 +1146,8 @@
         peers,
         (
             hidden_in.reshape(count, width), attn_gain.reshape(1, width),
-            query_back_mine, query_back_got, latent_back_mine, latent_back_got,
+            query_grads.reshape(2, count, group_width), latent_grads.reshape(2, count, latent_size),
+            joined.reshape(2, count, latent_size),
             query_weight, latent_weight, grad_resid, ffn_gain_part, key_part, value_part,
         ),
     )

time: 577 us -> 555 us (0.962)
  waiting for transfers between devices: 145 us -> 105 us
  Pallas kernels: 317 us -> 341 us
    ppermute x3 -> x2, waiting for transfers between devices: 42.2 us -> 1.16 us  [shards(): passing = lax.ppermute(joined, 'heads', down_chain)]
    pallas_call x1, Pallas kernels: 121 us -> 151 us  [finish(): pl.pallas_call(body, out_shape=[jax.ShapeDtypeStruct((2 * along, total, p...]
    reduce_scatter x1, waiting for transfers between devices: 0.01 us -> 14.7 us  [shards(): lax.psum_scatter(feed_grads, 'rows', scatter_dimension=0, tiled=True)[0]]
    ppermute x15 -> x13, waiting for transfers between devices: 78 us -> 64.5 us  [flip(): return lax.ppermute(array, axis, [(i, i ^ 1 << bit) for i in range(size)])]
    pallas_call x1, Pallas kernels: 60.3 us -> 50.4 us  [feed(): pl.pallas_call(feed_back_kernel, out_shape=outs, grid_spec=pltpu.Prefetch...]
    unnamed x43 -> x41, local copies, waits for them, and re-layouts: 13 us -> 12.3 us
    ppermute x15 -> x13, starting transfers between devices: 29.7 us -> 30 us  [flip(): return lax.ppermute(array, axis, [(i, i ^ 1 << bit) for i in range(size)])]
  transfers between devices with their start and end apart: 23 -> 20, of which waited for: 13 -> 11; matrix products, arithmetic and copies ran while one was open for 5% -> 5% of each run, Pallas kernels for 25% -> 24%
where the time goes in v4:
time: 555 us
  Pallas kernels  341 us (61%)
  waiting for transfers between devices  105 us (19%)
  starting transfers between devices  48.7 us (9%)
  local copies, waits for them, and re-layouts  18.1 us (3%)
  other arithmetic  16.8 us (3%)
  between operations  14.9 us (3%)
  matrix products  11.2 us (2%)
    pallas_call x1, Pallas kernels, finish(): pl.pallas_call(body, out_shape=[jax.ShapeDtypeStruct((2 * along, total, p...  151 us
    pallas_call x4, Pallas kernels, attend_back_part(): pl.pallas_call(functools.partial(attend_back_kernel, len(segs), begin, st...  67.3 us
    ppermute x13, waiting for transfers between devices, flip(): return lax.ppermute(array, axis, [(i, i ^ 1 << bit) for i in range(size)])  64.5 us
    pallas_call x1, Pallas kernels, feed(): pl.pallas_call(feed_back_kernel, out_shape=outs, grid_spec=pltpu.Prefetch...  50.4 us
    pallas_call x1, Pallas kernels, feed(): pl.pallas_call(feed_kernel, out_shape=outs, grid_spec=pltpu.PrefetchScala...  41.1 us
    ppermute x13, starting transfers between devices, flip(): return lax.ppermute(array, axis, [(i, i ^ 1 << bit) for i in range(size)])  30 us
    pallas_call x2, Pallas kernels, attend_part(): pl.pallas_call(functools.partial(attend_kernel, len(segs), state is None,...  29.4 us
    ppermute x3, waiting for transfers between devices, shards(): moving = lax.ppermute(moving, 'heads', up_chain)  24.4 us
  transfers between devices with their start and end apart: 20, of which 11 were waited for; matrix products, arithmetic and copies ran while one was open for 5% of the time, Pallas kernels for 24%

profile of v4, /device:TPU:0, one launch (start us, length us, event | category | flops | bytes accessed | tf_op | source)
XLA Modules:
  0.0 555.4 jit_solution(17402998406697833907)
XLA Ops:
  7.3 2.2 multiply_reduce_fusion
  9.5 0.5 multiply_convert_fusion
  10.1 0.7 copy-done.14
  10.7 0.7 convolution_convert_fusion.2
  11.5 0.6 copy-done.13
  12.1 0.5 collective-permute-start.2
  12.5 2.3 convolution_convert_fusion.3
  14.9 4.5 collective-permute-start.3
  19.5 0.4 iota_compare_fusion
  19.9 22.6 %collective-permute-done.3.refs_5_.refs_8_ = bf16[8,256,256]{2,1,0:T(8,128)(2,1)S(1)} collective-permute-done((bf16[8,256,256]{2,1,0:T(8,128)(2,1)S(1)}, bf16[8,256,256]{2,1,0:T(8,128)(2,1)S(1)}, u32[]{:S(2)}, u32[]{:S(2)}) %collective-permute-start.3) | collective-permute-done | bytes 1048608 | tf_op jit(solution)/shard_map/ppermute | solution.py:1066
  42.5 1.5 collective-permute-start.5
  44.0 5.4 collective-permute-start.4
  49.4 1.6 convert_reduce_fusion
  51.0 4.1 convolution_convert_fusion
  55.1 0.5 collective-permute-start.1
  55.6 0.6 collective-permute-start.9
  56.2 12.4 %collective-permute-done.5.refs_6_.refs_9_ = bf16[8,256,256]{2,1,0:T(8,128)(2,1)S(1)} collective-permute-done((bf16[8,256,256]{2,1,0:T(8,128)(2,1)S(1)}, bf16[8,256,256]{2,1,0:T(8,128)(2,1)S(1)}, u32[]{:S(2)}, u32[]{:S(2)}) %collective-permute-start.5) | collective-permute-done | bytes 1048608 | tf_op jit(solution)/shard_map/ppermute | solution.py:546
  68.5 1.8 collective-permute-done.4.refs_7_.refs_8_
  70.4 0.5 collective-permute-start.7
  70.9 6.0 %collective-permute-start.6 = (bf16[8,256,256]{2,1,0:T(8,128)(2,1)}, bf16[8,256,256]{2,1,0:T(8,128)(2,1)}, u32[]{:S(2)}, u32[]{:S(2)}) collective-permute-start(bf16[8,256,256]{2,1,0:T(8,128)(2,1)} %collective-permute-done.4.refs_7_.refs_8_), channel_id=1, source_target_pairs={{0,2},{1,3},{2,4},{3,5},{4,6},{5,7},{8,10},{9,11},{10,12},{11,13},... | collective-permute-start | bytes 3145736 | tf_op jit(solution)/shard_map/ppermute | solution.py:1066
  76.9 1.1 constant_dynamic-slice_fusion
  78.0 4.1 convolution_convert_fusion.1
  82.4 0.8 copy.39
  83.2 0.8 copy.38
  84.1 0.8 copy.42
  85.0 2.0 fusion
  87.2 3.2 pad_maximum_fusion
  90.4 21.9 %collective-permute-done.7.refs_8_.refs_9_ = bf16[8,256,256]{2,1,0:T(8,128)(2,1)} collective-permute-done((bf16[8,256,256]{2,1,0:T(8,128)(2,1)}, bf16[8,256,256]{2,1,0:T(8,128)(2,1)}, u32[]{:S(2)}, u32[]{:S(2)}) %collective-permute-start.7) | collective-permute-done | bytes 1048608 | tf_op jit(solution)/shard_map/ppermute | solution.py:546
  112.3 1.5 collective-permute-start.8
  113.9 18.1 %attend.2 = (f32[8,1,2048]{2,1,0:T(1,128)S(1)}, f32[8,1,2048]{2,1,0:T(1,128)S(1)}, bf16[8,256,2048]{2,1,0:T(8,128)(2,1)}) custom-call(s32[8]{0:T(128)S(1)} %fusion.9.lo, s32[7]{0:T(128)S(1)} %stack.66.bases, bf16[8,256,512]{2,1,0:T(8,128)(2,1)} %bitcast.73, s32[8,1,256]{2,1,0:T(1,128)S(1)} %broadcast_in_dim.6.refs_1_.refs_4_, ...), custom_call_target="tpu_custom_call" | custom-call | flops 25769803776 | bytes 16777216 | tf_op jit(solution)/shard_map/attend/pallas_call | solution.py:172
  132.0 4.4 collective-permute-done.8.refs_4_.refs_9_
  136.4 11.3 %attend.3 = (bf16[8,256,512]{2,1,0:T(8,128)(2,1)S(1)}, f32[8,1,2048]{2,1,0:T(1,128)S(1)}, bf16[8,256,2048]{2,1,0:T(8,128)(2,1)}) custom-call(s32[8]{0:T(128)S(1)} %fusion.9.lo, s32[3]{0:T(128)S(1)} %add_add_fusion.bases, bf16[8,256,512]{2,1,0:T(8,128)(2,1)} %bitcast.74, s32[8,1,256]{2,1,0:T(1,128)S(1)} %broadcast_in_dim.6.refs_1_.refs_4_, ...), custom_call_target="tpu_custom_call" | custom-call | flops 8589934592 | bytes 16777216 | tf_op jit(solution)/shard_map/attend/pallas_call | solution.py:172
  147.8 1.4 fusion.15
  149.2 1.0 copy.51
  150.3 2.0 collective-permute-done.10
  152.2 41.1 %feed.1 = (bf16[1024,1024]{1,0:T(8,128)(2,1)}, f32[1024,1024]{1,0:T(8,128)}, bf16[1024,1024]{1,0:T(8,128)(2,1)}, bf16[1024,1024]{1,0:T(8,128)(2,1)}, bf16[1024,2...) custom-call(s32[1]{0:T(128)} %bitcast.core_ref, bf16[1024,1024]{1,0:T(8,128)(2,1)} %bitcast.83, ...), custom_call_target="tpu_custom_call" | custom-call | flops 25769803776 | bytes 51380224 | tf_op jit(solution)/shard_map/feed/pallas_call | solution.py:487
  193.3 0.2 reduce-scatter.3.cloned.1.call-start
  193.5 50.4 %feed_back.1 = (f32[1024,1024]{1,0:T(8,128)}, bf16[1024,512]{1,0:T(8,128)(2,1)}, bf16[1024,512]{1,0:T(8,128)(2,1)}, f32[1,1024]{1,0:T(1,128)}, bf16[4,6656,256]{2,1,0:T(8,128)(2,1)}) custom-call(s32[1]{0:T(128)} %bitcast.core_ref, bf16[1024,512]{1,0:T(8,128)(2,1)} %bitcast.94, bf16[1024,512]{1,0:T(8,128)(2,1)} %bitcast.20.refs_2_.refs_1_, ...), custom_call_target="tpu_custom_call" | custom-call | flops 33822867456 | bytes 61341696 | tf_op jit(solution)/shard_map/feed_back/pallas_call | solution.py:514
  243.9 0.2 collective-permute-start.11
  244.2 2.7 collective-permute-done.11
  246.9 2.7 pad_maximum_fusion.1
  249.6 9.6 %attend_back.4 = (bf16[8,256,256]{2,1,0:T(8,128)(2,1)S(1)}, bf16[8,256,256]{2,1,0:T(8,128)(2,1)S(1)}, f32[8,512,256]{2,1,0:T(8,128)}, f32[256,512]{1,0:T(8,128)S(1)}) custom-call(s32[8]{0:T(128)S(1)} %fusion.9.lo, s32[3]{0:T(128)S(1)} %add_add_fusion.bases, bf16[8,256,512]{2,1,0:T(8,128)(2,1)} %bitcast.75, bf16[8,256,512]{2,1,0:T(8,128)(2,1)} %bitcast.79, ...), custom_call_target="tpu_custom_call" | custom-call | flops 2147483648 | bytes 4194304 | tf_op jit(solution)/shard_map/attend_back/pallas_call | solution.py:296
  259.2 4.3 collective-permute-start.13
  263.7 10.7 %attend_back.5 = (bf16[8,256,256]{2,1,0:T(8,128)(2,1)S(1)}, bf16[8,256,256]{2,1,0:T(8,128)(2,1)S(1)}, f32[8,512,256]{2,1,0:T(8,128)}, f32[256,512]{1,0:T(8,128)S(1)}) custom-call(s32[8]{0:T(128)S(1)} %fusion.9.lo, s32[3]{0:T(128)S(1)} %add_add_fusion.1.bases, bf16[8,256,512]{2,1,0:T(8,128)(2,1)} %bitcast.76, bf16[8,256,512]{2,1,0:T(8,128)(2,1)} %bitcast.80, ...), custom_call_target="tpu_custom_call" | custom-call | flops 2147483648 | bytes 4194304 | tf_op jit(solution)/shard_map/attend_back/pallas_call | solution.py:296
  274.5 13.1 %collective-permute-done.13 = bf16[8,256,256]{2,1,0:T(8,128)(2,1)S(1)} collective-permute-done((bf16[8,256,256]{2,1,0:T(8,128)(2,1)S(1)}, bf16[8,256,256]{2,1,0:T(8,128)(2,1)S(1)}, u32[]{:S(2)}, u32[]{:S(2)}) %collective-permute-start.13) | collective-permute-done | bytes 1048608 | tf_op jit(solution)/shard_map/ppermute | solution.py:546
  287.5 0.3 add_convert_fusion.2
  287.8 1.3 collective-permute-start.14
  289.2 14.1 %attend_back.6 = (bf16[8,256,256]{2,1,0:T(8,128)(2,1)S(1)}, bf16[8,256,256]{2,1,0:T(8,128)(2,1)S(1)}, bf16[8,256,256]{2,1,0:T(8,128)(2,1)S(1)}, f32[8,512,256]{2,1,0:T(8,128)}, f32[256,512]{1,0:T(8,128)S(1)}) custom-call(s32[8]{0:T(128)S(1)} %fusion.9.lo, s32[4]{0:T(128)S(1)} %pad_add_fusion.2.bases, bf16[8,256,512]{2,1,0:T(8,128)(2,1)} %bitcast.77, ...), custom_call_target="tpu_custom_call" | custom-call | flops 3221225472 | bytes 4194304 | tf_op jit(solution)/shard_map/attend_back/pallas_call | solution.py:296
  303.2 20.2 %collective-permute-start.15 = (bf16[8,256,256]{2,1,0:T(8,128)(2,1)S(1)}, bf16[8,256,256]{2,1,0:T(8,128)(2,1)S(1)}, u32[]{:S(2)}, u32[]{:S(2)}) collective-permute-start(bf16[8,256,256]{2,1,0:T(8,128)(2,1)S(1)} %get-tuple-element.100), channel_id=1, source_target_pairs={{0,1},{1,0},{2,3},{3,2},{4,5},{5,4},{6,7},{7,6},{8,9},{9,8},{10,11... | collective-permute-start | bytes 3145736 | tf_op jit(solution)/shard_map/ppermute | solution.py:546
  323.5 0.4 add_convert_fusion.1
  323.9 1.3 collective-permute-start.17
  325.3 32.8 %attend_back.7 = (bf16[8,256,256]{2,1,0:T(8,128)(2,1)S(1)}, bf16[8,256,512]{2,1,0:T(8,128)(2,1)}, f32[256,512]{1,0:T(8,128)S(1)}, f32[256,512]{1,0:T(8,128)S(1)}) custom-call(s32[8]{0:T(128)S(1)} %fusion.9.lo, s32[2]{0:T(128)S(1)} %pad_add_fusion.1.bases, bf16[8,256,512]{2,1,0:T(8,128)(2,1)} %bitcast.78, bf16[8,256,512]{2,1,0:T(8,128)(2,1)} %bitcast.82, ...), custom_call_target="tpu_custom_call" | custom-call | flops 1073741824 | bytes 4194304 | tf_op jit(solution)/shard_map/attend_back/pallas_call | solution.py:296
  358.2 1.6 convert_add_fusion
  359.8 8.1 %collective-permute-done.16 = bf16[8,256,256]{2,1,0:T(8,128)(2,1)S(1)} collective-permute-done((bf16[8,256,256]{2,1,0:T(8,128)(2,1)S(1)}, bf16[8,256,256]{2,1,0:T(8,128)(2,1)S(1)}, u32[]{:S(2)}, u32[]{:S(2)}) %collective-permute-start.16) | collective-permute-done | bytes 1048608 | tf_op jit(solution)/shard_map/ppermute | solution.py:546
  367.9 1.2 collective-permute-done.17
  369.1 1.4 add_convert_fusion
  370.5 14.7 %reduce-scatter.3.cloned.1.call-done = bf16[1,6656,256]{2,1,0:T(8,128)(2,1)} async-done(((bf16[4,6656,256]{2,1,0:T(8,128)(2,1)}), bf16[1,6656,256]{2,1,0:T(8,128)(2,1)}) %reduce-scatter.3.cloned.1.call-update) | async-done | bytes 3407888 | tf_op jit(solution)/shard_map/reduce_scatter | solution.py:1103
  385.1 150.5 %finish.1 = (bf16[4,1456,256]{2,1,0:T(8,128)(2,1)}, f32[1024,1024]{1,0:T(8,128)}) custom-call(bf16[6656,256]{1,0:T(8,128)(2,1)} %bitcast.88, bf16[2816,256]{1,0:T(8,128)(2,1)} %bitcast.91, bf16[1024,1024]{1,0:T(8,128)(2,1)} %bitcast.84, f32[1,1024]{1,0:T(1,128)} %bitcast.97, bf16[2,1024,512]{2,1,0:T(8,128)(2,1)} %bitcast.90, f32[2,1024,256]{2,1,0:T(8,128)} %bitcast.85, ...), custom_call_target="tpu_custom_call" | custom-call | tf_op jit(solution)/shard_map/finish/pallas_call | solution.py:898
  535.7 1.8 copy-done.3
  537.5 2.1 lay_out.1
  539.7 0.5 slice_bitcast_fusion
  540.2 1.6 copy.45
  541.7 1.6 copy.46
  543.3 4.8 copy.53
  (69 shorter events, 1.3 us)
Async XLA Ops:
  7.2 2.3 copy-start.12
  7.2 2.3 copy-start.16
  7.2 363.3 %reduce-scatter.5.cloned.1.call-start = ((), (), s32[]{:S(2)}) async-start(), calls=%async_computation.3 | async-start | bytes 7208960 | tf_op jit(solution)/shard_map/reduce_scatter | solution.py:1102
  9.5 1.2 copy-start.14
  10.7 1.3 copy-start.13
  12.1 2.8 collective-permute-start.2
  14.8 4.7 copy-start.15
  14.9 98.9 %copy-start.2 = (bf16[2048,256]{1,0:T(8,128)(2,1)}, bf16[2048,256]{1,0:T(8,128)(2,1)S(1)}, u32[]{:S(2)}) copy-start(bf16[2048,256]{1,0:T(8,128)(2,1)S(1)} %pad_maximum_fusion.2) | copy-start | bytes 3145732
  14.9 27.6 %collective-permute-start.3 = (bf16[8,256,256]{2,1,0:T(8,128)(2,1)S(1)}, bf16[8,256,256]{2,1,0:T(8,128)(2,1)S(1)}, u32[]{:S(2)}, u32[]{:S(2)}) collective-permute-start(bf16[8,256,256]{2,1,0:T(8,128)(2,1)S(1)} %bitcast.68), channel_id=1, source_target_pairs={{0,2},{1,3},{2,4},{3,5},{4,6},{5,7},{8,10},{9,11},{10,12},{11,13},... | collective-permute-start | bytes 3145736 | tf_op jit(solution)/shard_map/ppermute | solution.py:1066
  42.5 12.6 %copy-start.4 = (bf16[8,256,256]{2,1,0:T(8,128)(2,1)}, bf16[8,256,256]{2,1,0:T(8,128)(2,1)S(1)}, u32[]{:S(2)}) copy-start(bf16[8,256,256]{2,1,0:T(8,128)(2,1)S(1)} %collective-permute-done.3.refs_5_.refs_8_) | copy-start | bytes 3145732
  42.5 26.1 %collective-permute-start.5 = (bf16[8,256,256]{2,1,0:T(8,128)(2,1)S(1)}, bf16[8,256,256]{2,1,0:T(8,128)(2,1)S(1)}, u32[]{:S(2)}, u32[]{:S(2)}) collective-permute-start(bf16[8,256,256]{2,1,0:T(8,128)(2,1)S(1)} %collective-permute-done.3.refs_5_.refs_8_), channel_id=1, source_target_pairs={{0,1},{1,0},{2,3},{3,2},{4,5},{5,4},{6,7},{7,6},{8,9},{9,8},{10,11... | collective-permute-start | bytes 3145736 | tf_op jit(solution)/shard_map/ppermute | solution.py:546
  44.0 26.4 %collective-permute-start.4 = (bf16[8,256,256]{2,1,0:T(8,128)(2,1)S(1)}, bf16[8,256,256]{2,1,0:T(8,128)(2,1)}, u32[]{:S(2)}, u32[]{:S(2)}) collective-permute-start(bf16[8,256,256]{2,1,0:T(8,128)(2,1)S(1)} %collective-permute-done.3.refs_5_.refs_8_), channel_id=1, source_target_pairs={{0,2},{1,3},{2,4},{3,5},{4,6},{5,7},{8,10},{9,11},{10,12},{11,13},... | collective-permute-start | bytes 3145736 | tf_op jit(solution)/shard_map/ppermute | solution.py:1066
  50.9 36.1 %collective-permute-start = (s32[4,256]{1,0:T(4,128)S(1)}, s32[4,256]{1,0:T(4,128)S(1)}, u32[]{:S(2)}, u32[]{:S(2)}) collective-permute-start(s32[4,256]{1,0:T(4,128)S(1)} %broadcast_subtract_fusion), channel_id=1, source_target_pairs={{0,8},{8,0},{16,24},{24,16},{1,9},{9,1},{17,25},{25,17},{2,10},{10... | collective-permute-start | bytes 12296 | tf_op jit(solution)/shard_map/ppermute | solution.py:546
  55.1 32.1 %collective-permute-start.1 = (bf16[1024,512]{1,0:T(8,128)(2,1)}, bf16[1024,512]{1,0:T(8,128)(2,1)}, u32[]{:S(2)}, u32[]{:S(2)}) collective-permute-start(bf16[1024,512]{1,0:T(8,128)(2,1)} %convolution_convert_fusion), channel_id=1, source_target_pairs={{0,8},{8,0},{16,24},{24,16},{1,9},{9,1},{17,25},{25,17},{2,10},{10... | collective-permute-start | bytes 3145736 | tf_op jit(solution)/shard_map/ppermute | solution.py:546
  55.6 58.2 %collective-permute-start.9 = (bf16[8,256,256]{2,1,0:T(8,128)(2,1)S(1)}, bf16[8,256,256]{2,1,0:T(8,128)(2,1)}, u32[]{:S(2)}, u32[]{:S(2)}) collective-permute-start(bf16[8,256,256]{2,1,0:T(8,128)(2,1)S(1)} %bitcast.69), channel_id=1, source_target_pairs={{0,1},{1,0},{2,3},{3,2},{4,5},{5,4},{6,7},{7,6},{8,9},{9,8},{10,11... | collective-permute-start | bytes 3145736 | tf_op jit(solution)/shard_map/ppermute | solution.py:546
  68.5 13.5 %copy-start.6 = (bf16[8,256,256]{2,1,0:T(8,128)(2,1)}, bf16[8,256,256]{2,1,0:T(8,128)(2,1)S(1)}, u32[]{:S(2)}) copy-start(bf16[8,256,256]{2,1,0:T(8,128)(2,1)S(1)} %collective-permute-done.5.refs_6_.refs_9_) | copy-start | bytes 3145732
  70.4 41.9 %collective-permute-start.7 = (bf16[8,256,256]{2,1,0:T(8,128)(2,1)}, bf16[8,256,256]{2,1,0:T(8,128)(2,1)}, u32[]{:S(2)}, u32[]{:S(2)}) collective-permute-start(bf16[8,256,256]{2,1,0:T(8,128)(2,1)} %collective-permute-done.4.refs_7_.refs_8_), channel_id=1, source_target_pairs={{0,1},{1,0},{2,3},{3,2},{4,5},{5,4},{6,7},{7,6},{8,9},{9,8},{10,11... | collective-permute-start | bytes 3145736 | tf_op jit(solution)/shard_map/ppermute | solution.py:546
  70.9 41.4 %collective-permute-start.6 = (bf16[8,256,256]{2,1,0:T(8,128)(2,1)}, bf16[8,256,256]{2,1,0:T(8,128)(2,1)}, u32[]{:S(2)}, u32[]{:S(2)}) collective-permute-start(bf16[8,256,256]{2,1,0:T(8,128)(2,1)} %collective-permute-done.4.refs_7_.refs_8_), channel_id=1, source_target_pairs={{0,2},{1,3},{2,4},{3,5},{4,6},{5,7},{8,10},{9,11},{10,12},{11,13},... | collective-permute-start | bytes 3145736 | tf_op jit(solution)/shard_map/ppermute | solution.py:1066
  87.0 176.7 %copy-start = (bf16[2,1024,256]{2,1,0:T(8,128)(2,1)}, bf16[2,1024,256]{2,1,0:T(8,128)(2,1)S(1)}, u32[]{:S(2)}) copy-start(bf16[2,1024,256]{2,1,0:T(8,128)(2,1)S(1)} %get-tuple-element.160.refs_6_) | copy-start | bytes 3145732
  87.2 26.7 %copy-start.5 = (bf16[8,256,256]{2,1,0:T(8,128)(2,1)S(1)}, bf16[8,256,256]{2,1,0:T(8,128)(2,1)}, u32[]{:S(2)}) copy-start(bf16[8,256,256]{2,1,0:T(8,128)(2,1)} %copy-done.4) | copy-start | bytes 3145732
  87.2 26.7 %copy-start.7 = (bf16[8,256,256]{2,1,0:T(8,128)(2,1)S(1)}, bf16[8,256,256]{2,1,0:T(8,128)(2,1)}, u32[]{:S(2)}) copy-start(bf16[8,256,256]{2,1,0:T(8,128)(2,1)} %copy-done.6) | copy-start | bytes 3145732
  112.3 24.1 %collective-permute-start.8 = (bf16[8,256,256]{2,1,0:T(8,128)(2,1)}, bf16[8,256,256]{2,1,0:T(8,128)(2,1)S(1)}, u32[]{:S(2)}, u32[]{:S(2)}) collective-permute-start(bf16[8,256,256]{2,1,0:T(8,128)(2,1)} %collective-permute-done.6.refs_3_.refs_8_), channel_id=1, source_target_pairs={{0,1},{1,0},{2,3},{3,2},{4,5},{5,4},{6,7},{7,6},{8,9},{9,8},{10,11... | collective-permute-start | bytes 3145736 | tf_op jit(solution)/shard_map/ppermute | solution.py:546
  113.9 22.6 %copy-start.11 = (bf16[512,256]{1,0:T(8,128)(2,1)S(1)}, bf16[512,256]{1,0:T(8,128)(2,1)}, u32[]{:S(2)}) copy-start(bf16[512,256]{1,0:T(8,128)(2,1)} %copy.39) | copy-start | bytes 786436
  136.4 11.3 %copy-start.8 = (bf16[8,256,256]{2,1,0:T(8,128)(2,1)}, bf16[8,256,256]{2,1,0:T(8,128)(2,1)S(1)}, u32[]{:S(2)}) copy-start(bf16[8,256,256]{2,1,0:T(8,128)(2,1)S(1)} %collective-permute-done.8.refs_4_.refs_9_) | copy-start | bytes 3145732
  149.2 3.0 collective-permute-start.10
  193.3 191.8 %reduce-scatter.3.cloned.1.call-start = ((), (), s32[]{:S(2)}) async-start(), calls=%async_computation.2 | async-start | bytes 17039360 | tf_op jit(solution)/shard_map/reduce_scatter | solution.py:1103
  243.9 2.9 collective-permute-start.11
  259.2 28.3 %collective-permute-start.13 = (bf16[8,256,256]{2,1,0:T(8,128)(2,1)S(1)}, bf16[8,256,256]{2,1,0:T(8,128)(2,1)S(1)}, u32[]{:S(2)}, u32[]{:S(2)}) collective-permute-start(bf16[8,256,256]{2,1,0:T(8,128)(2,1)S(1)} %get-tuple-element.91), channel_id=1, source_target_pairs={{0,1},{1,0},{2,3},{3,2},{4,5},{5,4},{6,7},{7,6},{8,9},{9,8},{10,11... | collective-permute-start | bytes 3145736 | tf_op jit(solution)/shard_map/ppermute | solution.py:546
  274.4 49.1 %collective-permute-start.12 = (bf16[8,256,256]{2,1,0:T(8,128)(2,1)S(1)}, bf16[8,256,256]{2,1,0:T(8,128)(2,1)S(1)}, u32[]{:S(2)}, u32[]{:S(2)}) collective-permute-start(bf16[8,256,256]{2,1,0:T(8,128)(2,1)S(1)} %get-tuple-element.89), channel_id=1, source_target_pairs={{0,1},{1,0},{2,3},{3,2},{4,5},{5,4},{6,7},{7,6},{8,9},{9,8},{10,11... | collective-permute-start | bytes 3145736 | tf_op jit(solution)/shard_map/ppermute | solution.py:546
  287.8 35.7 %collective-permute-start.14 = (bf16[8,256,256]{2,1,0:T(8,128)(2,1)S(1)}, bf16[8,256,256]{2,1,0:T(8,128)(2,1)S(1)}, u32[]{:S(2)}, u32[]{:S(2)}) collective-permute-start(bf16[8,256,256]{2,1,0:T(8,128)(2,1)S(1)} %add_convert_fusion.2), channel_id=1, source_target_pairs={{2,0},{3,1},{4,2},{5,3},{6,4},{7,5},{10,8},{11,9},{12,10},{13,11},... | collective-permute-start | bytes 3145736 | tf_op jit(solution)/shard_map/ppermute | solution.py:1123
  303.2 55.0 %collective-permute-start.15 = (bf16[8,256,256]{2,1,0:T(8,128)(2,1)S(1)}, bf16[8,256,256]{2,1,0:T(8,128)(2,1)S(1)}, u32[]{:S(2)}, u32[]{:S(2)}) collective-permute-start(bf16[8,256,256]{2,1,0:T(8,128)(2,1)S(1)} %get-tuple-element.100), channel_id=1, source_target_pairs={{0,1},{1,0},{2,3},{3,2},{4,5},{5,4},{6,7},{7,6},{8,9},{9,8},{10,11... | collective-permute-start | bytes 3145736 | tf_op jit(solution)/shard_map/ppermute | solution.py:546
  323.4 44.5 %collective-permute-start.16 = (bf16[8,256,256]{2,1,0:T(8,128)(2,1)S(1)}, bf16[8,256,256]{2,1,0:T(8,128)(2,1)S(1)}, u32[]{:S(2)}, u32[]{:S(2)}) collective-permute-start(bf16[8,256,256]{2,1,0:T(8,128)(2,1)S(1)} %get-tuple-element.103), channel_id=1, source_target_pairs={{0,1},{1,0},{2,3},{3,2},{4,5},{5,4},{6,7},{7,6},{8,9},{9,8},{10,11... | collective-permute-start | bytes 3145736 | tf_op jit(solution)/shard_map/ppermute | solution.py:546
  323.5 1.9 copy-start.1
  323.9 45.2 %collective-permute-start.17 = (bf16[8,256,256]{2,1,0:T(8,128)(2,1)S(1)}, bf16[8,256,256]{2,1,0:T(8,128)(2,1)S(1)}, u32[]{:S(2)}, u32[]{:S(2)}) collective-permute-start(bf16[8,256,256]{2,1,0:T(8,128)(2,1)S(1)} %add_convert_fusion.1), channel_id=1, source_target_pairs={{2,0},{3,1},{4,2},{5,3},{6,4},{7,5},{10,8},{11,9},{12,10},{13,11},... | collective-permute-start | bytes 3145736 | tf_op jit(solution)/shard_map/ppermute | solution.py:1123
  358.2 1.7 copy-start.9
  358.2 1.7 copy-start.10
  535.7 1.8 copy-start.3
Sparse Core Ops, SparseCore 0:
  193.4 82.8 reduce-scatter.4
  279.1 105.9 reduce-scatter.2

commit v5 on v4

--- a/solution.py
+++ b/solution.py
@@ -81,23 +81,27 @@
 def attend_kernel(count, first, last, lo, bases, *refs):
     refs = list(refs)
     take = lambda k: [refs.pop(0) for _ in range(k)]
-    query_ref, start_ref, key_lift_ref = take(3)
+    (start_ref,) = take(1)
+    if first:
+        query_ref, key_lift_ref = take(2)
+    else:
+        expanded_ref, top_in, total_in, mix_in = take(4)
     seg_refs = take(count)
-    if not first:
-        top_in, total_in, mix_in = take(3)
     if last:
         (value_lift_ref,) = take(1)
         out_ref, lse_ref, mix_ref = take(3)
     else:
         top_out, total_out, mix_out = take(3)
-    expanded, top, total, mix, segs = take(5)
-    tokens = query_ref.shape[1]
+    if first:
+        (expanded_ref,) = take(1)
+    top, total, mix, segs = take(4)
+    expanded = expanded_ref.at[0]
+    tokens = start_ref.shape[2]
     heads = expanded.shape[1] // tokens
     row = pl.program_id(0)
-    scale = HEAD_WIDTH ** (-0.5) * LOG2E
     touched = lambda i: (bases[i] >= 0) & (bases[i] + tokens - 1 >= lo[row])
     if first:
-        expand_heads(query_ref[0], key_lift_ref, scale, expanded)
+        expand_heads(query_ref[0], key_lift_ref, HEAD_WIDTH ** (-0.5) * LOG2E, expanded)
         top[...] = jnp.full_like(top, blocked)
         total[...] = jnp.zeros_like(total)
         mix[...] = jnp.zeros_like(mix)
@@ -105,11 +109,6 @@
         top[...] = top_in[0]
         total[...] = total_in[0]
         mix[...] = mix_in[0].astype(f32)
-
-        @pl.when(functools.reduce(jnp.logical_or, [touched(i) for i in range(count)]))
-        def _():
-            expand_heads(query_ref[0], key_lift_ref, scale, expanded)
-
     for i in range(count):
         segs[i] = seg_refs[i][0]
 
@@ -145,29 +144,32 @@
     return pl.BlockSpec(array.shape, lambda *_: (0,) * len(array.shape))
 
 
-def by_row(shape, begin=0):
-    return pl.BlockSpec((1,) + tuple(shape[1:]), lambda r, *_: (r + begin,) + (0,) * (len(shape) - 1))
-
-
-def attend_part(queries, start, key_lift, value_lift_t, lo, segs, bases, state, last):
+def by_row(shape):
+    return pl.BlockSpec((1,) + tuple(shape[1:]), lambda r, *_: (r,) + (0,) * (len(shape) - 1))
+
+
+def attend_part(queries, start, key_lift, value_lift_t, lo, segs, bases, expanded, state, last):
     rows, tokens, width = queries.shape
     heads = width // HEAD_WIDTH
     latent = segs[0].shape[-1]
     shape = jax.ShapeDtypeStruct
     stat = shape((rows, 1, heads * tokens), f32)
-    state_shapes = [stat, stat, shape((rows, latent, heads * tokens), bf16)]
-    args = [queries, start, key_lift, *segs]
-    specs = [by_row(queries.shape), by_row(start.shape), whole(key_lift)]
+    flat = shape((rows, latent, heads * tokens), bf16)
+    if state is None:
+        args = [start, queries, key_lift, *segs]
+        specs = [by_row(start.shape), by_row(queries.shape), whole(key_lift)]
+    else:
+        args = [start, expanded, *state, *segs]
+        specs = [by_row(a.shape) for a in args[:5]]
     specs += [by_row(s.shape) for s in segs]
-    if state is not None:
-        args += list(state)
-        specs += [by_row(s.shape) for s in state_shapes]
     if last:
         args.append(value_lift_t)
         specs.append(whole(value_lift_t))
-        outs = [shape(queries.shape, bf16), stat, state_shapes[2]]
+        outs = [shape(queries.shape, bf16), stat, flat]
     else:
-        outs = state_shapes
+        outs = [stat, stat, flat]
+    if state is None:
+        outs.append(flat)
     blocks = rows * heads * len(segs)
     return pl.pallas_call(
         functools.partial(attend_kernel, len(segs), state is None, last),
@@ -178,7 +180,6 @@
             in_specs=specs,
             out_specs=[by_row(o.shape) for o in outs],
             scratch_shapes=[
-                pltpu.VMEM((latent, heads * tokens), bf16),
                 pltpu.VMEM((1, heads * tokens), f32),
                 pltpu.VMEM((1, heads * tokens), f32),
                 pltpu.VMEM((latent, heads * tokens), f32),
@@ -191,48 +192,52 @@
         cost_estimate=pl.CostEstimate(
             flops=blocks * tokens * tokens * latent * 4,
             bytes_accessed=rows * heads * latent * tokens * 4,
-            transcendentals=0,
+            transcendentals=blocks * tokens * tokens,
         ),
         name="attend",
     )(lo, bases, *args)
 
 
-def attend_back_kernel(count, begin, first, last, lo, bases, *refs):
+def attend_back_kernel(count, first, last, lo, bases, *refs):
     refs = list(refs)
     take = lambda k: [refs.pop(0) for _ in range(k)]
-    query_ref, grad_ref, lse_ref, mix_ref, start_ref, key_lift_ref, value_lift_ref, key_lift_t_ref = take(8)
+    query_ref, lse_ref, start_ref, expanded_ref, key_lift_t_ref = take(5)
     seg_refs = take(count)
-    if not first:
-        query_back_in, key_up_in = take(2)
-        if last:
-            (value_up_in,) = take(1)
+    if first or last:
+        grad_ref, mix_ref = take(2)
+    if first:
+        (value_lift_ref,) = take(1)
+    else:
+        expanded_grad_ref, delta_ref, query_back_in, key_up_in = take(4)
     grad_refs = take(count)
     query_back_ref, key_up_ref = take(2)
     if last:
         (value_up_ref,) = take(1)
-    expanded, expanded_grad, delta, back, query_back, segs, seg_grads = take(7)
-    latent_size = expanded.shape[0]
+    if first:
+        expanded_grad_ref, delta_ref = take(2)
+    back, query_back, segs, seg_grads = take(4)
+    expanded, expanded_grad = expanded_ref.at[0], expanded_grad_ref.at[0]
     tokens = query_ref.shape[1]
     heads = expanded.shape[1] // tokens
     row = pl.program_id(0)
     scale = HEAD_WIDTH ** (-0.5)
-    touched = lambda i: (bases[i] >= 0) & (bases[i] + tokens - 1 >= lo[row + begin])
+    touched = lambda i: (bases[i] >= 0) & (bases[i] + tokens - 1 >= lo[row])
     any_touched = functools.reduce(jnp.logical_or, [touched(i) for i in range(count)])
 
     @pl.when(row == 0)
     def _():
         key_up_ref[...] = jnp.zeros_like(key_up_ref) if first else key_up_in[...]
         if last:
-            value_up_ref[...] = value_up_in[...]
+            value_up_ref[...] = jnp.zeros_like(value_up_ref)
 
     query_back[...] = jnp.zeros_like(query_back) if first else query_back_in[0]
     seg_grads[...] = jnp.zeros_like(seg_grads)
+    if first:
+        expand_heads(grad_ref[0], value_lift_ref, 1.0, expanded_grad)
+        delta_ref[0] = jnp.sum(mix_ref[0].astype(f32) * expanded_grad[...].astype(f32), axis=0, keepdims=True)
 
     @pl.when(any_touched)
     def _():
-        expand_heads(query_ref[0], key_lift_ref, scale * LOG2E, expanded)
-        expand_heads(grad_ref[0], value_lift_ref, 1.0, expanded_grad)
-        delta[...] = jnp.sum(mix_ref[0].astype(f32) * expanded_grad[...].astype(f32), axis=0, keepdims=True)
         back[...] = jnp.zeros_like(back)
         for i in range(count):
             segs[i] = seg_refs[i][0]
@@ -247,7 +252,7 @@
             score = matmul(latent, expanded[...])
             probs = jnp.where(allow, jnp.exp2(score - lse_ref[0]), 0.0)
             dprobs = matmul(latent, expanded_grad[...])
-            dscore = (probs * (dprobs - delta[...])).astype(bf16)
+            dscore = (probs * (dprobs - delta_ref[0])).astype(bf16)
             by_key = matmul_nt(dscore, expanded[...])
             by_value = matmul_nt(probs.astype(bf16), expanded_grad[...])
             seg_grads[i] = (by_key * LN2 + by_value).astype(bf16)
@@ -269,32 +274,38 @@
         query_back_ref[0] = query_back[...]
 
 
-def attend_back_part(
-    queries, grads, lse, mix, start, key_lift, value_lift, key_lift_t, lo, segs, bases, state, last, begin, rows,
-):
-    _, tokens, width = queries.shape
+def attend_back_part(queries, grads, lse, mix, start, expanded, value_lift, key_lift_t, lo, segs, bases, kept, state, last):
+    rows, tokens, width = queries.shape
     heads = width // HEAD_WIDTH
     latent = segs[0].shape[-1]
     shape = jax.ShapeDtypeStruct
     back_shape = shape((rows, width, tokens), f32)
     up_shape = shape((latent, width), f32)
-    args = [queries, grads, lse, mix, start, key_lift, value_lift, key_lift_t, *segs]
-    specs = [by_row(a.shape, begin) for a in (queries, grads, lse, mix, start)]
-    specs += [whole(key_lift), whole(value_lift), whole(key_lift_t)]
-    specs += [by_row(s.shape, begin) for s in segs]
-    if state is not None:
-        args += list(state)
-        specs.append(by_row(state[0].shape, begin))
-        specs += [whole(up_shape)] * (len(state) - 1)
-    outs = [shape((rows, tokens, latent), bf16) for _ in segs]
-    outs += [shape((rows, tokens, width), bf16) if last else back_shape, up_shape]
+    first = state is None
+    args = [queries, lse, start, expanded, key_lift_t, *segs]
+    specs = [by_row(a.shape) for a in args[:4]] + [whole(key_lift_t)]
+    specs += [by_row(s.shape) for s in segs]
+    if first or last:
+        args += [grads, mix]
+        specs += [by_row(grads.shape), by_row(mix.shape)]
+    if first:
+        args.append(value_lift)
+        specs.append(whole(value_lift))
+    else:
+        args += [*kept, *state]
+        specs += [by_row(kept[0].shape), by_row(kept[1].shape), by_row(back_shape.shape), whole(up_shape)]
+    outs = [shape(s.shape, bf16) for s in segs]
+    outs += [shape(queries.shape, bf16) if last else back_shape, up_shape]
     out_specs = [by_row(o.shape) for o in outs[:-1]] + [whole(up_shape)]
     if last:
         outs.append(up_shape)
         out_specs.append(whole(up_shape))
+    if first:
+        outs += [shape(expanded.shape, bf16), shape(lse.shape, f32)]
+        out_specs += [by_row(expanded.shape), by_row(lse.shape)]
     blocks = rows * heads * len(segs)
     return pl.pallas_call(
-        functools.partial(attend_back_kernel, len(segs), begin, state is None, last),
+        functools.partial(attend_back_kernel, len(segs), first, last),
         out_shape=outs,
         grid_spec=pltpu.PrefetchScalarGridSpec(
             num_scalar_prefetch=2,
@@ -302,9 +313,6 @@
             in_specs=specs,
             out_specs=out_specs,
             scratch_shapes=[
-                pltpu.VMEM((latent, heads * tokens), bf16),
-                pltpu.VMEM((latent, heads * tokens), bf16),
-                pltpu.VMEM((1, heads * tokens), f32),
                 pltpu.VMEM((latent, heads * tokens), f32),
                 pltpu.VMEM((width, tokens), f32),
                 pltpu.VMEM((len(segs), tokens, latent), bf16),
@@ -546,90 +554,62 @@
     return lax.ppermute(array, axis, [(i, i ^ (1 << bit)) for i in range(size)])
 
 
-def late_parts(core, inputs_ref, gain_ref, back_refs, before, query_ref, latent_ref, resid_ref, other_gain_ref, up_refs, normed, own, sent, grad_ref):
-    along, count, _, piece = own.shape
-    tokens, width = inputs_ref.shape
-    query_mine, query_got, latent_mine, latent_got = back_refs
-    share = width // count
-    fold = share // 2
-    latent = latent_mine.shape[1]
-    half = query_mine.shape[1]
-    block = min(256, tokens)
-    mine = lambda ref, size: ref[:, pl.ds(pl.multiple_of(core * size, size), size)]
-    theirs = lambda ref, size: ref[:, pl.ds(pl.multiple_of((1 - core) * size, size), size)]
-    for t in range(0, tokens, block):
-        at = slice(t, t + block)
-        row = inputs_ref[at].astype(f32)
-        scale = lax.rsqrt(jnp.mean(row * row, axis=-1, keepdims=True) + epsilon)
-        normed[at] = (row * scale * gain_ref[...]).astype(bf16)
-    before()
-    gain_total = jnp.zeros((1, width), f32)
-    for t in range(0, tokens, block):
-        at = slice(t, t + block)
-        row = inputs_ref[at].astype(f32)
-        scale = lax.rsqrt(jnp.mean(row * row, axis=-1, keepdims=True) + epsilon)
-        unit = row * scale
-        grad = (
-            matmul_nt(query_mine[at], mine(query_ref, half))
-            + matmul_nt(query_got[at], theirs(query_ref, half))
-            + matmul_nt(latent_mine[at], mine(latent_ref, latent))
-            + matmul_nt(latent_got[at], theirs(latent_ref, latent))
-        )
-        gain_total += jnp.sum(grad * unit, axis=0, keepdims=True)
-        scaled = grad * gain_ref[...]
-        grad_ref[at] = resid_ref[at] + scale * (
-            scaled - unit * jnp.mean(scaled * unit, axis=-1, keepdims=True)
-        )
-    other = other_gain_ref[...]
-    gains = (jnp.where(core == 0, gain_total, other), jnp.where(core == 0, other, gain_total))
+def fill_shards(target, at, grad, count):
+    along, piece = target.shape[0], target.shape[3]
+    size = grad.shape[0] // count
+    for s in range(count):
+        for j in range(along):
+            target[j, s, at : at + size] = grad[s * size : (s + 1) * size, j * piece : (j + 1) * piece].astype(bf16)
+
+
+def fill_folded(target, at, grad, count):
+    along, piece = target.shape[0], target.shape[3]
+    size = grad.shape[0] // count
+    latent = grad.shape[1]
+    fold = size // 2
+    for s in range(count):
+        for j in range(along):
+            side, column = divmod(j * piece, latent)
+            first = s * size + side * fold
+            target[j, s, at : at + fold] = grad[first : first + fold, column : column + piece].astype(bf16)
+
+
+def fill_gains(target, at, gain, count):
+    along, piece = target.shape[0], target.shape[3]
+    share = gain.shape[1] // count
     lane = max(share, 128)
-    for target, query, latents, gain in (
-        (own, query_mine, latent_mine, gains[0]),
-        (sent, query_got, latent_got, gains[1]),
-    ):
-        query_grad = matmul_tn(normed[...], query[...]).astype(bf16)
-        latent_grad = matmul_tn(normed[...], latents[...]).astype(bf16)
-        for s in range(count):
-            first = s * share
-            begin = first // lane * lane
-            for j in range(along):
-                target[j, s, :share] = query_grad[first : first + share, j * piece : (j + 1) * piece]
-                side, column = divmod(j * piece, latent)
-                target[j, s, share : share + fold] = latent_grad[
-                    first + side * fold : first + (side + 1) * fold, column : column + piece
-                ]
-                rows = slice(share + fold, share + fold + 16)
-                if j == 0:
-                    kept = jnp.broadcast_to(gain[:, begin : begin + lane], (16, lane)).astype(bf16)
-                    target[j, s, rows, :lane] = kept
-                    if piece > lane:
-                        target[j, s, rows, lane:] = jnp.zeros((16, piece - lane), bf16)
-                else:
-                    target[j, s, rows] = jnp.zeros((16, piece), bf16)
-    lift = latent // count
-    at = share + fold + 16
-    for ref in up_refs:
-        for s in range(count):
-            for j in range(along):
-                own[j, s, at : at + lift] = ref[s * lift : (s + 1) * lift, j * piece : (j + 1) * piece].astype(bf16)
-        at += lift
-
-
-def finish_kernel(
-    sections, early_refs, late_compute, chain_refs, own_ref, sent_ref, out_ref, late_got, late_from, got_first, got_next,
-    chain_sems, core_sems, along_sems, first_sems, first_late_sems, next_sems, out_sems,
-):
+    for s in range(count):
+        begin = s * share // lane * lane
+        kept = jnp.broadcast_to(gain[:, begin : begin + lane], (16, lane)).astype(bf16)
+        target[0, s, at : at + 16, :lane] = kept
+        if piece > lane:
+            target[0, s, at : at + 16, lane:] = jnp.zeros((16, piece - lane), bf16)
+        for j in range(1, along):
+            target[j, s, at : at + 16] = jnp.zeros((16, piece), bf16)
+
+
+def finish_kernel(sections, groups, sizes, refs):
+    (
+        early_refs, inputs_ref, gain_ref, query_grad_ref, latent_grad_ref, joined_ref,
+        query_ref, latent_ref, resid_ref, other_gain_ref, key_up, value_up,
+        out_ref, grad_ref,
+        normed, own_ref, sent_ref, late_got, late_from, got_first, got_next,
+        chain_got, query_got, latent_low, latent_got,
+        chain_sems, core_sems, along_sems, first_sems, first_late_sems, next_sems, out_sems,
+    ) = refs
     along, count, late_rows, piece = own_ref.shape
-    shared_rows = sent_ref.shape[2]
-    early_rows = sum(section[2] for section in sections)
+    early_rows, share, fold, lift = sizes
     bits = count.bit_length() - 1
     row_at = lax.axis_index("rows")
     place = lax.axis_index("heads")
     core = row_at % 2
     x_at = row_at // 2
     mesh = pl.DeviceIdType.MESH
-    early_part = slice(0, early_rows)
-    late_part = slice(early_rows, early_rows + late_rows)
+    tokens, width = inputs_ref.shape
+    latent = latent_low.shape[2]
+    half = query_got.shape[1]
+    block = min(256, tokens)
+    parts = [slice(0, early_rows)] + [slice(early_rows + g[0], early_rows + g[1]) for g in groups]
 
     def turned(which):
         at = place
@@ -641,9 +621,9 @@
     x_others = [(x_at + d) % along for d in range(1, along)]
     x_peers = [(x * 2 + core, place) for x in x_others]
     head_peers = [(row_at, turned([bit])) for bit in range(bits)]
-    barrier = pltpu.get_barrier_semaphore()
     above = (row_at, (place + 2) % count)
     below = (row_at, (place + count - 2) % count)
+    barrier = pltpu.get_barrier_semaphore()
     everyone = [core_peer, above, below] + x_peers + head_peers
     for peer in everyone:
         pl.semaphore_signal(barrier, inc=1, device_id=peer, device_id_type=mesh)
@@ -663,146 +643,210 @@
         ]
 
     def add_rows(target, other, size):
-        block = size if size <= 600 else size // 2
+        step = size if size <= 600 else size // 2
 
         def one(i, carry):
-            at = pl.ds(pl.multiple_of(i * block, 16), block)
+            at = pl.ds(pl.multiple_of(i * step, 16), step)
             target[at] = (target[at].astype(f32) + other[at].astype(f32)).astype(bf16)
             return carry
 
-        lax.fori_loop(0, size // block, one, 0)
+        lax.fori_loop(0, size // step, one, 0)
+
+    def rows_of(part):
+        return pl.ds(part.start, part.stop - part.start)
 
     first = orders(0)
+    final = len(first) - 1
     pending = []
 
     def early_rows_of(n, shard):
-        which, start, share, _ = sections[n]
-        return early_refs[which].at[pl.ds(pl.multiple_of(start + shard * share, 16), share)]
+        which, start, size, _ = sections[n]
+        return early_refs[which].at[pl.ds(pl.multiple_of(start + shard * size, 16), size)]
 
     def first_early(i, n):
-        _, _, share, row = sections[n]
+        _, _, size, row = sections[n]
         return remote(
-            early_rows_of(n, turned([0] + first[i])), got_first.at[i, pl.ds(row, share)],
+            early_rows_of(n, turned([0] + first[i])), got_first.at[i, pl.ds(row, size)],
             first_sems, (i, n), head_peers[0],
         )
 
-    query_grad_ref, latent_grad_ref, joined_ref, chain_got, query_got, latent_low, latent_got = chain_refs
+    def next_copy(bit, j, i, which):
+        rows = rows_of(parts[which])
+        return remote(
+            got_first.at[i, rows], got_next[bit - 1].at[j, rows], next_sems[bit - 1], (j, which), head_peers[bit]
+        )
+
+    def settle(i, which):
+        rest = first[i]
+        level = rest[0] if rest else bits
+        rows = rows_of(parts[which])
+        for bit in range(1, level):
+            j = orders(bit).index(rest)
+            next_copy(bit, j, i, which).wait_recv()
+            add_rows(got_first.at[i, rows], got_next[bit - 1].at[j, rows], rows.size)
+        if rest:
+            copy = next_copy(level, orders(level).index(rest[1:]), i, which)
+            copy.start()
+            pending.append(copy)
+
+    def early_step(i):
+        for n, (_, _, size, row) in enumerate(sections):
+            first_early(i, n).wait()
+            add_rows(got_first.at[i, pl.ds(row, size)], early_rows_of(n, turned(first[i])), size)
+        settle(i, 0)
+
+    def core_copy(g):
+        _, _, begin, end = groups[g]
+        rows = pl.ds(begin, end - begin)
+        return remote(sent_ref.at[:, :, rows], late_got.at[:, :, rows], core_sems, (g,), core_peer)
+
+    def x_copies(g):
+        low, high, begin, end = groups[g]
+        shared = end - begin
+        copies = []
+        for d, (x, peer) in enumerate(zip(x_others, x_peers)):
+            copies.append(
+                remote(
+                    late_got.at[x, :, pl.ds(begin, shared)], late_from.at[d, :, pl.ds(low, shared)],
+                    along_sems, (d, g, 0), peer,
+                )
+            )
+            if low + shared < high:
+                rows = pl.ds(low + shared, high - low - shared)
+                copies.append(
+                    remote(own_ref.at[x, :, rows], late_from.at[d, :, rows], along_sems, (d, g, 1), peer)
+                )
+        return copies
+
+    def along_x(g):
+        low, _, begin, end = groups[g]
+        core_copy(g).wait()
+
+        def core_add(i, carry):
+            j, s = i // count, i % count
+            mine = own_ref[j, s, low : low + end - begin].astype(f32)
+            late_got[j, s, begin:end] = (mine + late_got[j, s, begin:end].astype(f32)).astype(bf16)
+            return carry
+
+        lax.fori_loop(0, along * count, core_add, 0)
+        for copy in x_copies(g):
+            copy.start()
+
+    def first_late(i, g):
+        low, high, _, _ = groups[g]
+        return remote(
+            late_from.at[0, turned([0] + first[i]), pl.ds(low, high - low)],
+            got_first.at[i, rows_of(parts[1 + g])], first_late_sems, (i, g), head_peers[0],
+        )
+
+    def over_heads(g):
+        low, high, begin, end = groups[g]
+        middle = low + end - begin
+        for copy in x_copies(g):
+            copy.wait()
+
+        def x_add(s, carry):
+            total = late_got[x_at, s, begin:end].astype(f32)
+            for d in range(along - 1):
+                total = total + late_from[d, s, low:middle].astype(f32)
+            late_from[0, s, low:middle] = total.astype(bf16)
+            if middle < high:
+                total = own_ref[x_at, s, middle:high].astype(f32)
+                for d in range(along - 1):
+                    total = total + late_from[d, s, middle:high].astype(f32)
+                late_from[0, s, middle:high] = total.astype(bf16)
+            return carry
+
+        lax.fori_loop(0, count, x_add, 0)
+        for i in range(len(first)):
+            first_late(i, g).start()
+
+    def late_step(i, g):
+        low, high, _, _ = groups[g]
+        first_late(i, g).wait()
+        add_rows(
+            got_first.at[i, rows_of(parts[1 + g])],
+            late_from.at[0, turned(first[i]), pl.ds(low, high - low)],
+            high - low,
+        )
+        settle(i, 1 + g)
+
+    mine = lambda ref, size: ref[:, pl.ds(pl.multiple_of(core * size, size), size)]
+    theirs = lambda ref, size: ref[:, pl.ds(pl.multiple_of((1 - core) * size, size), size)]
     chain_copy = remote(joined_ref, chain_got, chain_sems, (0,), below)
     chain_copy.start()
     query_copy = remote(query_grad_ref.at[1], query_got, chain_sems, (1,), core_peer)
     query_copy.start()
-    latent_copy = remote(latent_low.at[1], latent_got, chain_sems, (2,), core_peer)
     for i in range(len(first)):
         for n in range(len(sections)):
             first_early(i, n).start()
 
-    def settle_latents():
-        chain_copy.wait()
-        for side in (1, 0):
-            size = latent_low.shape[1] // 2
-            for t in range(2):
-                at = slice(t * size, (t + 1) * size)
-                latent_low[side, at] = (latent_grad_ref[side, at] + chain_got[side, at].astype(f32)).astype(bf16)
-            if side == 1:
-                latent_copy.start()
-        query_copy.wait()
-        latent_copy.wait()
-
-    def next_copy(bit, j, i, part, which):
-        rows = pl.ds(part.start, part.stop - part.start)
-        return remote(
-            got_first.at[i, rows], got_next[bit - 1].at[j, rows], next_sems[bit - 1], (j, which), head_peers[bit]
+    @pl.loop(0, tokens // block)
+    def _(t):
+        at = pl.ds(pl.multiple_of(t * block, block), block)
+        row = inputs_ref[at].astype(f32)
+        scale = lax.rsqrt(jnp.mean(row * row, axis=-1, keepdims=True) + epsilon)
+        normed[at] = (row * scale * gain_ref[...]).astype(bf16)
+
+    fill_shards(own_ref, 0, matmul_tn(normed[...], query_grad_ref[0]), count)
+    fill_shards(own_ref, share, key_up[...], count)
+    fill_shards(own_ref, share + lift, value_up[...], count)
+    query_copy.wait()
+    fill_shards(sent_ref, 0, matmul_tn(normed[...], query_got[...]), count)
+    core_copy(0).start()
+    early_step(0)
+    along_x(0)
+    for i in range(1, len(first) // 2):
+        early_step(i)
+
+    chain_copy.wait()
+    for side in (1, 0):
+        for t in range(0, tokens, block):
+            at = slice(t, t + block)
+            latent_low[side, at] = (latent_grad_ref[side, at] + chain_got[side, at].astype(f32)).astype(bf16)
+        if side == 1:
+            latent_copy = remote(latent_low.at[1], latent_got, chain_sems, (2,), core_peer)
+            latent_copy.start()
+    latent_copy.wait()
+
+    def back(t, gain_total):
+        at = pl.ds(pl.multiple_of(t * block, block), block)
+        row = inputs_ref[at].astype(f32)
+        scale = lax.rsqrt(jnp.mean(row * row, axis=-1, keepdims=True) + epsilon)
+        unit = row * scale
+        grad = (
+            matmul_nt(query_grad_ref[0, at], mine(query_ref, half))
+            + matmul_nt(query_got[at], theirs(query_ref, half))
+            + matmul_nt(latent_low[0, at], mine(latent_ref, latent))
+            + matmul_nt(latent_got[at], theirs(latent_ref, latent))
         )
-
-    def settle(i, part, which):
-        rest = first[i]
-        level = rest[0] if rest else bits
-        size = part.stop - part.start
-        rows = pl.ds(part.start, size)
-        for bit in range(1, level):
-            j = orders(bit).index(rest)
-            next_copy(bit, j, i, part, which).wait_recv()
-            add_rows(got_first.at[i, rows], got_next[bit - 1].at[j, rows], size)
-        if rest:
-            copy = next_copy(level, orders(level).index(rest[1:]), i, part, which)
-            copy.start()
-            pending.append(copy)
-
-    def early_step(i):
-        for n, (_, _, share, row) in enumerate(sections):
-            first_early(i, n).wait()
-            add_rows(got_first.at[i, pl.ds(row, share)], early_rows_of(n, turned(first[i])), share)
-        settle(i, early_part, 0)
-
-    def first_late(i):
-        return remote(
-            late_from.at[0, turned([0] + first[i])],
-            got_first.at[i, pl.ds(early_rows, late_rows)],
-            first_late_sems, (i,), head_peers[0],
+        scaled = grad * gain_ref[...]
+        grad_ref[at] = resid_ref[at] + scale * (
+            scaled - unit * jnp.mean(scaled * unit, axis=-1, keepdims=True)
         )
-
-    def late_begin():
-        for copy in x_copies:
-            copy.wait()
-
-        def x_add(s, carry):
-            shared = late_got[x_at, s].astype(f32)
-            alone = own_ref[x_at, s, shared_rows:].astype(f32)
-            for d in range(along - 1):
-                shared = shared + late_from[d, s, :shared_rows].astype(f32)
-                alone = alone + late_from[d, s, shared_rows:].astype(f32)
-            late_from[0, s, :shared_rows] = shared.astype(bf16)
-            late_from[0, s, shared_rows:] = alone.astype(bf16)
-            return carry
-
-        lax.fori_loop(0, count, x_add, 0)
-        for i in range(len(first)):
-            first_late(i).start()
-
-    def late_step(i):
-        first_late(i).wait()
-        add_rows(got_first.at[i, pl.ds(early_rows, late_rows)], late_from.at[0, turned(first[i])], late_rows)
-        settle(i, late_part, 1)
-
-    final = len(first) - 1
-    half = max(1, len(first) // 2)
-    for i in range(half):
+        return gain_total + jnp.sum(grad * unit, axis=0, keepdims=True)
+
+    gain_total = lax.fori_loop(0, tokens // block, back, jnp.zeros((1, width), f32))
+    other = other_gain_ref[...]
+    low = groups[1][0]
+    for target, at, latents, gain in (
+        (own_ref, low, latent_low[0], jnp.where(core == 0, gain_total, other)),
+        (sent_ref, groups[1][2], latent_got[...], jnp.where(core == 0, other, gain_total)),
+    ):
+        fill_folded(target, at, matmul_tn(normed[...], latents), count)
+        fill_gains(target, at + fold, gain, count)
+    core_copy(1).start()
+    over_heads(0)
+    along_x(1)
+    for i in range(max(1, len(first) // 2), final):
         early_step(i)
-    late_compute(core, settle_latents)
-    core_copy = remote(sent_ref, late_got, core_sems, (0,), core_peer)
-    core_copy.start()
-    core_copy.wait()
-
-    def core_add(i, carry):
-        j, s = i // count, i % count
-        late_got[j, s] = (own_ref[j, s, :shared_rows].astype(f32) + late_got[j, s].astype(f32)).astype(bf16)
-        return carry
-
-    lax.fori_loop(0, along * count, core_add, 0)
-    x_copies = []
-    for d, (x, peer) in enumerate(zip(x_others, x_peers)):
-        x_copies.append(
-            remote(late_got.at[x], late_from.at[d, :, pl.ds(0, shared_rows)], along_sems, (d, 0), peer)
-        )
-        x_copies.append(
-            remote(
-                own_ref.at[x, :, pl.ds(shared_rows, late_rows - shared_rows)],
-                late_from.at[d, :, pl.ds(shared_rows, late_rows - shared_rows)],
-                along_sems, (d, 1), peer,
-            )
-        )
-    for copy in x_copies:
-        copy.start()
-
-    early_step(half)
-    late_begin()
-    for i in range(half + 1, final):
-        early_step(i)
+    over_heads(1)
     for i in range(final):
-        late_step(i)
-
-    def spread(part, which):
-        rows = pl.ds(part.start, part.stop - part.start)
+        for g in range(len(groups)):
+            late_step(i, g)
+
+    def spread(which):
+        rows = rows_of(parts[which])
         out_ref[row_at, rows] = got_first[final, rows]
         copies = [remote(out_ref.at[row_at, rows], out_ref.at[row_at, rows], out_sems, (which, 0), core_peer)]
         for d, peer in enumerate(x_peers):
@@ -813,8 +857,8 @@
             copy.start()
         return copies
 
-    def pass_on(part, which, copies):
-        rows = pl.ds(part.start, part.stop - part.start)
+    def pass_on(which, copies):
+        rows = rows_of(parts[which])
         more = []
         for d in range(along - 1):
             copies[1 + d].wait_recv()
@@ -828,12 +872,12 @@
         return more
 
     early_step(final)
-    early_out = spread(early_part, 0)
-    late_step(final)
-    late_out = spread(late_part, 1)
-    early_more = pass_on(early_part, 0, early_out)
-    late_more = pass_on(late_part, 1, late_out)
-    for copies, more in ((early_out, early_more), (late_out, late_more)):
+    spreads = [spread(0)]
+    for g in range(len(groups)):
+        late_step(final, g)
+        spreads.append(spread(1 + g))
+    passes = [pass_on(which, copies) for which, copies in enumerate(spreads)]
+    for copies, more in zip(spreads, passes):
         copies[0].wait()
         for copy in copies[1:]:
             copy.wait_send()
@@ -844,14 +888,19 @@
 
 
 def finish(early, shares, count, late_args):
-    inputs = late_args[0]
+    inputs, _, query_grads, latent_grads = late_args[:4]
     tokens, width = inputs.shape
+    latent = latent_grads.shape[2]
     piece = early[0].shape[1]
     along = width // piece // 2
     share = width // count
+    fold, lift = share // 2, latent // count
     bits = count.bit_length() - 1
-    shared_rows = share + share // 2 + 16
-    late_rows = shared_rows + 2 * (late_args[3].shape[2] // count)
+    groups = [
+        (0, share + 2 * lift, 0, share),
+        (share + 2 * lift, share + 2 * lift + fold + 16, share, share + fold + 16),
+    ]
+    late_rows, shared_rows = groups[1][1], groups[1][3]
     sections = []
     row = 0
     for which, of_one in enumerate(shares):
@@ -867,33 +916,9 @@
     def body(*refs):
         refs = list(refs)
         take = lambda k: [refs.pop(0) for _ in range(k)]
-        early_refs = take(len(early))
-        late_refs = take(len(late_args))
-        out_ref, grad_ref = take(2)
-        normed, own_ref, sent_ref, late_got, late_from, got_first = take(6)
-        got_next = take(bits - 1)
-        chain_got, query_got, latent_low, latent_got, chain_sems = take(5)
-        core_sems, along_sems, first_sems, first_late_sems = take(4)
-        next_sems = take(bits - 1)
-        (out_sems,) = take(1)
-        (
-            inputs_ref, gain_ref, query_grad_ref, latent_grad_ref, joined_ref,
-            query_ref, latent_ref, resid_ref, other_gain_ref, key_up, value_up,
-        ) = late_refs
-
-        def late_compute(core, before):
-            late_parts(
-                core, inputs_ref, gain_ref, (query_grad_ref.at[0], query_got, latent_low.at[0], latent_got), before,
-                query_ref, latent_ref, resid_ref, other_gain_ref, (key_up, value_up),
-                normed, own_ref, sent_ref, grad_ref,
-            )
-
-        finish_kernel(
-            sections, early_refs, late_compute,
-            (query_grad_ref, latent_grad_ref, joined_ref, chain_got, query_got, latent_low, latent_got),
-            own_ref, sent_ref, out_ref, late_got, late_from,
-            got_first, got_next, chain_sems, core_sems, along_sems, first_sems, first_late_sems, next_sems, out_sems,
-        )
+        given = [take(len(early))] + take(len(late_args)) + take(2)
+        given += take(6) + [take(bits - 1)] + take(4) + take(5) + [take(bits - 1)] + take(1)
+        finish_kernel(sections, groups, (row, share, fold, lift), given)
 
     return pl.pallas_call(
         body,
@@ -913,18 +938,18 @@
         ]
         + [pltpu.VMEM((count >> (bit + 1), total, piece), bf16) for bit in range(1, bits)]
         + [
-            pltpu.VMEM(late_args[4].shape, bf16),
-            pltpu.VMEM(late_args[2].shape[1:], bf16),
-            pltpu.VMEM(late_args[4].shape, bf16),
-            pltpu.VMEM(late_args[4].shape[1:], bf16),
+            pltpu.VMEM((2, tokens, latent), bf16),
+            pltpu.VMEM(query_grads.shape[1:], bf16),
+            pltpu.VMEM((2, tokens, latent), bf16),
+            pltpu.VMEM((tokens, latent), bf16),
             dma((2, 3)),
-            dma((2, 1)),
-            dma((2, along - 1, 2)),
+            dma((2, 2)),
+            dma((2, along - 1, 2, 2)),
             dma((2, count // 2, len(sections))),
-            dma((2, count // 2)),
+            dma((2, count // 2, 2)),
         ]
-        + [dma((2, count >> (bit + 1), 2)) for bit in range(1, bits)]
-        + [dma((2, 2, 2 * along))],
+        + [dma((2, count >> (bit + 1), 3)) for bit in range(1, bits)]
+        + [dma((2, 3, 2 * along))],
         compiler_params=pltpu.CompilerParams(
             collective_id=0, has_side_effects=True, vmem_limit_bytes=60 << 20
         ),
@@ -935,13 +960,9 @@
 def lay_out_kernel(rows, latent, full_ref, gate_ref, up_ref, output_ref, down_ref, query_ref, latent_ref, key_ref, value_ref, gains_ref):
     pieces, _, piece = full_ref.shape
     at = 0
-    for ref, size, turn in zip((gate_ref, up_ref, output_ref, down_ref), rows, (True, True, False, False)):
+    for ref, size in zip((gate_ref, up_ref, output_ref, down_ref), rows):
         for j in range(pieces):
-            value = full_ref[j, at : at + size].astype(f32)
-            if turn:
-                ref[j * piece : (j + 1) * piece] = value.T
-            else:
-                ref[:, j * piece : (j + 1) * piece] = value
+            ref[:, j * piece : (j + 1) * piece] = full_ref[j, at : at + size].astype(f32)
         at += size
     share = query_ref.shape[0]
     fold = share // 2
@@ -955,6 +976,9 @@
             j, row : row + share
         ].astype(f32)
         row += share
+        for ref in (key_ref, value_ref):
+            ref[core, :, x * piece : (x + 1) * piece] = full_ref[j, row : row + lift].astype(f32)
+            row += lift
         side, column = divmod(x * piece, latent)
         column += core * latent
         latent_ref[side * fold : (side + 1) * fold, column : column + piece] = full_ref[
@@ -963,10 +987,6 @@
         row += fold
         if x == 0:
             gains_ref[core : core + 1] = full_ref[j, row : row + 16, :lane].astype(f32)[:1]
-        row += 16
-        for ref in (key_ref, value_ref):
-            ref[core, :, x * piece : (x + 1) * piece] = full_ref[j, row : row + lift].astype(f32)
-            row += lift
 
 
 def lay_out(full, rows, share, latent, half, count, width):
@@ -975,8 +995,8 @@
     lift = latent // count
     vmem = pl.BlockSpec(memory_space=pltpu.VMEM)
     outs = [
-        shape((width, gate), f32),
-        shape((width, up), f32),
+        shape((gate, width), f32),
+        shape((up, width), f32),
         shape((output, width), f32),
         shape((down, width), f32),
         shape((share, width), f32),
@@ -1064,9 +1084,8 @@
     for k in range(steps):
         if k > 0:
             moving = lax.ppermute(moving, "heads", up_chain)
-            if k > 1:
-                moving, crossed = lax.optimization_barrier((moving, segs[-1][1]))
-                segs[-1] = (segs[-1][0], crossed)
+            moving, crossed = lax.optimization_barrier((moving, segs[-1][1]))
+            segs[-1] = (segs[-1][0], crossed)
         segs.append((moving, flip(moving, "heads", 0)))
         base = ((level - k) * 2 + side) * tokens
         other = ((level - k) * 2 + 1 - side) * tokens
@@ -1082,12 +1101,15 @@
         )
 
     parts = [range(0, steps - 1), range(steps - 1, steps)]
-    state = None
+    state = expanded = None
     for i, ks in enumerate(parts):
         seg_list, base_list = pick([(k, j) for k in ks for j in range(2)])
-        state = attend_part(
-            queries, start, key_lift, value_lift_t, lo, seg_list, base_list, state, i == len(parts) - 1
+        made = attend_part(
+            queries, start, key_lift, value_lift_t, lo, seg_list, base_list, expanded, state, i == len(parts) - 1
         )
+        state = made[:3]
+        if i == 0:
+            expanded = made[3]
     head_out, lse, head_mix = state
     mixed_mine = head_out[:rows].reshape(count, group_width)
     mixed_got = swap(head_out[rows:]).reshape(count, group_width)
@@ -1105,7 +1127,7 @@
     calls = [[(k, 0), (k, 1)] for k in range(steps - 1, 0, -1)]
     calls[-1].append((0, 1))
     calls.append([(0, 0)])
-    state = None
+    state = kept = None
     pieces_in = []
     waiting = []
     passing = None
@@ -1123,20 +1145,21 @@
             passing = lax.ppermute(joined, "heads", down_chain)
         seg_list, base_list = pick(items)
         made = attend_back_part(
-            now, head_grads, lse, head_mix, start, key_lift, value_lift, key_lift_t, lo,
-            seg_list, base_list, state, len(items) == 1, 0, 2 * rows,
+            now, head_grads, lse, head_mix, start, expanded, value_lift, key_lift_t, lo,
+            seg_list, base_list, kept, state, len(items) == 1,
         )
-        state = list(made[len(items) :])
+        state = made[len(items) : len(items) + 2]
+        if i == 0:
+            kept = made[len(items) + 2 :]
         k = items[0][0]
         if k == 0:
             pieces_in.append(made[0])
             continue
         waiting.append((made[0], flip(made[1], "heads", 0)))
         if k == 1:
-            state.append(jnp.zeros_like(state[1]))
             pieces_in.append(flip(made[2], "heads", 0))
     joined = join(waiting.pop())
-    query_grads, key_part, value_part = state
+    query_grads, key_part, value_part = made[1:]
     latent_grads = sum(p.astype(f32) for p in pieces_in)
 
     ff_share = gate_weight.shape[1] // peers
@@ -1165,8 +1188,8 @@
         value_share,
         output_share,
         gains[1],
-        gate_share,
-        up_share,
+        gate_share.T,
+        up_share.T,
         down_share,
     )
 

time: 555 us -> 518 us (0.933)
  Pallas kernels: 341 us -> 322 us
  waiting for transfers between devices: 105 us -> 91.9 us
    pallas_call x1, Pallas kernels: 151 us -> 132 us  [finish(): pl.pallas_call(body, out_shape=[jax.ShapeDtypeStruct((2 * along, total, p...]
    ppermute x3, waiting for transfers between devices: 24.4 us -> 7.66 us  [shards(): moving = lax.ppermute(moving, 'heads', up_chain)]
    unnamed x41 -> x39, local copies, waits for them, and re-layouts: 12.3 us -> 9.62 us
  transfers between devices with their start and end apart: 20 -> 20, of which waited for: 11 -> 13; matrix products, arithmetic and copies ran while one was open for 5% -> 6% of each run, Pallas kernels for 24% -> 26%
where the time goes in v5:
time: 518 us; the launch traced here: 516 us
  Pallas kernels  322 us (62%)
  waiting for transfers between devices  91.9 us (18%)
  starting transfers between devices  44.3 us (9%)
  other arithmetic  16.7 us (3%)
  local copies, waits for them, and re-layouts  15.4 us (3%)
  between operations  14.6 us (3%)
  matrix products  11.2 us (2%)
    pallas_call x1, Pallas kernels, finish(): pl.pallas_call(body, out_shape=[jax.ShapeDtypeStruct((2 * along, total, p...  132 us
    pallas_call x4, Pallas kernels, attend_back_part(): pl.pallas_call(functools.partial(attend_back_kernel, len(segs), first, la...  66.6 us
    ppermute x13, waiting for transfers between devices, flip(): return lax.ppermute(array, axis, [(i, i ^ 1 << bit) for i in range(size)])  65.5 us
    pallas_call x1, Pallas kernels, feed(): pl.pallas_call(feed_back_kernel, out_shape=outs, grid_spec=pltpu.Prefetch...  50.1 us
    pallas_call x1, Pallas kernels, feed(): pl.pallas_call(feed_kernel, out_shape=outs, grid_spec=pltpu.PrefetchScala...  41 us
    pallas_call x2, Pallas kernels, attend_part(): pl.pallas_call(functools.partial(attend_kernel, len(segs), state is None,...  30.5 us
    ppermute x13, starting transfers between devices, flip(): return lax.ppermute(array, axis, [(i, i ^ 1 << bit) for i in range(size)])  26.9 us
    reduce_scatter x1, waiting for transfers between devices, shards(): lax.psum_scatter(feed_grads, 'rows', scatter_dimension=0, tiled=True)[0]  14.6 us
  transfers between devices with their start and end apart: 20, of which 13 were waited for; matrix products, arithmetic and copies ran while one was open for 6% of the time, Pallas kernels for 26%

profile of v5, /device:TPU:0, one launch (start us, length us, event | category | flops | bytes accessed | tf_op | source)
XLA Modules:
  0.0 516.5 jit_solution(2084616741597802112)
XLA Ops:
  7.3 2.2 multiply_reduce_fusion
  9.5 0.5 multiply_convert_fusion
  10.1 0.7 copy-done.13
  10.7 0.7 convolution_convert_fusion.2
  11.5 0.6 copy-done.12
  12.1 0.5 collective-permute-start.2
  12.5 2.3 convolution_convert_fusion.3
  14.9 2.6 collective-permute-start.4
  17.5 3.5 collective-permute-start.3
  21.1 0.4 iota_compare_fusion
  21.4 19.9 %collective-permute-done.4.refs_4_.refs_7_ = bf16[8,256,256]{2,1,0:T(8,128)(2,1)S(1)} collective-permute-done((bf16[8,256,256]{2,1,0:T(8,128)(2,1)S(1)}, bf16[8,256,256]{2,1,0:T(8,128)(2,1)S(1)}, u32[]{:S(2)}, u32[]{:S(2)}) %collective-permute-start.4) | collective-permute-done | bytes 1048608 | tf_op jit(solution)/shard_map/ppermute | solution.py:554
  41.3 2.4 collective-permute-done.3.refs_5_
  43.8 0.5 collective-permute-start.6
  44.3 5.4 %collective-permute-start.5 = (bf16[8,256,256]{2,1,0:T(8,128)(2,1)S(1)}, bf16[8,256,256]{2,1,0:T(8,128)(2,1)}, u32[]{:S(2)}, u32[]{:S(2)}) collective-permute-start(bf16[8,256,256]{2,1,0:T(8,128)(2,1)S(1)} %collective-permute-done.3.refs_5_), channel_id=1, source_target_pairs={{0,2},{1,3},{2,4},{3,5},{4,6},{5,7},{8,10},{9,11},{10,12},{11,13},... | collective-permute-start | bytes 3145736 | tf_op jit(solution)/shard_map/ppermute | solution.py:1086
  49.6 1.6 convert_reduce_fusion
  51.3 4.1 convolution_convert_fusion
  55.4 0.5 collective-permute-start.1
  55.9 12.5 %collective-permute-done.6.refs_6_ = bf16[8,256,256]{2,1,0:T(8,128)(2,1)} collective-permute-done((bf16[8,256,256]{2,1,0:T(8,128)(2,1)S(1)}, bf16[8,256,256]{2,1,0:T(8,128)(2,1)}, u32[]{:S(2)}, u32[]{:S(2)}) %collective-permute-start.6) | collective-permute-done | bytes 1048608 | tf_op jit(solution)/shard_map/ppermute | solution.py:554
  68.4 2.0 collective-permute-done.5.refs_7_.refs_5_
  70.4 1.5 collective-permute-start.8
  71.9 5.6 %collective-permute-start.7 = (bf16[8,256,256]{2,1,0:T(8,128)(2,1)}, bf16[8,256,256]{2,1,0:T(8,128)(2,1)}, u32[]{:S(2)}, u32[]{:S(2)}) collective-permute-start(bf16[8,256,256]{2,1,0:T(8,128)(2,1)} %collective-permute-done.5.refs_7_.refs_5_), channel_id=1, source_target_pairs={{0,2},{1,3},{2,4},{3,5},{4,6},{5,7},{8,10},{9,11},{10,12},{11,13},... | collective-permute-start | bytes 3145736 | tf_op jit(solution)/shard_map/ppermute | solution.py:1086
  77.5 1.1 constant_dynamic-slice_fusion
  78.6 4.1 convolution_convert_fusion.1
  83.0 0.8 copy.35
  83.8 0.8 copy.34
  84.7 0.8 copy.40
  85.6 2.1 fusion
  87.9 2.8 pad_maximum_fusion
  90.7 3.3 collective-permute-done.8.refs_8_.refs_6_
  93.9 3.2 collective-permute-done.7.refs_5_
  97.2 0.5 collective-permute-start.9
  97.7 18.3 %attend.2 = (f32[8,1,2048]{2,1,0:T(1,128)S(1)}, f32[8,1,2048]{2,1,0:T(1,128)S(1)}, bf16[8,256,2048]{2,1,0:T(8,128)(2,1)}, bf16[8,256,2048]{2,1,0:T(8,128)(2,1)}) custom-call(s32[8]{0:T(128)S(1)} %fusion.9.lo, s32[7]{0:T(128)S(1)} %stack.66.bases, s32[8,1,256]{2,1,0:T(1,128)S(1)} %broadcast_in_dim.4.refs_0_.refs_2_, bf16[8,256,512]{2,1,0:T(8,128)(2,1)} %bitcast.76, ...), custom_call_target="tpu_custom_call" | custom-call | flops 25769803776 | bytes 16777216 | tf_op jit(solution)/shard_map/attend/pallas_call | solution.py:174
  116.0 3.5 collective-permute-done.9.refs_6_
  119.5 12.2 %attend.3 = (bf16[8,256,512]{2,1,0:T(8,128)(2,1)S(1)}, f32[8,1,2048]{2,1,0:T(1,128)S(1)}, bf16[8,256,2048]{2,1,0:T(8,128)(2,1)}) custom-call(s32[8]{0:T(128)S(1)} %fusion.9.lo, s32[3]{0:T(128)S(1)} %add_add_fusion.bases, s32[8,1,256]{2,1,0:T(1,128)S(1)} %broadcast_in_dim.4.refs_0_.refs_2_, bf16[8,256,2048]{2,1,0:T(8,128)(2,1)} %get-tuple-element.76.refs_1_.refs_3_, ...), custom_call_target="tpu_custom_call" | custom-call | flops 8589934592 | bytes 16777216 | tf_op jit(solution)/shard_map/attend/pallas_call | solution.py:174
  131.7 1.4 fusion.15
  133.2 1.0 copy.45
  134.2 2.0 collective-permute-done.10
  136.1 41.0 %feed.1 = (bf16[1024,1024]{1,0:T(8,128)(2,1)}, f32[1024,1024]{1,0:T(8,128)}, bf16[1024,1024]{1,0:T(8,128)(2,1)}, bf16[1024,1024]{1,0:T(8,128)(2,1)}, bf16[1024,2...) custom-call(s32[1]{0:T(128)} %bitcast.core_ref, bf16[1024,1024]{1,0:T(8,128)(2,1)} %bitcast.83, ...), custom_call_target="tpu_custom_call" | custom-call | flops 25769803776 | bytes 51380224 | tf_op jit(solution)/shard_map/feed/pallas_call | solution.py:495
  177.2 0.3 reduce-scatter.3.cloned.1.call-start
  177.5 50.1 %feed_back.1 = (f32[1024,1024]{1,0:T(8,128)}, bf16[1024,512]{1,0:T(8,128)(2,1)}, bf16[1024,512]{1,0:T(8,128)(2,1)}, f32[1,1024]{1,0:T(1,128)}, bf16[4,6656,256]{2,1,0:T(8,128)(2,1)}) custom-call(s32[1]{0:T(128)} %bitcast.core_ref, bf16[1024,512]{1,0:T(8,128)(2,1)} %bitcast.93, bf16[1024,512]{1,0:T(8,128)(2,1)} %bitcast.20.refs_2_.refs_1_, ...), custom_call_target="tpu_custom_call" | custom-call | flops 33822867456 | bytes 61341696 | tf_op jit(solution)/shard_map/feed_back/pallas_call | solution.py:522
  227.6 0.2 collective-permute-start.11
  227.8 2.7 collective-permute-done.11
  230.5 2.8 pad_maximum_fusion.1
  233.3 15.2 %attend_back.4 = (bf16[8,256,256]{2,1,0:T(8,128)(2,1)S(1)}, bf16[8,256,256]{2,1,0:T(8,128)(2,1)S(1)}, f32[8,512,256]{2,1,0:T(8,128)}, f32[256,512]{1,0:T(8,128)S...) custom-call(s32[8]{0:T(128)S(1)} %fusion.9.lo, s32[3]{0:T(128)S(1)} %add_add_fusion.bases, ...), custom_call_target="tpu_custom_call" | custom-call | flops 2147483648 | bytes 4194304 | tf_op jit(solution)/shard_map/attend_back/pallas_call | solution.py:307
  248.5 6.7 %collective-permute-start.13 = (bf16[8,256,256]{2,1,0:T(8,128)(2,1)S(1)}, bf16[8,256,256]{2,1,0:T(8,128)(2,1)S(1)}, u32[]{:S(2)}, u32[]{:S(2)}) collective-permute-start(bf16[8,256,256]{2,1,0:T(8,128)(2,1)S(1)} %get-tuple-element.101), channel_id=1, source_target_pairs={{0,1},{1,0},{2,3},{3,2},{4,5},{5,4},{6,7},{7,6},{8,9},{9,8},{10,11... | collective-permute-start | bytes 3145736 | tf_op jit(solution)/shard_map/ppermute | solution.py:554
  255.3 12.3 %attend_back.5 = (bf16[8,256,256]{2,1,0:T(8,128)(2,1)S(1)}, bf16[8,256,256]{2,1,0:T(8,128)(2,1)S(1)}, f32[8,512,256]{2,1,0:T(8,128)}, f32[256,512]{1,0:T(8,128)S(1)}) custom-call(s32[8]{0:T(128)S(1)} %fusion.9.lo, s32[3]{0:T(128)S(1)} %add_add_fusion.1.bases, bf16[8,256,512]{2,1,0:T(8,128)(2,1)} %bitcast.78, f32[8,1,2048]{2,1,0:T(1,128)S(1)} %get-tuple-element.90.refs_1_, ...), custom_call_target="tpu_custom_call" | custom-call | flops 2147483648 | bytes 4194304 | tf_op jit(solution)/shard_map/attend_back/pallas_call | solution.py:307
  267.6 11.6 %collective-permute-done.13 = bf16[8,256,256]{2,1,0:T(8,128)(2,1)S(1)} collective-permute-done((bf16[8,256,256]{2,1,0:T(8,128)(2,1)S(1)}, bf16[8,256,256]{2,1,0:T(8,128)(2,1)S(1)}, u32[]{:S(2)}, u32[]{:S(2)}) %collective-permute-start.13) | collective-permute-done | bytes 1048608 | tf_op jit(solution)/shard_map/ppermute | solution.py:554
  279.1 0.3 add_convert_fusion.2
  279.4 1.3 collective-permute-start.14
  280.8 12.6 %attend_back.6 = (bf16[8,256,256]{2,1,0:T(8,128)(2,1)S(1)}, bf16[8,256,256]{2,1,0:T(8,128)(2,1)S(1)}, bf16[8,256,256]{2,1,0:T(8,128)(2,1)S(1)}, f32[8,512,256]{2,1,0:T(8,128)}, f32[256,512]{1,0:T(8,128)S(1)}) custom-call(s32[8]{0:T(128)S(1)} %fusion.9.lo, s32[4]{0:T(128)S(1)} %pad_add_fusion.2.bases, bf16[8,256,512]{2,1,0:T(8,128)(2,1)} %bitcast.79, ...), custom_call_target="tpu_custom_call" | custom-call | flops 3221225472 | bytes 4194304 | tf_op jit(solution)/shard_map/attend_back/pallas_call | solution.py:307
  293.3 13.8 %collective-permute-start.15 = (bf16[8,256,256]{2,1,0:T(8,128)(2,1)S(1)}, bf16[8,256,256]{2,1,0:T(8,128)(2,1)S(1)}, u32[]{:S(2)}, u32[]{:S(2)}) collective-permute-start(bf16[8,256,256]{2,1,0:T(8,128)(2,1)S(1)} %get-tuple-element.110), channel_id=1, source_target_pairs={{0,1},{1,0},{2,3},{3,2},{4,5},{5,4},{6,7},{7,6},{8,9},{9,8},{10,11... | collective-permute-start | bytes 3145736 | tf_op jit(solution)/shard_map/ppermute | solution.py:554
  307.2 4.1 collective-permute-done.14
  311.3 0.4 add_convert_fusion.1
  311.7 1.3 collective-permute-start.17
  313.1 26.5 %attend_back.7 = (bf16[8,256,256]{2,1,0:T(8,128)(2,1)S(1)}, bf16[8,256,512]{2,1,0:T(8,128)(2,1)S(1)}, f32[256,512]{1,0:T(8,128)S(1)}, f32[256,512]{1,0:T(8,128)S(1)}) custom-call(s32[8]{0:T(128)S(1)} %fusion.9.lo, s32[2]{0:T(128)S(1)} %pad_add_fusion.1.bases, bf16[8,256,512]{2,1,0:T(8,128)(2,1)} %bitcast.80, f32[8,1,2048]{2,1,0:T(1,128)S(1)} %get-tuple-element.90.refs_1_, ...), custom_call_target="tpu_custom_call" | custom-call | flops 1073741824 | bytes 4194304 | tf_op jit(solution)/shard_map/attend_back/pallas_call | solution.py:307
  339.7 1.8 convert_add_fusion
  342.0 10.1 %collective-permute-done.16 = bf16[8,256,256]{2,1,0:T(8,128)(2,1)S(1)} collective-permute-done((bf16[8,256,256]{2,1,0:T(8,128)(2,1)S(1)}, bf16[8,256,256]{2,1,0:T(8,128)(2,1)S(1)}, u32[]{:S(2)}, u32[]{:S(2)}) %collective-permute-start.16) | collective-permute-done | bytes 1048608 | tf_op jit(solution)/shard_map/ppermute | solution.py:554
  352.0 1.4 add_convert_fusion
  353.4 14.6 %reduce-scatter.3.cloned.1.call-done = bf16[1,6656,256]{2,1,0:T(8,128)(2,1)} async-done(((bf16[4,6656,256]{2,1,0:T(8,128)(2,1)}), bf16[1,6656,256]{2,1,0:T(8,128)(2,1)}) %reduce-scatter.3.cloned.1.call-update) | async-done | bytes 3407888 | tf_op jit(solution)/shard_map/reduce_scatter | solution.py:1125
  368.0 131.6 %finish.1 = (bf16[4,1456,256]{2,1,0:T(8,128)(2,1)}, f32[1024,1024]{1,0:T(8,128)}) custom-call(bf16[6656,256]{1,0:T(8,128)(2,1)} %bitcast.88, bf16[2816,256]{1,0:T(8,128)(2,1)} %bitcast.90, bf16[1024,1024]{1,0:T(8,128)(2,1)} %bitcast.84, f32[1,1024]{1,0:T(1,128)} %bitcast.96, bf16[2,1024,512]{2,1,0:T(8,128)(2,1)} %bitcast.74, f32[2,1024,256]{2,1,0:T(8,128)} %bitcast.85, ...), custom_call_target="tpu_custom_call" | custom-call | tf_op jit(solution)/shard_map/finish/pallas_call | solution.py:923
  499.7 1.8 copy-done
  501.5 2.6 lay_out.1
  504.1 0.5 slice_bitcast_fusion
  504.6 4.8 copy.47
  (66 shorter events, 1.7 us)
Async XLA Ops:
  7.2 2.3 copy-start.11
  7.2 2.3 copy-start.16
  7.2 346.2 %reduce-scatter.5.cloned.1.call-start = ((), (), s32[]{:S(2)}) async-start(), calls=%async_computation.3 | async-start | bytes 7208960 | tf_op jit(solution)/shard_map/reduce_scatter | solution.py:1124
  9.5 1.2 copy-start.13
  10.7 1.3 copy-start.12
  12.1 2.8 collective-permute-start.2
  14.8 6.2 %copy-start.15 = (s32[4,2048]{1,0:T(4,128)S(1)}, s32[4,2048]{1,0:T(4,128)}, u32[]{:S(2)}) copy-start(s32[4,2048]{1,0:T(4,128)} %param.14) | copy-start | bytes 98308
  14.9 26.4 %collective-permute-start.4 = (bf16[8,256,256]{2,1,0:T(8,128)(2,1)S(1)}, bf16[8,256,256]{2,1,0:T(8,128)(2,1)S(1)}, u32[]{:S(2)}, u32[]{:S(2)}) collective-permute-start(bf16[8,256,256]{2,1,0:T(8,128)(2,1)S(1)} %bitcast.70), channel_id=1, source_target_pairs={{0,1},{1,0},{2,3},{3,2},{4,5},{5,4},{6,7},{7,6},{8,9},{9,8},{10,11... | collective-permute-start | bytes 3145736 | tf_op jit(solution)/shard_map/ppermute | solution.py:554
  17.5 26.3 %collective-permute-start.3 = (bf16[8,256,256]{2,1,0:T(8,128)(2,1)S(1)}, bf16[8,256,256]{2,1,0:T(8,128)(2,1)S(1)}, u32[]{:S(2)}, u32[]{:S(2)}) collective-permute-start(bf16[8,256,256]{2,1,0:T(8,128)(2,1)S(1)} %bitcast.71), channel_id=1, source_target_pairs={{0,2},{1,3},{2,4},{3,5},{4,6},{5,7},{8,10},{9,11},{10,12},{11,13},... | collective-permute-start | bytes 3145736 | tf_op jit(solution)/shard_map/ppermute | solution.py:1086
  41.3 56.4 %copy-start.2 = (bf16[8,256,256]{2,1,0:T(8,128)(2,1)}, bf16[8,256,256]{2,1,0:T(8,128)(2,1)S(1)}, u32[]{:S(2)}) copy-start(bf16[8,256,256]{2,1,0:T(8,128)(2,1)S(1)} %collective-permute-done.4.refs_4_.refs_7_) | copy-start | bytes 3145732
  43.8 11.6 %copy-start.3 = (bf16[8,256,256]{2,1,0:T(8,128)(2,1)}, bf16[8,256,256]{2,1,0:T(8,128)(2,1)S(1)}, u32[]{:S(2)}) copy-start(bf16[8,256,256]{2,1,0:T(8,128)(2,1)S(1)} %collective-permute-done.3.refs_5_) | copy-start | bytes 3145732
  43.8 24.6 %collective-permute-start.6 = (bf16[8,256,256]{2,1,0:T(8,128)(2,1)S(1)}, bf16[8,256,256]{2,1,0:T(8,128)(2,1)}, u32[]{:S(2)}, u32[]{:S(2)}) collective-permute-start(bf16[8,256,256]{2,1,0:T(8,128)(2,1)S(1)} %collective-permute-done.3.refs_5_), channel_id=1, source_target_pairs={{0,1},{1,0},{2,3},{3,2},{4,5},{5,4},{6,7},{7,6},{8,9},{9,8},{10,11... | collective-permute-start | bytes 3145736 | tf_op jit(solution)/shard_map/ppermute | solution.py:554
  44.3 26.1 %collective-permute-start.5 = (bf16[8,256,256]{2,1,0:T(8,128)(2,1)S(1)}, bf16[8,256,256]{2,1,0:T(8,128)(2,1)}, u32[]{:S(2)}, u32[]{:S(2)}) collective-permute-start(bf16[8,256,256]{2,1,0:T(8,128)(2,1)S(1)} %collective-permute-done.3.refs_5_), channel_id=1, source_target_pairs={{0,2},{1,3},{2,4},{3,5},{4,6},{5,7},{8,10},{9,11},{10,12},{11,13},... | collective-permute-start | bytes 3145736 | tf_op jit(solution)/shard_map/ppermute | solution.py:1086
  51.2 36.5 %collective-permute-start = (s32[4,256]{1,0:T(4,128)S(1)}, s32[4,256]{1,0:T(4,128)S(1)}, u32[]{:S(2)}, u32[]{:S(2)}) collective-permute-start(s32[4,256]{1,0:T(4,128)S(1)} %broadcast_subtract_fusion), channel_id=1, source_target_pairs={{0,8},{8,0},{16,24},{24,16},{1,9},{9,1},{17,25},{25,17},{2,10},{10... | collective-permute-start | bytes 12296 | tf_op jit(solution)/shard_map/ppermute | solution.py:554
  55.4 32.5 %collective-permute-start.1 = (bf16[1024,512]{1,0:T(8,128)(2,1)}, bf16[1024,512]{1,0:T(8,128)(2,1)}, u32[]{:S(2)}, u32[]{:S(2)}) collective-permute-start(bf16[1024,512]{1,0:T(8,128)(2,1)} %convolution_convert_fusion), channel_id=1, source_target_pairs={{0,8},{8,0},{16,24},{24,16},{1,9},{9,1},{17,25},{25,17},{2,10},{10... | collective-permute-start | bytes 3145736 | tf_op jit(solution)/shard_map/ppermute | solution.py:554
  70.4 23.6 %collective-permute-start.8 = (bf16[8,256,256]{2,1,0:T(8,128)(2,1)}, bf16[8,256,256]{2,1,0:T(8,128)(2,1)}, u32[]{:S(2)}, u32[]{:S(2)}) collective-permute-start(bf16[8,256,256]{2,1,0:T(8,128)(2,1)} %collective-permute-done.5.refs_7_.refs_5_), channel_id=1, source_target_pairs={{0,1},{1,0},{2,3},{3,2},{4,5},{5,4},{6,7},{7,6},{8,9},{9,8},{10,11... | collective-permute-start | bytes 3145736 | tf_op jit(solution)/shard_map/ppermute | solution.py:554
  71.9 25.3 %collective-permute-start.7 = (bf16[8,256,256]{2,1,0:T(8,128)(2,1)}, bf16[8,256,256]{2,1,0:T(8,128)(2,1)}, u32[]{:S(2)}, u32[]{:S(2)}) collective-permute-start(bf16[8,256,256]{2,1,0:T(8,128)(2,1)} %collective-permute-done.5.refs_7_.refs_5_), channel_id=1, source_target_pairs={{0,2},{1,3},{2,4},{3,5},{4,6},{5,7},{8,10},{9,11},{10,12},{11,13},... | collective-permute-start | bytes 3145736 | tf_op jit(solution)/shard_map/ppermute | solution.py:1086
  85.6 2.3 copy-start.14
  87.9 9.8 %copy-start.4 = (bf16[8,256,256]{2,1,0:T(8,128)(2,1)S(1)}, bf16[8,256,256]{2,1,0:T(8,128)(2,1)}, u32[]{:S(2)}) copy-start(bf16[8,256,256]{2,1,0:T(8,128)(2,1)} %copy-done.3) | copy-start | bytes 3145732
  97.2 22.3 %collective-permute-start.9 = (bf16[8,256,256]{2,1,0:T(8,128)(2,1)}, bf16[8,256,256]{2,1,0:T(8,128)(2,1)S(1)}, u32[]{:S(2)}, u32[]{:S(2)}) collective-permute-start(bf16[8,256,256]{2,1,0:T(8,128)(2,1)} %collective-permute-done.7.refs_5_), channel_id=1, source_target_pairs={{0,1},{1,0},{2,3},{3,2},{4,5},{5,4},{6,7},{7,6},{8,9},{9,8},{10,11... | collective-permute-start | bytes 3145736 | tf_op jit(solution)/shard_map/ppermute | solution.py:554
  97.7 21.8 %copy-start.10 = (bf16[512,256]{1,0:T(8,128)(2,1)S(1)}, bf16[512,256]{1,0:T(8,128)(2,1)}, u32[]{:S(2)}) copy-start(bf16[512,256]{1,0:T(8,128)(2,1)} %copy.35) | copy-start | bytes 786436
  119.5 12.2 %copy-start.6 = (bf16[8,256,256]{2,1,0:T(8,128)(2,1)}, bf16[8,256,256]{2,1,0:T(8,128)(2,1)S(1)}, u32[]{:S(2)}) copy-start(bf16[8,256,256]{2,1,0:T(8,128)(2,1)S(1)} %collective-permute-done.9.refs_6_) | copy-start | bytes 3145732
  133.1 3.0 collective-permute-start.10
  177.2 190.8 %reduce-scatter.3.cloned.1.call-start = ((), (), s32[]{:S(2)}) async-start(), calls=%async_computation.2 | async-start | bytes 17039360 | tf_op jit(solution)/shard_map/reduce_scatter | solution.py:1125
  227.6 2.9 collective-permute-start.11
  230.5 2.8 copy-start.7
  248.5 30.6 %collective-permute-start.13 = (bf16[8,256,256]{2,1,0:T(8,128)(2,1)S(1)}, bf16[8,256,256]{2,1,0:T(8,128)(2,1)S(1)}, u32[]{:S(2)}, u32[]{:S(2)}) collective-permute-start(bf16[8,256,256]{2,1,0:T(8,128)(2,1)S(1)} %get-tuple-element.101), channel_id=1, source_target_pairs={{0,1},{1,0},{2,3},{3,2},{4,5},{5,4},{6,7},{7,6},{8,9},{9,8},{10,11... | collective-permute-start | bytes 3145736 | tf_op jit(solution)/shard_map/ppermute | solution.py:554
  267.5 13.2 %copy-start.5 = (bf16[8,256,256]{2,1,0:T(8,128)(2,1)S(1)}, bf16[8,256,256]{2,1,0:T(8,128)(2,1)}, u32[]{:S(2)}) copy-start(bf16[8,256,256]{2,1,0:T(8,128)(2,1)} %copy-done.3) | copy-start | bytes 3145732
  267.5 39.7 %collective-permute-start.12 = (bf16[8,256,256]{2,1,0:T(8,128)(2,1)S(1)}, bf16[8,256,256]{2,1,0:T(8,128)(2,1)S(1)}, u32[]{:S(2)}, u32[]{:S(2)}) collective-permute-start(bf16[8,256,256]{2,1,0:T(8,128)(2,1)S(1)} %get-tuple-element.99), channel_id=1, source_target_pairs={{0,1},{1,0},{2,3},{3,2},{4,5},{5,4},{6,7},{7,6},{8,9},{9,8},{10,11... | collective-permute-start | bytes 3145736 | tf_op jit(solution)/shard_map/ppermute | solution.py:554
  279.4 31.9 %collective-permute-start.14 = (bf16[8,256,256]{2,1,0:T(8,128)(2,1)S(1)}, bf16[8,256,256]{2,1,0:T(8,128)(2,1)S(1)}, u32[]{:S(2)}, u32[]{:S(2)}) collective-permute-start(bf16[8,256,256]{2,1,0:T(8,128)(2,1)S(1)} %add_convert_fusion.2), channel_id=1, source_target_pairs={{2,0},{3,1},{4,2},{5,3},{6,4},{7,5},{10,8},{11,9},{12,10},{13,11},... | collective-permute-start | bytes 3145736 | tf_op jit(solution)/shard_map/ppermute | solution.py:1145
  293.3 46.3 %collective-permute-start.15 = (bf16[8,256,256]{2,1,0:T(8,128)(2,1)S(1)}, bf16[8,256,256]{2,1,0:T(8,128)(2,1)S(1)}, u32[]{:S(2)}, u32[]{:S(2)}) collective-permute-start(bf16[8,256,256]{2,1,0:T(8,128)(2,1)S(1)} %get-tuple-element.110), channel_id=1, source_target_pairs={{0,1},{1,0},{2,3},{3,2},{4,5},{5,4},{6,7},{7,6},{8,9},{9,8},{10,11... | collective-permute-start | bytes 3145736 | tf_op jit(solution)/shard_map/ppermute | solution.py:554
  307.2 44.9 %collective-permute-start.16 = (bf16[8,256,256]{2,1,0:T(8,128)(2,1)S(1)}, bf16[8,256,256]{2,1,0:T(8,128)(2,1)S(1)}, u32[]{:S(2)}, u32[]{:S(2)}) collective-permute-start(bf16[8,256,256]{2,1,0:T(8,128)(2,1)S(1)} %get-tuple-element.113), channel_id=1, source_target_pairs={{0,1},{1,0},{2,3},{3,2},{4,5},{5,4},{6,7},{7,6},{8,9},{9,8},{10,11... | collective-permute-start | bytes 3145736 | tf_op jit(solution)/shard_map/ppermute | solution.py:554
  311.7 40.3 %collective-permute-start.17 = (bf16[8,256,256]{2,1,0:T(8,128)(2,1)S(1)}, bf16[8,256,256]{2,1,0:T(8,128)(2,1)S(1)}, u32[]{:S(2)}, u32[]{:S(2)}) collective-permute-start(bf16[8,256,256]{2,1,0:T(8,128)(2,1)S(1)} %add_convert_fusion.1), channel_id=1, source_target_pairs={{2,0},{3,1},{4,2},{5,3},{6,4},{7,5},{10,8},{11,9},{12,10},{13,11},... | collective-permute-start | bytes 3145736 | tf_op jit(solution)/shard_map/ppermute | solution.py:1145
  339.6 2.0 copy-start.1
  339.6 2.2 copy-start.8
  339.6 2.3 copy-start.9
  499.7 1.8 copy-start
Sparse Core Ops, SparseCore 0:
  177.3 81.9 reduce-scatter.4
  262.1 105.9 reduce-scatter.2

commit v6 on v5

--- a/solution.py
+++ b/solution.py
@@ -190,8 +190,8 @@
             dimension_semantics=("arbitrary",), vmem_limit_bytes=48 << 20
         ),
         cost_estimate=pl.CostEstimate(
-            flops=blocks * tokens * tokens * latent * 4,
-            bytes_accessed=rows * heads * latent * tokens * 4,
+            flops=blocks * tokens * tokens * latent * 64,
+            bytes_accessed=rows * heads * latent * tokens * 64,
             transcendentals=blocks * tokens * tokens,
         ),
         name="attend",
@@ -203,18 +203,14 @@
     take = lambda k: [refs.pop(0) for _ in range(k)]
     query_ref, lse_ref, start_ref, expanded_ref, key_lift_t_ref = take(5)
     seg_refs = take(count)
-    if first or last:
-        grad_ref, mix_ref = take(2)
     if first:
-        (value_lift_ref,) = take(1)
+        grad_mine, grad_got, mix_ref, value_lift_ref = take(4)
     else:
         expanded_grad_ref, delta_ref, query_back_in, key_up_in = take(4)
     grad_refs = take(count)
     query_back_ref, key_up_ref = take(2)
-    if last:
-        (value_up_ref,) = take(1)
     if first:
-        expanded_grad_ref, delta_ref = take(2)
+        expanded_grad_ref, delta_ref, value_up_ref = take(3)
     back, query_back, segs, seg_grads = take(4)
     expanded, expanded_grad = expanded_ref.at[0], expanded_grad_ref.at[0]
     tokens = query_ref.shape[1]
@@ -227,14 +223,16 @@
     @pl.when(row == 0)
     def _():
         key_up_ref[...] = jnp.zeros_like(key_up_ref) if first else key_up_in[...]
-        if last:
+        if first:
             value_up_ref[...] = jnp.zeros_like(value_up_ref)
 
     query_back[...] = jnp.zeros_like(query_back) if first else query_back_in[0]
     seg_grads[...] = jnp.zeros_like(seg_grads)
     if first:
-        expand_heads(grad_ref[0], value_lift_ref, 1.0, expanded_grad)
+        grads = jnp.where(row < pl.num_programs(0) // 2, grad_mine[0], grad_got[0])
+        expand_heads(grads, value_lift_ref, 1.0, expanded_grad)
         delta_ref[0] = jnp.sum(mix_ref[0].astype(f32) * expanded_grad[...].astype(f32), axis=0, keepdims=True)
+        lift_grad(mix_ref[0], grads, tokens, value_up_ref)
 
     @pl.when(any_touched)
     def _():
@@ -268,7 +266,6 @@
         lift_grad(part, query_ref[0], tokens, key_up_ref)
 
     if last:
-        lift_grad(mix_ref[0], grad_ref[0], tokens, value_up_ref)
         query_back_ref[0] = query_back[...].T.astype(bf16)
     else:
         query_back_ref[0] = query_back[...]
@@ -285,24 +282,21 @@
     args = [queries, lse, start, expanded, key_lift_t, *segs]
     specs = [by_row(a.shape) for a in args[:4]] + [whole(key_lift_t)]
     specs += [by_row(s.shape) for s in segs]
-    if first or last:
-        args += [grads, mix]
-        specs += [by_row(grads.shape), by_row(mix.shape)]
     if first:
-        args.append(value_lift)
-        specs.append(whole(value_lift))
+        args += [*grads, mix, value_lift]
+        half = (1, tokens, width)
+        specs.append(pl.BlockSpec(half, lambda r, *_: (jnp.minimum(r, rows // 2 - 1), 0, 0)))
+        specs.append(pl.BlockSpec(half, lambda r, *_: (jnp.maximum(r - rows // 2, 0), 0, 0)))
+        specs += [by_row(mix.shape), whole(value_lift)]
     else:
         args += [*kept, *state]
         specs += [by_row(kept[0].shape), by_row(kept[1].shape), by_row(back_shape.shape), whole(up_shape)]
     outs = [shape(s.shape, bf16) for s in segs]
     outs += [shape(queries.shape, bf16) if last else back_shape, up_shape]
     out_specs = [by_row(o.shape) for o in outs[:-1]] + [whole(up_shape)]
-    if last:
-        outs.append(up_shape)
-        out_specs.append(whole(up_shape))
     if first:
-        outs += [shape(expanded.shape, bf16), shape(lse.shape, f32)]
-        out_specs += [by_row(expanded.shape), by_row(lse.shape)]
+        outs += [shape(expanded.shape, bf16), shape(lse.shape, f32), up_shape]
+        out_specs += [by_row(expanded.shape), by_row(lse.shape), whole(up_shape)]
     blocks = rows * heads * len(segs)
     return pl.pallas_call(
         functools.partial(attend_back_kernel, len(segs), first, last),
@@ -356,10 +350,14 @@
     (
         inputs_ref, mine_ref, got_ref, output_ref, gain_ref, cotangent_ref, keep_ref,
         gate_ref, up_ref, down_ref,
-        hidden_out_ref, resid, normed, back, active_ref, slope_ref, down_grad_ref,
-        result, hidden,
+        hidden_out_ref, resid_out, normed_out, back_out, active_ref, slope_ref, down_grad_ref,
+        result, hidden, resid, normed, back, sems,
     ) = refs
     step = pl.program_id(0)
+    leaving = [
+        pltpu.make_async_copy(source, target, sems.at[i])
+        for i, (source, target) in enumerate(((resid, resid_out), (normed, normed_out), (back, back_out)))
+    ]
     count = inputs_ref.shape[0]
     block = min(256, count)
     core = core_ref[0]
@@ -375,6 +373,8 @@
             scale = lax.rsqrt(jnp.mean(row * row, axis=-1, keepdims=True) + epsilon)
             normed[at] = (row * scale * gain_ref[...]).astype(bf16)
             back[at] = (cotangent_ref[at].astype(f32) * keep_ref[at]).astype(bf16)
+        for copy in leaving:
+            copy.start()
         result[...] = jnp.zeros_like(result)
 
     part = count // 4
@@ -393,18 +393,27 @@
     @pl.when(step == pl.num_programs(0) - 1)
     def _():
         hidden_out_ref[...] = (resid[...] + result[...]).astype(bf16)
+        for copy in leaving:
+            copy.wait()
 
 
 def feed_back_kernel(core_ref, *refs):
     (
-        mine_ref, got_ref, output_ref, gain_ref, resid_ref, normed, back,
+        mine_in, got_in, output_in, resid_in, gain_ref, normed, back,
         active_ref, slope_ref, gate_ref, up_ref, down_ref,
-        grad_resid_ref, head_mine_ref, head_sent_ref, gain_grad_ref, grads_ref,
-        grad_two, both, low, staged, staged_out, sems, out_sem,
+        grad_resid_out, head_mine_out, head_sent_out, gain_grad_ref, grads_ref,
+        grad_two, both, low, staged, staged_out, mine_ref, got_ref, output_ref, resid_ref, head_mine_ref, head_sent_ref,
+        sems, out_sem, in_sems, leave_sems,
     ) = refs
     step = pl.program_id(0)
     steps = pl.num_programs(0)
     count, width = resid_ref.shape
+    coming = [
+        pltpu.make_async_copy(source, target, in_sems.at[i])
+        for i, (source, target) in enumerate(
+            ((mine_in, mine_ref), (got_in, got_ref), (output_in, output_ref), (resid_in, resid_ref))
+        )
+    ]
     chunk = down_ref.shape[0]
     ff = (grads_ref.shape[1] - width) // 2
     block = min(256, count)
@@ -425,6 +434,8 @@
 
     @pl.when(step == 0)
     def _():
+        for copy in coming:
+            copy.start()
         grad_two[...] = jnp.zeros_like(grad_two)
 
     part = count // 4
@@ -443,7 +454,10 @@
 
     @pl.when(step == steps - 1)
     def _():
+        for copy in coming:
+            copy.wait()
         gain_total = jnp.zeros((1, width), f32)
+        leaving = []
         for t in range(0, count, block):
             at = slice(t, t + block)
             row = resid_ref[at]
@@ -455,10 +469,17 @@
             grad = back[at].astype(f32) + scale * (
                 scaled - unit * jnp.mean(scaled * unit, axis=-1, keepdims=True)
             )
-            grad_resid_ref[at] = grad
+            grad_two[at] = grad
             low[at] = grad.astype(bf16)
             head_mine_ref[at] = matmul_nt(low[at], output_ref[core]).astype(bf16)
             head_sent_ref[at] = matmul_nt(low[at], output_ref[1 - core]).astype(bf16)
+            for i, (source, target) in enumerate(
+                ((grad_two, grad_resid_out), (head_mine_ref, head_mine_out), (head_sent_ref, head_sent_out))
+            ):
+                rows = pl.ds(t, block)
+                copy = pltpu.make_async_copy(source.at[rows], target.at[rows], leave_sems.at[t // block, i])
+                copy.start()
+                leaving.append(copy)
         gain_grad_ref[...] = gain_total
         half = mine_ref.shape[1]
         put_pieces(staged_out, matmul_tn(mine_ref[...], low[...]), core * half)
@@ -469,6 +490,8 @@
             leave(1 - slot, kind, step - 1).wait()
             leave(slot, kind, step).wait()
         last.wait()
+        for copy in leaving:
+            copy.wait()
 
 
 def once(array):
@@ -499,9 +522,17 @@
             num_scalar_prefetch=1,
             grid=(ff // chunk,),
             in_specs=[once(a) for a in firsts] + [by_columns, by_columns, by_rows],
-            out_specs=[once(o) for o in outs[:4]]
+            out_specs=[once(outs[0])]
+            + [pl.BlockSpec(memory_space=pl.ANY)] * 3
             + [kept_columns, kept_columns, pl.BlockSpec((pieces, chunk, piece), lambda c, *_: (0, c, 0))],
-            scratch_shapes=[pltpu.VMEM((count, width), f32), pltpu.VMEM((count, chunk), bf16)],
+            scratch_shapes=[
+                pltpu.VMEM((count, width), f32),
+                pltpu.VMEM((count, chunk), bf16),
+                pltpu.VMEM((count, width), f32),
+                pltpu.VMEM((count, width), bf16),
+                pltpu.VMEM((count, width), bf16),
+                pltpu.SemaphoreType.DMA((3,)),
+            ],
         ),
         compiler_params=params,
         cost_estimate=pl.CostEstimate(
@@ -511,7 +542,8 @@
         ),
         name="feed",
     )(core.reshape(1), *firsts, *weights)
-    firsts = [mixed_mine, mixed_got, output_weight, gain, resid, normed, back]
+    firsts = [mixed_mine, mixed_got, output_weight, resid, gain, normed, back]
+    anywhere = pl.BlockSpec(memory_space=pl.ANY)
     outs = [
         full_f,
         shape(mixed_mine.shape, bf16),
@@ -525,17 +557,26 @@
         grid_spec=pltpu.PrefetchScalarGridSpec(
             num_scalar_prefetch=1,
             grid=(ff // chunk,),
-            in_specs=[once(a) for a in firsts]
+            in_specs=[anywhere] * 4
+            + [once(a) for a in firsts[4:]]
             + [kept_columns, kept_columns, by_columns, by_columns, by_rows],
-            out_specs=[once(o) for o in outs[:4]] + [pl.BlockSpec(memory_space=pl.ANY)],
+            out_specs=[anywhere] * 3 + [once(outs[3]), anywhere],
             scratch_shapes=[
                 pltpu.VMEM((count, width), f32),
                 pltpu.VMEM((count, 2 * chunk), bf16),
                 pltpu.VMEM((count, width), bf16),
                 pltpu.VMEM((2, 2, pieces, chunk, piece), bf16),
                 pltpu.VMEM((pieces, width, piece), bf16),
+                pltpu.VMEM(mixed_mine.shape, bf16),
+                pltpu.VMEM(mixed_mine.shape, bf16),
+                pltpu.VMEM(output_weight.shape, bf16),
+                pltpu.VMEM((count, width), f32),
+                pltpu.VMEM(mixed_mine.shape, bf16),
+                pltpu.VMEM(mixed_mine.shape, bf16),
                 pltpu.SemaphoreType.DMA((2, 2)),
                 pltpu.SemaphoreType.DMA,
+                pltpu.SemaphoreType.DMA((4,)),
+                pltpu.SemaphoreType.DMA((max(1, count // 256), 3)),
             ],
         ),
         compiler_params=params,
@@ -957,7 +998,12 @@
     )(*early, *late_args)
 
 
-def lay_out_kernel(rows, latent, full_ref, gate_ref, up_ref, output_ref, down_ref, query_ref, latent_ref, key_ref, value_ref, gains_ref):
+def lay_out_kernel(
+    rows, latent, full_ref, grad_in, gate_ref, up_ref, output_ref, down_ref, query_ref, latent_ref, key_ref, value_ref,
+    gains_ref, grad_out, sem,
+):
+    copy = pltpu.make_async_copy(grad_in, grad_out, sem)
+    copy.start()
     pieces, _, piece = full_ref.shape
     at = 0
     for ref, size in zip((gate_ref, up_ref, output_ref, down_ref), rows):
@@ -987,9 +1033,10 @@
         row += fold
         if x == 0:
             gains_ref[core : core + 1] = full_ref[j, row : row + 16, :lane].astype(f32)[:1]
-
-
-def lay_out(full, rows, share, latent, half, count, width):
+    copy.wait()
+
+
+def lay_out(full, grad, rows, share, latent, half, count, width):
     shape = jax.ShapeDtypeStruct
     gate, up, output, down = rows
     lift = latent // count
@@ -1004,15 +1051,18 @@
         shape((2, lift, half), f32),
         shape((2, lift, half), f32),
         shape((2, max(share, 128)), f32),
+        shape(grad.shape, f32),
     ]
+    anywhere = pl.BlockSpec(memory_space=pl.ANY)
     return pl.pallas_call(
         functools.partial(lay_out_kernel, rows, latent),
         out_shape=outs,
-        in_specs=[vmem],
-        out_specs=[vmem] * len(outs),
+        in_specs=[vmem] * 2,
+        out_specs=[vmem] * (len(outs) - 1) + [anywhere],
+        scratch_shapes=[pltpu.SemaphoreType.DMA],
         compiler_params=pltpu.CompilerParams(vmem_limit_bytes=48 << 20),
         name="lay_out",
-    )(full)
+    )(full, grad)
 
 
 def shards(
@@ -1100,7 +1150,7 @@
             jnp.stack([bases[k][j] for k, j in items] + [own_base]).astype(jnp.int32),
         )
 
-    parts = [range(0, steps - 1), range(steps - 1, steps)]
+    parts = [p for p in (range(0, 2), range(2, steps - 1), range(steps - 1, steps)) if len(p) > 0]
     state = expanded = None
     for i, ks in enumerate(parts):
         seg_list, base_list = pick([(k, j) for k in ks for j in range(2)])
@@ -1118,9 +1168,7 @@
         core, hidden_in.reshape(count, width), mixed_mine, mixed_got, output_weight, ffn_gain,
         cotangent.reshape(count, width), keep, (gate_weight, up_weight, down_weight), pieces,
     )
-    head_grads = jnp.concatenate([grad_mixed_mine, swap(grad_mixed_sent)], axis=0).reshape(
-        2 * rows, tokens, group_width
-    )
+    head_grads = [a.reshape(rows, tokens, group_width) for a in (grad_mixed_mine, swap(grad_mixed_sent))]
     early_down = lax.psum_scatter(down_grad, "rows", scatter_dimension=0, tiled=True)[0]
     early_feed = lax.psum_scatter(feed_grads, "rows", scatter_dimension=0, tiled=True)[0]
 
@@ -1150,7 +1198,7 @@
         )
         state = made[len(items) : len(items) + 2]
         if i == 0:
-            kept = made[len(items) + 2 :]
+            *kept, value_part = made[len(items) + 2 :]
         k = items[0][0]
         if k == 0:
             pieces_in.append(made[0])
@@ -1159,7 +1207,7 @@
         if k == 1:
             pieces_in.append(flip(made[2], "heads", 0))
     joined = join(waiting.pop())
-    query_grads, key_part, value_part = made[1:]
+    query_grads, key_part = made[1:]
     latent_grads = sum(p.astype(f32) for p in pieces_in)
 
     ff_share = gate_weight.shape[1] // peers
@@ -1176,7 +1224,8 @@
     )
     (
         gate_share, up_share, output_share, down_share, query_share, latent_share, key_share, value_share, gains,
-    ) = lay_out(full, (ff_share, ff_share, share, ff_share), share, latent_size, group_width, peers, width)
+        hidden_grad,
+    ) = lay_out(full, hidden_grad, (ff_share, ff_share, share, ff_share), share, latent_size, group_width, peers, width)
     gains = lax.dynamic_slice_in_dim(gains, (place * share) % gains.shape[1], share, 1)
     return (
         hidden_out.reshape(rows, tokens, width),

time: 518 us -> 497 us (0.959); the launches traced: 516 us -> 489 us
  waiting for transfers between devices: 91.9 us -> 60.2 us
    ppermute x13, waiting for transfers between devices: 65.5 us -> 47.4 us  [flip(): return lax.ppermute(array, axis, [(i, i ^ 1 << bit) for i in range(size)])]
    reduce_scatter x1, waiting for transfers between devices: 14.6 us -> 2.34 us  [shards(): lax.psum_scatter(feed_grads, 'rows', scatter_dimension=0, tiled=True)[0]]
    pallas_call x2 -> x3, Pallas kernels: 30.5 us -> 42.3 us  [attend_part(): pl.pallas_call(functools.partial(attend_kernel, len(segs), state is None,...]
    pallas_call x1, Pallas kernels: 132 us -> 120 us  [finish(): pl.pallas_call(body, out_shape=[jax.ShapeDtypeStruct((2 * along, total, p...]
  transfers between devices with their start and end apart: 20 -> 20, of which waited for: 13 -> 11; matrix products, arithmetic and copies ran while one was open for 6% -> 7% of each run, Pallas kernels for 26% -> 30%
where the time goes in v6:
time: 497 us; the launch traced here: 489 us
  Pallas kernels  323 us (65%)
  waiting for transfers between devices  60.2 us (12%)
  starting transfers between devices  46.5 us (9%)
  local copies, waits for them, and re-layouts  18.7 us (4%)
  other arithmetic  15.1 us (3%)
  between operations  14.6 us (3%)
  matrix products  11.2 us (2%)
    pallas_call x1, Pallas kernels, finish(): pl.pallas_call(body, out_shape=[jax.ShapeDtypeStruct((2 * along, total, p...  120 us
    pallas_call x4, Pallas kernels, attend_back_part(): pl.pallas_call(functools.partial(attend_back_kernel, len(segs), first, la...  69.3 us
    ppermute x13, waiting for transfers between devices, flip(): return lax.ppermute(array, axis, [(i, i ^ 1 << bit) for i in range(size)])  47.4 us
    pallas_call x1, Pallas kernels, feed(): pl.pallas_call(feed_back_kernel, out_shape=outs, grid_spec=pltpu.Prefetch...  45.6 us
    pallas_call x3, Pallas kernels, attend_part(): pl.pallas_call(functools.partial(attend_kernel, len(segs), state is None,...  42.3 us
    pallas_call x1, Pallas kernels, feed(): pl.pallas_call(feed_kernel, out_shape=outs, grid_spec=pltpu.PrefetchScala...  38.4 us
    ppermute x13, starting transfers between devices, flip(): return lax.ppermute(array, axis, [(i, i ^ 1 << bit) for i in range(size)])  29.1 us
    ppermute x3, starting transfers between devices, shards(): moving = lax.ppermute(moving, 'heads', up_chain)  14.5 us
  transfers between devices with their start and end apart: 20, of which 11 were waited for; matrix products, arithmetic and copies ran while one was open for 7% of the time, Pallas kernels for 30%

profile of v6, /device:TPU:0, one launch (start us, length us, event | category | flops | bytes accessed | tf_op | source)
XLA Modules:
  0.0 489.0 jit_solution(251770562935311492)
XLA Ops:
  7.3 2.2 multiply_reduce_fusion
  9.5 0.5 multiply_convert_fusion
  10.1 0.7 copy-done.10
  10.7 0.7 convolution_convert_fusion.2
  11.5 0.6 copy-done.9
  12.1 0.5 collective-permute-start.2
  12.5 2.3 convolution_convert_fusion.3
  14.8 0.6 convert_bitcast_fusion
  15.9 2.6 collective-permute-start.4
  18.5 3.5 collective-permute-start.3
  22.0 1.6 convert_reduce_fusion
  23.7 4.1 convolution_convert_fusion
  27.8 0.5 collective-permute-start.1
  28.3 14.0 %collective-permute-done.4.refs_4_.refs_7_ = bf16[8,256,256]{2,1,0:T(8,128)(2,1)S(1)} collective-permute-done((bf16[8,256,256]{2,1,0:T(8,128)(2,1)S(1)}, bf16[8,256,256]{2,1,0:T(8,128)(2,1)S(1)}, u32[]{:S(2)}, u32[]{:S(2)}) %collective-permute-start.4) | collective-permute-done | bytes 1048608 | tf_op jit(solution)/shard_map/ppermute | solution.py:595
  42.3 2.4 collective-permute-done.3.refs_5_
  44.7 0.5 collective-permute-start.6
  45.3 5.3 %collective-permute-start.5 = (bf16[8,256,256]{2,1,0:T(8,128)(2,1)S(1)}, bf16[8,256,256]{2,1,0:T(8,128)(2,1)}, u32[]{:S(2)}, u32[]{:S(2)}) collective-permute-start(bf16[8,256,256]{2,1,0:T(8,128)(2,1)S(1)} %collective-permute-done.3.refs_5_), channel_id=1, source_target_pairs={{0,2},{1,3},{2,4},{3,5},{4,6},{5,7},{8,10},{9,11},{10,12},{11,13},... | collective-permute-start | bytes 3145736 | tf_op jit(solution)/shard_map/ppermute | solution.py:1136
  50.7 1.9 constant_dynamic-slice_fusion
  52.5 4.1 convolution_convert_fusion.1
  56.6 1.1 copy.42
  57.7 1.8 copy.39
  59.5 1.8 copy.35
  61.3 0.8 copy.34
  62.1 1.8 copy.40
  64.0 2.8 fusion
  67.0 2.7 pad_maximum_fusion
  69.7 1.6 collective-permute-done.5.refs_5_
  71.3 1.5 collective-permute-start.8
  72.8 5.6 %collective-permute-start.7 = (bf16[8,256,256]{2,1,0:T(8,128)(2,1)}, bf16[8,256,256]{2,1,0:T(8,128)(2,1)}, u32[]{:S(2)}, u32[]{:S(2)}) collective-permute-start(bf16[8,256,256]{2,1,0:T(8,128)(2,1)} %collective-permute-done.5.refs_5_), channel_id=1, source_target_pairs={{0,2},{1,3},{2,4},{3,5},{4,6},{5,7},{8,10},{9,11},{10,12},{11,13},... | collective-permute-start | bytes 3145736 | tf_op jit(solution)/shard_map/ppermute | solution.py:1136
  78.5 17.8 %attend.3 = (f32[8,1,2048]{2,1,0:T(1,128)S(1)}, f32[8,1,2048]{2,1,0:T(1,128)S(1)}, bf16[8,256,2048]{2,1,0:T(8,128)(2,1)}, bf16[8,256,2048]{2,1,0:T(8,128)(2,1)}) custom-call(s32[8]{0:T(128)S(1)} %fusion.9.lo, s32[5]{0:T(128)S(1)} %stack.66.bases, s32[8,1,256]{2,1,0:T(1,128)S(1)} %broadcast_in_dim.4.refs_0_.refs_2_, bf16[8,256,512]{2,1,0:T(8,128)(2,1)} %bitcast.77, ...), custom_call_target="tpu_custom_call" | custom-call | flops 274877906944 | bytes 268435456 | tf_op jit(solution)/shard_map/attend/pallas_call | solution.py:174
  96.2 1.9 collective-permute-done.7.refs_5_
  98.1 7.2 %collective-permute-start.9 = (bf16[8,256,256]{2,1,0:T(8,128)(2,1)}, bf16[8,256,256]{2,1,0:T(8,128)(2,1)S(1)}, u32[]{:S(2)}, u32[]{:S(2)}) collective-permute-start(bf16[8,256,256]{2,1,0:T(8,128)(2,1)} %collective-permute-done.7.refs_5_), channel_id=1, source_target_pairs={{0,1},{1,0},{2,3},{3,2},{4,5},{5,4},{6,7},{7,6},{8,9},{9,8},{10,11... | collective-permute-start | bytes 3145736 | tf_op jit(solution)/shard_map/ppermute | solution.py:595
  105.3 12.3 %attend.4 = (f32[8,1,2048]{2,1,0:T(1,128)S(1)}, f32[8,1,2048]{2,1,0:T(1,128)S(1)}, bf16[8,256,2048]{2,1,0:T(8,128)(2,1)}) custom-call(s32[8]{0:T(128)S(1)} %fusion.9.lo, s32[3]{0:T(128)S(1)} %get-tuple-element.149.bases, s32[8,1,256]{2,1,0:T(1,128)S(1)} %broadcast_in_dim.4.refs_0_.refs_2_, bf16[8,256,2048]{2,1,0:T(8,128)(2,1)} %get-tuple-element.78.refs_1_.refs_3_, ...), custom_call_target="tpu_custom_call" | custom-call | flops 137438953472 | bytes 268435456 | tf_op jit(solution)/shard_map/attend/pallas_call | solution.py:174
  117.6 8.9 %collective-permute-done.9.refs_6_ = bf16[8,256,256]{2,1,0:T(8,128)(2,1)S(1)} collective-permute-done((bf16[8,256,256]{2,1,0:T(8,128)(2,1)}, bf16[8,256,256]{2,1,0:T(8,128)(2,1)S(1)}, u32[]{:S(2)}, u32[]{:S(2)}) %collective-permute-start.9) | collective-permute-done | bytes 1048608 | tf_op jit(solution)/shard_map/ppermute | solution.py:595
  126.5 12.3 %attend.5 = (bf16[8,256,512]{2,1,0:T(8,128)(2,1)S(1)}, f32[8,1,2048]{2,1,0:T(1,128)S(1)}, bf16[8,256,2048]{2,1,0:T(8,128)(2,1)}) custom-call(s32[8]{0:T(128)S(1)} %fusion.9.lo, s32[3]{0:T(128)S(1)} %get-tuple-element.148.bases, s32[8,1,256]{2,1,0:T(1,128)S(1)} %broadcast_in_dim.4.refs_0_.refs_2_, bf16[8,256,2048]{2,1,0:T(8,128)(2,1)} %get-tuple-element.78.refs_1_.refs_3_, ...), custom_call_target="tpu_custom_call" | custom-call | flops 137438953472 | bytes 268435456 | tf_op jit(solution)/shard_map/attend/pallas_call | solution.py:174
  138.8 1.4 fusion.15
  140.2 1.0 copy.45
  141.3 2.0 collective-permute-done.10
  143.2 38.4 %feed.1 = (bf16[1024,1024]{1,0:T(8,128)(2,1)}, f32[1024,1024]{1,0:T(8,128)}, bf16[1024,1024]{1,0:T(8,128)(2,1)}, bf16[1024,1024]{1,0:T(8,128)(2,1)}, bf16[1024,2...) custom-call(s32[1]{0:T(128)} %bitcast.core_ref, bf16[1024,1024]{1,0:T(8,128)(2,1)} %bitcast.82, ...), custom_call_target="tpu_custom_call" | custom-call | flops 25769803776 | bytes 51380224 | tf_op jit(solution)/shard_map/feed/pallas_call | solution.py:518
  182.0 45.6 %feed_back.1 = (f32[1024,1024]{1,0:T(8,128)}, bf16[1024,512]{1,0:T(8,128)(2,1)}, bf16[1024,512]{1,0:T(8,128)(2,1)}, f32[1,1024]{1,0:T(1,128)}, bf16[4,6656,256]{2,1,0:T(8,128)(2,1)}) custom-call(s32[1]{0:T(128)} %bitcast.core_ref, bf16[1024,512]{1,0:T(8,128)(2,1)} %bitcast.93, bf16[1024,512]{1,0:T(8,128)(2,1)} %bitcast.20.refs_2_.refs_1_, ...), custom_call_target="tpu_custom_call" | custom-call | flops 33822867456 | bytes 61341696 | tf_op jit(solution)/shard_map/feed_back/pallas_call | solution.py:554
  227.8 2.7 collective-permute-done.11
  230.5 1.0 copy-done.11
  231.5 1.2 copy-done.4
  232.7 17.2 %attend_back.4 = (bf16[8,256,256]{2,1,0:T(8,128)(2,1)S(1)}, bf16[8,256,256]{2,1,0:T(8,128)(2,1)S(1)}, f32[8,512,256]{2,1,0:T(8,128)}, f32[256,512]{1,0:T(8,128)S...) custom-call(s32[8]{0:T(128)S(1)} %fusion.9.lo, ...), custom_call_target="tpu_custom_call" | custom-call | flops 2147483648 | bytes 4194304 | tf_op jit(solution)/shard_map/attend_back/pallas_call | solution.py:301
  249.9 0.8 copy-done.5
  250.7 1.8 collective-permute-start.13
  252.4 16.5 %attend_back.5 = (bf16[8,256,256]{2,1,0:T(8,128)(2,1)S(1)}, bf16[8,256,256]{2,1,0:T(8,128)(2,1)S(1)}, f32[8,512,256]{2,1,0:T(8,128)}, f32[256,512]{1,0:T(8,128)S(1)}) custom-call(s32[8]{0:T(128)S(1)} %fusion.9.lo, s32[3]{0:T(128)S(1)} %get-tuple-element.149.bases, bf16[8,256,512]{2,1,0:T(8,128)(2,1)} %bitcast.79, ...), custom_call_target="tpu_custom_call" | custom-call | flops 2147483648 | bytes 4194304 | tf_op jit(solution)/shard_map/attend_back/pallas_call | solution.py:301
  268.9 0.5 collective-permute-start.12
  269.4 7.3 %collective-permute-done.13 = bf16[8,256,256]{2,1,0:T(8,128)(2,1)S(1)} collective-permute-done((bf16[8,256,256]{2,1,0:T(8,128)(2,1)S(1)}, bf16[8,256,256]{2,1,0:T(8,128)(2,1)S(1)}, u32[]{:S(2)}, u32[]{:S(2)}) %collective-permute-start.13) | collective-permute-done | bytes 1048608 | tf_op jit(solution)/shard_map/ppermute | solution.py:595
  276.9 1.3 collective-permute-start.14
  278.3 12.2 %attend_back.6 = (bf16[8,256,256]{2,1,0:T(8,128)(2,1)S(1)}, bf16[8,256,256]{2,1,0:T(8,128)(2,1)S(1)}, bf16[8,256,256]{2,1,0:T(8,128)(2,1)S(1)}, f32[8,512,256]{2,1,0:T(8,128)}, f32[256,512]{1,0:T(8,128)S(1)}) custom-call(s32[8]{0:T(128)S(1)} %fusion.9.lo, s32[4]{0:T(128)S(1)} %pad_add_fusion.2.bases, bf16[8,256,512]{2,1,0:T(8,128)(2,1)} %bitcast.80, ...), custom_call_target="tpu_custom_call" | custom-call | flops 3221225472 | bytes 4194304 | tf_op jit(solution)/shard_map/attend_back/pallas_call | solution.py:301
  290.5 13.8 %collective-permute-start.15 = (bf16[8,256,256]{2,1,0:T(8,128)(2,1)S(1)}, bf16[8,256,256]{2,1,0:T(8,128)(2,1)S(1)}, u32[]{:S(2)}, u32[]{:S(2)}) collective-permute-start(bf16[8,256,256]{2,1,0:T(8,128)(2,1)S(1)} %get-tuple-element.117), channel_id=1, source_target_pairs={{0,1},{1,0},{2,3},{3,2},{4,5},{5,4},{6,7},{7,6},{8,9},{9,8},{10,11... | collective-permute-start | bytes 3145736 | tf_op jit(solution)/shard_map/ppermute | solution.py:595
  304.3 4.4 collective-permute-done.14
  308.8 0.4 add_convert_fusion.1
  309.2 1.3 collective-permute-start.17
  310.6 23.5 %attend_back.7 = (bf16[8,256,256]{2,1,0:T(8,128)(2,1)S(1)}, bf16[8,256,512]{2,1,0:T(8,128)(2,1)S(1)}, f32[256,512]{1,0:T(8,128)S(1)}) custom-call(s32[8]{0:T(128)S(1)} %fusion.9.lo, s32[2]{0:T(128)S(1)} %pad_add_fusion.1.bases, bf16[8,256,512]{2,1,0:T(8,128)(2,1)} %bitcast.81, f32[8,1,2048]{2,1,0:T(1,128)S(1)} %get-tuple-element.97.refs_1_, ...), custom_call_target="tpu_custom_call" | custom-call | flops 1073741824 | bytes 4194304 | tf_op jit(solution)/shard_map/attend_back/pallas_call | solution.py:301
  334.1 1.8 convert_add_fusion
  336.3 12.5 %collective-permute-done.16 = bf16[8,256,256]{2,1,0:T(8,128)(2,1)S(1)} collective-permute-done((bf16[8,256,256]{2,1,0:T(8,128)(2,1)S(1)}, bf16[8,256,256]{2,1,0:T(8,128)(2,1)S(1)}, u32[]{:S(2)}, u32[]{:S(2)}) %collective-permute-start.16) | collective-permute-done | bytes 1048608 | tf_op jit(solution)/shard_map/ppermute | solution.py:595
  348.8 1.4 add_convert_fusion
  350.2 2.3 reduce-scatter.3.cloned.1.call-done
  352.5 120.3 %finish.1 = (bf16[4,1456,256]{2,1,0:T(8,128)(2,1)}, f32[1024,1024]{1,0:T(8,128)}) custom-call(bf16[6656,256]{1,0:T(8,128)(2,1)} %bitcast.86, bf16[2816,256]{1,0:T(8,128)(2,1)} %bitcast.88, bf16[1024,1024]{1,0:T(8,128)(2,1)} %bitcast.83, f32[1,1024]{1,0:T(1,128)} %bitcast.96, bf16[2,1024,512]{2,1,0:T(8,128)(2,1)} %bitcast.75, f32[2,1024,256]{2,1,0:T(8,128)} %bitcast.84, ...), custom_call_target="tpu_custom_call" | custom-call | tf_op jit(solution)/shard_map/finish/pallas_call | solution.py:964
  472.8 1.8 copy-done
  474.7 6.7 %lay_out.1 = (f32[352,1024]{1,0:T(8,128)}, f32[352,1024]{1,0:T(8,128)}, f32[128,1024]{1,0:T(8,128)}, f32[352,1024]{1,0:T(8,128)}, f32[128,1024]{1,0:T(8,128)}, /...) custom-call(bf16[4,1456,256]{2,1,0:T(8,128)(2,1)S(1)} %copy-done, ...), custom_call_target="tpu_custom_call" | custom-call | tf_op jit(solution)/shard_map/lay_out/pallas_call | solution.py:1057
  481.4 0.5 slice_bitcast_fusion
  (62 shorter events, 2.3 us)
Async XLA Ops:
  7.2 2.3 copy-start.8
  7.2 2.3 copy-start.15
  7.2 343.0 %reduce-scatter.5.cloned.1.call-start = ((), (), s32[]{:S(2)}) async-start(), calls=%async_computation.3 | async-start | bytes 7208960 | tf_op jit(solution)/shard_map/reduce_scatter | solution.py:1172
  9.5 1.2 copy-start.10
  10.7 1.3 copy-start.9
  12.1 3.8 collective-permute-start.2
  12.5 2.3 copy-start.13
  15.9 26.4 %collective-permute-start.4 = (bf16[8,256,256]{2,1,0:T(8,128)(2,1)S(1)}, bf16[8,256,256]{2,1,0:T(8,128)(2,1)S(1)}, u32[]{:S(2)}, u32[]{:S(2)}) collective-permute-start(bf16[8,256,256]{2,1,0:T(8,128)(2,1)S(1)} %bitcast.71), channel_id=1, source_target_pairs={{0,1},{1,0},{2,3},{3,2},{4,5},{5,4},{6,7},{7,6},{8,9},{9,8},{10,11... | collective-permute-start | bytes 3145736 | tf_op jit(solution)/shard_map/ppermute | solution.py:595
  18.5 26.3 %collective-permute-start.3 = (bf16[8,256,256]{2,1,0:T(8,128)(2,1)S(1)}, bf16[8,256,256]{2,1,0:T(8,128)(2,1)S(1)}, u32[]{:S(2)}, u32[]{:S(2)}) collective-permute-start(bf16[8,256,256]{2,1,0:T(8,128)(2,1)S(1)} %bitcast.72), channel_id=1, source_target_pairs={{0,2},{1,3},{2,4},{3,5},{4,6},{5,7},{8,10},{9,11},{10,12},{11,13},... | collective-permute-start | bytes 3145736 | tf_op jit(solution)/shard_map/ppermute | solution.py:1136
  23.6 43.2 %collective-permute-start = (s32[4,256]{1,0:T(4,128)S(1)}, s32[4,256]{1,0:T(4,128)S(1)}, u32[]{:S(2)}, u32[]{:S(2)}) collective-permute-start(s32[4,256]{1,0:T(4,128)S(1)} %broadcast_subtract_fusion), channel_id=1, source_target_pairs={{0,8},{8,0},{16,24},{24,16},{1,9},{9,1},{17,25},{25,17},{2,10},{10... | collective-permute-start | bytes 12296 | tf_op jit(solution)/shard_map/ppermute | solution.py:595
  27.8 39.2 %collective-permute-start.1 = (bf16[1024,512]{1,0:T(8,128)(2,1)}, bf16[1024,512]{1,0:T(8,128)(2,1)}, u32[]{:S(2)}, u32[]{:S(2)}) collective-permute-start(bf16[1024,512]{1,0:T(8,128)(2,1)} %convolution_convert_fusion), channel_id=1, source_target_pairs={{0,8},{8,0},{16,24},{24,16},{1,9},{9,1},{17,25},{25,17},{2,10},{10... | collective-permute-start | bytes 3145736 | tf_op jit(solution)/shard_map/ppermute | solution.py:595
  42.3 36.1 %copy-start.2 = (bf16[8,256,256]{2,1,0:T(8,128)(2,1)}, bf16[8,256,256]{2,1,0:T(8,128)(2,1)S(1)}, u32[]{:S(2)}) copy-start(bf16[8,256,256]{2,1,0:T(8,128)(2,1)S(1)} %collective-permute-done.4.refs_4_.refs_7_) | copy-start | bytes 3145732
  44.7 24.9 %collective-permute-start.6 = (bf16[8,256,256]{2,1,0:T(8,128)(2,1)S(1)}, bf16[8,256,256]{2,1,0:T(8,128)(2,1)}, u32[]{:S(2)}, u32[]{:S(2)}) collective-permute-start(bf16[8,256,256]{2,1,0:T(8,128)(2,1)S(1)} %collective-permute-done.3.refs_5_), channel_id=1, source_target_pairs={{0,1},{1,0},{2,3},{3,2},{4,5},{5,4},{6,7},{7,6},{8,9},{9,8},{10,11... | collective-permute-start | bytes 3145736 | tf_op jit(solution)/shard_map/ppermute | solution.py:595
  45.3 26.1 %collective-permute-start.5 = (bf16[8,256,256]{2,1,0:T(8,128)(2,1)S(1)}, bf16[8,256,256]{2,1,0:T(8,128)(2,1)}, u32[]{:S(2)}, u32[]{:S(2)}) collective-permute-start(bf16[8,256,256]{2,1,0:T(8,128)(2,1)S(1)} %collective-permute-done.3.refs_5_), channel_id=1, source_target_pairs={{0,2},{1,3},{2,4},{3,5},{4,6},{5,7},{8,10},{9,11},{10,12},{11,13},... | collective-permute-start | bytes 3145736 | tf_op jit(solution)/shard_map/ppermute | solution.py:1136
  64.0 3.0 copy-start.12
  71.3 24.9 %collective-permute-start.8 = (bf16[8,256,256]{2,1,0:T(8,128)(2,1)}, bf16[8,256,256]{2,1,0:T(8,128)(2,1)}, u32[]{:S(2)}, u32[]{:S(2)}) collective-permute-start(bf16[8,256,256]{2,1,0:T(8,128)(2,1)} %collective-permute-done.5.refs_5_), channel_id=1, source_target_pairs={{0,1},{1,0},{2,3},{3,2},{4,5},{5,4},{6,7},{7,6},{8,9},{9,8},{10,11... | collective-permute-start | bytes 3145736 | tf_op jit(solution)/shard_map/ppermute | solution.py:595
  72.8 25.3 %collective-permute-start.7 = (bf16[8,256,256]{2,1,0:T(8,128)(2,1)}, bf16[8,256,256]{2,1,0:T(8,128)(2,1)}, u32[]{:S(2)}, u32[]{:S(2)}) collective-permute-start(bf16[8,256,256]{2,1,0:T(8,128)(2,1)} %collective-permute-done.5.refs_5_), channel_id=1, source_target_pairs={{0,2},{1,3},{2,4},{3,5},{4,6},{5,7},{8,10},{9,11},{10,12},{11,13},... | collective-permute-start | bytes 3145736 | tf_op jit(solution)/shard_map/ppermute | solution.py:1136
  98.1 28.4 %collective-permute-start.9 = (bf16[8,256,256]{2,1,0:T(8,128)(2,1)}, bf16[8,256,256]{2,1,0:T(8,128)(2,1)S(1)}, u32[]{:S(2)}, u32[]{:S(2)}) collective-permute-start(bf16[8,256,256]{2,1,0:T(8,128)(2,1)} %collective-permute-done.7.refs_5_), channel_id=1, source_target_pairs={{0,1},{1,0},{2,3},{3,2},{4,5},{5,4},{6,7},{7,6},{8,9},{9,8},{10,11... | collective-permute-start | bytes 3145736 | tf_op jit(solution)/shard_map/ppermute | solution.py:595
  105.3 21.2 %copy-start.7 = (bf16[512,256]{1,0:T(8,128)(2,1)S(1)}, bf16[512,256]{1,0:T(8,128)(2,1)}, u32[]{:S(2)}) copy-start(bf16[512,256]{1,0:T(8,128)(2,1)} %copy.35) | copy-start | bytes 786436
  126.5 12.3 %copy-start.3 = (bf16[8,256,256]{2,1,0:T(8,128)(2,1)}, bf16[8,256,256]{2,1,0:T(8,128)(2,1)S(1)}, u32[]{:S(2)}) copy-start(bf16[8,256,256]{2,1,0:T(8,128)(2,1)S(1)} %collective-permute-done.9.refs_6_) | copy-start | bytes 3145732
  138.8 1.5 copy-start.14
  140.2 3.0 collective-permute-start.10
  181.7 170.8 %reduce-scatter.3.cloned.1.call-start = ((), (), s32[]{:S(2)}) async-start(), calls=%async_computation.2 | async-start | bytes 17039360 | tf_op jit(solution)/shard_map/reduce_scatter | solution.py:1173
  227.6 2.9 collective-permute-start.11
  230.5 1.0 copy-start.11
  231.5 1.2 copy-start.4
  249.9 0.8 copy-start.5
  250.7 26.0 %collective-permute-start.13 = (bf16[8,256,256]{2,1,0:T(8,128)(2,1)S(1)}, bf16[8,256,256]{2,1,0:T(8,128)(2,1)S(1)}, u32[]{:S(2)}, u32[]{:S(2)}) collective-permute-start(bf16[8,256,256]{2,1,0:T(8,128)(2,1)S(1)} %get-tuple-element.108), channel_id=1, source_target_pairs={{0,1},{1,0},{2,3},{3,2},{4,5},{5,4},{6,7},{7,6},{8,9},{9,8},{10,11... | collective-permute-start | bytes 3145736 | tf_op jit(solution)/shard_map/ppermute | solution.py:595
  268.9 35.4 %collective-permute-start.12 = (bf16[8,256,256]{2,1,0:T(8,128)(2,1)S(1)}, bf16[8,256,256]{2,1,0:T(8,128)(2,1)S(1)}, u32[]{:S(2)}, u32[]{:S(2)}) collective-permute-start(bf16[8,256,256]{2,1,0:T(8,128)(2,1)S(1)} %get-tuple-element.106), channel_id=1, source_target_pairs={{0,1},{1,0},{2,3},{3,2},{4,5},{5,4},{6,7},{7,6},{8,9},{9,8},{10,11... | collective-permute-start | bytes 3145736 | tf_op jit(solution)/shard_map/ppermute | solution.py:595
  276.9 31.9 %collective-permute-start.14 = (bf16[8,256,256]{2,1,0:T(8,128)(2,1)S(1)}, bf16[8,256,256]{2,1,0:T(8,128)(2,1)S(1)}, u32[]{:S(2)}, u32[]{:S(2)}) collective-permute-start(bf16[8,256,256]{2,1,0:T(8,128)(2,1)S(1)} %add_convert_fusion.2), channel_id=1, source_target_pairs={{2,0},{3,1},{4,2},{5,3},{6,4},{7,5},{10,8},{11,9},{12,10},{13,11},... | collective-permute-start | bytes 3145736 | tf_op jit(solution)/shard_map/ppermute | solution.py:1193
  290.5 43.7 %collective-permute-start.15 = (bf16[8,256,256]{2,1,0:T(8,128)(2,1)S(1)}, bf16[8,256,256]{2,1,0:T(8,128)(2,1)S(1)}, u32[]{:S(2)}, u32[]{:S(2)}) collective-permute-start(bf16[8,256,256]{2,1,0:T(8,128)(2,1)S(1)} %get-tuple-element.117), channel_id=1, source_target_pairs={{0,1},{1,0},{2,3},{3,2},{4,5},{5,4},{6,7},{7,6},{8,9},{9,8},{10,11... | collective-permute-start | bytes 3145736 | tf_op jit(solution)/shard_map/ppermute | solution.py:595
  304.3 44.5 %collective-permute-start.16 = (bf16[8,256,256]{2,1,0:T(8,128)(2,1)S(1)}, bf16[8,256,256]{2,1,0:T(8,128)(2,1)S(1)}, u32[]{:S(2)}, u32[]{:S(2)}) collective-permute-start(bf16[8,256,256]{2,1,0:T(8,128)(2,1)S(1)} %get-tuple-element.120), channel_id=1, source_target_pairs={{0,1},{1,0},{2,3},{3,2},{4,5},{5,4},{6,7},{7,6},{8,9},{9,8},{10,11... | collective-permute-start | bytes 3145736 | tf_op jit(solution)/shard_map/ppermute | solution.py:595
  309.2 39.6 %collective-permute-start.17 = (bf16[8,256,256]{2,1,0:T(8,128)(2,1)S(1)}, bf16[8,256,256]{2,1,0:T(8,128)(2,1)S(1)}, u32[]{:S(2)}, u32[]{:S(2)}) collective-permute-start(bf16[8,256,256]{2,1,0:T(8,128)(2,1)S(1)} %add_convert_fusion.1), channel_id=1, source_target_pairs={{2,0},{3,1},{4,2},{5,3},{6,4},{7,5},{10,8},{11,9},{12,10},{13,11},... | collective-permute-start | bytes 3145736 | tf_op jit(solution)/shard_map/ppermute | solution.py:1193
  334.1 2.0 copy-start.1
  334.1 2.2 copy-start.6
  472.8 1.8 copy-start
Sparse Core Ops, SparseCore 0:
  181.8 61.8 reduce-scatter.4
  246.5 105.9 reduce-scatter.2
